TPU v7x, 128 devices: a whole 4x4x4 slice. The times are simulated.
128 devices in a mesh: tp: 4 (over x), fsdp: 32 (over z, y, core).
Axes of the slice: x: 4, y: 4, z: 4, core: 2. Of those that a mesh axis runs over, the one named last changes fastest.
Arguments:
- patches: bfloat16 [1024, 49, 3072], P('fsdp')
- labels: int32 [1024], P('fsdp')
- w_stem: float32 [3072, 1024], P('fsdp', 'tp')
- b_stem: float32 [1024], P(('tp', 'fsdp'))
- ln1_g: float32 [2, 1024], P(None, ('tp', 'fsdp'))
- ln1_b: float32 [2, 1024], P(None, ('tp', 'fsdp'))
- w_tok1: float32 [2, 49, 512], P(None, None, 'fsdp')
- b_tok1: float32 [2, 512], P(None, 'fsdp')
- w_tok2: float32 [2, 512, 49], P(None, 'fsdp')
- ln2_g: float32 [2, 1024], P(None, ('tp', 'fsdp'))
- ln2_b: float32 [2, 1024], P(None, ('tp', 'fsdp'))
- w_ch1: float32 [2, 1024, 4096], P(None, 'fsdp', 'tp')
- b_ch1: float32 [2, 4096], P(None, ('tp', 'fsdp'))
- w_ch2: float32 [2, 4096, 1024], P(None, ('tp', 'fsdp'))
- b_ch2: float32 [2, 1024], P(None, ('tp', 'fsdp'))
- lnf_g: float32 [1024], P(('tp', 'fsdp'))
- lnf_b: float32 [1024], P(('tp', 'fsdp'))
- w_head: float32 [1024, 1000], P('fsdp', 'tp')
- b_head: float32 [1000], P('tp')
Outputs:
- output 1: float32 [], replicated
- output 2: float32 [3072, 1024], P('fsdp', 'tp')
- output 3: float32 [1024], P(('tp', 'fsdp'))
- output 4: float32 [2, 1024], P(None, ('tp', 'fsdp'))
- output 5: float32 [2, 1024], P(None, ('tp', 'fsdp'))
- output 6: float32 [2, 49, 512], P(None, None, 'fsdp')
- output 7: float32 [2, 512], P(None, 'fsdp')
- output 8: float32 [2, 512, 49], P(None, 'fsdp')
- output 9: float32 [2, 1024], P(None, ('tp', 'fsdp'))
- output 10: float32 [2, 1024], P(None, ('tp', 'fsdp'))
- output 11: float32 [2, 1024, 4096], P(None, 'fsdp', 'tp')
- output 12: float32 [2, 4096], P(None, ('tp', 'fsdp'))
- output 13: float32 [2, 4096, 1024], P(None, ('tp', 'fsdp'))
- output 14: float32 [2, 1024], P(None, ('tp', 'fsdp'))
- output 15: float32 [1024], P(('tp', 'fsdp'))
- output 16: float32 [1024], P(('tp', 'fsdp'))
- output 17: float32 [1024, 1000], P('fsdp', 'tp')
- output 18: float32 [1000], P('tp')
All inputs are finite; a program needn't handle non-finite values.
Results may differ from a plain program's by a relative error of at most 0.014476.
Values are sent between devices in bfloat16 or wider.
A program may use at most 1 GiB of HBM per device.

v0:
```python
import jax
import jax.numpy as jnp
from jax import lax
from jax.sharding import PartitionSpec as P

EPS = 1e-6
CHANNEL_AXES = ('tp', 'fsdp')
LAYER_NAMES = ('ln1_g', 'ln1_b', 'w_tok1', 'b_tok1', 'w_tok2', 'ln2_g', 'ln2_b', 'w_ch1', 'b_ch1', 'w_ch2', 'b_ch2')


def product(form, left, right):
    return jnp.einsum(form, left, right, preferred_element_type=jnp.float32)


def gather_weight(weight, axis):
    return lax.all_gather(weight.astype(jnp.bfloat16), 'fsdp', axis=axis, tiled=True)


def gather_vector(values):
    return lax.all_gather(values, 'fsdp', axis=values.ndim - 1, tiled=True)


def sum_to_piece(grad_full, axis):
    return lax.psum_scatter(grad_full, 'fsdp', scatter_dimension=axis, tiled=True)


def lead_sum(values):
    return jnp.sum(values.reshape(-1, values.shape[-1]), axis=0)


def norm_forward(values, gain, shift, width):
    moments = jnp.concatenate([jnp.sum(values, axis=-1, keepdims=True),
                               jnp.sum(values * values, axis=-1, keepdims=True)], axis=-1)
    moments = lax.psum(moments, 'tp') / width
    mean_val = moments[..., :1]
    inv_std = lax.rsqrt(jnp.maximum(moments[..., 1:] - mean_val * mean_val, 0.0) + EPS)
    standard = (values - mean_val) * inv_std
    return standard * gain + shift, standard, inv_std


def norm_backward(grad_out, gain, standard, inv_std, width):
    grad_std = grad_out * gain
    moments = jnp.concatenate([jnp.sum(grad_std, axis=-1, keepdims=True),
                               jnp.sum(grad_std * standard, axis=-1, keepdims=True)], axis=-1)
    moments = lax.psum(moments, 'tp') / width
    return inv_std * (grad_std - moments[..., :1] - standard * moments[..., 1:])


def gelu_grad(pre_act, grad_out):
    return jax.vjp(jax.nn.gelu, pre_act)[1](grad_out)[0]


def weight_specs():
    vec_spec = P(CHANNEL_AXES)
    layer_vec = P(None, CHANNEL_AXES)
    return (P('fsdp', 'tp'), vec_spec, layer_vec, layer_vec, P(None, None, 'fsdp'), P(None, 'fsdp'),
            P(None, 'fsdp', None), layer_vec, layer_vec, P(None, 'fsdp', 'tp'), layer_vec,
            P(None, CHANNEL_AXES, None), layer_vec, vec_spec, vec_spec, P('fsdp', 'tp'), P('tp'))


def solution(mesh):
    fsdp_size = mesh.shape['fsdp']
    tp_size = mesh.shape['tp']

    def step(patches, labels, w_stem, b_stem, ln1_g, ln1_b, w_tok1, b_tok1, w_tok2,
             ln2_g, ln2_b, w_ch1, b_ch1, w_ch2, b_ch2, lnf_g, lnf_b, w_head, b_head):
        local_images = patches.shape[0]
        tokens = patches.shape[1]
        channels = w_stem.shape[1] * tp_size
        total_images = local_images * fsdp_size
        stem_bias = gather_vector(b_stem)
        ln1_gain = gather_vector(ln1_g)
        ln1_shift = gather_vector(ln1_b)
        tok_bias = gather_vector(b_tok1)
        ln2_gain = gather_vector(ln2_g)
        ln2_shift = gather_vector(ln2_b)
        ch_bias1 = gather_vector(b_ch1)
        ch_bias2 = gather_vector(b_ch2)
        lnf_gain = gather_vector(lnf_g)
        lnf_shift = gather_vector(lnf_b)

        resid = product('bsp,pc->bsc', patches, gather_weight(w_stem, 0)) + stem_bias
        saved = []
        for layer in range(w_tok1.shape[0]):
            normed, norm1_std, norm1_inv = norm_forward(resid, ln1_gain[layer], ln1_shift[layer], channels)
            normed = normed.astype(jnp.bfloat16)
            tok_pre = product('bsc,sj->bcj', normed, gather_weight(w_tok1[layer], 1)) + tok_bias[layer]
            tok_act = jax.nn.gelu(tok_pre).astype(jnp.bfloat16)
            resid = resid + product('bcj,js->bsc', tok_act, gather_weight(w_tok2[layer], 0))
            normed2, norm2_std, norm2_inv = norm_forward(resid, ln2_gain[layer], ln2_shift[layer], channels)
            full_in = lax.all_gather(normed2.astype(jnp.bfloat16), 'tp', axis=2, tiled=True)
            ch_pre = product('bsc,cd->bsd', full_in, gather_weight(w_ch1[layer], 0)) + ch_bias1[layer]
            ch_act = jax.nn.gelu(ch_pre).astype(jnp.bfloat16)
            part_sum = product('bsd,dc->bsc', ch_act, gather_weight(w_ch2[layer], 0))
            resid = resid + lax.psum_scatter(part_sum, 'tp', scatter_dimension=2, tiled=True) + ch_bias2[layer]
            saved.append(dict(normed=normed, norm1_std=norm1_std, norm1_inv=norm1_inv, tok_pre=tok_pre,
                              tok_act=tok_act, norm2_std=norm2_std, norm2_inv=norm2_inv,
                              full_in=full_in, ch_pre=ch_pre, ch_act=ch_act))

        pooled = jnp.mean(resid, axis=1)
        head_in, head_std, head_inv = norm_forward(pooled, lnf_gain, lnf_shift, channels)
        head_full = lax.all_gather(head_in.astype(jnp.bfloat16), 'tp', axis=1, tiled=True)
        head_w = gather_weight(w_head, 0)
        logits = product('bc,ck->bk', head_full, head_w) + b_head
        class_local = logits.shape[1]
        class_ids = lax.axis_index('tp') * class_local + jnp.arange(class_local)
        is_label = class_ids[None, :] == labels[:, None]
        row_max = lax.pmax(jnp.max(logits, axis=1), 'tp')
        shifted = jnp.exp(logits - row_max[:, None])
        class_sums = lax.psum(jnp.stack([jnp.sum(shifted, axis=1),
                                         jnp.sum(jnp.where(is_label, logits, 0.0), axis=1)]), 'tp')
        log_norm = row_max + jnp.log(class_sums[0])
        loss = lax.psum(jnp.sum(log_norm - class_sums[1]), 'fsdp') / total_images

        d_logits = (shifted / class_sums[0][:, None] - is_label.astype(jnp.float32)) / total_images
        d_logits_bf = d_logits.astype(jnp.bfloat16)
        g_w_head = sum_to_piece(product('bc,bk->ck', head_full, d_logits_bf), 0)
        g_b_head = lax.psum(jnp.sum(d_logits, axis=0), 'fsdp')
        d_head_in = lax.psum_scatter(product('bk,ck->bc', d_logits_bf, head_w), 'tp', scatter_dimension=1, tiled=True)
        g_lnf_g = sum_to_piece(jnp.sum(d_head_in * head_std, axis=0), 0)
        g_lnf_b = sum_to_piece(jnp.sum(d_head_in, axis=0), 0)
        d_pooled = norm_backward(d_head_in, lnf_gain, head_std, head_inv, channels)
        d_resid = jnp.broadcast_to((d_pooled / tokens)[:, None, :], resid.shape)

        grad_lists = {name: [] for name in LAYER_NAMES}
        for layer in reversed(range(w_tok1.shape[0])):
            keep = saved[layer]
            grad_lists['b_ch2'].append(sum_to_piece(lead_sum(d_resid), 0))
            d_out_full = lax.all_gather(d_resid.astype(jnp.bfloat16), 'tp', axis=2, tiled=True)
            ch_w1 = gather_weight(w_ch1[layer], 0)
            ch_w2 = gather_weight(w_ch2[layer], 0)
            grad_lists['w_ch2'].append(sum_to_piece(product('bsd,bsc->dc', keep['ch_act'], d_out_full), 0))
            d_ch_pre = gelu_grad(keep['ch_pre'], product('bsc,dc->bsd', d_out_full, ch_w2))
            grad_lists['b_ch1'].append(sum_to_piece(lead_sum(d_ch_pre), 0))
            d_ch_pre_bf = d_ch_pre.astype(jnp.bfloat16)
            grad_lists['w_ch1'].append(sum_to_piece(product('bsc,bsd->cd', keep['full_in'], d_ch_pre_bf), 0))
            d_norm2 = lax.psum_scatter(product('bsd,cd->bsc', d_ch_pre_bf, ch_w1), 'tp', scatter_dimension=2, tiled=True)
            grad_lists['ln2_g'].append(sum_to_piece(lead_sum(d_norm2 * keep['norm2_std']), 0))
            grad_lists['ln2_b'].append(sum_to_piece(lead_sum(d_norm2), 0))
            d_mid = d_resid + norm_backward(d_norm2, ln2_gain[layer], keep['norm2_std'], keep['norm2_inv'], channels)
            d_mid_bf = d_mid.astype(jnp.bfloat16)
            tok_w1 = gather_weight(w_tok1[layer], 1)
            tok_w2 = gather_weight(w_tok2[layer], 0)
            grad_lists['w_tok2'].append(lax.psum(sum_to_piece(product('bcj,bsc->js', keep['tok_act'], d_mid_bf), 0), 'tp'))
            d_tok_pre = gelu_grad(keep['tok_pre'], product('bsc,js->bcj', d_mid_bf, tok_w2))
            grad_lists['b_tok1'].append(lax.psum(sum_to_piece(lead_sum(d_tok_pre), 0), 'tp'))
            d_tok_pre_bf = d_tok_pre.astype(jnp.bfloat16)
            grad_lists['w_tok1'].append(lax.psum(sum_to_piece(product('bsc,bcj->sj', keep['normed'], d_tok_pre_bf), 1), 'tp'))
            d_norm1 = product('bcj,sj->bsc', d_tok_pre_bf, tok_w1)
            grad_lists['ln1_g'].append(sum_to_piece(lead_sum(d_norm1 * keep['norm1_std']), 0))
            grad_lists['ln1_b'].append(sum_to_piece(lead_sum(d_norm1), 0))
            d_resid = d_mid + norm_backward(d_norm1, ln1_gain[layer], keep['norm1_std'], keep['norm1_inv'], channels)

        g_b_stem = sum_to_piece(lead_sum(d_resid), 0)
        g_w_stem = sum_to_piece(product('bsp,bsc->pc', patches, d_resid.astype(jnp.bfloat16)), 0)
        stacked = [jnp.stack(grad_lists[name][::-1]) for name in LAYER_NAMES]
        return tuple([loss, g_w_stem, g_b_stem] + stacked + [g_lnf_g, g_lnf_b, g_w_head, g_b_head])

    specs = weight_specs()
    return jax.shard_map(step, mesh=mesh, in_specs=(P('fsdp', None, None), P('fsdp')) + specs,
                         out_specs=(P(),) + specs, check_vma=False)
```

profile of v0, /device:TPU:0, one launch (start us, length us, event | category | flops | bytes accessed | tf_op | source)
XLA Modules:
  0.0 1889.2 jit_solution(7175952412237633875)
XLA Ops:
  10.6 25.9 %all-gather.10 = f32[32,16,2]{1,2,0:T(2,128)S(1)} all-gather(f32[1,16,2]{1,2,0:T(2,128)} %bitcast.381), channel_id=1, replica_groups=mesh['tp'=4,'fsdp'=32] {'fsdp'}, dimensions={0}, use_global_device_ids=true | all-gather | bytes 4224 | tf_op jit(solution)/shard_map/all_gather | solution.py:20
  37.3 24.0 %all-gather = bf16[1,49,512]{1,2,0:T(8,128)(2,1)S(1)} all-gather(bf16[1,49,16]{1,2,0:T(8,128)(2,1)S(1)} %get-tuple-element.171), channel_id=3, replica_groups=mesh['tp'=4,'fsdp'=32] {'fsdp'}, dimensions={2}, use_global_device_ids=true | all-gather | bytes 51744 | tf_op jit(solution)/shard_map/all_gather | solution.py:16
  61.3 21.9 %all-gather.9 = f32[32,8,2]{1,2,0:T(2,128)S(1)} all-gather(f32[1,8,2]{1,2,0:T(2,128)} %bitcast.382), channel_id=1, replica_groups=mesh['tp'=4,'fsdp'=32] {'fsdp'}, dimensions={0}, use_global_device_ids=true | all-gather | bytes 2112 | tf_op jit(solution)/shard_map/all_gather | solution.py:20
  83.3 23.8 %all-gather.8 = f32[32,8,2]{1,2,0:T(2,128)S(1)} all-gather(f32[1,8,2]{1,2,0:T(2,128)} %bitcast.383), channel_id=1, replica_groups=mesh['tp'=4,'fsdp'=32] {'fsdp'}, dimensions={0}, use_global_device_ids=true | all-gather | bytes 2112 | tf_op jit(solution)/shard_map/all_gather | solution.py:20
  107.9 22.1 %all-gather.1 = bf16[1,512,49]{2,1,0:T(8,128)(2,1)S(1)} all-gather(bf16[1,16,49]{2,1,0:T(8,128)(2,1)S(1)} %get-tuple-element.169), channel_id=4, replica_groups=mesh['tp'=4,'fsdp'=32] {'fsdp'}, dimensions={1}, use_global_device_ids=true | all-gather | bytes 51744 | tf_op jit(solution)/shard_map/all_gather | solution.py:16
  130.0 23.7 %all-gather.12 = f32[32,8,2]{1,2,0:T(2,128)S(1)} all-gather(f32[1,8,2]{1,2,0:T(2,128)} %bitcast.384), channel_id=1, replica_groups=mesh['tp'=4,'fsdp'=32] {'fsdp'}, dimensions={0}, use_global_device_ids=true | all-gather | bytes 2112 | tf_op jit(solution)/shard_map/all_gather | solution.py:20
  153.9 21.9 %all-gather.11 = f32[32,8,2]{1,2,0:T(2,128)S(1)} all-gather(f32[1,8,2]{1,2,0:T(2,128)} %bitcast.385), channel_id=1, replica_groups=mesh['tp'=4,'fsdp'=32] {'fsdp'}, dimensions={0}, use_global_device_ids=true | all-gather | bytes 2112 | tf_op jit(solution)/shard_map/all_gather | solution.py:20
  180.4 65.8 %all-reduce.21 = (f32[256]{0:T(256)}, f32[256]{0:T(256)S(1)}, f32[256]{0:T(256)S(1)}) all-reduce(f32[256]{0:T(256)S(1)} %dynamic-update-slice.2, f32[256]{0:T(256)S(1)} %dynamic-update-slice.1, f32[256]{0:T(256)S(1)} %dynamic-update-slice), channel_id=1, replica_groups=mesh['tp'=4,'fsdp'=32] {'fsdp'}, use_global_device_ids=true, to_apply=%add.2 | all-reduce | flops 768 | bytes 6144
  253.3 18.1 psum.133
  303.8 21.4 %all-gather.13 = f32[32,32,2]{1,2,0:T(2,128)S(1)} all-gather(f32[1,32,2]{1,2,0:T(2,128)S(1)} %bitcast.386), channel_id=1, replica_groups=mesh['tp'=4,'fsdp'=32] {'fsdp'}, dimensions={0}, use_global_device_ids=true | all-gather | bytes 8448 | tf_op jit(solution)/shard_map/all_gather | solution.py:20
  354.1 33.4 %all-gather.34.cloned.1.call-done = bf16[1,1024,1024]{2,1,0:T(8,128)(2,1)} async-done(((bf16[1,32,1024]{2,1,0:T(8,128)(2,1)}), bf16[1,1024,1024]{2,1,0:T(8,128)(2,1)}) %all-gather.34.cloned.1.call-update) | async-done | bytes 2097168 | tf_op jit(solution)/shard_map/all_gather | solution.py:16
  398.2 23.6 %all-gather.14 = f32[32,8,2]{1,2,0:T(2,128)S(1)} all-gather(f32[1,8,2]{1,2,0:T(2,128)S(1)} %bitcast.387), channel_id=1, replica_groups=mesh['tp'=4,'fsdp'=32] {'fsdp'}, dimensions={0}, use_global_device_ids=true | all-gather | bytes 2112 | tf_op jit(solution)/shard_map/all_gather | solution.py:20
  421.9 22.4 %all-gather.4 = bf16[1,49,512]{1,2,0:T(8,128)(2,1)S(1)} all-gather(bf16[1,49,16]{1,2,0:T(8,128)(2,1)S(1)} %get-tuple-element.170), channel_id=7, replica_groups=mesh['tp'=4,'fsdp'=32] {'fsdp'}, dimensions={2}, use_global_device_ids=true | all-gather | bytes 51744 | tf_op jit(solution)/shard_map/all_gather | solution.py:16
  444.3 23.8 %all-gather.5 = bf16[1,512,49]{2,1,0:T(8,128)(2,1)} all-gather(bf16[1,16,49]{2,1,0:T(8,128)(2,1)S(1)} %get-tuple-element.168), channel_id=8, replica_groups=mesh['tp'=4,'fsdp'=32] {'fsdp'}, dimensions={1}, use_global_device_ids=true | all-gather | bytes 51744 | tf_op jit(solution)/shard_map/all_gather | solution.py:16
  470.2 17.5 psum.135
  519.9 38.8 %all-gather.28.cloned.1.call-done = bf16[32,49,1024]{2,0,1:T(8,128)(2,1)} async-done(((bf16[32,49,256]{2,0,1:T(8,128)(2,1)}), bf16[32,49,1024]{2,0,1:T(8,128)(2,1)}) %all-gather.28.cloned.1.call-update) | async-done | bytes 3211280 | tf_op jit(solution)/shard_map/all_gather | solution.py:91
  572.1 33.4 %all-gather.38.cloned.1.call-done = bf16[1,1024,1024]{2,1,0:T(8,128)(2,1)} async-done(((bf16[1,32,1024]{2,1,0:T(8,128)(2,1)}), bf16[1,1024,1024]{2,1,0:T(8,128)(2,1)}) %all-gather.38.cloned.1.call-update) | async-done | bytes 2097168 | tf_op jit(solution)/shard_map/all_gather | solution.py:16
  616.2 24.3 %all_gather.105 = bf16[1024,250]{1,0:T(8,128)(2,1)} all-gather(bf16[32,250]{1,0:T(8,128)(2,1)S(1)} %convert_element_type.125), channel_id=1, replica_groups=mesh['tp'=4,'fsdp'=32] {'fsdp'}, dimensions={0}, use_global_device_ids=true | all-gather | bytes 528000 | tf_op jit(solution)/shard_map/all_gather | solution.py:16
  640.4 39.4 %reduce-scatter.20.cloned.1.call-done = f32[32,49,256]{2,0,1:T(8,128)} async-done(((f32[32,49,1024]{2,0,1:T(8,128)}), f32[32,49,256]{2,0,1:T(8,128)}) %reduce-scatter.20.cloned.1.call-update) | async-done | bytes 1605648 | tf_op jit(solution)/shard_map/reduce_scatter | solution.py:95
  724.4 20.2 %reduce-scatter.22.cloned.1.call-done = f32[32,256]{1,0:T(8,128)} async-done(((f32[32,1024]{1,0:T(8,128)}), f32[32,256]{1,0:T(8,128)}) %reduce-scatter.22.cloned.1.call-update) | async-done | bytes 32784 | tf_op jit(solution)/shard_map/reduce_scatter | solution.py:119
  788.9 64.9 %reduce-scatter.24.cloned.1.call-done = f32[32,49,256]{2,0,1:T(8,128)} async-done(((f32[32,49,1024]{2,0,1:T(8,128)}), f32[32,49,256]{2,0,1:T(8,128)}) %reduce-scatter.24.cloned.1.call-update) | async-done | bytes 1605648 | tf_op jit(solution)/shard_map/reduce_scatter | solution.py:137
  922.8 41.9 %all-gather.30.cloned.1.call-done = bf16[32,49,1024]{2,0,1:T(8,128)(2,1)} async-done(((bf16[32,49,256]{2,0,1:T(8,128)(2,1)}), bf16[32,49,1024]{2,0,1:T(8,128)(2,1)}) %all-gather.30.cloned.1.call-update) | async-done | bytes 3211280 | tf_op jit(solution)/shard_map/all_gather | solution.py:129
  1148.9 75.7 %reduce-scatter.36.cloned.1.call-done = f32[32,1024]{1,0:T(8,128)} async-done(((f32[1024,1024]{1,0:T(8,128)}), f32[32,1024]{1,0:T(8,128)}) %reduce-scatter.36.cloned.1.call-update) | async-done | bytes 131088 | tf_op jit(solution)/shard_map/reduce_scatter | solution.py:24
  1226.2 83.5 %reduce-scatter.42.cloned.1.call-done = f32[32,1024]{1,0:T(8,128)} async-done(((f32[1024,1024]{1,0:T(8,128)}), f32[32,1024]{1,0:T(8,128)}) %reduce-scatter.42.cloned.1.call-update) | async-done | bytes 131088 | tf_op jit(solution)/shard_map/reduce_scatter | solution.py:24
  1309.7 85.2 %reduce-scatter.40.cloned.1.call-done = f32[32,1024]{1,0:T(8,128)} async-done(((f32[1024,1024]{1,0:T(8,128)}), f32[32,1024]{1,0:T(8,128)}) %reduce-scatter.40.cloned.1.call-update) | async-done | bytes 131088 | tf_op jit(solution)/shard_map/reduce_scatter | solution.py:24
  1396.7 124.2 %all-reduce.20 = (f32[]{:T(128)}, f32[256]{0:T(256)S(1)}, f32[256]{0:T(256)S(1)}, f32[256]{0:T(256)S(1)}, f32[256]{0:T(256)S(1)}, /*index=5*/f32[256]{0:T(256)S(...) all-reduce(f32[]{:T(128)} %fusion.131, ...), channel_id=1, replica_groups=mesh['tp'=4,'fsdp'=32] {'fsdp'}, use_global_device_ids=true, to_apply=%region_24.25 | all-reduce | flops 6651 | bytes 53208 | tf_op jit(solution)/shard_map/psum | solution.py:113
  1527.3 27.9 %reduce-scatter.34.cloned.1.call-done = f32[16,49]{1,0:T(8,128)} async-done(((f32[512,49]{1,0:T(8,128)}), f32[16,49]{1,0:T(8,128)}) %reduce-scatter.34.cloned.1.call-update) | async-done | bytes 3152 | tf_op jit(solution)/shard_map/reduce_scatter | solution.py:24
  1555.2 80.1 %reduce-scatter.28.cloned.1.call-done = f32[49,16]{0,1:T(8,128)} async-done(((f32[49,512]{0,1:T(8,128)}), f32[49,16]{0,1:T(8,128)}) %reduce-scatter.28.cloned.1.call-update) | async-done | bytes 3152 | tf_op jit(solution)/shard_map/reduce_scatter | solution.py:24
  1635.4 80.3 %reduce-scatter.32.cloned.1.call-done = f32[16,49]{1,0:T(8,128)} async-done(((f32[512,49]{1,0:T(8,128)}), f32[16,49]{1,0:T(8,128)}) %reduce-scatter.32.cloned.1.call-update) | async-done | bytes 3152 | tf_op jit(solution)/shard_map/reduce_scatter | solution.py:24
  1715.6 17.8 all-reduce.22
  1735.2 61.8 %reduce-scatter.44.cloned.1.call-done = f32[32,250]{1,0:T(8,128)} async-done(((f32[1024,250]{1,0:T(8,128)}), f32[32,250]{1,0:T(8,128)}) %reduce-scatter.44.cloned.1.call-update) | async-done | bytes 32016 | tf_op jit(solution)/shard_map/reduce_scatter | solution.py:24
  1797.0 84.2 %reduce-scatter.46.cloned.1.call-done = f32[96,256]{1,0:T(8,128)} async-done(((f32[3072,256]{1,0:T(8,128)}), f32[96,256]{1,0:T(8,128)}) %reduce-scatter.46.cloned.1.call-update) | async-done | bytes 98320
  (400 shorter events, 496.3 us)
Async XLA Ops:
  7.2 239.1 %all-gather.24.cloned.1.call-start = ((), (), s32[]{:S(2)}) async-start(), calls=%async_computation.15 | async-start | bytes 1622016 | tf_op jit(solution)/shard_map/all_gather | solution.py:16
  8.8 316.6 %all-gather.32.cloned.1.call-start = ((), (), s32[]{:S(2)}) async-start(), calls=%async_computation.33 | async-start | bytes 2162688 | tf_op jit(solution)/shard_map/all_gather | solution.py:16
  10.5 330.4 %all-gather.26.cloned.1.call-start = ((), (), s32[]{:S(2)}) async-start(), calls=%async_computation.16 | async-start | bytes 4014080 | tf_op jit(solution)/shard_map/all_gather | solution.py:91
  36.6 451.6 %copy-start.79 = (f32[1,512]{1,0:T(1,128)}, f32[1,512]{1,0:T(1,128)S(1)}, u32[]{:S(2)}) copy-start(f32[1,512]{1,0:T(1,128)S(1)} %get-tuple-element.172) | copy-start | bytes 6148
  107.2 380.5 %copy-start.47 = (f32[1,256]{1,0:T(1,128)}, f32[1,256]{1,0:T(1,128)S(1)}, u32[]{:S(2)}) copy-start(f32[1,256]{1,0:T(1,128)S(1)} %get-tuple-element.180) | copy-start | bytes 3076
  175.9 341.3 %copy-start.39 = (f32[1,256]{1,0:T(1,128)}, f32[1,256]{1,0:T(1,128)S(1)}, u32[]{:S(2)}) copy-start(f32[1,256]{1,0:T(1,128)S(1)} %get-tuple-element.176) | copy-start | bytes 3076
  246.3 498.4 %copy-start.51 = (f32[256]{0:T(256)}, f32[256]{0:T(256)S(1)}, u32[]{:S(2)}) copy-start(f32[256]{0:T(256)S(1)} %get-tuple-element.122) | copy-start | bytes 3076
  303.0 84.5 %all-gather.34.cloned.1.call-start = ((), (), s32[]{:S(2)}) async-start(), calls=%async_computation.34 | async-start | bytes 2162688 | tf_op jit(solution)/shard_map/all_gather | solution.py:16
  303.7 164.4 %reduce-scatter.18.cloned.1.call-start = ((), (), s32[]{:S(2)}) async-start(), calls=%async_computation.17 | async-start | bytes 8028160 | tf_op jit(solution)/shard_map/reduce_scatter | solution.py:95
  397.5 122.3 %all-gather.36.cloned.1.call-start = ((), (), s32[]{:S(2)}) async-start(), calls=%async_computation.35 | async-start | bytes 2162688 | tf_op jit(solution)/shard_map/all_gather | solution.py:16
  398.1 160.6 %all-gather.28.cloned.1.call-start = ((), (), s32[]{:S(2)}) async-start(), calls=%async_computation.18 | async-start | bytes 4014080 | tf_op jit(solution)/shard_map/all_gather | solution.py:91
  518.6 86.9 %all-gather.38.cloned.1.call-start = ((), (), s32[]{:S(2)}) async-start(), calls=%async_computation.36 | async-start | bytes 2162688 | tf_op jit(solution)/shard_map/all_gather | solution.py:16
  519.4 160.4 %reduce-scatter.20.cloned.1.call-start = ((), (), s32[]{:S(2)}) async-start(), calls=%async_computation.19 | async-start | bytes 8028160 | tf_op jit(solution)/shard_map/reduce_scatter | solution.py:95
  615.4 129.2 %reduce-scatter.22.cloned.1.call-start = ((), (), s32[]{:S(2)}) async-start(), calls=%async_computation.20 | async-start | bytes 163840 | tf_op jit(solution)/shard_map/reduce_scatter | solution.py:119
  724.4 129.4 %reduce-scatter.24.cloned.1.call-start = ((), (), s32[]{:S(2)}) async-start(), calls=%async_computation.21 | async-start | bytes 8028160 | tf_op jit(solution)/shard_map/reduce_scatter | solution.py:137
  788.9 175.8 %all-gather.30.cloned.1.call-start = ((), (), s32[]{:S(2)}) async-start(), calls=%async_computation.22 | async-start | bytes 4014080 | tf_op jit(solution)/shard_map/all_gather | solution.py:129
  922.3 131.4 %reduce-scatter.26.cloned.1.call-start = ((), (), s32[]{:S(2)}) async-start(), calls=%async_computation.23 | async-start | bytes 8028160 | tf_op jit(solution)/shard_map/reduce_scatter | solution.py:137
  987.6 161.3 %reduce-scatter.38.cloned.1.call-start = ((), (), s32[]{:S(2)}) async-start(), calls=%async_computation.29 | async-start | bytes 4325376 | tf_op jit(solution)/shard_map/reduce_scatter | solution.py:24
  998.2 226.4 %reduce-scatter.36.cloned.1.call-start = ((), (), s32[]{:S(2)}) async-start(), calls=%async_computation.28 | async-start | bytes 4325376 | tf_op jit(solution)/shard_map/reduce_scatter | solution.py:24
  1008.7 301.0 %reduce-scatter.42.cloned.1.call-start = ((), (), s32[]{:S(2)}) async-start(), calls=%async_computation.31 | async-start | bytes 4325376 | tf_op jit(solution)/shard_map/reduce_scatter | solution.py:24
  1017.2 377.7 %reduce-scatter.40.cloned.1.call-start = ((), (), s32[]{:S(2)}) async-start(), calls=%async_computation.30 | async-start | bytes 4325376 | tf_op jit(solution)/shard_map/reduce_scatter | solution.py:24
  1027.4 499.9 %reduce-scatter.30.cloned.1.call-start = ((), (), s32[]{:S(2)}) async-start(), calls=%async_computation.25 | async-start | bytes 270336 | tf_op jit(solution)/shard_map/reduce_scatter | solution.py:24
  1036.1 519.2 %reduce-scatter.34.cloned.1.call-start = ((), (), s32[]{:S(2)}) async-start(), calls=%async_computation.27 | async-start | bytes 270336 | tf_op jit(solution)/shard_map/reduce_scatter | solution.py:24
  1043.0 592.3 %reduce-scatter.28.cloned.1.call-start = ((), (), s32[]{:S(2)}) async-start(), calls=%async_computation.24 | async-start | bytes 270336 | tf_op jit(solution)/shard_map/reduce_scatter | solution.py:24
  1100.2 615.4 %reduce-scatter.32.cloned.1.call-start = ((), (), s32[]{:S(2)}) async-start(), calls=%async_computation.26 | async-start | bytes 270336 | tf_op jit(solution)/shard_map/reduce_scatter | solution.py:24
  1107.1 689.9 %reduce-scatter.44.cloned.1.call-start = ((), (), s32[]{:S(2)}) async-start(), calls=%async_computation.32 | async-start | bytes 1081344 | tf_op jit(solution)/shard_map/reduce_scatter | solution.py:24
  1108.6 772.5 %reduce-scatter.46.cloned.1.call-start = ((), (), s32[]{:S(2)}) async-start(), calls=%async_computation.37 | async-start | bytes 3244032
  1146.0 250.6 %copy-start.62 = (f32[256]{0:T(256)S(1)}, f32[256]{0:T(256)}, u32[]{:S(2)}) copy-start(f32[256]{0:T(256)} %get-tuple-element.74) | copy-start | bytes 3076
  1146.0 250.6 %copy-start.63 = (f32[256]{0:T(256)S(1)}, f32[256]{0:T(256)}, u32[]{:S(2)}) copy-start(f32[256]{0:T(256)} %get-tuple-element.84) | copy-start | bytes 3076
  1146.0 250.6 %copy-start.64 = (f32[256]{0:T(256)S(1)}, f32[256]{0:T(256)}, u32[]{:S(2)}) copy-start(f32[256]{0:T(256)} %get-tuple-element.72) | copy-start | bytes 3076
  1146.0 250.6 %copy-start.67 = (f32[1024]{0:T(1024)S(1)}, f32[1024]{0:T(1024)}, u32[]{:S(2)}) copy-start(f32[1024]{0:T(1024)} %get-tuple-element.143) | copy-start | bytes 12292
  1146.1 250.6 %copy-start.70 = (f32[1024]{0:T(1024)S(1)}, f32[1024]{0:T(1024)}, u32[]{:S(2)}) copy-start(f32[1024]{0:T(1024)} %get-tuple-element.141) | copy-start | bytes 12292
  (85 other events, 5389.7 us)
Sparse Core Ops, SparseCore 0:
  10.2 45.7 all-gather.23
  58.9 42.5 all-gather.31
  303.1 37.7 all-gather.25
  343.0 44.4 all-gather.33
  397.6 64.2 reduce-scatter.17
  464.6 43.2 all-gather.35
  518.7 39.8 all-gather.27
  560.9 44.4 all-gather.37
  615.5 64.1 reduce-scatter.19
  724.5 20.0 reduce-scatter.21
  789.0 64.7 reduce-scatter.23
  922.4 42.2 all-gather.29
  987.7 65.9 reduce-scatter.25
  1057.2 82.1 reduce-scatter.37
  1142.9 81.6 reduce-scatter.35
  1228.1 81.6 reduce-scatter.41
  1313.2 81.6 reduce-scatter.39
  1398.2 76.7 reduce-scatter.29
  1478.4 76.7 reduce-scatter.33
  1558.5 76.7 reduce-scatter.27
  1638.8 76.7 reduce-scatter.31
  1719.7 77.2 reduce-scatter.43
  1801.2 79.8 reduce-scatter.45
where the time goes:
time: 1900 us; the launch traced here: 1890 us
  waiting for transfers between devices  878 us (46%)
  blocking collectives  676 us (36%)
  matrix products  232 us (12%)
  other arithmetic  50.2 us (3%)
  local copies, waits for them, and re-layouts  31 us (2%)
  between operations  20.2 us (1%)
    reduce_scatter x9, waiting for transfers between devices, sum_to_piece(): lax.psum_scatter(grad_full, 'fsdp', scatter_dimension=axis, tiled=True)  494 us
    dot_general x29, matrix products, product(): return jnp.einsum(form, left, right, preferred_element_type=jnp.float32)  232 us
    all_gather x7, blocking collectives, gather_vector(): return lax.all_gather(values, 'fsdp', axis=values.ndim - 1, tiled=True)  162 us
    psum x1, blocking collectives, step(): loss = lax.psum(jnp.sum(log_norm - class_sums[1]), 'fsdp') / total_images  124 us
    all_gather x5, blocking collectives, gather_weight(): lax.all_gather(weight.astype(jnp.bfloat16), 'fsdp', axis=axis, tiled=True)  117 us
    unnamed x24, waiting for transfers between devices  85.7 us
    reduce_scatter x2, waiting for transfers between devices, step(): lax.psum_scatter(product('bsd,cd->bsc', d_ch_pre_bf, ch_w1), 'tp', scatte...  75.5 us
    psum x5, blocking collectives, norm_forward(): moments = lax.psum(moments, 'tp') / width  74 us
  transfers between devices with their start and end apart: 23, of which 17 were waited for; matrix products, arithmetic and copies ran while one was open for 10% of the time, Pallas kernels for 0%

commit v1 on v0

v1 whole, which is shorter than its diff:
```python
import jax
import jax.numpy as jnp
from jax import lax
from jax.sharding import PartitionSpec as P

EPS = 1e-6
CHANNEL_AXES = ('tp', 'fsdp')
ALL_AXES = ('tp', 'fsdp')
RS_DTYPE = jnp.float32


def product(form, left, right):
    return jnp.einsum(form, left, right, preferred_element_type=jnp.float32)


def bf(x):
    return x.astype(jnp.bfloat16)


def gather_all(x):
    g = lax.all_gather(x, ALL_AXES, axis=0, tiled=False)
    return g


def scatter_all(x):
    return lax.psum_scatter(x.astype(RS_DTYPE), ALL_AXES, scatter_dimension=0, tiled=True).astype(jnp.float32)[0]


def norm_forward(values, gain, shift):
    mean_val = jnp.mean(values, axis=-1, keepdims=True)
    cent = values - mean_val
    inv_std = lax.rsqrt(jnp.mean(cent * cent, axis=-1, keepdims=True) + EPS)
    standard = cent * inv_std
    return standard * gain + shift, standard, inv_std


def norm_backward(grad_out, gain, standard, inv_std):
    gs = grad_out * gain
    m0 = jnp.mean(gs, axis=-1, keepdims=True)
    m1 = jnp.mean(gs * standard, axis=-1, keepdims=True)
    return inv_std * (gs - m0 - standard * m1)


def gelu_grad(pre_act, grad_out):
    return jax.vjp(jax.nn.gelu, pre_act)[1](grad_out)[0]


def weight_specs():
    vec_spec = P(CHANNEL_AXES)
    layer_vec = P(None, CHANNEL_AXES)
    return (P('fsdp', 'tp'), vec_spec, layer_vec, layer_vec, P(None, None, 'fsdp'), P(None, 'fsdp'),
            P(None, 'fsdp', None), layer_vec, layer_vec, P(None, 'fsdp', 'tp'), layer_vec,
            P(None, CHANNEL_AXES, None), layer_vec, vec_spec, vec_spec, P('fsdp', 'tp'), P('tp'))


def solution(mesh):
    fs = mesh.shape['fsdp']
    tp = mesh.shape['tp']
    nd = fs * tp

    def step(patches, labels, w_stem, b_stem, ln1_g, ln1_b, w_tok1, b_tok1, w_tok2,
             ln2_g, ln2_b, w_ch1, b_ch1, w_ch2, b_ch2, lnf_g, lnf_b, w_head, b_head):
        t = lax.axis_index('tp')
        nl = w_tok1.shape[0]
        bl = patches.shape[0] // tp
        tokens = patches.shape[1]
        total_images = bl * nd
        pat = lax.dynamic_slice_in_dim(patches, t * bl, bl, 0)
        lab = lax.dynamic_slice_in_dim(labels, t * bl, bl, 0)

        vecs = [b_stem[None], ln1_g, ln1_b, ln2_g, ln2_b, b_ch2, lnf_g[None], lnf_b[None]]
        vec_rows = jnp.concatenate(vecs, axis=0)
        n_rows = vec_rows.shape[0]
        pieces = [vec_rows.reshape(-1), b_ch1.reshape(-1), b_tok1.reshape(-1), b_head.reshape(-1),
                  w_tok1.reshape(-1), w_tok2.reshape(-1)]
        sizes = [p.shape[0] for p in pieces]
        pack = jnp.concatenate(pieces)
        pad = (-pack.shape[0]) % 1024
        pack = jnp.pad(pack, (0, pad))
        small = gather_all(pack).reshape(tp, fs, -1)
        offs = []
        o = 0
        for s in sizes:
            offs.append(small[:, :, o:o + s])
            o += s
        vec_all = offs[0].reshape(tp, fs, n_rows, -1).transpose(2, 0, 1, 3).reshape(n_rows, -1)
        bch1 = offs[1].reshape(tp, fs, nl, -1).transpose(2, 0, 1, 3).reshape(nl, -1)
        btok1 = offs[2][0].reshape(fs, nl, -1).transpose(1, 0, 2).reshape(nl, -1)
        bhead = offs[3][:, 0].reshape(-1)
        wtok1 = bf(offs[4][0].reshape(fs, nl, tokens, -1).transpose(1, 2, 0, 3).reshape(nl, tokens, -1))
        wtok2 = bf(offs[5][0].reshape(fs, nl, -1, tokens).transpose(1, 0, 2, 3).reshape(nl, -1, tokens))
        bstem = vec_all[0]
        l1g, l1b, l2g, l2b, bc2 = [vec_all[1 + nl * i:1 + nl * (i + 1)] for i in range(5)]
        lfg, lfb = vec_all[1 + 5 * nl], vec_all[2 + 5 * nl]

        ws = gather_all(bf(w_stem)).reshape(tp, -1, w_stem.shape[1])
        wc1 = [gather_all(bf(w_ch1[l])).reshape(tp, -1, w_ch1.shape[2]) for l in range(nl)]
        wc2 = [gather_all(bf(w_ch2[l])).reshape(-1, w_ch2.shape[2]) for l in range(nl)]
        wh = gather_all(bf(w_head)).reshape(tp, -1, w_head.shape[1])

        c = w_stem.shape[1] * tp
        resid = product('bsp,tpc->bstc', pat, ws).reshape(bl, tokens, c) + bstem
        saved = []
        for l in range(nl):
            normed, n1s, n1i = norm_forward(resid, l1g[l], l1b[l])
            normed = bf(normed)
            tok_pre = product('bsc,sj->bcj', normed, wtok1[l]) + btok1[l]
            tok_act = bf(jax.nn.gelu(tok_pre))
            resid = resid + product('bcj,js->bsc', tok_act, wtok2[l])
            normed2, n2s, n2i = norm_forward(resid, l2g[l], l2b[l])
            full_in = bf(normed2)
            ch_pre = product('bsc,tcd->bstd', full_in, wc1[l]).reshape(bl, tokens, -1) + bch1[l]
            ch_act = bf(jax.nn.gelu(ch_pre))
            resid = resid + product('bsd,dc->bsc', ch_act, wc2[l]) + bc2[l]
            saved.append((normed, n1s, n1i, tok_pre, tok_act, n2s, n2i, full_in, ch_pre, ch_act))

        pooled = jnp.mean(resid, axis=1)
        head_in, hs, hi = norm_forward(pooled, lfg, lfb)
        head_bf = bf(head_in)
        logits = product('bc,tck->btk', head_bf, wh).reshape(bl, -1) + bhead
        is_label = jnp.arange(logits.shape[1])[None, :] == lab[:, None]
        row_max = jnp.max(logits, axis=1, keepdims=True)
        ex = jnp.exp(logits - row_max)
        es = jnp.sum(ex, axis=1, keepdims=True)
        log_norm = row_max + jnp.log(es)
        loss_loc = jnp.sum(log_norm) - jnp.sum(jnp.where(is_label, logits, 0.0))

        d_logits = (ex / es - is_label.astype(jnp.float32)) / total_images
        dlb = bf(d_logits).reshape(bl, tp, -1)
        g_bhead = jnp.sum(d_logits, axis=0)
        gh_full = product('bc,btk->tck', head_bf, dlb).reshape(nd, -1)
        gh_full = jnp.pad(gh_full, ((0, 0), (0, (-gh_full.shape[1]) % c))).reshape(nd, -1, c)
        gh_full = jnp.pad(gh_full, ((0, 0), (0, 8), (0, 0)))
        d_hin = product('btk,tck->bc', dlb, wh)
        g_lfg = jnp.sum(d_hin * hs, axis=0)
        g_lfb = jnp.sum(d_hin, axis=0)
        d_pooled = norm_backward(d_hin, lfg, hs, hi)
        d_resid = jnp.broadcast_to((d_pooled / tokens)[:, None, :], resid.shape)

        big1, big2 = [None] * nl, [None] * nl
        sm = {}
        for l in reversed(range(nl)):
            normed, n1s, n1i, tok_pre, tok_act, n2s, n2i, full_in, ch_pre, ch_act = saved[l]
            sm['b_ch2', l] = jnp.sum(d_resid, axis=(0, 1))
            dob = bf(d_resid)
            big2[l] = product('bsd,bsc->dc', ch_act, dob).reshape(nd, -1, c)
            d_pre = gelu_grad(ch_pre, product('bsc,dc->bsd', dob, wc2[l]))
            sm['b_ch1', l] = jnp.sum(d_pre, axis=(0, 1))
            dpb = bf(d_pre).reshape(bl, tokens, tp, -1)
            big1[l] = product('bsc,bstd->tcd', full_in, dpb).reshape(nd, -1, w_ch1.shape[2])
            d_n2 = product('bstd,tcd->bsc', dpb, wc1[l])
            sm['ln2_g', l] = jnp.sum(d_n2 * n2s, axis=(0, 1))
            sm['ln2_b', l] = jnp.sum(d_n2, axis=(0, 1))
            d_mid = d_resid + norm_backward(d_n2, l2g[l], n2s, n2i)
            dmb = bf(d_mid)
            sm['w_tok2', l] = product('bcj,bsc->js', tok_act, dmb)
            d_tp = gelu_grad(tok_pre, product('bsc,js->bcj', dmb, wtok2[l]))
            sm['b_tok1', l] = jnp.sum(d_tp, axis=(0, 1))
            dtb = bf(d_tp)
            sm['w_tok1', l] = product('bsc,bcj->sj', normed, dtb)
            d_n1 = product('bcj,sj->bsc', dtb, wtok1[l])
            sm['ln1_g', l] = jnp.sum(d_n1 * n1s, axis=(0, 1))
            sm['ln1_b', l] = jnp.sum(d_n1, axis=(0, 1))
            d_resid = d_mid + norm_backward(d_n1, l1g[l], n1s, n1i)
        g_bstem = jnp.sum(d_resid, axis=(0, 1))
        g_stem = scatter_all(product('bsp,bstc->tpc', pat, bf(d_resid).reshape(bl, tokens, tp, -1)).reshape(nd, -1, w_stem.shape[1]))

        half = w_ch2.shape[1] // 2
        ra = scatter_all(jnp.concatenate([big2[1], gh_full], axis=1))
        rb = scatter_all(jnp.concatenate([big1[1], big2[0][:, :half]], axis=1))
        rc = scatter_all(jnp.concatenate([big1[0], big2[0][:, half:]], axis=1))
        g_ch2 = jnp.stack([jnp.concatenate([rb[2 * half:], rc[2 * half:]], axis=0), ra[:2 * half]])
        g_ch1 = jnp.stack([rc[:2 * half], rb[:2 * half]])
        g_head = ra[2 * half:].reshape(-1)[:w_head.size].reshape(w_head.shape)
        st = lambda k: jnp.stack([sm[k, l] for l in range(nl)])
        parts = [g_bstem, st('ln1_g'), st('ln1_b'), st('ln2_g'), st('ln2_b'), st('b_ch2'), g_lfg, g_lfb,
                 st('b_ch1'), st('b_tok1'), g_bhead, st('w_tok1'), st('w_tok2'), loss_loc[None]]
        flat = jnp.concatenate([p.reshape(-1) for p in parts])
        flat = jnp.pad(flat, (0, (-flat.shape[0]) % 1024))
        tot = lax.psum(flat, ALL_AXES)
        out = []
        o = 0
        for p in parts:
            out.append(tot[o:o + p.size].reshape(p.shape))
            o += p.size
        f = lax.axis_index('fsdp')
        dev = t * fs + f

        def own(x, n, i, ax):
            k = x.shape[ax] // n
            return lax.dynamic_slice_in_dim(x, i * k, k, ax)
        (gb, g1g, g1b, g2g, g2b, gc2, gfg, gfb, gc1, gt1, gbh, gw1, gw2, ls) = out
        loss = ls[0] / total_images
        return (loss, g_stem, own(gb, nd, dev, 0), own(g1g, nd, dev, 1), own(g1b, nd, dev, 1),
                own(gw1, fs, f, 2), own(gt1, fs, f, 1), own(gw2, fs, f, 1),
                own(g2g, nd, dev, 1), own(g2b, nd, dev, 1), g_ch1, own(gc1, nd, dev, 1),
                g_ch2, own(gc2, nd, dev, 1), own(gfg, nd, dev, 0), own(gfb, nd, dev, 0),
                g_head, own(gbh, tp, t, 0))

    specs = weight_specs()
    return jax.shard_map(step, mesh=mesh, in_specs=(P('fsdp', None, None), P('fsdp')) + specs,
                         out_specs=(P(),) + specs, check_vma=False)
```

time: 1900 us -> 1790 us (0.942)
  blocking collectives: 676 us -> 0 us
  waiting for transfers between devices: 878 us -> 1270 us
  local copies, waits for them, and re-layouts: 31 us -> 216 us
    all_gather x14 -> x0, blocking collectives: 303 us -> none  [the longest x7 162 us: gather_vector(): return lax.all_gather(values, 'fsdp', axis=values.ndim - 1, tiled=True)]
    psum x13 -> x0, blocking collectives: 298 us -> none  [the longest x1 124 us: step(): loss = lax.psum(jnp.sum(log_norm - class_sums[1]), 'fsdp') / total_images]
    reduce_scatter x14 -> x4, waiting for transfers between devices: 629 us -> 908 us  [scatter_all(): lax.psum_scatter(x.astype(RS_DTYPE), ALL_AXES, scatter_dimension=0, tiled...]
    all_gather x8 -> x7, waiting for transfers between devices: 163 us -> 355 us  [gather_all(): g = lax.all_gather(x, ALL_AXES, axis=0, tiled=False)]
    unnamed x24 -> x12, waiting for transfers between devices: 85.7 us -> 1.39 us
    unnamed x1 -> x0, blocking collectives: 65.8 us -> none
    dot_general x0 -> x6, local copies, waits for them, and re-layouts: none -> 53 us  [product(): return jnp.einsum(form, left, right, preferred_element_type=jnp.float32)]
    reshape x0 -> x21, local copies, waits for them, and re-layouts: none -> 43.4 us  [the longest x2 15.9 us: step(): dpb = bf(d_pre).reshape(bl, tokens, tp, -1)]
  transfers between devices with their start and end apart: 23 -> 12, of which waited for: 17 -> 11; matrix products, arithmetic and copies ran while one was open for 10% -> 19% of each run, Pallas kernels for 0% -> 0%
where the time goes in v1:
time: 1790 us; the launch traced here: 1780 us
  waiting for transfers between devices  1270 us (71%)
  matrix products  219 us (12%)
  local copies, waits for them, and re-layouts  216 us (12%)
  other arithmetic  61.7 us (3%)
  between operations  19.1 us (1%)
    reduce_scatter x4, waiting for transfers between devices, scatter_all(): lax.psum_scatter(x.astype(RS_DTYPE), ALL_AXES, scatter_dimension=0, tiled...  908 us
    all_gather x7, waiting for transfers between devices, gather_all(): g = lax.all_gather(x, ALL_AXES, axis=0, tiled=False)  355 us
    dot_general x29, matrix products, product(): return jnp.einsum(form, left, right, preferred_element_type=jnp.float32)  219 us
    dot_general x6, local copies, waits for them, and re-layouts, product(): return jnp.einsum(form, left, right, preferred_element_type=jnp.float32)  53 us
  transfers between devices with their start and end apart: 12, of which 11 were waited for; matrix products, arithmetic and copies ran while one was open for 19% of the time, Pallas kernels for 0%

profile of v1, /device:TPU:0, one launch (start us, length us, event | category | flops | bytes accessed | tf_op | source)
XLA Modules:
  0.0 1782.0 jit_solution(9325775835095801683)
XLA Ops:
  26.5 53.1 %all-gather.23.cloned.1.call-done = bf16[4096,250]{1,0:T(8,128)(2,1)} async-done(((bf16[32,250]{1,0:T(8,128)(2,1)}), bf16[4096,250]{1,0:T(8,128)(2,1)}) %all-gather.23.cloned.1.call-update) | async-done | bytes 2048016 | tf_op jit(solution)/shard_map/all_gather | solution.py:21
  84.5 61.7 %all-gather.21.cloned.1.call-done = f32[524288]{0:T(1024)} async-done(((f32[4096]{0:T(1024)}), f32[524288]{0:T(1024)}) %all-gather.21.cloned.1.call-update) | async-done | bytes 2097168 | tf_op jit(solution)/shard_map/all_gather | solution.py:21
  159.1 55.9 %all-gather.19.cloned.1.call-done = bf16[12288,256]{1,0:T(8,128)(2,1)} async-done(((bf16[96,256]{1,0:T(8,128)(2,1)}), bf16[12288,256]{1,0:T(8,128)(2,1)}) %all-gather.19.cloned.1.call-update) | async-done | bytes 6291472 | tf_op jit(solution)/shard_map/all_gather | solution.py:21
  230.6 9.3 multiply_convert_fusion.1
  243.6 41.2 %all-gather.11.cloned.1.call-done = bf16[128,32,1024]{2,1,0:T(8,128)(2,1)} async-done(((bf16[1,32,1024]{2,1,0:T(8,128)(2,1)}), bf16[128,32,1024]{2,1,0:T(8,128)(2,1)}) %all-gather.11.cloned.1.call-update) | async-done | bytes 8388624 | tf_op jit(solution)/shard_map/all_gather | solution.py:21
  284.8 11.4 copy.224
  296.2 58.5 %all-gather.15.cloned.1.call-done = bf16[128,32,1024]{2,1,0:T(8,128)(2,1)} async-done(((bf16[1,32,1024]{2,1,0:T(8,128)(2,1)}), bf16[128,32,1024]{2,1,0:T(8,128)(2,1)}) %all-gather.15.cloned.1.call-update) | async-done | bytes 8388624 | tf_op jit(solution)/shard_map/all_gather | solution.py:21
  354.8 11.4 copy.237
  366.1 13.4 multiply_convert_fusion.3
  379.6 45.2 %all-gather.13.cloned.1.call-done = bf16[128,32,1024]{2,1,0:T(8,128)(2,1)} async-done(((bf16[1,32,1024]{2,1,0:T(8,128)(2,1)}), bf16[128,32,1024]{2,1,0:T(8,128)(2,1)}) %all-gather.13.cloned.1.call-update) | async-done | bytes 8388624 | tf_op jit(solution)/shard_map/all_gather | solution.py:21
  433.8 9.4 multiply_convert_fusion
  455.8 39.7 %all-gather.17.cloned.1.call-done = bf16[128,32,1024]{2,1,0:T(8,128)(2,1)} async-done(((bf16[1,32,1024]{2,1,0:T(8,128)(2,1)}), bf16[128,32,1024]{2,1,0:T(8,128)(2,1)}) %all-gather.17.cloned.1.call-update) | async-done | bytes 8388624 | tf_op jit(solution)/shard_map/all_gather | solution.py:21
  495.5 9.4 add_reduce_fusion
  510.6 11.6 fusion.101
  530.3 12.5 fusion.59
  543.6 16.4 fusion.117
  571.4 12.3 fusion.100
  591.6 12.8 fusion.57
  605.4 16.2 fusion.118
  679.1 11.6 dot_general.140
  690.7 13.8 copy.262
  704.5 10.4 convolution_bitcast_fusion
  724.1 29.7 %copy.267 = f32[128,48,1024]{2,1,0:T(8,128)} copy(f32[128,48,1024]{2,0,1:T(8,128)S(1)} %select_maximum_fusion) | data formatting | bytes 50331648 | tf_op jit(solution)/shard_map/concatenate | solution.py:169
  755.1 10.3 fusion.80
  765.4 9.6 fusion.99
  774.9 9.3 fusion.40
  784.2 15.6 pad_maximum_fusion.1
  830.3 12.6 copy.258
  857.9 191.0 %reduce-scatter.11.cloned.1.call-done = f32[1,48,1024]{2,1,0:T(8,128)} async-done(((f32[128,48,1024]{2,1,0:T(8,128)}), f32[1,48,1024]{2,1,0:T(8,128)}) %reduce-scatter.11.cloned.1.call-update) | async-done | bytes 196624 | tf_op jit(solution)/shard_map/reduce_scatter | solution.py:26
  1051.4 247.3 %reduce-scatter.9.cloned.1.call-done = f32[1,48,1024]{2,1,0:T(8,128)} async-done(((f32[128,48,1024]{2,1,0:T(8,128)}), f32[1,48,1024]{2,1,0:T(8,128)}) %reduce-scatter.9.cloned.1.call-update) | async-done | bytes 196624 | tf_op jit(solution)/shard_map/reduce_scatter | solution.py:26
  1299.6 249.1 %reduce-scatter.7.cloned.1.call-done = f32[1,48,1024]{2,1,0:T(8,128)} async-done(((f32[128,48,1024]{2,1,0:T(8,128)}), f32[1,48,1024]{2,1,0:T(8,128)}) %reduce-scatter.7.cloned.1.call-update) | async-done | bytes 196624 | tf_op jit(solution)/shard_map/reduce_scatter | solution.py:26
  1552.8 221.0 %reduce-scatter.5.cloned.1.call-done = f32[1,96,256]{2,1,0:T(8,128)} async-done(((f32[128,96,256]{2,1,0:T(8,128)}), f32[1,96,256]{2,1,0:T(8,128)}) %reduce-scatter.5.cloned.1.call-update) | async-done | bytes 98320 | tf_op jit(solution)/shard_map/reduce_scatter | solution.py:26
  (417 shorter events, 230.2 us)
Async XLA Ops:
  7.2 72.4 %all-gather.23.cloned.1.call-start = ((), (), s32[]{:S(2)}) async-start(), calls=%async_computation.15 | async-start | bytes 2113536 | tf_op jit(solution)/shard_map/all_gather | solution.py:21
  8.6 137.5 %all-gather.21.cloned.1.call-start = ((), (), s32[]{:S(2)}) async-start(), calls=%async_computation.14 | async-start | bytes 2113536 | tf_op jit(solution)/shard_map/all_gather | solution.py:21
  15.6 199.3 %all-gather.19.cloned.1.call-start = ((), (), s32[]{:S(2)}) async-start(), calls=%async_computation.13 | async-start | bytes 6340608 | tf_op jit(solution)/shard_map/all_gather | solution.py:21
  17.2 267.5 %all-gather.11.cloned.1.call-start = ((), (), s32[]{:S(2)}) async-start(), calls=%async_computation.4 | async-start | bytes 8454144 | tf_op jit(solution)/shard_map/all_gather | solution.py:21
  18.9 335.8 %all-gather.15.cloned.1.call-start = ((), (), s32[]{:S(2)}) async-start(), calls=%async_computation.6 | async-start | bytes 8454144 | tf_op jit(solution)/shard_map/all_gather | solution.py:21
  19.5 405.3 %all-gather.13.cloned.1.call-start = ((), (), s32[]{:S(2)}) async-start(), calls=%async_computation.5 | async-start | bytes 8454144 | tf_op jit(solution)/shard_map/all_gather | solution.py:21
  21.2 474.3 %all-gather.17.cloned.1.call-start = ((), (), s32[]{:S(2)}) async-start(), calls=%async_computation.7 | async-start | bytes 8454144 | tf_op jit(solution)/shard_map/all_gather | solution.py:21
  22.0 821.0 %all-reduce.6.cloned.1.call-start = ((), (), s32[]{:S(2)}) async-start(), calls=%async_computation.8 | async-start | bytes 991232 | tf_op jit(solution)/shard_map/psum | solution.py:180
  150.9 79.7 %copy-start.83 = (f32[512]{0:T(512)}, f32[512]{0:T(512)S(1)}, u32[]{:S(2)}) copy-start(f32[512]{0:T(512)S(1)} %add.300) | copy-start | bytes 6148
  151.4 79.1 %copy-start.30 = (bf16[1,49,32,16]{1,3,2,0:T(8,128)(2,1)}, bf16[1,49,32,16]{1,3,2,0:T(8,128)(2,1)S(1)}, u32[]{:S(2)}) copy-start(bf16[1,49,32,16]{1,3,2,0:T(8,128)(2,1)S(1)} %copy.217) | copy-start | bytes 150532
  152.4 78.2 %copy-start.56 = (f32[1024]{0:T(1024)}, f32[1024]{0:T(1024)S(1)}, u32[]{:S(2)}) copy-start(f32[1024]{0:T(1024)S(1)} %add.297) | copy-start | bytes 12292
  153.3 77.3 %copy-start.48 = (f32[1024]{0:T(1024)}, f32[1024]{0:T(1024)S(1)}, u32[]{:S(2)}) copy-start(f32[1024]{0:T(1024)S(1)} %mul.451) | copy-start | bytes 12292
  154.2 85.8 %copy-start.40 = (f32[1024]{0:T(1024)}, f32[1024]{0:T(1024)S(1)}, u32[]{:S(2)}) copy-start(f32[1024]{0:T(1024)S(1)} %add.293) | copy-start | bytes 12292
  154.5 211.7 %copy-start.69 = (f32[4096]{0:T(1024)}, f32[4096]{0:T(1024)S(1)}, u32[]{:S(2)}) copy-start(f32[4096]{0:T(1024)S(1)} %add.310) | copy-start | bytes 49156
  156.3 86.9 %copy-start.58 = (f32[1024]{0:T(1024)}, f32[1024]{0:T(1024)S(1)}, u32[]{:S(2)}) copy-start(f32[1024]{0:T(1024)S(1)} %mul.461) | copy-start | bytes 12292
  156.7 277.1 %copy-start.34 = (bf16[1,49,32,16]{1,3,2,0:T(8,128)(2,1)}, bf16[1,49,32,16]{1,3,2,0:T(8,128)(2,1)S(1)}, u32[]{:S(2)}) copy-start(bf16[1,49,32,16]{1,3,2,0:T(8,128)(2,1)S(1)} %copy.231) | copy-start | bytes 150532
  157.7 276.2 %copy-start.62 = (f32[1024]{0:T(1024)}, f32[1024]{0:T(1024)S(1)}, u32[]{:S(2)}) copy-start(f32[1024]{0:T(1024)S(1)} %add.320) | copy-start | bytes 12292
  157.8 276.0 %copy-start.50 = (f32[1024]{0:T(1024)}, f32[1024]{0:T(1024)S(1)}, u32[]{:S(2)}) copy-start(f32[1024]{0:T(1024)S(1)} %mul.471) | copy-start | bytes 12292
  158.7 351.8 %copy-start.52 = (f32[1024]{0:T(1024)}, f32[1024]{0:T(1024)S(1)}, u32[]{:S(2)}) copy-start(f32[1024]{0:T(1024)S(1)} %mul.491) | copy-start | bytes 12292
  159.0 346.3 %copy-start.60 = (f32[1024]{0:T(1024)}, f32[1024]{0:T(1024)S(1)}, u32[]{:S(2)}) copy-start(f32[1024]{0:T(1024)S(1)} %add.343) | copy-start | bytes 12292
  159.1 80.9 %copy-start.32 = (bf16[1,32,16,49]{3,2,0,1:T(8,128)(2,1)}, bf16[1,32,16,49]{3,2,0,1:T(8,128)(2,1)S(1)}, u32[]{:S(2)}) copy-start(bf16[1,32,16,49]{3,2,0,1:T(8,128)(2,1)S(1)} %get-tuple-element.158) | copy-start | bytes 150532
  242.7 182.1 %copy-start.7 = (f32[8,49,1024]{2,1,0:T(8,128)}, f32[8,49,1024]{2,1,0:T(8,128)S(1)}, u32[]{:S(2)}) copy-start(f32[8,49,1024]{2,1,0:T(8,128)S(1)} %get-tuple-element.187) | copy-start | bytes 4816900
  242.7 53.5 %copy-start.54 = (f32[8,49]{1,0:T(8,128)}, f32[8,49]{1,0:T(8,128)S(1)}, u32[]{:S(2)}) copy-start(f32[8,49]{1,0:T(8,128)S(1)} %broadcast_multiply_fusion.10) | copy-start | bytes 4708
  243.2 53.0 %copy-start.64 = (f32[8,49]{1,0:T(8,128)}, f32[8,49]{1,0:T(8,128)S(1)}, u32[]{:S(2)}) copy-start(f32[8,49]{1,0:T(8,128)S(1)} %add_rsqrt_fusion.2) | copy-start | bytes 4708
  243.6 122.5 %copy-start.25 = (bf16[8,49,1024]{2,1,0:T(8,128)(2,1)}, bf16[8,49,1024]{2,1,0:T(8,128)(2,1)S(1)}, u32[]{:S(2)}) copy-start(bf16[8,49,1024]{2,1,0:T(8,128)(2,1)S(1)} %add_convert_fusion.2) | copy-start | bytes 2408452
  366.1 58.7 %copy-start.79 = (f32[1024]{0:T(1024)S(1)}, f32[1024]{0:T(1024)}, u32[]{:S(2)}) copy-start(f32[1024]{0:T(1024)} %add.316) | copy-start | bytes 12292
  504.9 17.2 copy-start.23
  505.1 17.1 copy-start.73
  651.7 397.2 %reduce-scatter.11.cloned.1.call-start = ((), (), s32[]{:S(2)}) async-start(), calls=%async_computation.12 | async-start | bytes 25362432 | tf_op jit(solution)/shard_map/reduce_scatter | solution.py:26
  753.9 544.8 %reduce-scatter.9.cloned.1.call-start = ((), (), s32[]{:S(2)}) async-start(), calls=%async_computation.11 | async-start | bytes 25362432 | tf_op jit(solution)/shard_map/reduce_scatter | solution.py:26
  799.8 748.9 %reduce-scatter.7.cloned.1.call-start = ((), (), s32[]{:S(2)}) async-start(), calls=%async_computation.10 | async-start | bytes 25362432 | tf_op jit(solution)/shard_map/reduce_scatter | solution.py:26
  819.3 954.5 %reduce-scatter.5.cloned.1.call-start = ((), (), s32[]{:S(2)}) async-start(), calls=%async_computation.9 | async-start | bytes 12681216 | tf_op jit(solution)/shard_map/reduce_scatter | solution.py:26
  (73 other events, 631.6 us)
Sparse Core Ops, SparseCore 0:
  11.7 67.8 all-gather.22
  83.4 62.7 all-gather.20
  149.3 65.6 all-gather.18
  217.8 66.9 all-gather.10
  287.6 67.1 all-gather.14
  357.6 67.1 all-gather.12
  428.3 67.1 all-gather.16
  651.8 145.7 all-reduce.5
  803.0 245.8 reduce-scatter.10
  1054.1 244.6 reduce-scatter.8
  1304.1 244.6 reduce-scatter.6
  1554.1 219.6 reduce-scatter.4

commit v2 on v1

v2 whole, which is shorter than its diff:
```python
import functools

import jax
import jax.numpy as jnp
from jax import lax
from jax.experimental import pallas as pl
from jax.experimental.pallas import tpu as pltpu
from jax.sharding import PartitionSpec as P

MESH = pl.DeviceIdType.MESH
ORDERS = (('x', 'y', 'z'), ('y', 'z', 'x'), ('z', 'x', 'y'))
COLS = ((0, 384), (384, 384), (768, 256))
N_CH = 4
STEM, HEAD = 4, 5
bf16, f32 = jnp.bfloat16, jnp.float32


def my_place():
    f = lax.axis_index('fsdp')
    return {'x': lax.axis_index('tp'), 'z': f // 8, 'y': (f // 2) % 4, 'k': f % 2}


def moved(place, dim, step):
    new = dict(place)
    new[dim] = 1 - place['k'] if dim == 'k' else (place[dim] + step) % 4
    return new


def device(place):
    return {'tp': place['x'], 'fsdp': (place['z'] * 4 + place['y']) * 2 + place['k']}


def meet_neighbours(me):
    barrier = pltpu.get_barrier_semaphore()
    for dim in 'xyz':
        for step in (1, 3):
            pl.semaphore_signal(barrier, inc=1, device_id=device(moved(me, dim, step)), device_id_type=MESH)
    pl.semaphore_signal(barrier, inc=1, device_id=device(moved(me, 'k', 1)), device_id_type=MESH)
    pl.semaphore_wait(barrier, 7)


class Sender:
    def __init__(self, send_sems, recv_sems):
        self.send_sems, self.recv_sems, self.count, self.started = send_sems, recv_sems, 0, []

    def start(self, src, dst, target):
        n = self.count
        self.count += 1
        copy = pltpu.make_async_remote_copy(src_ref=src, dst_ref=dst, send_sem=self.send_sems.at[n],
                                            recv_sem=self.recv_sems.at[n], device_id=device(target),
                                            device_id_type=MESH)
        copy.start()
        self.started.append(copy)
        return copy


GATHER_COPIES = 7 * 8 + 16 * 4 + 16 * 4


def gather_kernel(pc, ps, ph, wc, ws, wh, send_sems, recv_sems, local_sems):
    me = my_place()
    other = moved(me, 'k', 1)
    meet_neighbours(me)
    sender = Sender(send_sems, recv_sems)
    every = pl.ds(0, 4)

    def view(kind, colour, block, half=None, group=None, k=None):
        k = me['k'] if k is None else k
        x, z, y = block['x'], block['z'], block['y']
        r0, rn = (0, 32) if half is None else (16 * half, 16)
        if kind == 'ch':
            c0, cn = COLS[colour]
            return wc.at[every if group is None else group, x, z, y, k, pl.ds(r0, rn), pl.ds(c0, cn)]
        cols = pl.ds(0, 1024) if x is every else pl.ds(pl.multiple_of(x * 256, 256), 256)
        if kind == 'stem':
            return ws.at[z, y, k, pl.ds(32 * colour + r0, rn), cols]
        return wh.at[z, y, k, pl.ds(r0, rn), cols]

    def piece(kind, colour):
        if kind == 'ch':
            c0, cn = COLS[colour]
            return pc.at[:, :, pl.ds(c0, cn)]
        if kind == 'stem':
            return ps.at[pl.ds(32 * colour, 32), :]
        return ph.at[:, :]

    early = [('stem', 0), ('stem', 1), ('stem', 2), ('ch', 0), ('ch', 1), ('ch', 2), ('head', 2)]
    late = [('stem', c, None) for c in range(3)] + [('ch', c, g) for g in range(N_CH) for c in range(3)]
    late += [('head', 2, None)]

    own = [pltpu.make_async_copy(piece(kind, c), view(kind, c, me), local_sems.at[i])
           for i, (kind, c) in enumerate(early)]
    for copy in own:
        copy.start()

    def exchange(unit, dim, block, src=None):
        kind, c = unit[:2]
        g = unit[2] if len(unit) > 2 else None
        mine = view(kind, c, block, group=g)
        source = mine if src is None else src
        return [sender.start(source, mine, moved(me, dim, step)) for step in (1, 3)]

    def forward(unit, dim, block):
        kind, c = unit[:2]
        g = unit[2] if len(unit) > 2 else None
        out = []
        for half, (origin, target) in enumerate(((3, 1), (1, 3))):
            part = view(kind, c, {**block, dim: (me[dim] + origin) % 4}, half=half, group=g)
            out.append(sender.start(part, part, moved(me, dim, target)))
        return out

    def arrived(copies):
        for copy in copies:
            copy.wait_recv()

    first, second, third, swaps = {}, {}, {}, []
    for u in early:
        first[u] = exchange(u, ORDERS[u[1]][0], me, piece(*u))
    for copy in own:
        copy.wait()
    for u in early:
        arrived(first[u])
        first[u] = forward(u, ORDERS[u[1]][0], me)
    for u in early:
        d1, d2, _ = ORDERS[u[1]]
        arrived(first[u])
        second[u] = exchange(u, d2, {**me, d1: every})
    for u in early:
        d1, d2, _ = ORDERS[u[1]]
        arrived(second[u])
        second[u] = forward(u, d2, {**me, d1: every})
    done = set()
    for u in late:
        d1, d2, d3 = ORDERS[u[1]]
        if u[:2] not in done:
            arrived(second[u[:2]])
            done.add(u[:2])
        plane = {**me, d1: every, d2: every}
        third[u] = exchange(u, d3, plane)
        mine = view(u[0], u[1], plane, group=u[2])
        swaps.append(sender.start(mine, mine, other))
    for u in late:
        d1, d2, d3 = ORDERS[u[1]]
        plane = {**me, d1: every, d2: every}
        arrived(third[u])
        third[u] = forward(u, d3, plane)
        for step in (1, 3):
            part = view(u[0], u[1], {**plane, d3: (me[d3] + step) % 4}, group=u[2])
            swaps.append(sender.start(part, part, other))
    for u in late:
        d1, d2, d3 = ORDERS[u[1]]
        plane = {**me, d1: every, d2: every}
        arrived(third[u])
        part = view(u[0], u[1], {**plane, d3: (me[d3] + 2) % 4}, group=u[2])
        swaps.append(sender.start(part, part, other))
    arrived(swaps)
    for copy in sender.started:
        copy.wait_send()
    assert sender.count == GATHER_COPIES, sender.count


def gather_weights(pc, ps, ph):
    any_spec = pl.BlockSpec(memory_space=pl.ANY)
    vmem = pl.BlockSpec(memory_space=pltpu.VMEM)
    return pl.pallas_call(
        gather_kernel, name='gather_weights',
        out_shape=[jax.ShapeDtypeStruct((N_CH, 4, 4, 4, 2, 32, 1024), bf16),
                   jax.ShapeDtypeStruct((4, 4, 2, 96, 1024), bf16),
                   jax.ShapeDtypeStruct((4, 4, 2, 32, 1024), bf16)],
        in_specs=[vmem] * 3, out_specs=[any_spec] * 3,
        scratch_shapes=[pltpu.SemaphoreType.DMA((GATHER_COPIES,)), pltpu.SemaphoreType.DMA((GATHER_COPIES,)),
                        pltpu.SemaphoreType.DMA((7,))],
        compiler_params=pltpu.CompilerParams(collective_id=0, has_side_effects=True),
        cost_estimate=pl.CostEstimate(flops=90_000_000_000, bytes_accessed=80_000_000, transcendentals=0),
    )(pc, ps, ph)


GROUPS = (STEM, 3, 2, 1, 0, HEAD)
UNITS = tuple((g, c) for g in GROUPS for c in (2, 0, 1) if g != HEAD or c == 2)
REDUCE_COPIES = 13 * len(UNITS)


def reduce_scratch():
    per = []
    for c in range(3):
        n = COLS[c][1]
        many = sum(1 for u in UNITS if u[1] == c)
        lead = ((4, 4), (4,), ())
        b = {'C': pltpu.VMEM((4, 4, 4, 2, 32, n), bf16), 'D': pltpu.VMEM((4, 4, 4, 32, n), bf16),
             'S1': pltpu.VMEM((4, 4, 32, n), f32), 'S2': pltpu.VMEM((4, 32, n), f32)}
        for ph in range(3):
            for name in ('opp', 'rig', 'lef'):
                b[f'{name}{ph}'] = pltpu.VMEM(lead[ph] + (32, n), bf16)
            for name in ('half0', 'half1'):
                b[f'{name}{ph}'] = pltpu.VMEM((many,) + lead[ph] + (16, n), bf16)
            for name in ('froml', 'fromr'):
                b[f'{name}{ph}'] = pltpu.VMEM((many,) + lead[ph] + (32, n), bf16)
        per.append(b)
    return per


def transposed_product(left, right):
    return lax.dot_general(left, right, (((0,), (0,)), ((), ())), preferred_element_type=f32)


def reduce_kernel(*refs):
    wides, narrows, (head_l, head_r) = refs[:5], refs[5:10], refs[10:12]
    out_c, out_s, out_h = refs[12:15]
    wide, narrow, per, send_sems, recv_sems, load_sems, credit = refs[15:]
    me = my_place()
    other = moved(me, 'k', 1)
    k = me['k']
    loads = {}

    def load(i):
        g = GROUPS[i]
        if g == HEAD:
            return
        cols = 3072 if g == STEM else 4096
        loads[g] = [pltpu.make_async_copy(wides[g], wide.at[i % 2, :, pl.ds(0, cols)], load_sems.at[i % 2, 0]),
                    pltpu.make_async_copy(narrows[g], narrow.at[i % 2], load_sems.at[i % 2, 1])]
        for copy in loads[g]:
            copy.start()

    load(0)
    meet_neighbours(me)
    sender = Sender(send_sems, recv_sems)
    busy = {}

    def free(key):
        for copy in busy.pop(key, ()):
            copy.wait_send()

    def make(g, c):
        i = GROUPS.index(g)
        slot = i % 2
        if g != HEAD and c == 2:
            for copy in loads[g]:
                copy.wait()
            load(i + 1)
        if g == STEM:
            if c != 2:
                return
            for d in range(3):
                free(('C', d))

            @pl.loop(0, 32)
            def _(j):
                b = j // 4
                t = j % 4
                z, y2 = b // 2, b % 2
                left = wide[slot, :, pl.ds(pl.multiple_of(b * 384, 128), 384)]
                right = narrow[slot, :, pl.ds(pl.multiple_of(t * 256, 128), 256)]
                prod = transposed_product(left, right).astype(bf16).reshape(2, 2, 3, 32, 256)
                for d in range(3):
                    per[d]['C'][t, z, pl.ds(y2 * 2, 2), :, :, pl.ds(0, 256)] = prod[:, :, d]
        elif g == HEAD:
            free(('C', c))

            @pl.loop(0, 4)
            def _(t):
                right = head_r[:, pl.ds(pl.multiple_of(t * 256, 128), 256)]
                prod = transposed_product(head_l[...], right)
                per[c]['C'][t] = prod.astype(bf16).reshape(4, 4, 2, 32, 256)
        else:
            free(('C', c))
            c0, n = COLS[c]

            @pl.loop(0, 16)
            def _(j):
                t, z = j // 4, j % 4
                if g % 2 == 0:
                    left = narrow[slot, :, pl.ds(pl.multiple_of(z * 256, 128), 256)]
                    right = wide[slot, :, pl.ds(pl.multiple_of(t * 1024 + c0, 128), n)]
                else:
                    left = wide[slot, :, pl.ds(pl.multiple_of(j * 256, 128), 256)]
                    right = narrow[slot, :, pl.ds(c0, n)]
                per[c]['C'][t, z] = transposed_product(left, right).astype(bf16).reshape(4, 2, 32, n)

    class Unit:
        def __init__(self, g, c):
            self.g, self.c = g, c
            same = [u for u in UNITS if u[1] == c]
            self.index = same.index((g, c))
            self.last = self.index == len(same) - 1
            self.n = COLS[c][1] if g < N_CH else 256
            self.buf = per[c]
            self.dims = ORDERS[c]

        def cut(self, name, *at):
            ref = self.buf[name]
            rest = len(ref.shape) - len(at) - 1
            return ref.at[(*at, *[slice(None)] * rest, pl.ds(0, self.n))]

        def share(self, phase, p, e, rows):
            r = pl.ds(*rows)
            cols = pl.ds(0, self.n)
            if phase == 0:
                at = dict(zip(self.dims, (p, *e)))
                at = (at['x'], at['z'], at['y'])
                return (self.buf['C'][(*at, k, r, cols)].astype(f32) + self.buf['D'][(*at, r, cols)].astype(f32))
            return self.buf[f'S{phase}'][(p, *e, r, cols)]

        def each(self, phase, body):
            if phase == 2:
                body(())
            elif phase == 1:
                pl.loop(0, 4)(lambda i: body((i,)))
            else:
                pl.loop(0, 16)(lambda i: body((i // 4, i % 4)))

        def start(self):
            make(self.g, self.c)
            if self.index:
                pl.semaphore_wait(credit.at[self.c], 1)
            cols = pl.ds(0, self.n)
            src = self.buf['C'].at[:, :, :, 1 - k, :, cols]
            self.swap = sender.start(src, self.buf['D'].at[:, :, :, :, cols], other)
            busy['C', self.c] = [self.swap]

        def opposite(self, phase):
            if phase == 0:
                self.swap.wait_recv()
            p = (me[self.dims[phase]] + 2) % 4
            free((f'opp{phase}', self.c))
            cols = pl.ds(0, self.n)

            def body(e):
                self.buf[f'opp{phase}'][(*e, slice(None), cols)] = self.share(phase, p, e, (0, 32)).astype(bf16)
            self.each(phase, body)
            lead = [slice(None)] * (2 - phase)
            copies = []
            for half, step in ((0, 1), (1, 3)):
                src = self.buf[f'opp{phase}'].at[(*lead, pl.ds(16 * half, 16), cols)]
                dst = self.cut(f'half{half}{phase}', self.index)
                copies.append(sender.start(src, dst, moved(me, self.dims[phase], step)))
            busy[f'opp{phase}', self.c] = copies
            self.halves = copies

        def beside(self, phase):
            copies = []
            for half, step, name, dst in ((0, 1, 'rig', 'froml'), (1, 3, 'lef', 'fromr')):
                self.halves[half].wait_recv()
                free((f'{name}{phase}', self.c))
                p = (me[self.dims[phase]] + step) % 4
                cols = pl.ds(0, self.n)
                whole, got = self.buf[f'{name}{phase}'], self.buf[f'half{half}{phase}']

                def body(e):
                    mine = self.share(phase, p, e, (16 * half, 16)) + got[(self.index, *e, slice(None), cols)].astype(f32)
                    whole[(*e, pl.ds(16 * half, 16), cols)] = mine.astype(bf16)
                    plain = self.share(phase, p, e, (16 - 16 * half, 16))
                    whole[(*e, pl.ds(16 - 16 * half, 16), cols)] = plain.astype(bf16)
                self.each(phase, body)
                copy = sender.start(self.cut(f'{name}{phase}'), self.cut(f'{dst}{phase}', self.index),
                                    moved(me, self.dims[phase], step))
                busy[f'{name}{phase}', self.c] = [copy]
                copies.append(copy)
            self.wholes = copies

        def total(self, phase):
            for copy in self.wholes:
                copy.wait_recv()
            p = me[self.dims[phase]]
            cols = pl.ds(0, self.n)

            def body(e):
                got = [self.buf[f'{name}{phase}'][(self.index, *e, slice(None), cols)].astype(f32)
                       for name in ('froml', 'fromr')]
                value = self.share(phase, p, e, (0, 32)) + got[0] + got[1]
                if phase < 2:
                    self.buf[f'S{phase + 1}'][(*e, slice(None), cols)] = value
                elif self.g == STEM:
                    out_s[pl.ds(32 * self.c, 32), :] = value
                elif self.g == HEAD:
                    out_h[...] = value
                else:
                    out_c[self.g, :, pl.ds(*COLS[self.c])] = value
            self.each(phase, body)
            if phase == 0 and not self.last:
                pl.semaphore_signal(credit.at[self.c], inc=1, device_id=device(other), device_id_type=MESH)

        def run(self, stage):
            if stage == 0:
                self.start()
            elif stage == 7:
                self.total(2)
            elif stage % 2 == 0:
                self.beside(stage // 2 - 1)
            else:
                if stage > 1:
                    self.total(stage // 2 - 1)
                self.opposite(stage // 2)

    units = [Unit(g, c) for g, c in UNITS]
    for slot in range(len(units) + 7):
        for stage in range(7, -1, -1):
            if 0 <= slot - stage < len(units):
                units[slot - stage].run(stage)
    for key in list(busy):
        free(key)
    assert sender.count == REDUCE_COPIES, sender.count


def reduce_gradients(wides, narrows, head_l, head_r):
    any_spec = pl.BlockSpec(memory_space=pl.ANY)
    vmem = pl.BlockSpec(memory_space=pltpu.VMEM)
    rows = narrows[0].shape[0]
    return pl.pallas_call(
        reduce_kernel, name='reduce_gradients',
        out_shape=[jax.ShapeDtypeStruct((N_CH, 32, 1024), f32), jax.ShapeDtypeStruct((96, 256), f32),
                   jax.ShapeDtypeStruct((32, 256), f32)],
        in_specs=[any_spec] * 10 + [vmem] * 2, out_specs=[vmem] * 3,
        scratch_shapes=[pltpu.VMEM((2, rows, 4096), bf16), pltpu.VMEM((2, rows, 1024), bf16), reduce_scratch(),
                        pltpu.SemaphoreType.DMA((REDUCE_COPIES,)), pltpu.SemaphoreType.DMA((REDUCE_COPIES,)),
                        pltpu.SemaphoreType.DMA((2, 2)), pltpu.SemaphoreType.REGULAR((3,))],
        compiler_params=pltpu.CompilerParams(collective_id=1, has_side_effects=True, vmem_limit_bytes=64 * 1024 * 1024 - 65536),
        cost_estimate=pl.CostEstimate(flops=100_000_000_000, bytes_accessed=80_000_000, transcendentals=0),
    )(*wides, *narrows, head_l, head_r)


EPS = 1e-6
CHANNEL_AXES = ('tp', 'fsdp')


def product(form, left, right):
    return jnp.einsum(form, left, right, preferred_element_type=f32)


def bf(x):
    return x.astype(bf16)


def norm_forward(values, gain, shift):
    mean_val = jnp.mean(values, axis=-1, keepdims=True)
    cent = values - mean_val
    inv_std = lax.rsqrt(jnp.mean(cent * cent, axis=-1, keepdims=True) + EPS)
    standard = cent * inv_std
    return standard * gain + shift, standard, inv_std


def norm_backward(grad_out, gain, standard, inv_std):
    gs = grad_out * gain
    m0 = jnp.mean(gs, axis=-1, keepdims=True)
    m1 = jnp.mean(gs * standard, axis=-1, keepdims=True)
    return inv_std * (gs - m0 - standard * m1)


def gelu_grad(pre_act, grad_out):
    return jax.vjp(jax.nn.gelu, pre_act)[1](grad_out)[0]


def weight_specs():
    vec_spec = P(CHANNEL_AXES)
    layer_vec = P(None, CHANNEL_AXES)
    return (P('fsdp', 'tp'), vec_spec, layer_vec, layer_vec, P(None, None, 'fsdp'), P(None, 'fsdp'),
            P(None, 'fsdp', None), layer_vec, layer_vec, P(None, 'fsdp', 'tp'), layer_vec,
            P(None, CHANNEL_AXES, None), layer_vec, vec_spec, vec_spec, P('fsdp', 'tp'), P('tp'))


def solution(mesh):
    fs = mesh.shape['fsdp']
    tp = mesh.shape['tp']
    nd = fs * tp

    def step(patches, labels, w_stem, b_stem, ln1_g, ln1_b, w_tok1, b_tok1, w_tok2,
             ln2_g, ln2_b, w_ch1, b_ch1, w_ch2, b_ch2, lnf_g, lnf_b, w_head, b_head):
        t = lax.axis_index('tp')
        nl = w_tok1.shape[0]
        bl = patches.shape[0] // tp
        tokens = patches.shape[1]
        rows = bl * tokens
        total_images = bl * nd
        pat = lax.dynamic_slice_in_dim(patches, t * bl, bl, 0)
        pat = pat.transpose(1, 0, 2).reshape(rows, -1)
        lab = lax.dynamic_slice_in_dim(labels, t * bl, bl, 0)

        vecs = [b_stem[None], ln1_g, ln1_b, ln2_g, ln2_b, b_ch2, lnf_g[None], lnf_b[None]]
        vec_rows = jnp.concatenate(vecs, axis=0)
        n_rows = vec_rows.shape[0]
        pieces = [vec_rows.reshape(-1), b_ch1.reshape(-1), b_tok1.reshape(-1), b_head.reshape(-1),
                  w_tok1.reshape(-1), w_tok2.reshape(-1)]
        pack = jnp.concatenate(pieces)
        pack = jnp.pad(pack, (0, (-pack.shape[0]) % 1024))
        small = lax.all_gather(pack, CHANNEL_AXES, axis=0, tiled=False).reshape(tp, fs, -1)
        offs = []
        o = 0
        for p in pieces:
            offs.append(small[:, :, o:o + p.shape[0]])
            o += p.shape[0]
        vec_all = offs[0].reshape(tp, fs, n_rows, -1).transpose(2, 0, 1, 3).reshape(n_rows, -1)
        bch1 = offs[1].reshape(tp, fs, nl, -1).transpose(2, 0, 1, 3).reshape(nl, -1)
        btok1 = offs[2][0].reshape(fs, nl, -1).transpose(1, 0, 2).reshape(nl, -1)
        bhead = offs[3][:, 0]
        wtok1 = bf(offs[4][0].reshape(fs, nl, tokens, -1).transpose(1, 2, 0, 3).reshape(nl, tokens, -1))
        wtok2 = bf(offs[5][0].reshape(fs, nl, -1, tokens).transpose(1, 0, 2, 3).reshape(nl, -1, tokens))
        bstem = vec_all[0]
        l1g, l1b, l2g, l2b, bc2 = [vec_all[1 + nl * i:1 + nl * (i + 1)] for i in range(5)]
        lfg, lfb = vec_all[1 + 5 * nl], vec_all[2 + 5 * nl]

        classes = w_head.shape[1]
        pad_cls = 256 - classes
        pc = jnp.stack([bf(w_ch1[0]), bf(w_ch2[0]), bf(w_ch1[1]), bf(w_ch2[1])])
        ph = jnp.pad(bf(w_head), ((0, 0), (0, pad_cls)))
        wc, ws, wh = gather_weights(pc, bf(w_stem), ph)
        c = w_stem.shape[1] * tp
        ws = ws.reshape(-1, c)
        wh = wh.reshape(c, -1)
        wc = wc.reshape(2 * nl, tp, c, c)
        bhead = jnp.pad(bhead, ((0, 0), (0, pad_cls)), constant_values=-1e30).reshape(-1)
        col = lab // classes * 256 + lab % classes

        resid = product('rp,pc->rc', pat, ws) + bstem
        saved = []
        for l in range(nl):
            normed, n1s, n1i = norm_forward(resid, l1g[l], l1b[l])
            normed = bf(normed).reshape(tokens, bl, c)
            tok_pre = product('sbc,sj->bcj', normed, wtok1[l]) + btok1[l]
            tok_act = bf(jax.nn.gelu(tok_pre))
            resid = resid + product('bcj,js->sbc', tok_act, wtok2[l]).reshape(rows, c)
            normed2, n2s, n2i = norm_forward(resid, l2g[l], l2b[l])
            full_in = bf(normed2)
            ch_pre = [product('rc,cd->rd', full_in, wc[2 * l, i]) + bch1[l, i * c:(i + 1) * c] for i in range(tp)]
            ch_act = [bf(jax.nn.gelu(p)) for p in ch_pre]
            for i in range(tp):
                resid = resid + product('rd,dc->rc', ch_act[i], wc[2 * l + 1, i])
            resid = resid + bc2[l]
            saved.append((normed, n1s, n1i, tok_pre, tok_act, n2s, n2i, full_in, ch_pre, ch_act))

        pooled = jnp.mean(resid.reshape(tokens, bl, c), axis=0)
        head_in, hs, hi = norm_forward(pooled, lfg, lfb)
        head_bf = bf(head_in)
        logits = product('bc,ck->bk', head_bf, wh) + bhead
        is_label = jnp.arange(logits.shape[1])[None, :] == col[:, None]
        row_max = jnp.max(logits, axis=1, keepdims=True)
        ex = jnp.exp(logits - row_max)
        es = jnp.sum(ex, axis=1, keepdims=True)
        log_norm = row_max + jnp.log(es)
        loss_loc = jnp.sum(log_norm) - jnp.sum(jnp.where(is_label, logits, 0.0))

        d_logits = (ex / es - is_label.astype(f32)) / total_images
        dlb = bf(d_logits)
        g_bhead = jnp.sum(d_logits, axis=0)
        d_hin = product('bk,ck->bc', dlb, wh)
        g_lfg = jnp.sum(d_hin * hs, axis=0)
        g_lfb = jnp.sum(d_hin, axis=0)
        d_pooled = norm_backward(d_hin, lfg, hs, hi)
        d_resid = jnp.broadcast_to((d_pooled / tokens)[None], (tokens, bl, c)).reshape(rows, c)

        wides, narrows = [None] * 5, [None] * 5
        sm = {}
        for l in reversed(range(nl)):
            normed, n1s, n1i, tok_pre, tok_act, n2s, n2i, full_in, ch_pre, ch_act = saved[l]
            sm['b_ch2', l] = jnp.sum(d_resid, axis=0)
            dob = bf(d_resid)
            wides[2 * l + 1], narrows[2 * l + 1] = jnp.concatenate(ch_act, axis=1), dob
            d_pre = [gelu_grad(ch_pre[i], product('rc,dc->rd', dob, wc[2 * l + 1, i])) for i in range(tp)]
            sm['b_ch1', l] = jnp.concatenate([jnp.sum(d, axis=0) for d in d_pre])
            dpb = [bf(d) for d in d_pre]
            wides[2 * l], narrows[2 * l] = jnp.concatenate(dpb, axis=1), full_in
            d_n2 = sum(product('rd,cd->rc', dpb[i], wc[2 * l, i]) for i in range(tp))
            sm['ln2_g', l] = jnp.sum(d_n2 * n2s, axis=0)
            sm['ln2_b', l] = jnp.sum(d_n2, axis=0)
            d_mid = d_resid + norm_backward(d_n2, l2g[l], n2s, n2i)
            dmb = bf(d_mid).reshape(tokens, bl, c)
            sm['w_tok2', l] = product('bcj,sbc->js', tok_act, dmb)
            d_tp = gelu_grad(tok_pre, product('sbc,js->bcj', dmb, wtok2[l]))
            sm['b_tok1', l] = jnp.sum(d_tp, axis=(0, 1))
            dtb = bf(d_tp)
            sm['w_tok1', l] = product('sbc,bcj->sj', normed, dtb)
            d_n1 = product('bcj,sj->sbc', dtb, wtok1[l]).reshape(rows, c)
            sm['ln1_g', l] = jnp.sum(d_n1 * n1s, axis=0)
            sm['ln1_b', l] = jnp.sum(d_n1, axis=0)
            d_resid = d_mid + norm_backward(d_n1, l1g[l], n1s, n1i)
        g_bstem = jnp.sum(d_resid, axis=0)
        wides[4], narrows[4] = pat, bf(d_resid)

        def st(key):
            return jnp.stack([sm[key, l] for l in range(nl)])
        parts = [g_bstem, st('ln1_g'), st('ln1_b'), st('ln2_g'), st('ln2_b'), st('b_ch2'), g_lfg, g_lfb,
                 st('b_ch1'), st('b_tok1'), g_bhead, st('w_tok1'), st('w_tok2'), loss_loc[None]]
        flat = jnp.concatenate([p.reshape(-1) for p in parts])
        flat = jnp.pad(flat, (0, (-flat.shape[0]) % 1024))
        tot = lax.psum(flat, CHANNEL_AXES)

        g_c, g_s, g_h = reduce_gradients(wides, narrows, head_bf, dlb)
        g_ch1, g_ch2 = g_c[0::2], g_c[1::2]
        g_head = g_h[:, :classes]

        out = []
        o = 0
        for p in parts:
            out.append(tot[o:o + p.size].reshape(p.shape))
            o += p.size
        f = lax.axis_index('fsdp')
        dev = t * fs + f

        def own(x, n, i, ax):
            size = x.shape[ax] // n
            return lax.dynamic_slice_in_dim(x, i * size, size, ax)
        (gb, g1g, g1b, g2g, g2b, gc2, gfg, gfb, gc1, gt1, gbh, gw1, gw2, ls) = out
        loss = ls[0] / total_images
        return (loss, g_s, own(gb, nd, dev, 0), own(g1g, nd, dev, 1), own(g1b, nd, dev, 1),
                own(gw1, fs, f, 2), own(gt1, fs, f, 1), own(gw2, fs, f, 1),
                own(g2g, nd, dev, 1), own(g2b, nd, dev, 1), g_ch1, own(gc1, nd, dev, 1),
                g_ch2, own(gc2, nd, dev, 1), own(gfg, nd, dev, 0), own(gfb, nd, dev, 0),
                g_head, own(gbh.reshape(tp, 256), tp, t, 0)[0, :classes])

    specs = weight_specs()
    return jax.shard_map(step, mesh=mesh, in_specs=(P('fsdp', None, None), P('fsdp')) + specs,
                         out_specs=(P(),) + specs, check_vma=False)
```

time: 1790 us -> 605 us (0.34)
  waiting for transfers between devices: 1270 us -> 0.04 us
  Pallas kernels: 0 us -> 299 us
  local copies, waits for them, and re-layouts: 216 us -> 50.3 us
  matrix products: 219 us -> 185 us
  other arithmetic: 61.7 us -> 41.7 us
    reduce_scatter x4 -> x0, waiting for transfers between devices: 908 us -> none  [scatter_all(): lax.psum_scatter(x.astype(RS_DTYPE), ALL_AXES, scatter_dimension=0, tiled...]
    all_gather x7 -> x1, waiting for transfers between devices: 355 us -> 0.01 us  [step(): lax.all_gather(pack, CHANNEL_AXES, axis=0, tiled=False).reshape(tp, fs, -1)]
    pallas_call x0 -> x2, Pallas kernels: none -> 299 us  [the longest x1 198 us: reduce_gradients(): pl.pallas_call(reduce_kernel, name='reduce_gradients', out_shape=[jax.Sha...]
    dot_general x6 -> x0, local copies, waits for them, and re-layouts: 53 us -> none  [product(): return jnp.einsum(form, left, right, preferred_element_type=jnp.float32)]
    reshape x9 -> x2, local copies, waits for them, and re-layouts: 39.8 us -> 5.02 us  [the longest x1 3.27 us: step(): pat = pat.transpose(1, 0, 2).reshape(rows, -1)]
    dot_general x29 -> x47, matrix products: 219 us -> 185 us  [product(): return jnp.einsum(form, left, right, preferred_element_type=f32)]
    concatenate x1 -> x0, local copies, waits for them, and re-layouts: 29.7 us -> none  [step(): ra = scatter_all(jnp.concatenate([big2[1], gh_full], axis=1))]
    concatenate x3 -> x6, other arithmetic: 34 us -> 8.13 us  [the longest x2 4.11 us: step(): jnp.concatenate(ch_act, axis=1)]
  transfers between devices with their start and end apart: 12 -> 2, of which waited for: 11 -> 0; matrix products, arithmetic and copies ran while one was open for 19% -> 2% of each run, Pallas kernels for 0% -> 50%
where the time goes in v2:
time: 605 us; the launch traced here: 595 us
  Pallas kernels  299 us (49%)
  matrix products  185 us (31%)
  local copies, waits for them, and re-layouts  50.3 us (8%)
  other arithmetic  41.7 us (7%)
  between operations  19.1 us (3%)
    pallas_call x1, Pallas kernels, reduce_gradients(): pl.pallas_call(reduce_kernel, name='reduce_gradients', out_shape=[jax.Sha...  198 us
    dot_general x47, matrix products, product(): return jnp.einsum(form, left, right, preferred_element_type=f32)  185 us
    pallas_call x1, Pallas kernels, gather_weights(): pl.pallas_call(gather_kernel, name='gather_weights', out_shape=[jax.Shape...  101 us
  transfers between devices with their start and end apart: 2, of which 0 were waited for; matrix products, arithmetic and copies ran while one was open for 2% of the time, Pallas kernels for 50%

profile of v2, /device:TPU:0, one launch (start us, length us, event | category | flops | bytes accessed | tf_op | source)
XLA Modules:
  0.0 595.0 jit_solution(14974239764828709614)
XLA Ops:
  19.8 100.8 %gather_weights.1 = (bf16[4,4,4,4,2,32,1024]{6,5,4,3,2,1,0:T(8,128)(2,1)}, bf16[4,4,2,96,1024]{4,3,2,1,0:T(8,128)(2,1)}, bf16[4,4,2,32,1024]{4,3,2,1,0:T(8,128)(2,1)}) custom-call(bf16[4,32,1024]{2,1,0:T(8,128)(2,1)} %pad_maximum_fusion.4.pc, bf16[96,256]{1,0:T(8,128)(2,1)} %convert_element_type.136.ps, bf16[32,256]{1,0:T(8,128)(2,1)} %pad.16.ph), custom_call_target="tpu_custom_call" | custom-call | flops 89999998976 | bytes 80000000 | tf_op jit(solution)/shard_map/gather_weights/pallas_call | solution.py:165
  121.3 3.3 dynamic-slice_bitcast_fusion.refs_4_
  135.3 5.0 fusion.174
  141.3 9.5 %multiply_convert_fusion.1 = (bf16[8,1024,512]{2,1,0:T(8,128)(2,1)S(1)}, f32[8,1024,512]{2,1,0:T(8,128)}) fusion(f32[512]{0:T(512)S(1)} %copy-done.58, bf16[49,512,1]{0,1,2:T(8,128)(2,1)S(1)} %bitcast.435, bf16[49,8,1024]{2,1,0:T(8,128)(2,1)S(1)} %fusion.138), kind=kOutput, calls=%fused_computation.17 | convolution fusion | flops 452984832 | bytes 26020864 | tf_op jit(solution)/shard_map/sbc,sj->bcj/dot_general | solution.py:427
  156.3 4.1 multiply_convert_fusion.6
  160.4 4.1 multiply_convert_fusion.7
  167.1 4.1 multiply_convert_fusion.8
  173.9 4.1 multiply_convert_fusion.9
  182.5 3.0 fusion.175
  186.7 9.8 %multiply_convert_fusion = (bf16[8,1024,512]{2,1,0:T(8,128)(2,1)S(1)}, f32[8,1024,512]{2,1,0:T(8,128)}) fusion(f32[512]{0:T(512)S(1)} %copy-done.60, bf16[49,512,1]{0,1,2:T(8,128)(2,1)S(1)} %bitcast.439, bf16[49,8,1024]{2,1,0:T(8,128)(2,1)S(1)} %fusion.139), kind=kOutput, calls=%fused_computation.16 | convolution fusion | flops 452984832 | bytes 26020864 | tf_op jit(solution)/shard_map/sbc,sj->bcj/dot_general | solution.py:427
  201.1 3.3 multiply_convert_fusion.2
  204.3 3.0 multiply_convert_fusion.3
  209.9 3.0 multiply_convert_fusion.4
  215.5 3.0 multiply_convert_fusion.5
  223.3 3.0 bitcast_reduce_fusion
  232.2 4.1 fusion.161
  236.3 4.1 fusion.160
  240.4 4.1 fusion.159
  244.4 4.1 fusion.158
  258.5 3.8 multiply_reduce_fusion.2
  266.4 17.0 %fusion.177 = (f32[512]{0:T(512)}, bf16[8,1024,512]{2,1,0:T(8,128)(2,1)S(1)}) fusion(f32[8,1024,512]{2,1,0:T(8,128)} %get-tuple-element.200, f32[512]{0:T(512)S(1)} %copy-done.60, bf16[512,49,1]{1,0,2:T(8,128)(2,1)S(1)} %bitcast.438, bf16[49,8,1024]{2,1,0:T(8,128)(2,1)S(1)} %get-tuple-element.114), kind=kOutput, calls=%fused_computation.334 | convolution fusion | flops 503315968 | bytes 26022912 | tf_op jit(solution)/shard_map/sbc,js->bcj/dot_general | solution.py:427
  285.8 3.2 fusion.147
  291.1 3.7 fusion.150
  296.5 3.6 fusion.157
  300.1 3.6 fusion.156
  303.7 3.6 fusion.155
  307.3 3.6 fusion.154
  320.8 4.3 multiply_reduce_fusion.3
  329.1 16.4 %fusion.178 = (f32[512]{0:T(512)S(1)}, bf16[8,1024,512]{2,1,0:T(8,128)(2,1)S(1)}) fusion(f32[8,1024,512]{2,1,0:T(8,128)} %get-tuple-element.188, f32[512]{0:T(512)S(1)} %copy-done.59, bf16[512,49,1]{1,0,2:T(8,128)(2,1)S(1)} %bitcast.434, bf16[49,8,1024]{2,1,0:T(8,128)(2,1)S(1)} %get-tuple-element.112), kind=kOutput, calls=%fused_computation.335 | convolution fusion | flops 503315968 | bytes 26022912 | tf_op jit(solution)/shard_map/sbc,js->bcj/dot_general | solution.py:427
  347.3 3.4 fusion.146
  362.9 4.0 fusion.148
  371.2 198.2 %reduce_gradients.1 = (f32[4,32,1024]{2,1,0:T(8,128)}, f32[96,256]{1,0:T(8,128)}, f32[32,256]{1,0:T(8,128)}) custom-call(bf16[392,4096]{1,0:T(8,128)(2,1)} %pad_maximum_fusion.refs_0_, bf16[392,4096]{1,0:T(8,128)(2,1)} %pad_maximum_fusion.1.refs_1_, bf16[392,4096]{1,0:T(8,128)(2,1)} %pad_maximum_fusion.2.refs_2_, ...), custom_call_target="tpu_custom_call" | custom-call | flops 99999997952 | bytes 80000000 | tf_op jit(solution)/shard_map/reduce_gradients/pallas_call | solution.py:409
  (352 shorter events, 128.1 us)
Async XLA Ops:
  7.2 117.3 %all-gather.3.cloned.1.call-start = ((), (), s32[]{:S(2)}) async-start(), calls=%async_computation.1 | async-start | bytes 2113536 | tf_op jit(solution)/shard_map/all_gather | solution.py:485
  14.2 557.2 %all-reduce.6.cloned.1.call-start = ((), (), s32[]{:S(2)}) async-start(), calls=%async_computation | async-start | bytes 999424 | tf_op jit(solution)/shard_map/psum | solution.py:584
  19.8 100.8 %copy-start.62 = (s32[32]{0:T(128)S(1)}, s32[32]{0:T(128)}, u32[]{:S(2)}) copy-start(s32[32]{0:T(128)} %param.20) | copy-start | bytes 388
  130.0 3.8 copy-start.20
  131.8 23.8 %copy-start.26 = (f32[1024]{0:T(1024)}, f32[1024]{0:T(1024)S(1)}, u32[]{:S(2)}) copy-start(f32[1024]{0:T(1024)S(1)} %mul.711) | copy-start | bytes 12292
  132.2 8.5 %copy-start.22 = (f32[1024]{0:T(1024)}, f32[1024]{0:T(1024)S(1)}, u32[]{:S(2)}) copy-start(f32[1024]{0:T(1024)S(1)} %mul.701) | copy-start | bytes 12292
  133.8 17.2 %copy-start.13 = (bf16[1,32,16,49]{3,2,0,1:T(8,128)(2,1)}, bf16[1,32,16,49]{3,2,0,1:T(8,128)(2,1)S(1)}, u32[]{:S(2)}) copy-start(bf16[1,32,16,49]{3,2,0,1:T(8,128)(2,1)S(1)} %get-tuple-element.157) | copy-start | bytes 150532
  135.3 6.0 %copy-start.15 = (bf16[1,49,32,16]{1,3,2,0:T(8,128)(2,1)}, bf16[1,49,32,16]{1,3,2,0:T(8,128)(2,1)S(1)}, u32[]{:S(2)}) copy-start(bf16[1,49,32,16]{1,3,2,0:T(8,128)(2,1)S(1)} %copy.141) | copy-start | bytes 150532
  140.4 13.3 %copy-start = (f32[392,1024]{1,0:T(8,128)}, f32[392,1024]{1,0:T(8,128)S(1)}, u32[]{:S(2)}) copy-start(f32[392,1024]{1,0:T(8,128)S(1)} %get-tuple-element.186) | copy-start | bytes 4816900
  140.7 10.2 %copy-start.35 = (f32[392]{0:T(512)}, f32[392]{0:T(512)S(1)}, u32[]{:S(2)}) copy-start(f32[392]{0:T(512)S(1)} %add_rsqrt_fusion.3) | copy-start | bytes 4708
  141.3 9.6 %copy-start.5 = (bf16[49,8,1024]{2,1,0:T(8,128)(2,1)}, bf16[49,8,1024]{2,1,0:T(8,128)(2,1)S(1)}, u32[]{:S(2)}) copy-start(bf16[49,8,1024]{2,1,0:T(8,128)(2,1)S(1)} %fusion.138) | copy-start | bytes 2408452
  155.6 4.8 copy-start.37
  156.0 17.9 %copy-start.8 = (bf16[392,1024]{1,0:T(8,128)(2,1)}, bf16[392,1024]{1,0:T(8,128)(2,1)S(1)}, u32[]{:S(2)}) copy-start(bf16[392,1024]{1,0:T(8,128)(2,1)S(1)} %add_convert_fusion.2.refs_5_) | copy-start | bytes 2408452
  201.1 14.4 %copy-start.9 = (bf16[392,1024]{1,0:T(8,128)(2,1)}, bf16[392,1024]{1,0:T(8,128)(2,1)S(1)}, u32[]{:S(2)}) copy-start(bf16[392,1024]{1,0:T(8,128)(2,1)S(1)} %add_convert_fusion.refs_7_) | copy-start | bytes 2408452
  223.3 3.4 copy-start.4
  226.7 3.8 copy-start.28
  229.2 7.1 %copy-start.29 = (bf16[8,1024]{1,0:T(8,128)(2,1)}, bf16[8,1024]{1,0:T(8,128)(2,1)S(1)}, u32[]{:S(2)}) copy-start(bf16[8,1024]{1,0:T(8,128)(2,1)S(1)} %get-tuple-element.109.refs_11_) | copy-start | bytes 49156
  294.9 12.4 %copy-start.10 = (bf16[392,1024]{1,0:T(8,128)(2,1)}, bf16[392,1024]{1,0:T(8,128)(2,1)S(1)}, u32[]{:S(2)}) copy-start(bf16[392,1024]{1,0:T(8,128)(2,1)S(1)} %convert_element_type.167.refs_6_) | copy-start | bytes 2408452
  296.5 3.6 copy-start.63
  300.1 3.6 copy-start.64
  303.7 3.6 copy-start.65
  318.9 8.0 %slice-start = ((s8[8388608]{0:T(1024)(128)(4,1)}), s8[4194304]{0:T(1024)(128)(4,1)S(1)}, s32[]{:S(2)}) async-start(s8[8388608]{0:T(1024)(128)(4,1)} %bitcast.394), calls=%async_computation.2 | async-start | bytes 8388608
  320.8 6.1 %slice-start.1 = ((s8[8388608]{0:T(1024)(128)(4,1)}), s8[4194304]{0:T(1024)(128)(4,1)S(1)}, s32[]{:S(2)}) async-start(s8[8388608]{0:T(1024)(128)(4,1)} %bitcast.394), calls=%async_computation.3 | async-start | bytes 8388608
  329.1 16.4 %copy-start.6 = (bf16[49,8,1024]{2,1,0:T(8,128)(2,1)S(1)}, bf16[49,8,1024]{2,1,0:T(8,128)(2,1)}, u32[]{:S(2)}) copy-start(bf16[49,8,1024]{2,1,0:T(8,128)(2,1)} %copy-done.5) | copy-start | bytes 2408452
  347.2 3.4 copy-start.53
  347.3 3.4 copy-start.54
  347.3 4.1 copy-start.61
  347.3 4.7 copy-start.19
  347.3 7.0 %copy-start.18 = (f32[1,512,49]{1,2,0:T(8,128)S(1)}, f32[1,512,49]{1,2,0:T(8,128)}, u32[]{:S(2)}) copy-start(f32[1,512,49]{1,2,0:T(8,128)} %convolution_bitcast_fusion) | copy-start | bytes 301060
  350.7 10.0 %copy-start.1 = (f32[392,1024]{1,0:T(8,128)S(1)}, f32[392,1024]{1,0:T(8,128)}, u32[]{:S(2)}) copy-start(f32[392,1024]{1,0:T(8,128)} %copy-done) | copy-start | bytes 4816900
  569.4 15.8 %copy-start.25 = (f32[96,256]{1,0:T(8,128)S(1)}, f32[96,256]{1,0:T(8,128)}, u32[]{:S(2)}) copy-start(f32[96,256]{1,0:T(8,128)} %get-tuple-element.255) | copy-start | bytes 294916
  571.4 14.6 %copy-start.34 = (f32[32,256]{1,0:T(8,128)S(1)}, f32[32,256]{1,0:T(8,128)}, u32[]{:S(2)}) copy-start(f32[32,256]{1,0:T(8,128)} %get-tuple-element.29) | copy-start | bytes 98308
  (39 other events, 93.3 us)
Sparse Core Ops, SparseCore 0:
  14.3 69.6 all-gather.2
  371.4 146.6 all-reduce.5

commit v3 on v2

--- a/solution.py
+++ b/solution.py
@@ -178,6 +178,10 @@
 GROUPS = (STEM, 3, 2, 1, 0, HEAD)
 UNITS = tuple((g, c) for g in GROUPS for c in (2, 0, 1) if g != HEAD or c == 2)
 REDUCE_COPIES = 13 * len(UNITS)
+ORDER = (0, 1, 2, 3, 4, 0, 5, 1, 2, 0, 3, 1, 2, 0, 4, 6, 3, 1, 7, 5, 0, 6, 4, 1, 2, 8, 0, 6, 7, 5, 2, 3, 1, 9, 0, 8, 4, 10, 7, 9, 1, 2,
+         3, 0, 5, 11, 8, 9, 10, 1, 4, 5, 2, 11, 3, 6, 12, 10, 2, 5, 8, 6, 4, 7, 13, 11, 12, 3, 4, 7, 8, 14, 5, 12, 6, 13, 4, 9,
+         15, 5, 8, 11, 3, 14, 13, 6, 7, 8, 9, 10, 11, 15, 7, 14, 6, 11, 10, 15, 7, 8, 9, 12, 11, 12, 14, 11, 10, 9, 13, 12, 15,
+         14, 10, 9, 13, 12, 15, 14, 10, 13, 15, 12, 14, 13, 15, 14, 15, 13)
 
 
 def reduce_scratch():
@@ -186,8 +190,8 @@
         n = COLS[c][1]
         many = sum(1 for u in UNITS if u[1] == c)
         lead = ((4, 4), (4,), ())
-        b = {'C': pltpu.VMEM((4, 4, 4, 2, 32, n), bf16), 'D': pltpu.VMEM((4, 4, 4, 32, n), bf16),
-             'S1': pltpu.VMEM((4, 4, 32, n), f32), 'S2': pltpu.VMEM((4, 32, n), f32)}
+        b = {'C': pltpu.VMEM((2, 4, 4, 4, 2, 32, n), bf16), 'D': pltpu.VMEM((2, 4, 4, 4, 32, n), bf16),
+             'S1': pltpu.VMEM((4, 4, 32, n), f32), 'S2': pltpu.VMEM((3, 4, 32, n), f32)}
         for ph in range(3):
             for name in ('opp', 'rig', 'lef'):
                 b[f'{name}{ph}'] = pltpu.VMEM(lead[ph] + (32, n), bf16)
@@ -231,7 +235,7 @@
         for copy in busy.pop(key, ()):
             copy.wait_send()
 
-    def make(g, c):
+    def make(g, c, cslot):
         i = GROUPS.index(g)
         slot = i % 2
         if g != HEAD and c == 2:
@@ -241,9 +245,6 @@
         if g == STEM:
             if c != 2:
                 return
-            for d in range(3):
-                free(('C', d))
-
             @pl.loop(0, 32)
             def _(j):
                 b = j // 4
@@ -253,17 +254,15 @@
                 right = narrow[slot, :, pl.ds(pl.multiple_of(t * 256, 128), 256)]
                 prod = transposed_product(left, right).astype(bf16).reshape(2, 2, 3, 32, 256)
                 for d in range(3):
-                    per[d]['C'][t, z, pl.ds(y2 * 2, 2), :, :, pl.ds(0, 256)] = prod[:, :, d]
+                    per[d]['C'][0, t, z, pl.ds(y2 * 2, 2), :, :, pl.ds(0, 256)] = prod[:, :, d]
         elif g == HEAD:
-            free(('C', c))
 
             @pl.loop(0, 4)
             def _(t):
                 right = head_r[:, pl.ds(pl.multiple_of(t * 256, 128), 256)]
                 prod = transposed_product(head_l[...], right)
-                per[c]['C'][t] = prod.astype(bf16).reshape(4, 4, 2, 32, 256)
+                per[c]['C'][cslot, t] = prod.astype(bf16).reshape(4, 4, 2, 32, 256)
         else:
-            free(('C', c))
             c0, n = COLS[c]
 
             @pl.loop(0, 16)
@@ -275,14 +274,15 @@
                 else:
                     left = wide[slot, :, pl.ds(pl.multiple_of(j * 256, 128), 256)]
                     right = narrow[slot, :, pl.ds(c0, n)]
-                per[c]['C'][t, z] = transposed_product(left, right).astype(bf16).reshape(4, 2, 32, n)
+                per[c]['C'][cslot, t, z] = transposed_product(left, right).astype(bf16).reshape(4, 2, 32, n)
 
     class Unit:
         def __init__(self, g, c):
             self.g, self.c = g, c
             same = [u for u in UNITS if u[1] == c]
             self.index = same.index((g, c))
-            self.last = self.index == len(same) - 1
+            self.slot = self.index % 2
+            self.last = self.index >= len(same) - 2
             self.n = COLS[c][1] if g < N_CH else 256
             self.buf = per[c]
             self.dims = ORDERS[c]
@@ -298,8 +298,10 @@
             if phase == 0:
                 at = dict(zip(self.dims, (p, *e)))
                 at = (at['x'], at['z'], at['y'])
-                return (self.buf['C'][(*at, k, r, cols)].astype(f32) + self.buf['D'][(*at, r, cols)].astype(f32))
-            return self.buf[f'S{phase}'][(p, *e, r, cols)]
+                return (self.buf['C'][(self.slot, *at, k, r, cols)].astype(f32)
+                        + self.buf['D'][(self.slot, *at, r, cols)].astype(f32))
+            lead = () if phase == 1 else (self.index % 3,)
+            return self.buf[f'S{phase}'][(*lead, p, *e, r, cols)]
 
         def each(self, phase, body):
             if phase == 2:
@@ -310,13 +312,14 @@
                 pl.loop(0, 16)(lambda i: body((i // 4, i % 4)))
 
         def start(self):
-            make(self.g, self.c)
-            if self.index:
+            free(('C', self.c, self.slot))
+            make(self.g, self.c, self.slot)
+            if self.index > 1:
                 pl.semaphore_wait(credit.at[self.c], 1)
             cols = pl.ds(0, self.n)
-            src = self.buf['C'].at[:, :, :, 1 - k, :, cols]
-            self.swap = sender.start(src, self.buf['D'].at[:, :, :, :, cols], other)
-            busy['C', self.c] = [self.swap]
+            src = self.buf['C'].at[self.slot, :, :, :, 1 - k, :, cols]
+            self.swap = sender.start(src, self.buf['D'].at[self.slot, :, :, :, :, cols], other)
+            busy['C', self.c, self.slot] = [self.swap]
 
         def opposite(self, phase):
             if phase == 0:
@@ -368,8 +371,10 @@
                 got = [self.buf[f'{name}{phase}'][(self.index, *e, slice(None), cols)].astype(f32)
                        for name in ('froml', 'fromr')]
                 value = self.share(phase, p, e, (0, 32)) + got[0] + got[1]
-                if phase < 2:
-                    self.buf[f'S{phase + 1}'][(*e, slice(None), cols)] = value
+                if phase == 0:
+                    self.buf['S1'][(*e, slice(None), cols)] = value
+                elif phase == 1:
+                    self.buf['S2'][(self.index % 3, *e, slice(None), cols)] = value
                 elif self.g == STEM:
                     out_s[pl.ds(32 * self.c, 32), :] = value
                 elif self.g == HEAD:
@@ -393,10 +398,11 @@
                 self.opposite(stage // 2)
 
     units = [Unit(g, c) for g, c in UNITS]
-    for slot in range(len(units) + 7):
-        for stage in range(7, -1, -1):
-            if 0 <= slot - stage < len(units):
-                units[slot - stage].run(stage)
+    stage_of = [0] * len(units)
+    for u in ORDER:
+        units[u].run(stage_of[u])
+        stage_of[u] += 1
+    assert stage_of == [8] * len(units)
     for key in list(busy):
         free(key)
     assert sender.count == REDUCE_COPIES, sender.count

time: 605 us -> 556 us (0.919)
  Pallas kernels: 299 us -> 251 us
    pallas_call x1, Pallas kernels: 198 us -> 150 us  [reduce_gradients(): pl.pallas_call(reduce_kernel, name='reduce_gradients', out_shape=[jax.Sha...]
  transfers between devices with their start and end apart: 2 -> 2, of which waited for: 0 -> 0; matrix products, arithmetic and copies ran while one was open for 2% -> 2% of each run, Pallas kernels for 50% -> 46%
where the time goes in v3:
time: 556 us; the launch traced here: 547 us
  Pallas kernels  251 us (45%)
  matrix products  185 us (33%)
  local copies, waits for them, and re-layouts  50.3 us (9%)
  other arithmetic  41.7 us (8%)
  between operations  19.1 us (3%)
    dot_general x47, matrix products, product(): return jnp.einsum(form, left, right, preferred_element_type=f32)  185 us
    pallas_call x1, Pallas kernels, reduce_gradients(): pl.pallas_call(reduce_kernel, name='reduce_gradients', out_shape=[jax.Sha...  150 us
    pallas_call x1, Pallas kernels, gather_weights(): pl.pallas_call(gather_kernel, name='gather_weights', out_shape=[jax.Shape...  101 us
  transfers between devices with their start and end apart: 2, of which 0 were waited for; matrix products, arithmetic and copies ran while one was open for 2% of the time, Pallas kernels for 46%

profile of v3, /device:TPU:0, one launch (start us, length us, event | category | flops | bytes accessed | tf_op | source)
XLA Modules:
  0.0 546.6 jit_solution(4339813264051159176)
XLA Ops:
  19.8 100.8 %gather_weights.1 = (bf16[4,4,4,4,2,32,1024]{6,5,4,3,2,1,0:T(8,128)(2,1)}, bf16[4,4,2,96,1024]{4,3,2,1,0:T(8,128)(2,1)}, bf16[4,4,2,32,1024]{4,3,2,1,0:T(8,128)(2,1)}) custom-call(bf16[4,32,1024]{2,1,0:T(8,128)(2,1)} %pad_maximum_fusion.4.pc, bf16[96,256]{1,0:T(8,128)(2,1)} %convert_element_type.136.ps, bf16[32,256]{1,0:T(8,128)(2,1)} %pad.16.ph), custom_call_target="tpu_custom_call" | custom-call | flops 89999998976 | bytes 80000000 | tf_op jit(solution)/shard_map/gather_weights/pallas_call | solution.py:165
  121.3 3.3 dynamic-slice_bitcast_fusion.refs_4_
  135.3 5.0 fusion.174
  141.3 9.5 %multiply_convert_fusion.1 = (bf16[8,1024,512]{2,1,0:T(8,128)(2,1)S(1)}, f32[8,1024,512]{2,1,0:T(8,128)}) fusion(f32[512]{0:T(512)S(1)} %copy-done.58, bf16[49,512,1]{0,1,2:T(8,128)(2,1)S(1)} %bitcast.435, bf16[49,8,1024]{2,1,0:T(8,128)(2,1)S(1)} %fusion.138), kind=kOutput, calls=%fused_computation.17 | convolution fusion | flops 452984832 | bytes 26020864 | tf_op jit(solution)/shard_map/sbc,sj->bcj/dot_general | solution.py:433
  156.3 4.1 multiply_convert_fusion.6
  160.4 4.1 multiply_convert_fusion.7
  167.1 4.1 multiply_convert_fusion.8
  173.9 4.1 multiply_convert_fusion.9
  182.5 3.0 fusion.175
  186.7 9.8 %multiply_convert_fusion = (bf16[8,1024,512]{2,1,0:T(8,128)(2,1)S(1)}, f32[8,1024,512]{2,1,0:T(8,128)}) fusion(f32[512]{0:T(512)S(1)} %copy-done.60, bf16[49,512,1]{0,1,2:T(8,128)(2,1)S(1)} %bitcast.439, bf16[49,8,1024]{2,1,0:T(8,128)(2,1)S(1)} %fusion.139), kind=kOutput, calls=%fused_computation.16 | convolution fusion | flops 452984832 | bytes 26020864 | tf_op jit(solution)/shard_map/sbc,sj->bcj/dot_general | solution.py:433
  201.1 3.3 multiply_convert_fusion.2
  204.3 3.0 multiply_convert_fusion.3
  209.9 3.0 multiply_convert_fusion.4
  215.5 3.0 multiply_convert_fusion.5
  223.3 3.0 bitcast_reduce_fusion
  232.2 4.1 fusion.161
  236.3 4.1 fusion.160
  240.4 4.1 fusion.159
  244.4 4.1 fusion.158
  258.5 3.8 multiply_reduce_fusion.2
  266.4 17.0 %fusion.177 = (f32[512]{0:T(512)}, bf16[8,1024,512]{2,1,0:T(8,128)(2,1)S(1)}) fusion(f32[8,1024,512]{2,1,0:T(8,128)} %get-tuple-element.200, f32[512]{0:T(512)S(1)} %copy-done.60, bf16[512,49,1]{1,0,2:T(8,128)(2,1)S(1)} %bitcast.438, bf16[49,8,1024]{2,1,0:T(8,128)(2,1)S(1)} %get-tuple-element.114), kind=kOutput, calls=%fused_computation.334 | convolution fusion | flops 503315968 | bytes 26022912 | tf_op jit(solution)/shard_map/sbc,js->bcj/dot_general | solution.py:433
  285.8 3.2 fusion.147
  291.1 3.7 fusion.150
  296.5 3.6 fusion.157
  300.1 3.6 fusion.156
  303.7 3.6 fusion.155
  307.3 3.6 fusion.154
  320.8 4.3 multiply_reduce_fusion.3
  329.1 16.4 %fusion.178 = (f32[512]{0:T(512)S(1)}, bf16[8,1024,512]{2,1,0:T(8,128)(2,1)S(1)}) fusion(f32[8,1024,512]{2,1,0:T(8,128)} %get-tuple-element.188, f32[512]{0:T(512)S(1)} %copy-done.59, bf16[512,49,1]{1,0,2:T(8,128)(2,1)S(1)} %bitcast.434, bf16[49,8,1024]{2,1,0:T(8,128)(2,1)S(1)} %get-tuple-element.112), kind=kOutput, calls=%fused_computation.335 | convolution fusion | flops 503315968 | bytes 26022912 | tf_op jit(solution)/shard_map/sbc,js->bcj/dot_general | solution.py:433
  347.3 3.4 fusion.146
  362.9 4.0 fusion.148
  371.2 149.8 %reduce_gradients.1 = (f32[4,32,1024]{2,1,0:T(8,128)}, f32[96,256]{1,0:T(8,128)}, f32[32,256]{1,0:T(8,128)}) custom-call(bf16[392,4096]{1,0:T(8,128)(2,1)} %pad_maximum_fusion.refs_0_, bf16[392,4096]{1,0:T(8,128)(2,1)} %pad_maximum_fusion.1.refs_1_, bf16[392,4096]{1,0:T(8,128)(2,1)} %pad_maximum_fusion.2.refs_2_, ...), custom_call_target="tpu_custom_call" | custom-call | flops 99999997952 | bytes 80000000 | tf_op jit(solution)/shard_map/reduce_gradients/pallas_call | solution.py:415
  (352 shorter events, 128.1 us)
Async XLA Ops:
  7.2 117.3 %all-gather.3.cloned.1.call-start = ((), (), s32[]{:S(2)}) async-start(), calls=%async_computation.1 | async-start | bytes 2113536 | tf_op jit(solution)/shard_map/all_gather | solution.py:491
  14.2 508.8 %all-reduce.6.cloned.1.call-start = ((), (), s32[]{:S(2)}) async-start(), calls=%async_computation | async-start | bytes 999424 | tf_op jit(solution)/shard_map/psum | solution.py:590
  19.8 100.8 %copy-start.62 = (s32[32]{0:T(128)S(1)}, s32[32]{0:T(128)}, u32[]{:S(2)}) copy-start(s32[32]{0:T(128)} %param.20) | copy-start | bytes 388
  130.0 3.8 copy-start.20
  131.8 23.8 %copy-start.26 = (f32[1024]{0:T(1024)}, f32[1024]{0:T(1024)S(1)}, u32[]{:S(2)}) copy-start(f32[1024]{0:T(1024)S(1)} %mul.711) | copy-start | bytes 12292
  132.2 8.5 %copy-start.22 = (f32[1024]{0:T(1024)}, f32[1024]{0:T(1024)S(1)}, u32[]{:S(2)}) copy-start(f32[1024]{0:T(1024)S(1)} %mul.701) | copy-start | bytes 12292
  133.8 17.2 %copy-start.13 = (bf16[1,32,16,49]{3,2,0,1:T(8,128)(2,1)}, bf16[1,32,16,49]{3,2,0,1:T(8,128)(2,1)S(1)}, u32[]{:S(2)}) copy-start(bf16[1,32,16,49]{3,2,0,1:T(8,128)(2,1)S(1)} %get-tuple-element.157) | copy-start | bytes 150532
  135.3 6.0 %copy-start.15 = (bf16[1,49,32,16]{1,3,2,0:T(8,128)(2,1)}, bf16[1,49,32,16]{1,3,2,0:T(8,128)(2,1)S(1)}, u32[]{:S(2)}) copy-start(bf16[1,49,32,16]{1,3,2,0:T(8,128)(2,1)S(1)} %copy.141) | copy-start | bytes 150532
  140.4 13.3 %copy-start = (f32[392,1024]{1,0:T(8,128)}, f32[392,1024]{1,0:T(8,128)S(1)}, u32[]{:S(2)}) copy-start(f32[392,1024]{1,0:T(8,128)S(1)} %get-tuple-element.186) | copy-start | bytes 4816900
  140.7 10.2 %copy-start.35 = (f32[392]{0:T(512)}, f32[392]{0:T(512)S(1)}, u32[]{:S(2)}) copy-start(f32[392]{0:T(512)S(1)} %add_rsqrt_fusion.3) | copy-start | bytes 4708
  141.3 9.6 %copy-start.5 = (bf16[49,8,1024]{2,1,0:T(8,128)(2,1)}, bf16[49,8,1024]{2,1,0:T(8,128)(2,1)S(1)}, u32[]{:S(2)}) copy-start(bf16[49,8,1024]{2,1,0:T(8,128)(2,1)S(1)} %fusion.138) | copy-start | bytes 2408452
  155.6 4.8 copy-start.37
  156.0 17.9 %copy-start.8 = (bf16[392,1024]{1,0:T(8,128)(2,1)}, bf16[392,1024]{1,0:T(8,128)(2,1)S(1)}, u32[]{:S(2)}) copy-start(bf16[392,1024]{1,0:T(8,128)(2,1)S(1)} %add_convert_fusion.2.refs_5_) | copy-start | bytes 2408452
  201.1 14.4 %copy-start.9 = (bf16[392,1024]{1,0:T(8,128)(2,1)}, bf16[392,1024]{1,0:T(8,128)(2,1)S(1)}, u32[]{:S(2)}) copy-start(bf16[392,1024]{1,0:T(8,128)(2,1)S(1)} %add_convert_fusion.refs_7_) | copy-start | bytes 2408452
  223.3 3.4 copy-start.4
  226.7 3.8 copy-start.28
  229.2 7.1 %copy-start.29 = (bf16[8,1024]{1,0:T(8,128)(2,1)}, bf16[8,1024]{1,0:T(8,128)(2,1)S(1)}, u32[]{:S(2)}) copy-start(bf16[8,1024]{1,0:T(8,128)(2,1)S(1)} %get-tuple-element.109.refs_11_) | copy-start | bytes 49156
  294.9 12.4 %copy-start.10 = (bf16[392,1024]{1,0:T(8,128)(2,1)}, bf16[392,1024]{1,0:T(8,128)(2,1)S(1)}, u32[]{:S(2)}) copy-start(bf16[392,1024]{1,0:T(8,128)(2,1)S(1)} %convert_element_type.167.refs_6_) | copy-start | bytes 2408452
  296.5 3.6 copy-start.63
  300.1 3.6 copy-start.64
  303.7 3.6 copy-start.65
  318.9 8.0 %slice-start = ((s8[8388608]{0:T(1024)(128)(4,1)}), s8[4194304]{0:T(1024)(128)(4,1)S(1)}, s32[]{:S(2)}) async-start(s8[8388608]{0:T(1024)(128)(4,1)} %bitcast.394), calls=%async_computation.2 | async-start | bytes 8388608
  320.8 6.1 %slice-start.1 = ((s8[8388608]{0:T(1024)(128)(4,1)}), s8[4194304]{0:T(1024)(128)(4,1)S(1)}, s32[]{:S(2)}) async-start(s8[8388608]{0:T(1024)(128)(4,1)} %bitcast.394), calls=%async_computation.3 | async-start | bytes 8388608
  329.1 16.4 %copy-start.6 = (bf16[49,8,1024]{2,1,0:T(8,128)(2,1)S(1)}, bf16[49,8,1024]{2,1,0:T(8,128)(2,1)}, u32[]{:S(2)}) copy-start(bf16[49,8,1024]{2,1,0:T(8,128)(2,1)} %copy-done.5) | copy-start | bytes 2408452
  347.2 3.4 copy-start.53
  347.3 3.4 copy-start.54
  347.3 4.1 copy-start.61
  347.3 4.7 copy-start.19
  347.3 7.0 %copy-start.18 = (f32[1,512,49]{1,2,0:T(8,128)S(1)}, f32[1,512,49]{1,2,0:T(8,128)}, u32[]{:S(2)}) copy-start(f32[1,512,49]{1,2,0:T(8,128)} %convolution_bitcast_fusion) | copy-start | bytes 301060
  350.7 10.0 %copy-start.1 = (f32[392,1024]{1,0:T(8,128)S(1)}, f32[392,1024]{1,0:T(8,128)}, u32[]{:S(2)}) copy-start(f32[392,1024]{1,0:T(8,128)} %copy-done) | copy-start | bytes 4816900
  521.1 15.8 %copy-start.25 = (f32[96,256]{1,0:T(8,128)S(1)}, f32[96,256]{1,0:T(8,128)}, u32[]{:S(2)}) copy-start(f32[96,256]{1,0:T(8,128)} %get-tuple-element.255) | copy-start | bytes 294916
  523.0 14.6 %copy-start.34 = (f32[32,256]{1,0:T(8,128)S(1)}, f32[32,256]{1,0:T(8,128)}, u32[]{:S(2)}) copy-start(f32[32,256]{1,0:T(8,128)} %get-tuple-element.29) | copy-start | bytes 98308
  (39 other events, 93.3 us)
Sparse Core Ops, SparseCore 0:
  14.3 69.6 all-gather.2
  371.4 146.4 all-reduce.5

commit v4 on v3

--- a/solution.py
+++ b/solution.py
@@ -208,9 +208,11 @@
 
 
 def reduce_kernel(*refs):
-    wides, narrows, (head_l, head_r) = refs[:5], refs[5:10], refs[10:12]
-    out_c, out_s, out_h = refs[12:15]
-    wide, narrow, per, send_sems, recv_sems, load_sems, credit = refs[15:]
+    dpre, act, pat, vin, dout, dstem, head_l, head_r = refs[:8]
+    wides = [dpre.at[0], act.at[0], dpre.at[1], act.at[1], pat]
+    narrows = [vin.at[0], dout.at[0], vin.at[1], dout.at[1], dstem]
+    out_c, out_s, out_h = refs[8:11]
+    wide, narrow, per, send_sems, recv_sems, load_sems, credit = refs[11:]
     me = my_place()
     other = moved(me, 'k', 1)
     k = me['k']
@@ -408,52 +410,355 @@
     assert sender.count == REDUCE_COPIES, sender.count
 
 
-def reduce_gradients(wides, narrows, head_l, head_r):
+def reduce_gradients(*operands):
     any_spec = pl.BlockSpec(memory_space=pl.ANY)
     vmem = pl.BlockSpec(memory_space=pltpu.VMEM)
-    rows = narrows[0].shape[0]
+    rows = operands[2].shape[0]
     return pl.pallas_call(
         reduce_kernel, name='reduce_gradients',
         out_shape=[jax.ShapeDtypeStruct((N_CH, 32, 1024), f32), jax.ShapeDtypeStruct((96, 256), f32),
                    jax.ShapeDtypeStruct((32, 256), f32)],
-        in_specs=[any_spec] * 10 + [vmem] * 2, out_specs=[vmem] * 3,
+        in_specs=[any_spec] * 6 + [vmem] * 2, out_specs=[vmem] * 3,
         scratch_shapes=[pltpu.VMEM((2, rows, 4096), bf16), pltpu.VMEM((2, rows, 1024), bf16), reduce_scratch(),
                         pltpu.SemaphoreType.DMA((REDUCE_COPIES,)), pltpu.SemaphoreType.DMA((REDUCE_COPIES,)),
                         pltpu.SemaphoreType.DMA((2, 2)), pltpu.SemaphoreType.REGULAR((3,))],
         compiler_params=pltpu.CompilerParams(collective_id=1, has_side_effects=True, vmem_limit_bytes=64 * 1024 * 1024 - 65536),
         cost_estimate=pl.CostEstimate(flops=100_000_000_000, bytes_accessed=80_000_000, transcendentals=0),
-    )(*wides, *narrows, head_l, head_r)
+    )(*operands)
 
 
 EPS = 1e-6
+TOK, TPAD = 49, 56
+IMG = 8
+ROWS = IMG * TPAD
+CH, TOKH, CHH = 1024, 512, 4096
+BLK = 512
+NBLK = CHH // BLK
+GELU_C, GELU_A = 0.7978845608028654, 0.044715
+
+
+def dot_nn(a, b):
+    return lax.dot_general(a, b, (((1,), (0,)), ((), ())), preferred_element_type=f32)
+
+
+def dot_nt(a, b):
+    return lax.dot_general(a, b, (((1,), (1,)), ((), ())), preferred_element_type=f32)
+
+
+def dot_tn(a, b):
+    return lax.dot_general(a, b, (((0,), (0,)), ((), ())), preferred_element_type=f32)
+
+
+def gelu(x):
+    half = 0.5 * x
+    return half + half * jnp.tanh(x * (GELU_C + (GELU_C * GELU_A) * (x * x)))
+
+
+def gelu_both(x):
+    sq = x * x
+    th = jnp.tanh(x * (GELU_C + (GELU_C * GELU_A) * sq))
+    half = 0.5 * x
+    rise = 0.5 + 0.5 * th
+    slope = (1.0 - th * th) * (GELU_C + (3.0 * GELU_C * GELU_A) * sq)
+    return x * rise, rise + half * slope
+
+
+def standardize(x):
+    mean = jnp.mean(x, axis=-1, keepdims=True)
+    cent = x - mean
+    inv = lax.rsqrt(jnp.mean(cent * cent, axis=-1, keepdims=True) + EPS)
+    return cent * inv, inv
+
+
+def norm_grad(d, gain, std, inv):
+    gs = d * gain
+    m0 = jnp.mean(gs, axis=-1, keepdims=True)
+    m1 = jnp.mean(gs * std, axis=-1, keepdims=True)
+    return inv * (gs - m0 - std * m1)
+
+
+def row_mask(rows=TPAD):
+    return lax.broadcasted_iota(jnp.int32, (rows, 1), 0) < TOK
+
+
+def image(b):
+    return pl.ds(pl.multiple_of(b * TPAD, 8), TPAD)
+
+
+def pair(p):
+    return pl.ds(pl.multiple_of(p * 2 * TPAD, 16), 2 * TPAD)
+
+
+class Stream:
+    def __init__(self, sem, copies, count):
+        self.sem, self.copies, self.count = sem, copies, count
+
+    def make(self, i, slot):
+        return [pltpu.make_async_copy(src, dst, self.sem.at[slot, n]) for n, (src, dst) in enumerate(self.copies(i, slot))]
+
+    def start(self, i, slot):
+        for copy in self.make(i, slot):
+            copy.start()
+
+    def wait(self, i, slot):
+        for copy in self.make(i, slot):
+            copy.wait()
+
+
+def for_blocks(stream, body, out=None):
+    n = stream.count
+    stream.start(0, 0)
+
+    @pl.loop(0, n)
+    def _(i):
+        slot = i % 2
+        stream.wait(i, slot)
+
+        @pl.when(i + 1 < n)
+        def _():
+            stream.start(i + 1, 1 - slot)
+        if out is not None:
+            @pl.when(i >= 2)
+            def _():
+                out.wait(i - 2, slot)
+        body(i, slot)
+        if out is not None:
+            out.start(i, slot)
+    if out is not None:
+        out.wait(n - 2, n % 2)
+        out.wait(n - 1, 1 - n % 2)
+
+
+def forward_kernel(pat, ws, wc, wh, wt1, wt2, bt1, vec, bch1, bhead, label,
+                   xin, xmid, vout, pre_out, act_out, hl, hr, dx0, hstat, gbh,
+                   p_v, x_v, v_v, w1_v, w2_v, ws_v, wh_v, pre_v, act_v, g_v, sem, sem_w, sem_o, sem_x):
+    load_p = pltpu.make_async_copy(pat, p_v, sem.at[0])
+    load_p.start()
+    load_h = pltpu.make_async_copy(wh, wh_v, sem.at[1])
+    load_h.start()
+    load_p.wait()
+
+    def stem_copies(i, slot):
+        return [(ws.at[:, pl.ds(pl.multiple_of(i * 256, 256), 256)], ws_v.at[slot])]
+
+    def stem(i, slot):
+        cols = pl.ds(pl.multiple_of(i * 256, 256), 256)
+        mask = (lax.broadcasted_iota(jnp.int32, (ROWS, 1), 0) % TPAD) < TOK
+        x_v[:, cols] = jnp.where(mask, dot_nn(p_v[...], ws_v[slot]) + vec[0:1, cols], 0.0)
+    for_blocks(Stream(sem_w, stem_copies, 4), stem)
+
+    saves = []
+
+    def save(src, dst, n):
+        copy = pltpu.make_async_copy(src, dst, sem_x.at[n])
+        copy.start()
+        saves.append(copy)
+
+    for l in range(2):
+        r = 1 + 5 * l
+        for copy in saves:
+            copy.wait()
+        saves.clear()
+        first = pltpu.make_async_copy(x_v, xin.at[l], sem_x.at[0])
+        first.start()
+        first.wait()
+
+        @pl.loop(0, IMG)
+        def _(b):
+            x = x_v[image(b), :]
+            std, _ = standardize(x)
+            a = (std * vec[r:r + 1, :] + vec[r + 1:r + 2, :]).astype(bf16)
+            h = dot_nn(wt1[l], a) + bt1[l]
+            g_v[...] = gelu(h).astype(bf16)
+            x_v[image(b), :] = x + dot_tn(wt2[l], g_v[...])
+        save(x_v, xmid.at[l], 0)
+
+        @pl.loop(0, IMG // 2)
+        def _(p):
+            std, _ = standardize(x_v[pair(p), :])
+            v_v[pair(p), :] = (std * vec[r + 2:r + 3, :] + vec[r + 3:r + 4, :]).astype(bf16)
+        save(v_v, vout.at[l], 1)
+        saves[0].wait()
+        saves.pop(0)
+
+        def blocks(i, slot):
+            t, h = i // 2, i % 2
+            part = pl.ds(pl.multiple_of(h * BLK, BLK), BLK)
+            return [(wc.at[2 * l, t, :, part], w1_v.at[slot]), (wc.at[2 * l + 1, t, part, :], w2_v.at[slot])]
+
+        def outs(i, slot):
+            part = pl.ds(pl.multiple_of(i * BLK, BLK), BLK)
+            return [(pre_v.at[slot], pre_out.at[l, :, part]), (act_v.at[slot], act_out.at[l, :, part])]
+
+        def channel(i, slot):
+            part = pl.ds(pl.multiple_of(i * BLK, BLK), BLK)
+            h = dot_nn(v_v[...], w1_v[slot]) + bch1[l:l + 1, part]
+            pre_v[slot] = h
+            act_v[slot] = gelu(h).astype(bf16)
+            x_v[...] += dot_nn(act_v[slot], w2_v[slot])
+        for_blocks(Stream(sem_w, blocks, NBLK), channel, Stream(sem_o, outs, NBLK))
+        x_v[...] += vec[r + 4:r + 5, :]
+    for copy in saves:
+        copy.wait()
+
+    load_h.wait()
+    last = 11
+    mask = row_mask()
+    pooled = jnp.concatenate([jnp.sum(jnp.where(mask, x_v[b * TPAD:(b + 1) * TPAD, :], 0.0), axis=0, keepdims=True)
+                              for b in range(IMG)], axis=0) * (1.0 / TOK)
+    std, inv = standardize(pooled)
+    head_in = (std * vec[last:last + 1, :] + vec[last + 1:last + 2, :]).astype(bf16)
+    hl[...] = head_in
+    logits = dot_nn(head_in, wh_v[...]) + bhead[...]
+    is_label = lax.broadcasted_iota(jnp.int32, logits.shape, 1) == label[...]
+    top = jnp.max(logits, axis=-1, keepdims=True)
+    ex = jnp.exp(logits - top)
+    es = jnp.sum(ex, axis=-1, keepdims=True)
+    nll = top + jnp.log(es) - jnp.sum(jnp.where(is_label, logits, 0.0), axis=-1, keepdims=True)
+    d_logits = (ex / es - jnp.where(is_label, 1.0, 0.0)) * (1.0 / 1024)
+    gbh[...] = jnp.sum(d_logits, axis=0, keepdims=True)
+    d_bf = d_logits.astype(bf16)
+    hr[...] = d_bf
+    d_in = dot_nt(d_bf, wh_v[...])
+    hstat[0:1, :] = jnp.sum(d_in * std, axis=0, keepdims=True)
+    hstat[1:2, :] = jnp.sum(d_in, axis=0, keepdims=True)
+    hstat[2:3, :] = jnp.broadcast_to(jnp.sum(nll, axis=0, keepdims=True), (1, CH))
+    dx0[...] = norm_grad(d_in, vec[last:last + 1, :], std, inv) * (1.0 / TOK)
+
+
+def forward(pat, ws, wc, wh, wt1, wt2, bt1, vec, bch1, bhead, label):
+    a, v = pl.BlockSpec(memory_space=pl.ANY), pl.BlockSpec(memory_space=pltpu.VMEM)
+    S = jax.ShapeDtypeStruct
+    return pl.pallas_call(
+        forward_kernel, name='forward',
+        in_specs=[a, a, a, a] + [v] * 7,
+        out_specs=[a] * 5 + [v] * 5,
+        out_shape=[S((2, ROWS, CH), f32), S((2, ROWS, CH), f32), S((2, ROWS, CH), bf16), S((2, ROWS, CHH), f32),
+                   S((2, ROWS, CHH), bf16), S((IMG, CH), bf16), S((IMG, CH), bf16), S((IMG, CH), f32), S((8, CH), f32),
+                   S((1, CH), f32)],
+        scratch_shapes=[pltpu.VMEM((ROWS, 3072), bf16), pltpu.VMEM((ROWS, CH), f32), pltpu.VMEM((ROWS, CH), bf16),
+                        pltpu.VMEM((2, CH, BLK), bf16), pltpu.VMEM((2, BLK, CH), bf16), pltpu.VMEM((2, 3072, 256), bf16),
+                        pltpu.VMEM((CH, CH), bf16), pltpu.VMEM((2, ROWS, BLK), f32), pltpu.VMEM((2, ROWS, BLK), bf16),
+                        pltpu.VMEM((TOKH, CH), bf16), pltpu.SemaphoreType.DMA((2,)), pltpu.SemaphoreType.DMA((2, 2)),
+                        pltpu.SemaphoreType.DMA((2, 2)), pltpu.SemaphoreType.DMA((2,))],
+        compiler_params=pltpu.CompilerParams(vmem_limit_bytes=60 * 1024 * 1024),
+        cost_estimate=pl.CostEstimate(flops=50_000_000_000, bytes_accessed=100_000_000, transcendentals=0),
+    )(pat, ws, wc, wh, wt1, wt2, bt1, vec, bch1, bhead, label)
+
+
+def backward_kernel(xin, xmid, pre_in, wc, wt1, wt2, bt1, vec, dx0,
+                    dpre, dout, dstem, gvec, gbch1, gt1, gt2, gbt,
+                    x_v, d_v, dv_v, do_v, w1_v, w2_v, pre_v, dp_v, g_v, dh_v, sem, sem_w, sem_o):
+    mask = row_mask()
+    for b in range(IMG):
+        d_v[b * TPAD:(b + 1) * TPAD, :] = jnp.where(mask, jnp.broadcast_to(dx0[b:b + 1, :], (TPAD, CH)), 0.0)
+    gvec[...] = jnp.zeros_like(gvec)
+    gt1[...] = jnp.zeros_like(gt1)
+    gt2[...] = jnp.zeros_like(gt2)
+    gbt[...] = jnp.zeros_like(gbt)
+
+    def add(row, value):
+        gvec[row:row + 1, :] += jnp.sum(value, axis=0, keepdims=True)
+
+    for l in (1, 0):
+        r = 1 + 5 * l
+        load = pltpu.make_async_copy(xmid.at[l], x_v, sem.at[0])
+        load.start()
+
+        @pl.loop(0, IMG // 2)
+        def _(p):
+            d = d_v[pair(p), :]
+            add(r + 4, d)
+            do_v[pair(p), :] = d.astype(bf16)
+        send = pltpu.make_async_copy(do_v, dout.at[l], sem.at[1])
+        send.start()
+
+        def blocks(i, slot):
+            t, h = i // 2, i % 2
+            part = pl.ds(pl.multiple_of(h * BLK, BLK), BLK)
+            whole = pl.ds(pl.multiple_of(i * BLK, BLK), BLK)
+            return [(wc.at[2 * l, t, :, part], w1_v.at[slot]), (wc.at[2 * l + 1, t, part, :], w2_v.at[slot]),
+                    (pre_in.at[l, :, whole], pre_v.at[slot])]
+
+        def outs(i, slot):
+            return [(dp_v.at[slot], dpre.at[l, :, pl.ds(pl.multiple_of(i * BLK, BLK), BLK)])]
+
+        def channel(i, slot):
+            _, slope = gelu_both(pre_v[slot])
+            d = dot_nt(do_v[...], w2_v[slot]) * slope
+            gbch1[l:l + 1, pl.ds(pl.multiple_of(i * BLK, BLK), BLK)] = jnp.sum(d, axis=0, keepdims=True)
+            dp_v[slot] = d.astype(bf16)
+            part = dot_nt(dp_v[slot], w1_v[slot])
+
+            @pl.when(i == 0)
+            def _():
+                dv_v[...] = part
+
+            @pl.when(i > 0)
+            def _():
+                dv_v[...] += part
+        for_blocks(Stream(sem_w, blocks, NBLK), channel, Stream(sem_o, outs, NBLK))
+        load.wait()
+        send.wait()
+
+        @pl.loop(0, IMG)
+        def _(b):
+            std, inv = standardize(x_v[image(b), :])
+            d = dv_v[image(b), :]
+            add(r + 2, d * std)
+            add(r + 3, d)
+            d_v[image(b), :] += norm_grad(d, vec[r + 2:r + 3, :], std, inv)
+        load = pltpu.make_async_copy(xin.at[l], x_v, sem.at[0])
+        load.start()
+        load.wait()
+
+        @pl.loop(0, IMG)
+        def _(b):
+            std, inv = standardize(x_v[image(b), :])
+            a = (std * vec[r:r + 1, :] + vec[r + 1:r + 2, :]).astype(bf16)
+            d_mid = d_v[image(b), :]
+            dm = d_mid.astype(bf16)
+            act, slope = gelu_both(dot_nn(wt1[l], a) + bt1[l])
+            g_v[...] = act.astype(bf16)
+            dh = dot_nn(wt2[l], dm) * slope
+            gbt[l] += jnp.sum(dh, axis=-1, keepdims=True)
+            dh_v[...] = dh.astype(bf16)
+            gt2[l] += dot_nt(g_v[...], dm)
+            gt1[l] += dot_nt(dh_v[...], a)
+            d = dot_tn(wt1[l], dh_v[...])
+            add(r, d * std)
+            add(r + 1, d)
+            d_v[image(b), :] = d_mid + norm_grad(d, vec[r:r + 1, :], std, inv)
+
+    @pl.loop(0, IMG // 2)
+    def _(p):
+        d = d_v[pair(p), :]
+        add(0, d)
+        do_v[pair(p), :] = d.astype(bf16)
+    send = pltpu.make_async_copy(do_v, dstem, sem.at[1])
+    send.start()
+    send.wait()
+
+
+def backward(xin, xmid, pre, wc, wt1, wt2, bt1, vec, dx0):
+    a, v = pl.BlockSpec(memory_space=pl.ANY), pl.BlockSpec(memory_space=pltpu.VMEM)
+    S = jax.ShapeDtypeStruct
+    return pl.pallas_call(
+        backward_kernel, name='backward',
+        in_specs=[a] * 4 + [v] * 5,
+        out_specs=[a] * 3 + [v] * 5,
+        out_shape=[S((2, ROWS, CHH), bf16), S((2, ROWS, CH), bf16), S((ROWS, CH), bf16), S((16, CH), f32), S((2, CHH), f32),
+                   S((2, TOKH, TPAD), f32), S((2, TOKH, TPAD), f32), S((2, TOKH, 1), f32)],
+        scratch_shapes=[pltpu.VMEM((ROWS, CH), f32), pltpu.VMEM((ROWS, CH), f32), pltpu.VMEM((ROWS, CH), f32),
+                        pltpu.VMEM((ROWS, CH), bf16), pltpu.VMEM((2, CH, BLK), bf16), pltpu.VMEM((2, BLK, CH), bf16),
+                        pltpu.VMEM((2, ROWS, BLK), f32), pltpu.VMEM((2, ROWS, BLK), bf16), pltpu.VMEM((TOKH, CH), bf16),
+                        pltpu.VMEM((TOKH, CH), bf16), pltpu.SemaphoreType.DMA((2,)), pltpu.SemaphoreType.DMA((2, 3)),
+                        pltpu.SemaphoreType.DMA((2, 1))],
+        compiler_params=pltpu.CompilerParams(vmem_limit_bytes=60 * 1024 * 1024),
+        cost_estimate=pl.CostEstimate(flops=50_000_000_000, bytes_accessed=100_000_000, transcendentals=0),
+    )(xin, xmid, pre, wc, wt1, wt2, bt1, vec, dx0)
+
 CHANNEL_AXES = ('tp', 'fsdp')
-
-
-def product(form, left, right):
-    return jnp.einsum(form, left, right, preferred_element_type=f32)
-
-
-def bf(x):
-    return x.astype(bf16)
-
-
-def norm_forward(values, gain, shift):
-    mean_val = jnp.mean(values, axis=-1, keepdims=True)
-    cent = values - mean_val
-    inv_std = lax.rsqrt(jnp.mean(cent * cent, axis=-1, keepdims=True) + EPS)
-    standard = cent * inv_std
-    return standard * gain + shift, standard, inv_std
-
-
-def norm_backward(grad_out, gain, standard, inv_std):
-    gs = grad_out * gain
-    m0 = jnp.mean(gs, axis=-1, keepdims=True)
-    m1 = jnp.mean(gs * standard, axis=-1, keepdims=True)
-    return inv_std * (gs - m0 - standard * m1)
-
-
-def gelu_grad(pre_act, grad_out):
-    return jax.vjp(jax.nn.gelu, pre_act)[1](grad_out)[0]
 
 
 def weight_specs():
@@ -473,19 +778,18 @@
              ln2_g, ln2_b, w_ch1, b_ch1, w_ch2, b_ch2, lnf_g, lnf_b, w_head, b_head):
         t = lax.axis_index('tp')
         nl = w_tok1.shape[0]
-        bl = patches.shape[0] // tp
-        tokens = patches.shape[1]
-        rows = bl * tokens
-        total_images = bl * nd
-        pat = lax.dynamic_slice_in_dim(patches, t * bl, bl, 0)
-        pat = pat.transpose(1, 0, 2).reshape(rows, -1)
-        lab = lax.dynamic_slice_in_dim(labels, t * bl, bl, 0)
-
-        vecs = [b_stem[None], ln1_g, ln1_b, ln2_g, ln2_b, b_ch2, lnf_g[None], lnf_b[None]]
-        vec_rows = jnp.concatenate(vecs, axis=0)
+        total_images = IMG * nd
+        pat = lax.dynamic_slice_in_dim(patches, t * IMG, IMG, 0)
+        pat = jnp.pad(pat, ((0, 0), (0, TPAD - TOK), (0, 0))).reshape(ROWS, -1)
+        lab = lax.dynamic_slice_in_dim(labels, t * IMG, IMG, 0)
+
+        vecs = [b_stem[None]]
+        for l in range(nl):
+            vecs += [a[l:l + 1] for a in (ln1_g, ln1_b, ln2_g, ln2_b, b_ch2)]
+        vec_rows = jnp.concatenate(vecs + [lnf_g[None], lnf_b[None]], axis=0)
         n_rows = vec_rows.shape[0]
-        pieces = [vec_rows.reshape(-1), b_ch1.reshape(-1), b_tok1.reshape(-1), b_head.reshape(-1),
-                  w_tok1.reshape(-1), w_tok2.reshape(-1)]
+        toks = jnp.pad(jnp.concatenate([w_tok1.transpose(0, 2, 1), w_tok2], axis=0), ((0, 0), (0, 0), (0, TPAD - TOK)))
+        pieces = [vec_rows.reshape(-1), b_ch1.reshape(-1), b_tok1.reshape(-1), b_head.reshape(-1), toks.reshape(-1)]
         pack = jnp.concatenate(pieces)
         pack = jnp.pad(pack, (0, (-pack.shape[0]) % 1024))
         small = lax.all_gather(pack, CHANNEL_AXES, axis=0, tiled=False).reshape(tp, fs, -1)
@@ -494,104 +798,34 @@
         for p in pieces:
             offs.append(small[:, :, o:o + p.shape[0]])
             o += p.shape[0]
-        vec_all = offs[0].reshape(tp, fs, n_rows, -1).transpose(2, 0, 1, 3).reshape(n_rows, -1)
+        vec = offs[0].reshape(tp, fs, n_rows, -1).transpose(2, 0, 1, 3).reshape(n_rows, -1)
         bch1 = offs[1].reshape(tp, fs, nl, -1).transpose(2, 0, 1, 3).reshape(nl, -1)
-        btok1 = offs[2][0].reshape(fs, nl, -1).transpose(1, 0, 2).reshape(nl, -1)
+        bt1 = offs[2][0].reshape(fs, nl, -1).transpose(1, 0, 2).reshape(nl, -1)[:, :, None]
         bhead = offs[3][:, 0]
-        wtok1 = bf(offs[4][0].reshape(fs, nl, tokens, -1).transpose(1, 2, 0, 3).reshape(nl, tokens, -1))
-        wtok2 = bf(offs[5][0].reshape(fs, nl, -1, tokens).transpose(1, 0, 2, 3).reshape(nl, -1, tokens))
-        bstem = vec_all[0]
-        l1g, l1b, l2g, l2b, bc2 = [vec_all[1 + nl * i:1 + nl * (i + 1)] for i in range(5)]
-        lfg, lfb = vec_all[1 + 5 * nl], vec_all[2 + 5 * nl]
+        wt = offs[4][0].reshape(fs, 2 * nl, -1, TPAD).transpose(1, 0, 2, 3).reshape(2 * nl, TOKH, TPAD).astype(bf16)
 
         classes = w_head.shape[1]
         pad_cls = 256 - classes
-        pc = jnp.stack([bf(w_ch1[0]), bf(w_ch2[0]), bf(w_ch1[1]), bf(w_ch2[1])])
-        ph = jnp.pad(bf(w_head), ((0, 0), (0, pad_cls)))
-        wc, ws, wh = gather_weights(pc, bf(w_stem), ph)
-        c = w_stem.shape[1] * tp
-        ws = ws.reshape(-1, c)
-        wh = wh.reshape(c, -1)
-        wc = wc.reshape(2 * nl, tp, c, c)
-        bhead = jnp.pad(bhead, ((0, 0), (0, pad_cls)), constant_values=-1e30).reshape(-1)
-        col = lab // classes * 256 + lab % classes
-
-        resid = product('rp,pc->rc', pat, ws) + bstem
-        saved = []
-        for l in range(nl):
-            normed, n1s, n1i = norm_forward(resid, l1g[l], l1b[l])
-            normed = bf(normed).reshape(tokens, bl, c)
-            tok_pre = product('sbc,sj->bcj', normed, wtok1[l]) + btok1[l]
-            tok_act = bf(jax.nn.gelu(tok_pre))
-            resid = resid + product('bcj,js->sbc', tok_act, wtok2[l]).reshape(rows, c)
-            normed2, n2s, n2i = norm_forward(resid, l2g[l], l2b[l])
-            full_in = bf(normed2)
-            ch_pre = [product('rc,cd->rd', full_in, wc[2 * l, i]) + bch1[l, i * c:(i + 1) * c] for i in range(tp)]
-            ch_act = [bf(jax.nn.gelu(p)) for p in ch_pre]
-            for i in range(tp):
-                resid = resid + product('rd,dc->rc', ch_act[i], wc[2 * l + 1, i])
-            resid = resid + bc2[l]
-            saved.append((normed, n1s, n1i, tok_pre, tok_act, n2s, n2i, full_in, ch_pre, ch_act))
-
-        pooled = jnp.mean(resid.reshape(tokens, bl, c), axis=0)
-        head_in, hs, hi = norm_forward(pooled, lfg, lfb)
-        head_bf = bf(head_in)
-        logits = product('bc,ck->bk', head_bf, wh) + bhead
-        is_label = jnp.arange(logits.shape[1])[None, :] == col[:, None]
-        row_max = jnp.max(logits, axis=1, keepdims=True)
-        ex = jnp.exp(logits - row_max)
-        es = jnp.sum(ex, axis=1, keepdims=True)
-        log_norm = row_max + jnp.log(es)
-        loss_loc = jnp.sum(log_norm) - jnp.sum(jnp.where(is_label, logits, 0.0))
-
-        d_logits = (ex / es - is_label.astype(f32)) / total_images
-        dlb = bf(d_logits)
-        g_bhead = jnp.sum(d_logits, axis=0)
-        d_hin = product('bk,ck->bc', dlb, wh)
-        g_lfg = jnp.sum(d_hin * hs, axis=0)
-        g_lfb = jnp.sum(d_hin, axis=0)
-        d_pooled = norm_backward(d_hin, lfg, hs, hi)
-        d_resid = jnp.broadcast_to((d_pooled / tokens)[None], (tokens, bl, c)).reshape(rows, c)
-
-        wides, narrows = [None] * 5, [None] * 5
-        sm = {}
-        for l in reversed(range(nl)):
-            normed, n1s, n1i, tok_pre, tok_act, n2s, n2i, full_in, ch_pre, ch_act = saved[l]
-            sm['b_ch2', l] = jnp.sum(d_resid, axis=0)
-            dob = bf(d_resid)
-            wides[2 * l + 1], narrows[2 * l + 1] = jnp.concatenate(ch_act, axis=1), dob
-            d_pre = [gelu_grad(ch_pre[i], product('rc,dc->rd', dob, wc[2 * l + 1, i])) for i in range(tp)]
-            sm['b_ch1', l] = jnp.concatenate([jnp.sum(d, axis=0) for d in d_pre])
-            dpb = [bf(d) for d in d_pre]
-            wides[2 * l], narrows[2 * l] = jnp.concatenate(dpb, axis=1), full_in
-            d_n2 = sum(product('rd,cd->rc', dpb[i], wc[2 * l, i]) for i in range(tp))
-            sm['ln2_g', l] = jnp.sum(d_n2 * n2s, axis=0)
-            sm['ln2_b', l] = jnp.sum(d_n2, axis=0)
-            d_mid = d_resid + norm_backward(d_n2, l2g[l], n2s, n2i)
-            dmb = bf(d_mid).reshape(tokens, bl, c)
-            sm['w_tok2', l] = product('bcj,sbc->js', tok_act, dmb)
-            d_tp = gelu_grad(tok_pre, product('sbc,js->bcj', dmb, wtok2[l]))
-            sm['b_tok1', l] = jnp.sum(d_tp, axis=(0, 1))
-            dtb = bf(d_tp)
-            sm['w_tok1', l] = product('sbc,bcj->sj', normed, dtb)
-            d_n1 = product('bcj,sj->sbc', dtb, wtok1[l]).reshape(rows, c)
-            sm['ln1_g', l] = jnp.sum(d_n1 * n1s, axis=0)
-            sm['ln1_b', l] = jnp.sum(d_n1, axis=0)
-            d_resid = d_mid + norm_backward(d_n1, l1g[l], n1s, n1i)
-        g_bstem = jnp.sum(d_resid, axis=0)
-        wides[4], narrows[4] = pat, bf(d_resid)
-
-        def st(key):
-            return jnp.stack([sm[key, l] for l in range(nl)])
-        parts = [g_bstem, st('ln1_g'), st('ln1_b'), st('ln2_g'), st('ln2_b'), st('b_ch2'), g_lfg, g_lfb,
-                 st('b_ch1'), st('b_tok1'), g_bhead, st('w_tok1'), st('w_tok2'), loss_loc[None]]
+        pc = jnp.stack([w_ch1[0], w_ch2[0], w_ch1[1], w_ch2[1]]).astype(bf16)
+        ph = jnp.pad(w_head.astype(bf16), ((0, 0), (0, pad_cls)))
+        wc, ws, wh = gather_weights(pc, w_stem.astype(bf16), ph)
+        ws = ws.reshape(-1, CH)
+        wh = wh.reshape(CH, -1)
+        wc = wc.reshape(2 * nl, tp, CH, CH)
+        bhead = jnp.pad(bhead, ((0, 0), (0, pad_cls)), constant_values=-1e30).reshape(1, -1)
+        label = (lab // classes * 256 + lab % classes).reshape(IMG, 1)
+
+        xin, xmid, vin, pre, act, hl, hr, dx0, hstat, gbh = forward(pat, ws, wc, wh, wt[:nl], wt[nl:], bt1, vec, bch1,
+                                                                    bhead, label)
+        dpre, dout, dstem, gvec, gbch1, gt1, gt2, gbt = backward(xin, xmid, pre, wc, wt[:nl], wt[nl:], bt1, vec, dx0)
+
+        gvec = jnp.concatenate([gvec[:11], hstat[:2]], axis=0)
+        parts = [gvec, gbch1, gbt[:, :, 0], gbh, gt1, gt2, hstat[2, :1]]
         flat = jnp.concatenate([p.reshape(-1) for p in parts])
         flat = jnp.pad(flat, (0, (-flat.shape[0]) % 1024))
         tot = lax.psum(flat, CHANNEL_AXES)
 
-        g_c, g_s, g_h = reduce_gradients(wides, narrows, head_bf, dlb)
-        g_ch1, g_ch2 = g_c[0::2], g_c[1::2]
-        g_head = g_h[:, :classes]
+        g_c, g_s, g_h = reduce_gradients(dpre, act, pat, vin, dout, dstem, hl, hr)
 
         out = []
         o = 0
@@ -599,18 +833,21 @@
             out.append(tot[o:o + p.size].reshape(p.shape))
             o += p.size
         f = lax.axis_index('fsdp')
-        dev = t * fs + f
 
         def own(x, n, i, ax):
             size = x.shape[ax] // n
             return lax.dynamic_slice_in_dim(x, i * size, size, ax)
-        (gb, g1g, g1b, g2g, g2b, gc2, gfg, gfb, gc1, gt1, gbh, gw1, gw2, ls) = out
-        loss = ls[0] / total_images
-        return (loss, g_s, own(gb, nd, dev, 0), own(g1g, nd, dev, 1), own(g1b, nd, dev, 1),
-                own(gw1, fs, f, 2), own(gt1, fs, f, 1), own(gw2, fs, f, 1),
-                own(g2g, nd, dev, 1), own(g2b, nd, dev, 1), g_ch1, own(gc1, nd, dev, 1),
-                g_ch2, own(gc2, nd, dev, 1), own(gfg, nd, dev, 0), own(gfb, nd, dev, 0),
-                g_head, own(gbh.reshape(tp, 256), tp, t, 0)[0, :classes])
+        dev = t * fs + f
+        gv = own(out[0], nd, dev, 1)
+        gc1 = own(out[1], nd, dev, 1)
+        gtb = own(out[2], fs, f, 1)
+        gbh = own(out[3].reshape(tp, 256), tp, t, 0)[0, :classes]
+        gw1 = own(out[4], fs, f, 1)[:, :, :TOK].transpose(0, 2, 1)
+        gw2 = own(out[5], fs, f, 1)[:, :, :TOK]
+        loss = out[6][0] / total_images
+        per = [jnp.stack([gv[1 + i], gv[6 + i]]) for i in range(5)]
+        return (loss, g_s, gv[0], per[0], per[1], gw1, gtb, gw2, per[2], per[3], g_c[0::2], gc1, g_c[1::2], per[4],
+                gv[11], gv[12], g_h[:, :classes], gbh)
 
     specs = weight_specs()
     return jax.shard_map(step, mesh=mesh, in_specs=(P('fsdp', None, None), P('fsdp')) + specs,

time: 556 us -> 477 us (0.86); the launches traced: 547 us -> 474 us
  matrix products: 185 us -> 0 us
  Pallas kernels: 251 us -> 406 us
  other arithmetic: 41.7 us -> 10.7 us
  local copies, waits for them, and re-layouts: 50.3 us -> 41.2 us
    dot_general x47 -> x0, matrix products: 185 us -> none  [product(): return jnp.einsum(form, left, right, preferred_element_type=f32)]
    pallas_call x0 -> x2, Pallas kernels: none -> 155 us  [the longest x1 89.2 us: backward(): pl.pallas_call(backward_kernel, name='backward', in_specs=[a] * 4 + [v] *...]
    reduce_sum x16 -> x0, other arithmetic: 15.6 us -> none  [the longest x2 4.37 us: step(): sm['b_ch2', l] = jnp.sum(d_resid, axis=0)]
    concatenate x6 -> x2, other arithmetic: 8.13 us -> 1.6 us  [the longest x1 0.85 us: step(): gvec = jnp.concatenate([gvec[:11], hstat[:2]], axis=0)]
    dynamic_slice x12 -> x2, local copies, waits for them, and re-layouts: 6.88 us -> 1.27 us  [own(): return lax.dynamic_slice_in_dim(x, i * size, size, ax)]
  transfers between devices with their start and end apart: 2 -> 2, of which waited for: 0 -> 0; matrix products, arithmetic and copies ran while one was open for 2% -> 3% of each run, Pallas kernels for 46% -> 53%
where the time goes in v4:
time: 477 us; the launch traced here: 474 us
  Pallas kernels  406 us (85%)
  local copies, waits for them, and re-layouts  41.2 us (9%)
  between operations  16.2 us (3%)
  other arithmetic  10.7 us (2%)
    pallas_call x1, Pallas kernels, reduce_gradients(): pl.pallas_call(reduce_kernel, name='reduce_gradients', out_shape=[jax.Sha...  150 us
    pallas_call x1, Pallas kernels, gather_weights(): pl.pallas_call(gather_kernel, name='gather_weights', out_shape=[jax.Shape...  101 us
    pallas_call x1, Pallas kernels, backward(): pl.pallas_call(backward_kernel, name='backward', in_specs=[a] * 4 + [v] *...  89.2 us
    pallas_call x1, Pallas kernels, forward(): pl.pallas_call(forward_kernel, name='forward', in_specs=[a, a, a, a] + [v...  65.8 us
  transfers between devices with their start and end apart: 2, of which 0 were waited for; matrix products, arithmetic and copies ran while one was open for 3% of the time, Pallas kernels for 53%

profile of v4, /device:TPU:0, one launch (start us, length us, event | category | flops | bytes accessed | tf_op | source)
XLA Modules:
  0.0 474.2 jit_solution(4873916612172770173)
XLA Ops:
  8.0 0.8 fusion.9
  8.8 0.8 fusion.11
  9.5 1.4 concatenate.15
  11.8 0.8 reshape.143
  14.8 1.0 convert.15
  15.7 1.0 convert.16
  16.7 1.5 convert_element_type.25.ps
  18.2 0.8 convert_element_type.26
  20.4 100.8 %gather_weights.1 = (bf16[4,4,4,4,2,32,1024]{6,5,4,3,2,1,0:T(8,128)(2,1)}, bf16[4,4,2,96,1024]{4,3,2,1,0:T(8,128)(2,1)}, bf16[4,4,2,32,1024]{4,3,2,1,0:T(8,128)(2,1)}) custom-call(bf16[4,32,1024]{2,1,0:T(8,128)(2,1)} %pad_maximum_fusion.pc, bf16[96,256]{1,0:T(8,128)(2,1)} %convert_element_type.25.ps, bf16[32,256]{1,0:T(8,128)(2,1)} %pad.25.ph), custom_call_target="tpu_custom_call" | custom-call | flops 89999998976 | bytes 80000000 | tf_op jit(solution)/shard_map/gather_weights/pallas_call | solution.py:165
  121.2 1.8 constant_dynamic-slice_fusion.5
  123.0 1.4 copy.63
  124.4 1.8 pad.24.clone
  127.0 1.7 reshape.146
  129.1 1.1 convert_element_type.27
  132.1 1.1 reshape.148.vec
  133.3 1.1 broadcast_in_dim_reshape.4.bt1
  135.9 65.8 %forward.1 = (f32[2,448,1024]{2,1,0:T(8,128)}, f32[2,448,1024]{2,1,0:T(8,128)}, bf16[2,448,1024]{2,1,0:T(8,128)(2,1)}, f32[2,448,4096]{2,1,0:T(8,128)}, bf16[2,4...) custom-call(bf16[448,3072]{1,0:T(8,128)(2,1)} %bitcast.52, ...), custom_call_target="tpu_custom_call" | custom-call | flops 49999998976 | bytes 100000000 | tf_op jit(solution)/shard_map/forward/pallas_call | solution.py:632
  201.8 0.8 slice.223
  202.5 1.2 slice.224
  203.7 89.2 %backward.1 = (bf16[2,448,4096]{2,1,0:T(8,128)(2,1)}, bf16[2,448,1024]{2,1,0:T(8,128)(2,1)}, bf16[448,1024]{1,0:T(8,128)(2,1)}, f32[16,1024]{1,0:T(8,128)}, f32[...) custom-call(f32[2,448,1024]{2,1,0:T(8,128)} %get-tuple-element.45.xin, ...), custom_call_target="tpu_custom_call" | custom-call | flops 49999998976 | bytes 100000000 | tf_op jit(solution)/shard_map/backward/pallas_call | solution.py:746
  292.9 0.9 pad_maximum_fusion.1
  293.8 0.8 copy.65
  294.6 1.2 reduce
  295.8 1.4 reshape.156
  297.2 1.4 reshape.157
  299.4 0.9 pad.29
  300.3 150.2 %reduce_gradients.1 = (f32[4,32,1024]{2,1,0:T(8,128)}, f32[96,256]{1,0:T(8,128)}, f32[32,256]{1,0:T(8,128)}) custom-call(bf16[2,448,4096]{2,1,0:T(8,128)(2,1)} %get-tuple-element.56.refs_0_, bf16[2,448,4096]{2,1,0:T(8,128)(2,1)} %get-tuple-element.57.refs_1_, bf16[448,3072]{1,0:T(8,128)(2,1)} %bitcast.53, bf16[2,448,1024]{2,1,0:T(8,128)(2,1)} %get-tuple-element.58.refs_3_, ...), custom_call_target="tpu_custom_call" | custom-call | flops 99999997952 | bytes 80000000 | tf_op jit(solution)/shard_map/reduce_gradients/pallas_call | solution.py:417
  450.5 1.9 fusion.5
  452.4 0.8 slice.266
  453.2 1.1 fusion.4
  456.4 0.8 slice.270
  463.1 1.2 slice.265
  (73 shorter events, 19.9 us)
Async XLA Ops:
  7.2 119.8 %all-gather.3.cloned.1.call-start = ((), (), s32[]{:S(2)}) async-start(), calls=%async_computation.1 | async-start | bytes 2113536 | tf_op jit(solution)/shard_map/all_gather | solution.py:795
  14.7 437.7 %all-reduce.8.cloned.1.call-start = ((), (), s32[]{:S(2)}) async-start(), calls=%async_computation | async-start | bytes 1114112 | tf_op jit(solution)/shard_map/psum | solution.py:826
  124.4 1.8 copy-start.3
  203.7 94.9 %copy-start.2 = (f32[1,1024]{1,0:T(1,128)S(1)}, f32[1,1024]{1,0:T(1,128)}, u32[]{:S(2)}) copy-start(f32[1,1024]{1,0:T(1,128)} %get-tuple-element.53) | copy-start | bytes 12292
  450.5 14.5 %copy-start = (f32[96,256]{1,0:T(8,128)S(1)}, f32[96,256]{1,0:T(8,128)}, u32[]{:S(2)}) copy-start(f32[96,256]{1,0:T(8,128)} %get-tuple-element.126) | copy-start | bytes 294916
  450.5 15.1 %copy-start.1 = (f32[32,256]{1,0:T(8,128)S(1)}, f32[32,256]{1,0:T(8,128)}, u32[]{:S(2)}) copy-start(f32[32,256]{1,0:T(8,128)} %get-tuple-element.65) | copy-start | bytes 98308
Sparse Core Ops, SparseCore 0:
  14.8 69.6 all-gather.2
  300.4 146.4 all-reduce.7

commit v5 on v4

--- a/solution.py
+++ b/solution.py
@@ -52,127 +52,6 @@
         copy.start()
         self.started.append(copy)
         return copy
-
-
-GATHER_COPIES = 7 * 8 + 16 * 4 + 16 * 4
-
-
-def gather_kernel(pc, ps, ph, wc, ws, wh, send_sems, recv_sems, local_sems):
-    me = my_place()
-    other = moved(me, 'k', 1)
-    meet_neighbours(me)
-    sender = Sender(send_sems, recv_sems)
-    every = pl.ds(0, 4)
-
-    def view(kind, colour, block, half=None, group=None, k=None):
-        k = me['k'] if k is None else k
-        x, z, y = block['x'], block['z'], block['y']
-        r0, rn = (0, 32) if half is None else (16 * half, 16)
-        if kind == 'ch':
-            c0, cn = COLS[colour]
-            return wc.at[every if group is None else group, x, z, y, k, pl.ds(r0, rn), pl.ds(c0, cn)]
-        cols = pl.ds(0, 1024) if x is every else pl.ds(pl.multiple_of(x * 256, 256), 256)
-        if kind == 'stem':
-            return ws.at[z, y, k, pl.ds(32 * colour + r0, rn), cols]
-        return wh.at[z, y, k, pl.ds(r0, rn), cols]
-
-    def piece(kind, colour):
-        if kind == 'ch':
-            c0, cn = COLS[colour]
-            return pc.at[:, :, pl.ds(c0, cn)]
-        if kind == 'stem':
-            return ps.at[pl.ds(32 * colour, 32), :]
-        return ph.at[:, :]
-
-    early = [('stem', 0), ('stem', 1), ('stem', 2), ('ch', 0), ('ch', 1), ('ch', 2), ('head', 2)]
-    late = [('stem', c, None) for c in range(3)] + [('ch', c, g) for g in range(N_CH) for c in range(3)]
-    late += [('head', 2, None)]
-
-    own = [pltpu.make_async_copy(piece(kind, c), view(kind, c, me), local_sems.at[i])
-           for i, (kind, c) in enumerate(early)]
-    for copy in own:
-        copy.start()
-
-    def exchange(unit, dim, block, src=None):
-        kind, c = unit[:2]
-        g = unit[2] if len(unit) > 2 else None
-        mine = view(kind, c, block, group=g)
-        source = mine if src is None else src
-        return [sender.start(source, mine, moved(me, dim, step)) for step in (1, 3)]
-
-    def forward(unit, dim, block):
-        kind, c = unit[:2]
-        g = unit[2] if len(unit) > 2 else None
-        out = []
-        for half, (origin, target) in enumerate(((3, 1), (1, 3))):
-            part = view(kind, c, {**block, dim: (me[dim] + origin) % 4}, half=half, group=g)
-            out.append(sender.start(part, part, moved(me, dim, target)))
-        return out
-
-    def arrived(copies):
-        for copy in copies:
-            copy.wait_recv()
-
-    first, second, third, swaps = {}, {}, {}, []
-    for u in early:
-        first[u] = exchange(u, ORDERS[u[1]][0], me, piece(*u))
-    for copy in own:
-        copy.wait()
-    for u in early:
-        arrived(first[u])
-        first[u] = forward(u, ORDERS[u[1]][0], me)
-    for u in early:
-        d1, d2, _ = ORDERS[u[1]]
-        arrived(first[u])
-        second[u] = exchange(u, d2, {**me, d1: every})
-    for u in early:
-        d1, d2, _ = ORDERS[u[1]]
-        arrived(second[u])
-        second[u] = forward(u, d2, {**me, d1: every})
-    done = set()
-    for u in late:
-        d1, d2, d3 = ORDERS[u[1]]
-        if u[:2] not in done:
-            arrived(second[u[:2]])
-            done.add(u[:2])
-        plane = {**me, d1: every, d2: every}
-        third[u] = exchange(u, d3, plane)
-        mine = view(u[0], u[1], plane, group=u[2])
-        swaps.append(sender.start(mine, mine, other))
-    for u in late:
-        d1, d2, d3 = ORDERS[u[1]]
-        plane = {**me, d1: every, d2: every}
-        arrived(third[u])
-        third[u] = forward(u, d3, plane)
-        for step in (1, 3):
-            part = view(u[0], u[1], {**plane, d3: (me[d3] + step) % 4}, group=u[2])
-            swaps.append(sender.start(part, part, other))
-    for u in late:
-        d1, d2, d3 = ORDERS[u[1]]
-        plane = {**me, d1: every, d2: every}
-        arrived(third[u])
-        part = view(u[0], u[1], {**plane, d3: (me[d3] + 2) % 4}, group=u[2])
-        swaps.append(sender.start(part, part, other))
-    arrived(swaps)
-    for copy in sender.started:
-        copy.wait_send()
-    assert sender.count == GATHER_COPIES, sender.count
-
-
-def gather_weights(pc, ps, ph):
-    any_spec = pl.BlockSpec(memory_space=pl.ANY)
-    vmem = pl.BlockSpec(memory_space=pltpu.VMEM)
-    return pl.pallas_call(
-        gather_kernel, name='gather_weights',
-        out_shape=[jax.ShapeDtypeStruct((N_CH, 4, 4, 4, 2, 32, 1024), bf16),
-                   jax.ShapeDtypeStruct((4, 4, 2, 96, 1024), bf16),
-                   jax.ShapeDtypeStruct((4, 4, 2, 32, 1024), bf16)],
-        in_specs=[vmem] * 3, out_specs=[any_spec] * 3,
-        scratch_shapes=[pltpu.SemaphoreType.DMA((GATHER_COPIES,)), pltpu.SemaphoreType.DMA((GATHER_COPIES,)),
-                        pltpu.SemaphoreType.DMA((7,))],
-        compiler_params=pltpu.CompilerParams(collective_id=0, has_side_effects=True),
-        cost_estimate=pl.CostEstimate(flops=90_000_000_000, bytes_accessed=80_000_000, transcendentals=0),
-    )(pc, ps, ph)
 
 
 GROUPS = (STEM, 3, 2, 1, 0, HEAD)
@@ -529,124 +408,7 @@
         out.wait(n - 1, 1 - n % 2)
 
 
-def forward_kernel(pat, ws, wc, wh, wt1, wt2, bt1, vec, bch1, bhead, label,
-                   xin, xmid, vout, pre_out, act_out, hl, hr, dx0, hstat, gbh,
-                   p_v, x_v, v_v, w1_v, w2_v, ws_v, wh_v, pre_v, act_v, g_v, sem, sem_w, sem_o, sem_x):
-    load_p = pltpu.make_async_copy(pat, p_v, sem.at[0])
-    load_p.start()
-    load_h = pltpu.make_async_copy(wh, wh_v, sem.at[1])
-    load_h.start()
-    load_p.wait()
-
-    def stem_copies(i, slot):
-        return [(ws.at[:, pl.ds(pl.multiple_of(i * 256, 256), 256)], ws_v.at[slot])]
-
-    def stem(i, slot):
-        cols = pl.ds(pl.multiple_of(i * 256, 256), 256)
-        mask = (lax.broadcasted_iota(jnp.int32, (ROWS, 1), 0) % TPAD) < TOK
-        x_v[:, cols] = jnp.where(mask, dot_nn(p_v[...], ws_v[slot]) + vec[0:1, cols], 0.0)
-    for_blocks(Stream(sem_w, stem_copies, 4), stem)
-
-    saves = []
-
-    def save(src, dst, n):
-        copy = pltpu.make_async_copy(src, dst, sem_x.at[n])
-        copy.start()
-        saves.append(copy)
-
-    for l in range(2):
-        r = 1 + 5 * l
-        for copy in saves:
-            copy.wait()
-        saves.clear()
-        first = pltpu.make_async_copy(x_v, xin.at[l], sem_x.at[0])
-        first.start()
-        first.wait()
-
-        @pl.loop(0, IMG)
-        def _(b):
-            x = x_v[image(b), :]
-            std, _ = standardize(x)
-            a = (std * vec[r:r + 1, :] + vec[r + 1:r + 2, :]).astype(bf16)
-            h = dot_nn(wt1[l], a) + bt1[l]
-            g_v[...] = gelu(h).astype(bf16)
-            x_v[image(b), :] = x + dot_tn(wt2[l], g_v[...])
-        save(x_v, xmid.at[l], 0)
-
-        @pl.loop(0, IMG // 2)
-        def _(p):
-            std, _ = standardize(x_v[pair(p), :])
-            v_v[pair(p), :] = (std * vec[r + 2:r + 3, :] + vec[r + 3:r + 4, :]).astype(bf16)
-        save(v_v, vout.at[l], 1)
-        saves[0].wait()
-        saves.pop(0)
-
-        def blocks(i, slot):
-            t, h = i // 2, i % 2
-            part = pl.ds(pl.multiple_of(h * BLK, BLK), BLK)
-            return [(wc.at[2 * l, t, :, part], w1_v.at[slot]), (wc.at[2 * l + 1, t, part, :], w2_v.at[slot])]
-
-        def outs(i, slot):
-            part = pl.ds(pl.multiple_of(i * BLK, BLK), BLK)
-            return [(pre_v.at[slot], pre_out.at[l, :, part]), (act_v.at[slot], act_out.at[l, :, part])]
-
-        def channel(i, slot):
-            part = pl.ds(pl.multiple_of(i * BLK, BLK), BLK)
-            h = dot_nn(v_v[...], w1_v[slot]) + bch1[l:l + 1, part]
-            pre_v[slot] = h
-            act_v[slot] = gelu(h).astype(bf16)
-            x_v[...] += dot_nn(act_v[slot], w2_v[slot])
-        for_blocks(Stream(sem_w, blocks, NBLK), channel, Stream(sem_o, outs, NBLK))
-        x_v[...] += vec[r + 4:r + 5, :]
-    for copy in saves:
-        copy.wait()
-
-    load_h.wait()
-    last = 11
-    mask = row_mask()
-    pooled = jnp.concatenate([jnp.sum(jnp.where(mask, x_v[b * TPAD:(b + 1) * TPAD, :], 0.0), axis=0, keepdims=True)
-                              for b in range(IMG)], axis=0) * (1.0 / TOK)
-    std, inv = standardize(pooled)
-    head_in = (std * vec[last:last + 1, :] + vec[last + 1:last + 2, :]).astype(bf16)
-    hl[...] = head_in
-    logits = dot_nn(head_in, wh_v[...]) + bhead[...]
-    is_label = lax.broadcasted_iota(jnp.int32, logits.shape, 1) == label[...]
-    top = jnp.max(logits, axis=-1, keepdims=True)
-    ex = jnp.exp(logits - top)
-    es = jnp.sum(ex, axis=-1, keepdims=True)
-    nll = top + jnp.log(es) - jnp.sum(jnp.where(is_label, logits, 0.0), axis=-1, keepdims=True)
-    d_logits = (ex / es - jnp.where(is_label, 1.0, 0.0)) * (1.0 / 1024)
-    gbh[...] = jnp.sum(d_logits, axis=0, keepdims=True)
-    d_bf = d_logits.astype(bf16)
-    hr[...] = d_bf
-    d_in = dot_nt(d_bf, wh_v[...])
-    hstat[0:1, :] = jnp.sum(d_in * std, axis=0, keepdims=True)
-    hstat[1:2, :] = jnp.sum(d_in, axis=0, keepdims=True)
-    hstat[2:3, :] = jnp.broadcast_to(jnp.sum(nll, axis=0, keepdims=True), (1, CH))
-    dx0[...] = norm_grad(d_in, vec[last:last + 1, :], std, inv) * (1.0 / TOK)
-
-
-def forward(pat, ws, wc, wh, wt1, wt2, bt1, vec, bch1, bhead, label):
-    a, v = pl.BlockSpec(memory_space=pl.ANY), pl.BlockSpec(memory_space=pltpu.VMEM)
-    S = jax.ShapeDtypeStruct
-    return pl.pallas_call(
-        forward_kernel, name='forward',
-        in_specs=[a, a, a, a] + [v] * 7,
-        out_specs=[a] * 5 + [v] * 5,
-        out_shape=[S((2, ROWS, CH), f32), S((2, ROWS, CH), f32), S((2, ROWS, CH), bf16), S((2, ROWS, CHH), f32),
-                   S((2, ROWS, CHH), bf16), S((IMG, CH), bf16), S((IMG, CH), bf16), S((IMG, CH), f32), S((8, CH), f32),
-                   S((1, CH), f32)],
-        scratch_shapes=[pltpu.VMEM((ROWS, 3072), bf16), pltpu.VMEM((ROWS, CH), f32), pltpu.VMEM((ROWS, CH), bf16),
-                        pltpu.VMEM((2, CH, BLK), bf16), pltpu.VMEM((2, BLK, CH), bf16), pltpu.VMEM((2, 3072, 256), bf16),
-                        pltpu.VMEM((CH, CH), bf16), pltpu.VMEM((2, ROWS, BLK), f32), pltpu.VMEM((2, ROWS, BLK), bf16),
-                        pltpu.VMEM((TOKH, CH), bf16), pltpu.SemaphoreType.DMA((2,)), pltpu.SemaphoreType.DMA((2, 2)),
-                        pltpu.SemaphoreType.DMA((2, 2)), pltpu.SemaphoreType.DMA((2,))],
-        compiler_params=pltpu.CompilerParams(vmem_limit_bytes=60 * 1024 * 1024),
-        cost_estimate=pl.CostEstimate(flops=50_000_000_000, bytes_accessed=100_000_000, transcendentals=0),
-    )(pat, ws, wc, wh, wt1, wt2, bt1, vec, bch1, bhead, label)
-
-
-def backward_kernel(xin, xmid, pre_in, wc, wt1, wt2, bt1, vec, dx0,
+def backward_kernel(xin, xmid, pre_in, wc, wt, vec, dx0,
                     dpre, dout, dstem, gvec, gbch1, gt1, gt2, gbt,
                     x_v, d_v, dv_v, do_v, w1_v, w2_v, pre_v, dp_v, g_v, dh_v, sem, sem_w, sem_o):
     mask = row_mask()
@@ -677,7 +439,8 @@
             t, h = i // 2, i % 2
             part = pl.ds(pl.multiple_of(h * BLK, BLK), BLK)
             whole = pl.ds(pl.multiple_of(i * BLK, BLK), BLK)
-            return [(wc.at[2 * l, t, :, part], w1_v.at[slot]), (wc.at[2 * l + 1, t, part, :], w2_v.at[slot]),
+            return [(wc.at[2 * l, t, :, :, :, :, part], w1_v.at[slot]),
+                    (wc.at[2 * l + 1, t, pl.ds(pl.multiple_of(h * 2, 2), 2)], w2_v.at[slot]),
                     (pre_in.at[l, :, whole], pre_v.at[slot])]
 
         def outs(i, slot):
@@ -685,10 +448,10 @@
 
         def channel(i, slot):
             _, slope = gelu_both(pre_v[slot])
-            d = dot_nt(do_v[...], w2_v[slot]) * slope
+            d = dot_nt(do_v[...], w2_v[slot].reshape(BLK, CH)) * slope
             gbch1[l:l + 1, pl.ds(pl.multiple_of(i * BLK, BLK), BLK)] = jnp.sum(d, axis=0, keepdims=True)
             dp_v[slot] = d.astype(bf16)
-            part = dot_nt(dp_v[slot], w1_v[slot])
+            part = dot_nt(dp_v[slot], w1_v[slot].reshape(CH, BLK))
 
             @pl.when(i == 0)
             def _():
@@ -715,17 +478,17 @@
         @pl.loop(0, IMG)
         def _(b):
             std, inv = standardize(x_v[image(b), :])
-            a = (std * vec[r:r + 1, :] + vec[r + 1:r + 2, :]).astype(bf16)
+            a = with_bias_rows(std * vec[r:r + 1, :] + vec[r + 1:r + 2, :])
             d_mid = d_v[image(b), :]
             dm = d_mid.astype(bf16)
-            act, slope = gelu_both(dot_nn(wt1[l], a) + bt1[l])
+            act, slope = gelu_both(dot_nn(wt[l, :, 0:TPAD], a))
             g_v[...] = act.astype(bf16)
-            dh = dot_nn(wt2[l], dm) * slope
+            dh = dot_nn(wt[2 + l, :, 0:TPAD], dm) * slope
             gbt[l] += jnp.sum(dh, axis=-1, keepdims=True)
             dh_v[...] = dh.astype(bf16)
             gt2[l] += dot_nt(g_v[...], dm)
             gt1[l] += dot_nt(dh_v[...], a)
-            d = dot_tn(wt1[l], dh_v[...])
+            d = jnp.where(mask, dot_tn(wt[l, :, 0:TPAD], dh_v[...]), 0.0)
             add(r, d * std)
             add(r + 1, d)
             d_v[image(b), :] = d_mid + norm_grad(d, vec[r:r + 1, :], std, inv)
@@ -740,23 +503,419 @@
     send.wait()
 
 
-def backward(xin, xmid, pre, wc, wt1, wt2, bt1, vec, dx0):
+def backward(*operands):
     a, v = pl.BlockSpec(memory_space=pl.ANY), pl.BlockSpec(memory_space=pltpu.VMEM)
     S = jax.ShapeDtypeStruct
     return pl.pallas_call(
         backward_kernel, name='backward',
-        in_specs=[a] * 4 + [v] * 5,
+        in_specs=[a] * 4 + [v] * 3,
         out_specs=[a] * 3 + [v] * 5,
         out_shape=[S((2, ROWS, CHH), bf16), S((2, ROWS, CH), bf16), S((ROWS, CH), bf16), S((16, CH), f32), S((2, CHH), f32),
                    S((2, TOKH, TPAD), f32), S((2, TOKH, TPAD), f32), S((2, TOKH, 1), f32)],
         scratch_shapes=[pltpu.VMEM((ROWS, CH), f32), pltpu.VMEM((ROWS, CH), f32), pltpu.VMEM((ROWS, CH), f32),
-                        pltpu.VMEM((ROWS, CH), bf16), pltpu.VMEM((2, CH, BLK), bf16), pltpu.VMEM((2, BLK, CH), bf16),
+                        pltpu.VMEM((ROWS, CH), bf16), pltpu.VMEM((2, 4, 4, 2, 32, BLK), bf16),
+                        pltpu.VMEM((2, 2, 4, 2, 32, CH), bf16),
                         pltpu.VMEM((2, ROWS, BLK), f32), pltpu.VMEM((2, ROWS, BLK), bf16), pltpu.VMEM((TOKH, CH), bf16),
                         pltpu.VMEM((TOKH, CH), bf16), pltpu.SemaphoreType.DMA((2,)), pltpu.SemaphoreType.DMA((2, 3)),
                         pltpu.SemaphoreType.DMA((2, 1))],
         compiler_params=pltpu.CompilerParams(vmem_limit_bytes=60 * 1024 * 1024),
         cost_estimate=pl.CostEstimate(flops=50_000_000_000, bytes_accessed=100_000_000, transcendentals=0),
-    )(xin, xmid, pre, wc, wt1, wt2, bt1, vec, dx0)
+    )(*operands)
+
+
+FRONT_COPIES = 240
+EARLY = [('stem', 0), ('stem', 1), ('stem', 2), ('ch', 0), ('ch', 1), ('ch', 2), ('head', 2)]
+LATE = [('stem', c, None) for c in range(3)] + [('ch', c, g) for g in range(N_CH) for c in range(3)] + [('head', 2, None)]
+UNIT_GROUP = {('stem', None): 0, ('ch', 0): 1, ('ch', 1): 2, ('ch', 2): 3, ('ch', 3): 4, ('head', None): 5}
+EVERY = pl.ds(0, 4)
+FRONT_ORDER = (
+    ('prep', (('M0', ('sm',)), ('M0', ('tk',)), ('A0', ('stem', 0)), ('A0', ('stem', 1)), ('A0', ('stem', 2)),
+        ('A0', ('ch', 0)), ('A0', ('ch', 1)), ('A0', ('ch', 2)), ('A0', ('head', 2)),)),
+    ('unpack', (('M1', ('sm',)), ('M1', ('tk',)), ('A', ('stem', 0)), ('A', ('stem', 1)), ('A', ('stem', 2)),
+        ('A', ('head', 2)), ('A', ('ch', 2)), ('A', ('ch', 0)), ('A', ('ch', 1)), ('B', ('stem', 0)), ('M2', ('sm',)),
+        ('B', ('stem', 1)), ('M2', ('tk',)), ('B', ('stem', 2)), ('B', ('ch', 0)), ('B', ('head', 2)), ('B', ('ch', 1)),
+        ('C', ('stem', 0)), ('B', ('ch', 2)), ('M3', ('sm',)), ('C', ('stem', 2)), ('C', ('stem', 1)), ('C', ('head', 2)),)),
+    ('stem0', (('D', ('stem', 2, None)), ('D', ('stem', 0, None)), ('C', ('ch', 2)), ('C', ('ch', 0)),
+        ('D', ('stem', 1, None)), ('C', ('ch', 1)), ('D', ('ch', 2, 0)), ('D', ('ch', 2, 1)), ('E', ('stem', 2, None)),
+        ('E', ('stem', 0, None)), ('E', ('stem', 1, None)), ('D', ('ch', 0, 0)), ('D', ('ch', 0, 1)), ('D', ('ch', 1, 0)),
+        ('D', ('ch', 1, 1)), ('F', ('stem', 0, None)), ('F', ('stem', 1, None)), ('E', ('ch', 2, 0)), ('E', ('ch', 2, 1)),
+        ('E', ('ch', 0, 0)), ('E', ('ch', 1, 0)), ('F', ('stem', 2, None)), ('F', ('ch', 2, 0)),)),
+    ('stem1', (('F', ('ch', 2, 1)), ('E', ('ch', 0, 1)), ('E', ('ch', 1, 1)), ('D', ('ch', 0, 2)), ('D', ('ch', 1, 2)),
+        ('D', ('ch', 2, 2)), ('D', ('ch', 0, 3)), ('D', ('ch', 1, 3)), ('D', ('ch', 2, 3)),)),
+    ('stem3', (('F', ('ch', 0, 0)),)),
+    ('tok0_0', (('F', ('ch', 1, 0)),)),
+    ('tok0_3', (('F', ('ch', 0, 1)),)),
+    ('tok0_4', (('F', ('ch', 1, 1)),)),
+    ('tok0_5', (('E', ('ch', 2, 2)),)),
+    ('ch0_0', (('E', ('ch', 2, 3)), ('E', ('ch', 0, 2)), ('E', ('ch', 1, 2)), ('F', ('ch', 2, 2)),)),
+    ('ch0_3', (('F', ('ch', 2, 3)),)),
+    ('ch0_5', (('E', ('ch', 0, 3)), ('E', ('ch', 1, 3)), ('D', ('head', 2, None)),)),
+    ('ch0_7', (('F', ('ch', 0, 2)), ('F', ('ch', 1, 2)),)),
+    ('tok1_2', (('F', ('ch', 0, 3)),)),
+    ('tok1_3', (('F', ('ch', 1, 3)), ('E', ('head', 2, None)),)),
+    ('ln1', (('F', ('head', 2, None)),)),
+)
+
+
+class Net:
+    def __init__(self, send_sems, recv_sems):
+        self.send_sems, self.recv_sems, self.names, self.builds = send_sems, recv_sems, {}, []
+
+    def copy(self, name):
+        n = self.names[name]
+        src, dst, target = self.builds[n]()
+        return pltpu.make_async_remote_copy(src_ref=src, dst_ref=dst, send_sem=self.send_sems.at[n],
+                                            recv_sem=self.recv_sems.at[n], device_id=target, device_id_type=MESH)
+
+    def start(self, name, build):
+        self.names[name] = len(self.builds)
+        self.builds.append(build)
+        self.copy(name).start()
+
+    def arrived(self, *names):
+        for name in names:
+            self.copy(name).wait_recv()
+
+    def finish(self):
+        for name in self.names:
+            self.copy(name).wait_send()
+
+
+def three_parts(x):
+    hi = x.astype(bf16)
+    rest = x - hi.astype(f32)
+    mid = rest.astype(bf16)
+    return hi, mid, (rest - mid.astype(f32)).astype(bf16)
+
+
+def with_bias_rows(a):
+    row = lax.broadcasted_iota(jnp.int32, (TPAD, 1), 0)
+    return jnp.where(row < TOK, a, jnp.where(row < TOK + 3, 1.0, 0.0)).astype(bf16)
+
+
+def front_kernel(labels, patches, w_stem, w_ch1, w_ch2, w_head, w_tok1, w_tok2, b_tok1, b_ch1, b_head, vecs,
+                 wc, pat_out, xin, xmid, vout, pre_out, act_out, hl, hr, dx0, hstat, gbh, vec, wt,
+                 pc, ps, ph, tk_f, tk_p, sm_p, bh_p, ws, wh, tk_v, sm_v, sm_2, bh_v, bch1,
+                 stage_v, pair_v, p_v, x_v, v_v, w1_v, w2_v, pre_v, act_v, g_v,
+                 send_sems, recv_sems, sem, sem_w, sem_o, sem_x):
+    me = my_place()
+    other = moved(me, 'k', 1)
+    load_p = pltpu.make_async_copy(patches.at[pl.ds(me['x'] * IMG, IMG)], stage_v, sem.at[0])
+    load_p.start()
+
+    for l in range(2):
+        pc[2 * l] = w_ch1[l].astype(bf16)
+        pc[2 * l + 1] = w_ch2[l].astype(bf16)
+    ps[...] = w_stem[...].astype(bf16)
+    ph[...] = jnp.zeros_like(ph)
+    ph[:, pl.ds(0, 250)] = w_head[...].astype(bf16)
+    tk_f[...] = jnp.zeros_like(tk_f)
+    for l in range(2):
+        tk_f[l, :, pl.ds(0, TOK)] = w_tok1[l]
+        tk_f[2 + l, :, pl.ds(0, TOK)] = w_tok2[l]
+        for n, part in enumerate(three_parts(b_tok1[l])):
+            tk_f[l, :, pl.ds(TOK + n, 1)] = part.astype(f32)
+    tk_p[...] = tk_f[...].astype(bf16)
+    sm_p[...] = jnp.zeros_like(sm_p)
+    sm_p[:, pl.ds(0, 13)] = vecs[...]
+    sm_p[pl.ds(0, 2), pl.ds(32, 32)] = b_ch1[...]
+    bh_p[...] = jnp.full_like(bh_p, -1e30)
+    bh_p[pl.ds(0, 1), pl.ds(0, 250)] = b_head[...]
+
+    barrier = pltpu.get_barrier_semaphore()
+    for dim in 'xyz':
+        for step in (1, 2, 3):
+            pl.semaphore_signal(barrier, inc=1, device_id=device(moved(me, dim, step)), device_id_type=MESH)
+    pl.semaphore_signal(barrier, inc=1, device_id=device(other), device_id_type=MESH)
+    net = Net(send_sems, recv_sems)
+    core = me['k']
+    ring = {d: [moved(me, d, n)[d] for n in range(4)] for d in 'xyz'}
+    columns = [pl.ds(pl.multiple_of(x * 256, 256), 256) for x in ring['x']]
+    peers = {(d, n): device(moved(me, d, n)) for d in 'xyz' for n in (1, 2, 3)}
+    partner = device(other)
+    here = {'x': 0, 'y': 0, 'z': 0}
+
+    def view(unit, block, half=None):
+        kind, colour = unit[:2]
+        x, z, y = (EVERY if block[d] is None else ring[d][block[d]] for d in 'xzy')
+        r0, rn = (0, 32) if half is None else (16 * half, 16)
+        if kind == 'ch':
+            c0, cn = COLS[colour]
+            g = EVERY if len(unit) == 2 else unit[2]
+            return wc.at[g, x, z, y, core, pl.ds(r0, rn), pl.ds(c0, cn)]
+        cols = pl.ds(0, CH) if x is EVERY else columns[block['x']]
+        if kind == 'stem':
+            return ws.at[z, y, core, pl.ds(32 * colour + r0, rn), cols]
+        return wh.at[z, y, core, pl.ds(r0, rn), cols]
+
+    def piece(unit):
+        kind, colour = unit
+        if kind == 'ch':
+            return pc.at[:, :, pl.ds(*COLS[colour])]
+        return ps.at[pl.ds(32 * colour, 32), :] if kind == 'stem' else ph.at[:, :]
+
+    def exchange(unit, tag, dim, block):
+        for side, step in (('l', 1), ('r', 3)):
+            def build(step=step):
+                part = view(unit, block)
+                return (piece(unit) if tag == '1' else part), part, peers[dim, step]
+            net.start((unit, tag, side), build)
+
+    def forward_half(unit, tag, dim, block):
+        for half, (origin, target, side) in enumerate(((3, 1, 'l'), (1, 3, 'r'))):
+            def build(half=half, origin=origin, target=target):
+                part = view(unit, {**block, dim: origin}, half)
+                return part, part, peers[dim, target]
+            net.start((unit, tag, side), build)
+
+    def swap(unit, tag, block):
+        def build():
+            part = view(unit, block)
+            return part, part, partner
+        net.start((unit, tag), build)
+
+    own = pltpu.make_async_copy(pc, wc.at[:, me['x'], me['z'], me['y'], me['k']], sem.at[1])
+    own.start()
+    mine = pl.ds(pl.multiple_of(me['x'] * 256, 256), 256)
+    ws[me['z'], me['y'], me['k'], :, mine] = ps[...]
+    wh[me['z'], me['y'], me['k'], :, mine] = ph[...]
+    sm_v[me['x'], me['z'], me['y'], me['k']] = sm_p[...]
+    tk_v[:, me['z'], me['y'], me['k']] = tk_p[...]
+    bh_v[:, mine] = bh_p[...]
+    own.wait()
+    pl.semaphore_wait(barrier, 10)
+
+    def small(kind, n):
+        dims = 'xyz' if kind == 'sm' else 'yz'
+        at = {d: EVERY if d in dims[:n] else ring[d][0] for d in 'xyz'}
+
+        def part():
+            if kind == 'sm':
+                return sm_v.at[at['x'], at['z'], at['y'], core]
+            return tk_v.at[:, at['z'], at['y'], core]
+        if n > 0:
+            net.arrived(*[(kind, n - 1, s) for s in (1, 2, 3)])
+        if n < len(dims):
+            for s in (1, 2, 3):
+                net.start((kind, n, s), lambda s=s: (part(), part(), peers[dims[n], s]))
+            if kind == 'sm' and n == 0:
+                def head_bias():
+                    return bh_v.at[:, columns[0]]
+                for s in (1, 2, 3):
+                    net.start(('bh', s), lambda s=s: (head_bias(), head_bias(), peers['x', s]))
+        else:
+            net.start((kind, 'k'), lambda: (part(), part(), partner))
+
+    def step(name, unit):
+        if name[0] == 'M':
+            small(unit[0], int(name[1]))
+            return
+        d1, d2, d3 = ORDERS[unit[1]]
+        early = unit[:2]
+        plane = {**here, d1: None, d2: None}
+        if name == 'A0':
+            exchange(unit, '1', d1, here)
+        elif name == 'A':
+            net.arrived((unit, '1', 'l'), (unit, '1', 'r'))
+            forward_half(unit, '1h', d1, here)
+        elif name == 'B':
+            net.arrived((unit, '1h', 'l'), (unit, '1h', 'r'))
+            exchange(unit, '2', d2, {**here, d1: None})
+        elif name == 'C':
+            net.arrived((unit, '2', 'l'), (unit, '2', 'r'))
+            forward_half(unit, '2h', d2, {**here, d1: None})
+        elif name == 'D':
+            if early not in planes:
+                planes.add(early)
+                net.arrived((early, '2h', 'l'), (early, '2h', 'r'))
+            exchange(unit, '3', d3, plane)
+            swap(unit, 'k0', plane)
+        elif name == 'E':
+            net.arrived((unit, '3', 'l'), (unit, '3', 'r'))
+            forward_half(unit, '3h', d3, plane)
+            for n in (1, 3):
+                swap(unit, f'k{n}', {**plane, d3: n})
+        else:
+            net.arrived((unit, '3h', 'l'), (unit, '3h', 'r'))
+            swap(unit, 'k2', {**plane, d3: 2})
+
+    planes = set()
+    awaited = set()
+
+    def need(group):
+        for u in LATE:
+            if UNIT_GROUP[u[0], u[2]] <= group and u not in awaited:
+                awaited.add(u)
+                net.arrived(*[(u, f'k{n}') for n in range(4)])
+
+    bursts = {name: steps for name, steps in FRONT_ORDER}
+
+    def burst(name):
+        for s in bursts.get(name, ()):
+            step(*s)
+
+    def during(name, count):
+        def run(i):
+            for n in range(1, count):
+                if bursts.get(f'{name}{n}'):
+                    pl.when(i == n)(functools.partial(burst, f'{name}{n}'))
+        return run
+
+    burst('prep')
+    load_p.wait()
+    pair_v[...] = jnp.zeros_like(pair_v)
+
+    @pl.loop(0, IMG // 2)
+    def _(p):
+        for n in range(2):
+            pair_v[pl.ds(TPAD * n, TOK), :] = stage_v[2 * p + n].astype(f32)
+        p_v[pair(p), :] = pair_v[...].astype(bf16)
+    keep_p = pltpu.make_async_copy(p_v, pat_out, sem.at[0])
+    keep_p.start()
+
+    burst('unpack')
+    net.arrived(('sm', 'k'), ('tk', 'k'), ('bh', 1), ('bh', 2), ('bh', 3))
+    sm_2[...] = sm_v[...].reshape(1024, 128)
+    for n in range(8):
+        vec[:, pl.ds(128 * n, 128)] = sm_2[pl.ds(128 * n, 128), :].T[0:16, :]
+    wt[...] = tk_v[...].reshape(4, TOKH, 128)
+    for l in range(2):
+        rows = jnp.concatenate(three_parts(sm_2[pl.ds(l, 128, stride=8), :]), axis=0)
+
+        @pl.loop(0, 8)
+        def _(n):
+            lane = lax.broadcasted_iota(jnp.int32, (128, 512), 0)
+            col = lax.broadcasted_iota(jnp.int32, (128, 512), 1)
+            pick = jnp.where(lane == 32 + col % 32, 1.0, 0.0).astype(bf16)
+            spread = dot_nn(rows, pick)
+            value = spread[0:128] + spread[128:256] + spread[256:384]
+            mine = lane == n * 16 + col // 32
+            bch1[l:l + 1, pl.ds(pl.multiple_of(n * 512, 512), 512)] = jnp.sum(jnp.where(mine, value, 0.0), axis=0, keepdims=True)
+
+    burst('stem0')
+    need(0)
+    mask_all = (lax.broadcasted_iota(jnp.int32, (ROWS, 1), 0) % TPAD) < TOK
+    run = during('stem', 4)
+
+    @pl.loop(0, 4)
+    def _(i):
+        run(i)
+        cols = pl.ds(pl.multiple_of(i * 256, 256), 256)
+        w = ws[:, :, :, :, cols].reshape(3072, 256)
+        x_v[:, cols] = jnp.where(mask_all, dot_nn(p_v[...], w) + vec[0:1, cols], 0.0)
+
+    wc_all = wc
+    for l in range(2):
+        r = 1 + 5 * l
+        burst(f'tok{l}_0')
+        run = during(f'tok{l}_', IMG)
+        save_in = pltpu.make_async_copy(x_v, xin.at[l], sem_x.at[0])
+        save_in.start()
+        save_in.wait()
+
+        @pl.loop(0, IMG)
+        def _(b):
+            run(b)
+            x = x_v[image(b), :]
+            std, _ = standardize(x)
+            a = with_bias_rows(std * vec[r:r + 1, :] + vec[r + 1:r + 2, :])
+            g_v[...] = gelu(dot_nn(wt[l, :, 0:TPAD], a)).astype(bf16)
+            x_v[image(b), :] = x + dot_tn(wt[2 + l, :, 0:TPAD], g_v[...])
+        save_mid = pltpu.make_async_copy(x_v, xmid.at[l], sem_x.at[0])
+        save_mid.start()
+        burst(f'ln{l}')
+
+        @pl.loop(0, IMG // 2)
+        def _(p):
+            std, _ = standardize(x_v[pair(p), :])
+            v_v[pair(p), :] = (std * vec[r + 2:r + 3, :] + vec[r + 3:r + 4, :]).astype(bf16)
+        save_v = pltpu.make_async_copy(v_v, vout.at[l], sem_x.at[1])
+        save_v.start()
+        burst(f'ch{l}_0')
+        need(2 + 2 * l)
+        save_mid.wait()
+
+        def blocks(i, slot):
+            t, h = i // 2, i % 2
+            part = pl.ds(pl.multiple_of(h * BLK, BLK), BLK)
+            half = [pl.ds(pl.multiple_of(h * 2, 2), 2)]
+            return [(wc_all.at[2 * l, t, :, :, :, :, part], w1_v.at[slot]), (wc_all.at[2 * l + 1, t, *half], w2_v.at[slot])]
+
+        def outs(i, slot):
+            part = pl.ds(pl.multiple_of(i * BLK, BLK), BLK)
+            return [(pre_v.at[slot], pre_out.at[l, :, part]), (act_v.at[slot], act_out.at[l, :, part])]
+        run = during(f'ch{l}_', NBLK)
+
+        def channel(i, slot):
+            run(i)
+            part = pl.ds(pl.multiple_of(i * BLK, BLK), BLK)
+            h = dot_nn(v_v[...], w1_v[slot].reshape(CH, BLK)) + bch1[l:l + 1, part]
+            pre_v[slot] = h
+            act_v[slot] = gelu(h).astype(bf16)
+            x_v[...] += dot_nn(act_v[slot], w2_v[slot].reshape(BLK, CH))
+        for_blocks(Stream(sem_w, blocks, NBLK), channel, Stream(sem_o, outs, NBLK))
+        x_v[...] += vec[r + 4:r + 5, :]
+        save_v.wait()
+
+    burst('head')
+    need(5)
+    keep_p.wait()
+    last = 11
+    mask = row_mask()
+    pooled = jnp.concatenate([jnp.sum(jnp.where(mask, x_v[b * TPAD:(b + 1) * TPAD, :], 0.0), axis=0, keepdims=True)
+                              for b in range(IMG)], axis=0) * (1.0 / TOK)
+    std, inv = standardize(pooled)
+    head_in = (std * vec[last:last + 1, :] + vec[last + 1:last + 2, :]).astype(bf16)
+    hl[...] = head_in
+    w_h = wh[...].reshape(CH, CH)
+    logits = dot_nn(head_in, w_h) + bh_v[0:1, :]
+    row = lax.broadcasted_iota(jnp.int32, (IMG, 1), 0)
+    label = jnp.zeros((IMG, 1), jnp.int32)
+    for b in range(IMG):
+        value = labels[me['x'] * IMG + b]
+        label = jnp.where(row == b, value, label)
+    label = label + 6 * sum(jnp.where(label >= edge, 1, 0) for edge in (250, 500, 750))
+    is_label = lax.broadcasted_iota(jnp.int32, logits.shape, 1) == label
+    top = jnp.max(logits, axis=-1, keepdims=True)
+    ex = jnp.exp(logits - top)
+    es = jnp.sum(ex, axis=-1, keepdims=True)
+    nll = top + jnp.log(es) - jnp.sum(jnp.where(is_label, logits, 0.0), axis=-1, keepdims=True)
+    d_logits = (ex / es - jnp.where(is_label, 1.0, 0.0)) * (1.0 / 1024)
+    gbh[...] = jnp.sum(d_logits, axis=0, keepdims=True)
+    d_bf = d_logits.astype(bf16)
+    hr[...] = d_bf
+    d_in = dot_nt(d_bf, w_h)
+    hstat[0:1, :] = jnp.sum(d_in * std, axis=0, keepdims=True)
+    hstat[1:2, :] = jnp.sum(d_in, axis=0, keepdims=True)
+    hstat[2:3, :] = jnp.broadcast_to(jnp.sum(nll, axis=0, keepdims=True), (1, CH))
+    dx0[...] = norm_grad(d_in, vec[last:last + 1, :], std, inv) * (1.0 / TOK)
+    burst('end')
+    net.finish()
+    assert len(net.builds) <= FRONT_COPIES, len(net.builds)
+
+
+def front(*operands):
+    a, v = pl.BlockSpec(memory_space=pl.ANY), pl.BlockSpec(memory_space=pltpu.VMEM)
+    S, V, DMA = jax.ShapeDtypeStruct, pltpu.VMEM, pltpu.SemaphoreType.DMA
+    return pl.pallas_call(
+        front_kernel, name='front',
+        in_specs=[pl.BlockSpec(memory_space=pltpu.SMEM), a] + [v] * 10,
+        out_specs=[a] * 7 + [v] * 7,
+        out_shape=[S((N_CH, 4, 4, 4, 2, 32, 1024), bf16), S((ROWS, 3072), bf16), S((2, ROWS, CH), f32), S((2, ROWS, CH), f32),
+                   S((2, ROWS, CH), bf16), S((2, ROWS, CHH), f32), S((2, ROWS, CHH), bf16), S((IMG, CH), bf16),
+                   S((IMG, CH), bf16), S((IMG, CH), f32), S((8, CH), f32), S((1, CH), f32), S((16, CH), f32),
+                   S((4, TOKH, 128), bf16)],
+        scratch_shapes=[V((N_CH, 32, 1024), bf16), V((96, 256), bf16), V((32, 256), bf16), V((4, 16, 128), f32),
+                        V((4, 16, 128), bf16), V((8, 128), f32), V((8, 256), f32), V((4, 4, 2, 96, CH), bf16),
+                        V((4, 4, 2, 32, CH), bf16), V((4, 4, 4, 2, 16, 128), bf16), V((4, 4, 4, 2, 8, 128), f32),
+                        V((1024, 128), f32), V((8, CH), f32), V((2, CHH), f32),
+                        V((IMG, TOK, 3072), bf16), V((2 * TPAD, 3072), f32), V((ROWS, 3072), bf16), V((ROWS, CH), f32),
+                        V((ROWS, CH), bf16), V((2, 4, 4, 2, 32, BLK), bf16), V((2, 2, 4, 2, 32, CH), bf16),
+                        V((2, ROWS, BLK), f32), V((2, ROWS, BLK), bf16), V((TOKH, CH), bf16),
+                        DMA((FRONT_COPIES,)), DMA((FRONT_COPIES,)), DMA((2,)), DMA((2, 2)), DMA((2, 2)), DMA((2,))],
+        compiler_params=pltpu.CompilerParams(collective_id=0, has_side_effects=True, vmem_limit_bytes=62 * 1024 * 1024),
+        cost_estimate=pl.CostEstimate(flops=90_000_000_000, bytes_accessed=180_000_000, transcendentals=0),
+    )(*operands)
 
 CHANNEL_AXES = ('tp', 'fsdp')
 
@@ -779,45 +938,15 @@
         t = lax.axis_index('tp')
         nl = w_tok1.shape[0]
         total_images = IMG * nd
-        pat = lax.dynamic_slice_in_dim(patches, t * IMG, IMG, 0)
-        pat = jnp.pad(pat, ((0, 0), (0, TPAD - TOK), (0, 0))).reshape(ROWS, -1)
-        lab = lax.dynamic_slice_in_dim(labels, t * IMG, IMG, 0)
-
         vecs = [b_stem[None]]
         for l in range(nl):
             vecs += [a[l:l + 1] for a in (ln1_g, ln1_b, ln2_g, ln2_b, b_ch2)]
-        vec_rows = jnp.concatenate(vecs + [lnf_g[None], lnf_b[None]], axis=0)
-        n_rows = vec_rows.shape[0]
-        toks = jnp.pad(jnp.concatenate([w_tok1.transpose(0, 2, 1), w_tok2], axis=0), ((0, 0), (0, 0), (0, TPAD - TOK)))
-        pieces = [vec_rows.reshape(-1), b_ch1.reshape(-1), b_tok1.reshape(-1), b_head.reshape(-1), toks.reshape(-1)]
-        pack = jnp.concatenate(pieces)
-        pack = jnp.pad(pack, (0, (-pack.shape[0]) % 1024))
-        small = lax.all_gather(pack, CHANNEL_AXES, axis=0, tiled=False).reshape(tp, fs, -1)
-        offs = []
-        o = 0
-        for p in pieces:
-            offs.append(small[:, :, o:o + p.shape[0]])
-            o += p.shape[0]
-        vec = offs[0].reshape(tp, fs, n_rows, -1).transpose(2, 0, 1, 3).reshape(n_rows, -1)
-        bch1 = offs[1].reshape(tp, fs, nl, -1).transpose(2, 0, 1, 3).reshape(nl, -1)
-        bt1 = offs[2][0].reshape(fs, nl, -1).transpose(1, 0, 2).reshape(nl, -1)[:, :, None]
-        bhead = offs[3][:, 0]
-        wt = offs[4][0].reshape(fs, 2 * nl, -1, TPAD).transpose(1, 0, 2, 3).reshape(2 * nl, TOKH, TPAD).astype(bf16)
-
+        vecs = jnp.concatenate(vecs + [lnf_g[None], lnf_b[None]], axis=0).T
         classes = w_head.shape[1]
-        pad_cls = 256 - classes
-        pc = jnp.stack([w_ch1[0], w_ch2[0], w_ch1[1], w_ch2[1]]).astype(bf16)
-        ph = jnp.pad(w_head.astype(bf16), ((0, 0), (0, pad_cls)))
-        wc, ws, wh = gather_weights(pc, w_stem.astype(bf16), ph)
-        ws = ws.reshape(-1, CH)
-        wh = wh.reshape(CH, -1)
-        wc = wc.reshape(2 * nl, tp, CH, CH)
-        bhead = jnp.pad(bhead, ((0, 0), (0, pad_cls)), constant_values=-1e30).reshape(1, -1)
-        label = (lab // classes * 256 + lab % classes).reshape(IMG, 1)
-
-        xin, xmid, vin, pre, act, hl, hr, dx0, hstat, gbh = forward(pat, ws, wc, wh, wt[:nl], wt[nl:], bt1, vec, bch1,
-                                                                    bhead, label)
-        dpre, dout, dstem, gvec, gbch1, gt1, gt2, gbt = backward(xin, xmid, pre, wc, wt[:nl], wt[nl:], bt1, vec, dx0)
+        wc, pat, xin, xmid, vin, pre, act, hl, hr, dx0, hstat, gbh, vec, wt = front(
+            labels, patches, w_stem, w_ch1, w_ch2, w_head, w_tok1.transpose(0, 2, 1), w_tok2, b_tok1[:, :, None], b_ch1,
+            b_head[None], vecs)
+        dpre, dout, dstem, gvec, gbch1, gt1, gt2, gbt = backward(xin, xmid, pre, wc, wt, vec, dx0)
 
         gvec = jnp.concatenate([gvec[:11], hstat[:2]], axis=0)
         parts = [gvec, gbch1, gbt[:, :, 0], gbh, gt1, gt2, hstat[2, :1]]

time: 477 us -> 425 us (0.89)
  Pallas kernels: 406 us -> 362 us
  other arithmetic: 10.7 us -> 3.82 us
    pallas_call x2 -> x1, Pallas kernels: 167 us -> 128 us  [front(): pl.pallas_call(front_kernel, name='front', in_specs=[pl.BlockSpec(memory_...]
    unnamed x22 -> x25, local copies, waits for them, and re-layouts: 4.06 us -> 16.7 us
    reshape x10 -> x0, local copies, waits for them, and re-layouts: 6.04 us -> none  [the longest x1 1.75 us: step(): lax.all_gather(pack, CHANNEL_AXES, axis=0, tiled=False).reshape(tp, fs, -1)]
  transfers between devices with their start and end apart: 2 -> 1, of which waited for: 0 -> 0; matrix products, arithmetic and copies ran while one was open for 3% -> 0% of each run, Pallas kernels for 53% -> 35%
where the time goes in v5:
time: 425 us; the launch traced here: 423 us
  Pallas kernels  362 us (85%)
  local copies, waits for them, and re-layouts  40.6 us (10%)
  between operations  16 us (4%)
    pallas_call x1, Pallas kernels, reduce_gradients(): pl.pallas_call(reduce_kernel, name='reduce_gradients', out_shape=[jax.Sha...  147 us
    pallas_call x1, Pallas kernels, front(): pl.pallas_call(front_kernel, name='front', in_specs=[pl.BlockSpec(memory_...  128 us
    pallas_call x1, Pallas kernels, backward(): pl.pallas_call(backward_kernel, name='backward', in_specs=[a] * 4 + [v] *...  87.9 us
    unnamed x25, local copies, waits for them, and re-layouts  16.7 us
  transfers between devices with their start and end apart: 1, of which 0 were waited for; matrix products, arithmetic and copies ran while one was open for 0% of the time, Pallas kernels for 35%

profile of v5, /device:TPU:0, one launch (start us, length us, event | category | flops | bytes accessed | tf_op | source)
XLA Modules:
  0.0 422.8 jit_solution(899857357401516393)
XLA Ops:
  7.2 0.8 fusion.8
  8.1 0.8 fusion.7
  8.9 0.8 fusion.6
  9.8 0.8 fusion.5
  10.6 0.8 fusion.4
  11.8 0.7 copy.62
  12.6 0.7 copy.63
  13.3 0.7 copy.64
  14.0 12.2 %copy.65.patches = bf16[32,49,3072]{2,1,0:T(8,128)(2,1)} copy(bf16[32,49,3072]{2,0,1:T(8,128)(2,1)} %param.19) | data formatting | bytes 19267584 | tf_op args[0]
  26.2 0.7 copy.66.b_tok1
  26.9 0.7 concatenate.9
  27.6 127.6 %front.1 = (bf16[4,4,4,4,2,32,1024]{6,5,4,3,2,1,0:T(8,128)(2,1)}, bf16[448,3072]{1,0:T(8,128)(2,1)}, f32[2,448,1024]{2,1,0:T(8,128)}, f32[2,448,1024]{2,1,0:T(8,...) custom-call(s32[32]{0:T(128)} %labels.1, ...), custom_call_target="tpu_custom_call" | custom-call | flops 89999998976 | bytes 180000000 | tf_op jit(solution)/shard_map/front/pallas_call | solution.py:900
  155.2 0.8 slice.158
  156.0 1.2 slice.159
  157.2 87.9 %backward.1 = (bf16[2,448,4096]{2,1,0:T(8,128)(2,1)}, bf16[2,448,1024]{2,1,0:T(8,128)(2,1)}, bf16[448,1024]{1,0:T(8,128)(2,1)}, f32[16,1024]{1,0:T(8,128)}, f32[...) custom-call(f32[2,448,1024]{2,1,0:T(8,128)} %get-tuple-element.43.xin, ...), custom_call_target="tpu_custom_call" | custom-call | flops 49999998976 | bytes 100000000 | tf_op jit(solution)/shard_map/backward/pallas_call | solution.py:509
  245.0 0.9 pad_maximum_fusion
  245.9 0.8 copy.77
  246.7 1.2 reduce
  248.0 1.4 reshape.91
  249.4 1.4 reshape.92
  250.8 0.6 constant_dynamic-update-slice_fusion
  251.5 0.8 pad.4
  252.4 146.8 %reduce_gradients.1 = (f32[4,32,1024]{2,1,0:T(8,128)}, f32[96,256]{1,0:T(8,128)}, f32[32,256]{1,0:T(8,128)}) custom-call(bf16[2,448,4096]{2,1,0:T(8,128)(2,1)} %get-tuple-element.57.refs_0_, bf16[2,448,4096]{2,1,0:T(8,128)(2,1)} %get-tuple-element.58.refs_1_, bf16[448,3072]{1,0:T(8,128)(2,1)} %get-tuple-element.59.refs_2_, ...), custom_call_target="tpu_custom_call" | custom-call | flops 99999997952 | bytes 80000000 | tf_op jit(solution)/shard_map/reduce_gradients/pallas_call | solution.py:296
  399.2 1.9 fusion.3
  401.1 0.8 slice.190
  401.9 1.1 fusion.2
  403.8 0.8 slice.194
  404.6 0.7 fusion.1
  406.5 0.6 constant_dynamic-slice_fusion.4
  409.0 1.2 slice.189
  411.9 1.5 copy.88
  413.5 1.4 copy.89
  (38 shorter events, 5.9 us)
Async XLA Ops:
  7.2 393.9 %all-reduce.3.cloned.1.call-start = ((), (), s32[]{:S(2)}) async-start(), calls=%async_computation | async-start | bytes 1114112 | tf_op jit(solution)/shard_map/psum | solution.py:955
  14.0 12.2 %copy-start.1 = (f32[2,16]{1,0:T(2,128)S(1)}, f32[2,16]{1,0:T(2,128)}, u32[]{:S(2)}) copy-start(f32[2,16]{1,0:T(2,128)} %param.26) | copy-start | bytes 388
  157.2 93.6 %copy-start = (f32[1,1024]{1,0:T(1,128)S(1)}, f32[1,1024]{1,0:T(1,128)}, u32[]{:S(2)}) copy-start(f32[1,1024]{1,0:T(1,128)} %get-tuple-element.54) | copy-start | bytes 12292
Sparse Core Ops, SparseCore 0:
  252.5 145.7 all-reduce.2

commit v6 on v5

--- a/solution.py
+++ b/solution.py
@@ -309,7 +309,8 @@
 EPS = 1e-6
 TOK, TPAD = 49, 56
 IMG = 8
-ROWS = IMG * TPAD
+ROWS, XROWS = IMG * TOK, IMG * TPAD
+CHUNKS = ((0, 112), (112, 112), (224, 112), (336, 56))
 CH, TOKH, CHH = 1024, 512, 4096
 BLK = 512
 NBLK = CHH // BLK
@@ -361,11 +362,16 @@
 
 
 def image(b):
-    return pl.ds(pl.multiple_of(b * TPAD, 8), TPAD)
-
-
-def pair(p):
-    return pl.ds(pl.multiple_of(p * 2 * TPAD, 16), 2 * TPAD)
+    return pl.ds(b, TPAD, stride=IMG)
+
+
+def get(ref, rows):
+    return jnp.concatenate([ref[n, rows, :] for n in range(CH // 128)], axis=1)
+
+
+def put(ref, rows, value):
+    for n in range(CH // 128):
+        ref[n, rows, :] = value[:, 128 * n:128 * (n + 1)]
 
 
 class Stream:
@@ -412,8 +418,13 @@
                     dpre, dout, dstem, gvec, gbch1, gt1, gt2, gbt,
                     x_v, d_v, dv_v, do_v, w1_v, w2_v, pre_v, dp_v, g_v, dh_v, sem, sem_w, sem_o):
     mask = row_mask()
-    for b in range(IMG):
-        d_v[b * TPAD:(b + 1) * TPAD, :] = jnp.where(mask, jnp.broadcast_to(dx0[b:b + 1, :], (TPAD, CH)), 0.0)
+    rest = pl.ds(ROWS, XROWS - ROWS)
+    put(d_v, rest, jnp.zeros((XROWS - ROWS, CH), f32))
+    put(x_v, rest, jnp.zeros((XROWS - ROWS, CH), f32))
+
+    @pl.loop(0, TOK)
+    def _(s):
+        put(d_v, pl.ds(pl.multiple_of(s * IMG, IMG), IMG), dx0[...])
     gvec[...] = jnp.zeros_like(gvec)
     gt1[...] = jnp.zeros_like(gt1)
     gt2[...] = jnp.zeros_like(gt2)
@@ -424,14 +435,13 @@
 
     for l in (1, 0):
         r = 1 + 5 * l
-        load = pltpu.make_async_copy(xmid.at[l], x_v, sem.at[0])
+        load = pltpu.make_async_copy(xmid.at[l], x_v.at[:, pl.ds(0, ROWS)], sem.at[0])
         load.start()
 
-        @pl.loop(0, IMG // 2)
-        def _(p):
-            d = d_v[pair(p), :]
+        for at, size in CHUNKS:
+            d = get(d_v, pl.ds(at, size))
             add(r + 4, d)
-            do_v[pair(p), :] = d.astype(bf16)
+            do_v[pl.ds(at, size), :] = d.astype(bf16)
         send = pltpu.make_async_copy(do_v, dout.at[l], sem.at[1])
         send.start()
 
@@ -464,22 +474,23 @@
         load.wait()
         send.wait()
 
+        @pl.loop(0, ROWS // TPAD)
+        def _(n):
+            rows = pl.ds(pl.multiple_of(n * TPAD, TPAD), TPAD)
+            std, inv = standardize(get(x_v, rows))
+            d = dv_v[rows, :]
+            add(r + 2, d * std)
+            add(r + 3, d)
+            put(d_v, rows, get(d_v, rows) + norm_grad(d, vec[r + 2:r + 3, :], std, inv))
+        load = pltpu.make_async_copy(xin.at[l], x_v.at[:, pl.ds(0, ROWS)], sem.at[0])
+        load.start()
+        load.wait()
+
         @pl.loop(0, IMG)
         def _(b):
-            std, inv = standardize(x_v[image(b), :])
-            d = dv_v[image(b), :]
-            add(r + 2, d * std)
-            add(r + 3, d)
-            d_v[image(b), :] += norm_grad(d, vec[r + 2:r + 3, :], std, inv)
-        load = pltpu.make_async_copy(xin.at[l], x_v, sem.at[0])
-        load.start()
-        load.wait()
-
-        @pl.loop(0, IMG)
-        def _(b):
-            std, inv = standardize(x_v[image(b), :])
+            std, inv = standardize(get(x_v, image(b)))
             a = with_bias_rows(std * vec[r:r + 1, :] + vec[r + 1:r + 2, :])
-            d_mid = d_v[image(b), :]
+            d_mid = get(d_v, image(b))
             dm = d_mid.astype(bf16)
             act, slope = gelu_both(dot_nn(wt[l, :, 0:TPAD], a))
             g_v[...] = act.astype(bf16)
@@ -491,13 +502,12 @@
             d = jnp.where(mask, dot_tn(wt[l, :, 0:TPAD], dh_v[...]), 0.0)
             add(r, d * std)
             add(r + 1, d)
-            d_v[image(b), :] = d_mid + norm_grad(d, vec[r:r + 1, :], std, inv)
-
-    @pl.loop(0, IMG // 2)
-    def _(p):
-        d = d_v[pair(p), :]
+            put(d_v, image(b), d_mid + norm_grad(d, vec[r:r + 1, :], std, inv))
+
+    for at, size in CHUNKS:
+        d = get(d_v, pl.ds(at, size))
         add(0, d)
-        do_v[pair(p), :] = d.astype(bf16)
+        do_v[pl.ds(at, size), :] = d.astype(bf16)
     send = pltpu.make_async_copy(do_v, dstem, sem.at[1])
     send.start()
     send.wait()
@@ -512,7 +522,7 @@
         out_specs=[a] * 3 + [v] * 5,
         out_shape=[S((2, ROWS, CHH), bf16), S((2, ROWS, CH), bf16), S((ROWS, CH), bf16), S((16, CH), f32), S((2, CHH), f32),
                    S((2, TOKH, TPAD), f32), S((2, TOKH, TPAD), f32), S((2, TOKH, 1), f32)],
-        scratch_shapes=[pltpu.VMEM((ROWS, CH), f32), pltpu.VMEM((ROWS, CH), f32), pltpu.VMEM((ROWS, CH), f32),
+        scratch_shapes=[pltpu.VMEM((CH // 128, XROWS, 128), f32), pltpu.VMEM((CH // 128, XROWS, 128), f32), pltpu.VMEM((ROWS, CH), f32),
                         pltpu.VMEM((ROWS, CH), bf16), pltpu.VMEM((2, 4, 4, 2, 32, BLK), bf16),
                         pltpu.VMEM((2, 2, 4, 2, 32, CH), bf16),
                         pltpu.VMEM((2, ROWS, BLK), f32), pltpu.VMEM((2, ROWS, BLK), bf16), pltpu.VMEM((TOKH, CH), bf16),
@@ -593,14 +603,15 @@
     return jnp.where(row < TOK, a, jnp.where(row < TOK + 3, 1.0, 0.0)).astype(bf16)
 
 
-def front_kernel(labels, patches, w_stem, w_ch1, w_ch2, w_head, w_tok1, w_tok2, b_tok1, b_ch1, b_head, vecs,
+def front_kernel(labels, patches, w_stem, w_ch1, w_ch2, w_head, w_tok1, w_tok2, b_tok1, b_ch1, b_head, b_stem, ln1_g, ln1_b,
+                 ln2_g, ln2_b, b_ch2, lnf_g, lnf_b,
                  wc, pat_out, xin, xmid, vout, pre_out, act_out, hl, hr, dx0, hstat, gbh, vec, wt,
                  pc, ps, ph, tk_f, tk_p, sm_p, bh_p, ws, wh, tk_v, sm_v, sm_2, bh_v, bch1,
-                 stage_v, pair_v, p_v, x_v, v_v, w1_v, w2_v, pre_v, act_v, g_v,
+                 turn, p_v, x_v, v_v, w1_v, w2_v, pre_v, act_v, g_v,
                  send_sems, recv_sems, sem, sem_w, sem_o, sem_x):
     me = my_place()
     other = moved(me, 'k', 1)
-    load_p = pltpu.make_async_copy(patches.at[pl.ds(me['x'] * IMG, IMG)], stage_v, sem.at[0])
+    load_p = pltpu.make_async_copy(patches.at[:, pl.ds(pl.multiple_of(me['x'] * IMG, IMG), IMG)], p_v, sem.at[0])
     load_p.start()
 
     for l in range(2):
@@ -609,18 +620,26 @@
     ps[...] = w_stem[...].astype(bf16)
     ph[...] = jnp.zeros_like(ph)
     ph[:, pl.ds(0, 250)] = w_head[...].astype(bf16)
+    turn[...] = jnp.zeros_like(turn)
+    for n, ref in ((0, b_stem), (11, lnf_g), (12, lnf_b)):
+        turn[n, pl.ds(0, 8)] = ref[...]
+    for n, ref in enumerate((ln1_g, ln1_b, ln2_g, ln2_b, b_ch2)):
+        for l in range(2):
+            turn[pl.ds(1 + 5 * l + n, 1), pl.ds(0, 8)] = ref[pl.ds(l, 1), :]
+    turn[pl.ds(16, 2), pl.ds(0, 16)] = b_tok1[...]
+    turned = turn[...].T
     tk_f[...] = jnp.zeros_like(tk_f)
     for l in range(2):
         tk_f[l, :, pl.ds(0, TOK)] = w_tok1[l]
         tk_f[2 + l, :, pl.ds(0, TOK)] = w_tok2[l]
-        for n, part in enumerate(three_parts(b_tok1[l])):
+        for n, part in enumerate(three_parts(turned[0:16, 16 + l:17 + l])):
             tk_f[l, :, pl.ds(TOK + n, 1)] = part.astype(f32)
     tk_p[...] = tk_f[...].astype(bf16)
     sm_p[...] = jnp.zeros_like(sm_p)
-    sm_p[:, pl.ds(0, 13)] = vecs[...]
+    sm_p[:, pl.ds(0, 16)] = turned[0:8, 0:16]
     sm_p[pl.ds(0, 2), pl.ds(32, 32)] = b_ch1[...]
     bh_p[...] = jnp.full_like(bh_p, -1e30)
-    bh_p[pl.ds(0, 1), pl.ds(0, 250)] = b_head[...]
+    bh_p[0, pl.ds(0, 250)] = b_head[...]
 
     barrier = pltpu.get_barrier_semaphore()
     for dim in 'xyz':
@@ -763,13 +782,6 @@
 
     burst('prep')
     load_p.wait()
-    pair_v[...] = jnp.zeros_like(pair_v)
-
-    @pl.loop(0, IMG // 2)
-    def _(p):
-        for n in range(2):
-            pair_v[pl.ds(TPAD * n, TOK), :] = stage_v[2 * p + n].astype(f32)
-        p_v[pair(p), :] = pair_v[...].astype(bf16)
     keep_p = pltpu.make_async_copy(p_v, pat_out, sem.at[0])
     keep_p.start()
 
@@ -794,41 +806,47 @@
 
     burst('stem0')
     need(0)
-    mask_all = (lax.broadcasted_iota(jnp.int32, (ROWS, 1), 0) % TPAD) < TOK
     run = during('stem', 4)
+    put(x_v, pl.ds(ROWS, XROWS - ROWS), jnp.zeros((XROWS - ROWS, CH), f32))
 
     @pl.loop(0, 4)
     def _(i):
         run(i)
         cols = pl.ds(pl.multiple_of(i * 256, 256), 256)
         w = ws[:, :, :, :, cols].reshape(3072, 256)
-        x_v[:, cols] = jnp.where(mask_all, dot_nn(p_v[...], w) + vec[0:1, cols], 0.0)
+        value = dot_nn(p_v[...].reshape(ROWS, 3072), w) + vec[0:1, cols]
+        for n in range(2):
+            x_v[2 * i + n, pl.ds(0, ROWS), :] = value[:, 128 * n:128 * (n + 1)]
 
     wc_all = wc
+
+    def add_rows(value):
+        for n in range(CH // 128):
+            x_v[n, pl.ds(0, ROWS), :] += value[:, 128 * n:128 * (n + 1)]
+
     for l in range(2):
         r = 1 + 5 * l
         burst(f'tok{l}_0')
         run = during(f'tok{l}_', IMG)
-        save_in = pltpu.make_async_copy(x_v, xin.at[l], sem_x.at[0])
+        save_in = pltpu.make_async_copy(x_v.at[:, pl.ds(0, ROWS)], xin.at[l], sem_x.at[0])
         save_in.start()
         save_in.wait()
 
         @pl.loop(0, IMG)
         def _(b):
             run(b)
-            x = x_v[image(b), :]
+            x = get(x_v, image(b))
             std, _ = standardize(x)
             a = with_bias_rows(std * vec[r:r + 1, :] + vec[r + 1:r + 2, :])
             g_v[...] = gelu(dot_nn(wt[l, :, 0:TPAD], a)).astype(bf16)
-            x_v[image(b), :] = x + dot_tn(wt[2 + l, :, 0:TPAD], g_v[...])
-        save_mid = pltpu.make_async_copy(x_v, xmid.at[l], sem_x.at[0])
+            put(x_v, image(b), x + dot_tn(wt[2 + l, :, 0:TPAD], g_v[...]))
+        save_mid = pltpu.make_async_copy(x_v.at[:, pl.ds(0, ROWS)], xmid.at[l], sem_x.at[0])
         save_mid.start()
         burst(f'ln{l}')
 
-        @pl.loop(0, IMG // 2)
-        def _(p):
-            std, _ = standardize(x_v[pair(p), :])
-            v_v[pair(p), :] = (std * vec[r + 2:r + 3, :] + vec[r + 3:r + 4, :]).astype(bf16)
+        for at, size in CHUNKS:
+            std, _ = standardize(get(x_v, pl.ds(at, size)))
+            v_v[pl.ds(at, size), :] = (std * vec[r + 2:r + 3, :] + vec[r + 3:r + 4, :]).astype(bf16)
         save_v = pltpu.make_async_copy(v_v, vout.at[l], sem_x.at[1])
         save_v.start()
         burst(f'ch{l}_0')
@@ -852,18 +870,16 @@
             h = dot_nn(v_v[...], w1_v[slot].reshape(CH, BLK)) + bch1[l:l + 1, part]
             pre_v[slot] = h
             act_v[slot] = gelu(h).astype(bf16)
-            x_v[...] += dot_nn(act_v[slot], w2_v[slot].reshape(BLK, CH))
+            add_rows(dot_nn(act_v[slot], w2_v[slot].reshape(BLK, CH)))
         for_blocks(Stream(sem_w, blocks, NBLK), channel, Stream(sem_o, outs, NBLK))
-        x_v[...] += vec[r + 4:r + 5, :]
+        add_rows(jnp.broadcast_to(vec[r + 4:r + 5, :], (ROWS, CH)))
         save_v.wait()
 
     burst('head')
     need(5)
     keep_p.wait()
     last = 11
-    mask = row_mask()
-    pooled = jnp.concatenate([jnp.sum(jnp.where(mask, x_v[b * TPAD:(b + 1) * TPAD, :], 0.0), axis=0, keepdims=True)
-                              for b in range(IMG)], axis=0) * (1.0 / TOK)
+    pooled = jnp.sum(get(x_v, pl.ds(0, ROWS)).reshape(TOK, IMG, CH), axis=0) * (1.0 / TOK)
     std, inv = standardize(pooled)
     head_in = (std * vec[last:last + 1, :] + vec[last + 1:last + 2, :]).astype(bf16)
     hl[...] = head_in
@@ -899,9 +915,10 @@
     S, V, DMA = jax.ShapeDtypeStruct, pltpu.VMEM, pltpu.SemaphoreType.DMA
     return pl.pallas_call(
         front_kernel, name='front',
-        in_specs=[pl.BlockSpec(memory_space=pltpu.SMEM), a] + [v] * 10,
+        in_specs=[pl.BlockSpec(memory_space=pltpu.SMEM), a] + [v] * 17,
         out_specs=[a] * 7 + [v] * 7,
-        out_shape=[S((N_CH, 4, 4, 4, 2, 32, 1024), bf16), S((ROWS, 3072), bf16), S((2, ROWS, CH), f32), S((2, ROWS, CH), f32),
+        out_shape=[S((N_CH, 4, 4, 4, 2, 32, 1024), bf16), S((TOK, IMG, 3072), bf16), S((2, CH // 128, ROWS, 128), f32),
+                   S((2, CH // 128, ROWS, 128), f32),
                    S((2, ROWS, CH), bf16), S((2, ROWS, CHH), f32), S((2, ROWS, CHH), bf16), S((IMG, CH), bf16),
                    S((IMG, CH), bf16), S((IMG, CH), f32), S((8, CH), f32), S((1, CH), f32), S((16, CH), f32),
                    S((4, TOKH, 128), bf16)],
@@ -909,7 +926,7 @@
                         V((4, 16, 128), bf16), V((8, 128), f32), V((8, 256), f32), V((4, 4, 2, 96, CH), bf16),
                         V((4, 4, 2, 32, CH), bf16), V((4, 4, 4, 2, 16, 128), bf16), V((4, 4, 4, 2, 8, 128), f32),
                         V((1024, 128), f32), V((8, CH), f32), V((2, CHH), f32),
-                        V((IMG, TOK, 3072), bf16), V((2 * TPAD, 3072), f32), V((ROWS, 3072), bf16), V((ROWS, CH), f32),
+                        V((128, 128), f32), V((TOK, IMG, 3072), bf16), V((CH // 128, XROWS, 128), f32),
                         V((ROWS, CH), bf16), V((2, 4, 4, 2, 32, BLK), bf16), V((2, 2, 4, 2, 32, CH), bf16),
                         V((2, ROWS, BLK), f32), V((2, ROWS, BLK), bf16), V((TOKH, CH), bf16),
                         DMA((FRONT_COPIES,)), DMA((FRONT_COPIES,)), DMA((2,)), DMA((2, 2)), DMA((2, 2)), DMA((2,))],
@@ -938,14 +955,11 @@
         t = lax.axis_index('tp')
         nl = w_tok1.shape[0]
         total_images = IMG * nd
-        vecs = [b_stem[None]]
-        for l in range(nl):
-            vecs += [a[l:l + 1] for a in (ln1_g, ln1_b, ln2_g, ln2_b, b_ch2)]
-        vecs = jnp.concatenate(vecs + [lnf_g[None], lnf_b[None]], axis=0).T
         classes = w_head.shape[1]
         wc, pat, xin, xmid, vin, pre, act, hl, hr, dx0, hstat, gbh, vec, wt = front(
-            labels, patches, w_stem, w_ch1, w_ch2, w_head, w_tok1.transpose(0, 2, 1), w_tok2, b_tok1[:, :, None], b_ch1,
-            b_head[None], vecs)
+            labels, patches.transpose(1, 0, 2), w_stem, w_ch1, w_ch2, w_head, w_tok1.transpose(0, 2, 1), w_tok2, b_tok1, b_ch1,
+            b_head, b_stem, ln1_g, ln1_b, ln2_g, ln2_b, b_ch2, lnf_g, lnf_b)
+        pat = pat.reshape(ROWS, -1)
         dpre, dout, dstem, gvec, gbch1, gt1, gt2, gbt = backward(xin, xmid, pre, wc, wt, vec, dx0)
 
         gvec = jnp.concatenate([gvec[:11], hstat[:2]], axis=0)

time: 425 us -> 402 us (0.946)
  local copies, waits for them, and re-layouts: 40.6 us -> 20.3 us
    unnamed x25 -> x12, local copies, waits for them, and re-layouts: 16.7 us -> 3.74 us
  transfers between devices with their start and end apart: 1 -> 1, of which waited for: 0 -> 0; matrix products, arithmetic and copies ran while one was open for 0% -> 0% of each run, Pallas kernels for 35% -> 37%
where the time goes in v6:
time: 402 us; the launch traced here: 400 us
  Pallas kernels  360 us (90%)
  local copies, waits for them, and re-layouts  20.3 us (5%)
  between operations  16 us (4%)
    pallas_call x1, Pallas kernels, reduce_gradients(): pl.pallas_call(reduce_kernel, name='reduce_gradients', out_shape=[jax.Sha...  146 us
    pallas_call x1, Pallas kernels, front(): pl.pallas_call(front_kernel, name='front', in_specs=[pl.BlockSpec(memory_...  128 us
    pallas_call x1, Pallas kernels, backward(): pl.pallas_call(backward_kernel, name='backward', in_specs=[a] * 4 + [v] *...  85.7 us
  transfers between devices with their start and end apart: 1, of which 0 were waited for; matrix products, arithmetic and copies ran while one was open for 0% of the time, Pallas kernels for 37%

profile of v6, /device:TPU:0, one launch (start us, length us, event | category | flops | bytes accessed | tf_op | source)
XLA Modules:
  0.0 400.2 jit_solution(16799330260844250500)
XLA Ops:
  7.2 0.0 all-reduce.3.cloned.1.call-start
  7.2 128.2 %front.1 = (bf16[4,4,4,4,2,32,1024]{6,5,4,3,2,1,0:T(8,128)(2,1)}, bf16[49,8,3072]{2,1,0:T(8,128)(2,1)}, f32[2,8,392,128]{3,2,1,0:T(8,128)}, f32[2,8,392,128]{3,2...) custom-call(s32[32]{0:T(128)} %labels.1, ...), custom_call_target="tpu_custom_call" | custom-call | flops 89999998976 | bytes 180000000 | tf_op jit(solution)/shard_map/front/pallas_call | solution.py:916
  135.4 0.8 slice.118
  136.2 1.2 slice.119
  137.4 85.7 %backward.1 = (bf16[2,392,4096]{2,1,0:T(8,128)(2,1)}, bf16[2,392,1024]{2,1,0:T(8,128)(2,1)}, bf16[392,1024]{1,0:T(8,128)(2,1)}, f32[16,1024]{1,0:T(8,128)}, f32[...) custom-call(f32[2,8,392,128]{3,2,1,0:T(8,128)} %get-tuple-element.43.xin, ...), custom_call_target="tpu_custom_call" | custom-call | flops 49999998976 | bytes 100000000 | tf_op jit(solution)/shard_map/backward/pallas_call | solution.py:519
  223.1 0.9 pad_maximum_fusion
  224.0 0.8 copy.37
  224.7 1.2 reduce
  226.0 1.4 reshape.94
  227.4 1.4 reshape.95
  228.9 0.6 constant_dynamic-update-slice_fusion
  229.5 0.9 pad.4
  230.4 0.0 all-reduce.3.cloned.1.call-update
  230.5 146.1 %reduce_gradients.1 = (f32[4,32,1024]{2,1,0:T(8,128)}, f32[96,256]{1,0:T(8,128)}, f32[32,256]{1,0:T(8,128)}) custom-call(bf16[2,392,4096]{2,1,0:T(8,128)(2,1)} %get-tuple-element.57.refs_0_, bf16[2,392,4096]{2,1,0:T(8,128)(2,1)} %get-tuple-element.58.refs_1_, bf16[392,3072]{1,0:T(8,128)(2,1)} %bitcast.32, bf16[2,392,1024]{2,1,0:T(8,128)(2,1)} %get-tuple-element.60.refs_3_, ...), custom_call_target="tpu_custom_call" | custom-call | flops 99999997952 | bytes 80000000 | tf_op jit(solution)/shard_map/reduce_gradients/pallas_call | solution.py:296
  376.6 1.9 fusion.3
  378.5 0.8 slice.150
  379.3 1.1 fusion.2
  380.4 0.4 reshape.97
  380.8 0.4 reshape.98
  381.2 0.8 slice.154
  382.0 0.7 fusion.1
  382.7 0.6 dynamic-slice_bitcast_fusion.1
  383.3 0.6 pad_maximum_fusion.5
  383.9 0.6 constant_dynamic-slice_fusion.4
  384.5 0.6 dynamic-slice_bitcast_fusion
  385.2 0.6 constant_dynamic-slice_fusion.2
  385.8 0.6 constant_dynamic-slice_fusion.1
  386.4 1.2 slice.149
  388.2 0.6 pad_maximum_fusion.3
  388.8 0.6 pad_maximum_fusion.1
  389.3 1.5 copy.48
  390.9 1.4 copy.49
  (15 shorter events, 0.1 us)
Async XLA Ops:
  7.2 371.3 %all-reduce.3.cloned.1.call-start = ((), (), s32[]{:S(2)}) async-start(), calls=%async_computation | async-start | bytes 1114112 | tf_op jit(solution)/shard_map/psum | solution.py:969
  137.4 91.4 %copy-start = (f32[1,1024]{1,0:T(1,128)S(1)}, f32[1,1024]{1,0:T(1,128)}, u32[]{:S(2)}) copy-start(f32[1,1024]{1,0:T(1,128)} %get-tuple-element.54) | copy-start | bytes 12292
Sparse Core Ops, SparseCore 0:
  230.6 145.8 all-reduce.2

commit v7 on v6

--- a/solution.py
+++ b/solution.py
@@ -28,15 +28,6 @@
 
 def device(place):
     return {'tp': place['x'], 'fsdp': (place['z'] * 4 + place['y']) * 2 + place['k']}
-
-
-def meet_neighbours(me):
-    barrier = pltpu.get_barrier_semaphore()
-    for dim in 'xyz':
-        for step in (1, 3):
-            pl.semaphore_signal(barrier, inc=1, device_id=device(moved(me, dim, step)), device_id_type=MESH)
-    pl.semaphore_signal(barrier, inc=1, device_id=device(moved(me, 'k', 1)), device_id_type=MESH)
-    pl.semaphore_wait(barrier, 7)
 
 
 class Sender:
@@ -56,7 +47,8 @@
 
 GROUPS = (STEM, 3, 2, 1, 0, HEAD)
 UNITS = tuple((g, c) for g in GROUPS for c in (2, 0, 1) if g != HEAD or c == 2)
-REDUCE_COPIES = 13 * len(UNITS)
+REDUCE_COPIES = 13 * len(UNITS) + 20
+SMALL_AT = (2, 10, 20, 32, 44, 56)
 ORDER = (0, 1, 2, 3, 4, 0, 5, 1, 2, 0, 3, 1, 2, 0, 4, 6, 3, 1, 7, 5, 0, 6, 4, 1, 2, 8, 0, 6, 7, 5, 2, 3, 1, 9, 0, 8, 4, 10, 7, 9, 1, 2,
          3, 0, 5, 11, 8, 9, 10, 1, 4, 5, 2, 11, 3, 6, 12, 10, 2, 5, 8, 6, 4, 7, 13, 11, 12, 3, 4, 7, 8, 14, 5, 12, 6, 13, 4, 9,
          15, 5, 8, 11, 3, 14, 13, 6, 7, 8, 9, 10, 11, 15, 7, 14, 6, 11, 10, 15, 7, 8, 9, 12, 11, 12, 14, 11, 10, 9, 13, 12, 15,
@@ -70,7 +62,7 @@
         many = sum(1 for u in UNITS if u[1] == c)
         lead = ((4, 4), (4,), ())
         b = {'C': pltpu.VMEM((2, 4, 4, 4, 2, 32, n), bf16), 'D': pltpu.VMEM((2, 4, 4, 4, 32, n), bf16),
-             'S1': pltpu.VMEM((4, 4, 32, n), f32), 'S2': pltpu.VMEM((3, 4, 32, n), f32)}
+             'S1': pltpu.VMEM((4, 4, 32, n), f32), 'S2': pltpu.VMEM((2, 4, 32, n), f32)}
         for ph in range(3):
             for name in ('opp', 'rig', 'lef'):
                 b[f'{name}{ph}'] = pltpu.VMEM(lead[ph] + (32, n), bf16)
@@ -88,10 +80,13 @@
 
 def reduce_kernel(*refs):
     dpre, act, pat, vin, dout, dstem, head_l, head_r = refs[:8]
+    sm_in, tk_in, refs = refs[8], refs[9], refs[:8] + refs[10:]
     wides = [dpre.at[0], act.at[0], dpre.at[1], act.at[1], pat]
     narrows = [vin.at[0], dout.at[0], vin.at[1], dout.at[1], dstem]
-    out_c, out_s, out_h = refs[8:11]
-    wide, narrow, per, send_sems, recv_sems, load_sems, credit = refs[11:]
+    (loss, out_s, o_bstem, o_ln1g, o_ln1b, o_wt1, o_bt1, o_wt2, o_ln2g, o_ln2b, out_c1, o_bch1, out_c2, o_bch2, o_lnfg, o_lnfb,
+     out_h, o_bhead) = refs[8:26]
+    wide, narrow, per, small, send_sems, recv_sems, load_sems, credit = refs[26:]
+    out_c = (out_c1, out_c2)
     me = my_place()
     other = moved(me, 'k', 1)
     k = me['k']
@@ -108,7 +103,16 @@
             copy.start()
 
     load(0)
-    meet_neighbours(me)
+    barrier = pltpu.get_barrier_semaphore()
+    for dim in 'xyz':
+        for step in (1, 2, 3):
+            pl.semaphore_signal(barrier, inc=1, device_id=device(moved(me, dim, step)), device_id_type=MESH)
+    pl.semaphore_signal(barrier, inc=1, device_id=device(other), device_id_type=MESH)
+    mine = [pltpu.make_async_copy(sm_in.at[:, :, :, k], small['sm0'], load_sems.at[2, 0]),
+            pltpu.make_async_copy(tk_in.at[:, :, :, k], small['tk0'], load_sems.at[2, 1])]
+    for copy in mine:
+        copy.start()
+    pl.semaphore_wait(barrier, 10)
     sender = Sender(send_sems, recv_sems)
     busy = {}
 
@@ -181,7 +185,7 @@
                 at = (at['x'], at['z'], at['y'])
                 return (self.buf['C'][(self.slot, *at, k, r, cols)].astype(f32)
                         + self.buf['D'][(self.slot, *at, r, cols)].astype(f32))
-            lead = () if phase == 1 else (self.index % 3,)
+            lead = () if phase == 1 else (self.index % 2,)
             return self.buf[f'S{phase}'][(*lead, p, *e, r, cols)]
 
         def each(self, phase, body):
@@ -255,13 +259,13 @@
                 if phase == 0:
                     self.buf['S1'][(*e, slice(None), cols)] = value
                 elif phase == 1:
-                    self.buf['S2'][(self.index % 3, *e, slice(None), cols)] = value
+                    self.buf['S2'][(self.index % 2, *e, slice(None), cols)] = value
                 elif self.g == STEM:
                     out_s[pl.ds(32 * self.c, 32), :] = value
                 elif self.g == HEAD:
-                    out_h[...] = value
+                    out_h[...] = value[:, 0:250]
                 else:
-                    out_c[self.g, :, pl.ds(*COLS[self.c])] = value
+                    out_c[self.g % 2][self.g // 2, :, pl.ds(*COLS[self.c])] = value
             self.each(phase, body)
             if phase == 0 and not self.last:
                 pl.semaphore_signal(credit.at[self.c], inc=1, device_id=device(other), device_id_type=MESH)
@@ -280,27 +284,124 @@
 
     units = [Unit(g, c) for g, c in UNITS]
     stage_of = [0] * len(units)
-    for u in ORDER:
+    for copy in mine:
+        copy.wait()
+    sums = SmallSums(me, sender, small, sm_in, tk_in)
+    for n, u in enumerate(ORDER):
+        if n in SMALL_AT:
+            sums.step(SMALL_AT.index(n))
         units[u].run(stage_of[u])
         stage_of[u] += 1
     assert stage_of == [8] * len(units)
+    sums.wait_sent()
+    small_unpack(small, loss, (o_bstem, o_lnfg, o_lnfb), (o_ln1g, o_ln1b, o_ln2g, o_ln2b, o_bch2), o_bch1, o_bhead, o_wt1,
+                 o_wt2, o_bt1)
     for key in list(busy):
         free(key)
     assert sender.count == REDUCE_COPIES, sender.count
+
+
+SMALL = dict(sm=((4, 4, 4, 8, 128), (4, 4, 4, 8, 128), (3, 4, 4, 8, 128), (3, 4, 8, 128), (3, 8, 128)),
+             tk=((4, 4, 4, 16, 128), (4, 4, 4, 16, 128), (3, 4, 4, 16, 128), (3, 4, 16, 128), (3, 4, 16, 128)))
+
+
+def small_scratch():
+    b = {f'{kind}{n}': pltpu.VMEM(shape, f32) for kind, shapes in SMALL.items() for n, shape in enumerate(shapes)}
+    b.update(sm_s1=pltpu.VMEM((4, 4, 8, 128), f32), sm_s2=pltpu.VMEM((4, 8, 128), f32), sm_own=pltpu.VMEM((8, 128), f32),
+             tk_s1=pltpu.VMEM((4, 4, 16, 128), f32), tk_s2=pltpu.VMEM((4, 16, 128), f32), tk_own=pltpu.VMEM((4, 16, 128), f32))
+    return b
+
+
+class SmallSums:
+    def __init__(self, me, sender, b, sm_in, tk_in):
+        self.me, self.sender, self.b, self.sent, self.last = me, sender, b, [], []
+        self.sm_in, self.tk_in = sm_in, tk_in
+
+    def send(self, src, dst, target):
+        copy = self.sender.start(src, dst, target)
+        self.sent.append(copy)
+        self.last.append(copy)
+
+    def wait_sent(self):
+        for copy in self.sent:
+            copy.wait_send()
+
+    def arrived(self):
+        for copy in self.last:
+            copy.wait_recv()
+        self.last = []
+
+    def step(self, n):
+        me, b = self.me, self.b
+        x, z, y, k = me['x'], me['z'], me['y'], me['k']
+        self.arrived()
+        if n == 0:
+            self.send(self.sm_in.at[:, :, :, 1 - k], b['sm1'], moved(me, 'k', 1))
+            self.send(self.tk_in.at[:, :, :, 1 - k], b['tk1'], moved(me, 'k', 1))
+        elif n == 1:
+            b['sm1'][...] += b['sm0'][...]
+            b['tk1'][...] += b['tk0'][...]
+            for s in (1, 2, 3):
+                self.send(b['sm1'].at[(x + s) % 4], b['sm2'].at[s - 1], moved(me, 'x', s))
+                self.send(b['tk1'].at[:, (z + s) % 4], b['tk2'].at[s - 1], moved(me, 'z', s))
+        elif n == 2:
+            b['sm_s1'][...] = b['sm1'][x] + b['sm2'][0] + b['sm2'][1] + b['sm2'][2]
+            b['tk_s1'][...] = b['tk1'][:, z] + b['tk2'][0] + b['tk2'][1] + b['tk2'][2]
+            for s in (1, 2, 3):
+                self.send(b['sm_s1'].at[(z + s) % 4], b['sm3'].at[s - 1], moved(me, 'z', s))
+                self.send(b['tk_s1'].at[:, (y + s) % 4], b['tk3'].at[s - 1], moved(me, 'y', s))
+        elif n == 3:
+            b['sm_s2'][...] = b['sm_s1'][z] + b['sm3'][0] + b['sm3'][1] + b['sm3'][2]
+            b['tk_s2'][...] = b['tk_s1'][:, y] + b['tk3'][0] + b['tk3'][1] + b['tk3'][2]
+            for s in (1, 2, 3):
+                self.send(b['sm_s2'].at[(y + s) % 4], b['sm4'].at[s - 1], moved(me, 'y', s))
+                self.send(b['tk_s2'], b['tk4'].at[s - 1], moved(me, 'x', s))
+        elif n == 4:
+            b['sm_own'][...] = b['sm_s2'][y] + b['sm4'][0] + b['sm4'][1] + b['sm4'][2]
+            parts = [b['tk_s2'][...]] + [b['tk4'][s] for s in range(3)]
+            ordered = []
+            for place in range(4):
+                value = parts[0]
+                for s in (1, 2, 3):
+                    value = jnp.where((x + 4 - s) % 4 == place, parts[s], value)
+                ordered.append(value)
+            b['tk_own'][...] = (ordered[0] + ordered[1]) + (ordered[2] + ordered[3])
+
+
+def small_unpack(b, loss, singles, pairs, o_bch1, o_bhead, o_wt1, o_wt2, o_bt1):
+    own = b['sm_own'][...]
+    turned = jnp.concatenate([own, jnp.zeros((120, 128), f32)], axis=0).T
+    for ref, n in zip(singles, (0, 11, 12)):
+        ref[...] = turned[n, 0:8]
+    for n, ref in enumerate(pairs):
+        for l in range(2):
+            ref[pl.ds(l, 1), :] = turned[1 + 5 * l + n:2 + 5 * l + n, 0:8]
+    o_bch1[...] = own[0:2, 32:64]
+    classes = jnp.concatenate([own[2 + q:3 + q, 64:128] for q in range(4)], axis=1)
+    o_bhead[...] = classes[0, 0:250]
+    loss[...] = own[6:7, 64:65] * (1.0 / 1024)
+    tk = b['tk_own'][...]
+    for l in range(2):
+        o_wt1[l] = tk[l, :, 0:TOK]
+        o_wt2[l] = tk[2 + l, :, 0:TOK]
+        tall = jnp.concatenate([tk[l], jnp.zeros((112, 128), f32)], axis=0).T
+        o_bt1[pl.ds(l, 1), :] = tall[64:65, 0:16]
 
 
 def reduce_gradients(*operands):
     any_spec = pl.BlockSpec(memory_space=pl.ANY)
     vmem = pl.BlockSpec(memory_space=pltpu.VMEM)
     rows = operands[2].shape[0]
+    S = jax.ShapeDtypeStruct
     return pl.pallas_call(
         reduce_kernel, name='reduce_gradients',
-        out_shape=[jax.ShapeDtypeStruct((N_CH, 32, 1024), f32), jax.ShapeDtypeStruct((96, 256), f32),
-                   jax.ShapeDtypeStruct((32, 256), f32)],
-        in_specs=[any_spec] * 6 + [vmem] * 2, out_specs=[vmem] * 3,
-        scratch_shapes=[pltpu.VMEM((2, rows, 4096), bf16), pltpu.VMEM((2, rows, 1024), bf16), reduce_scratch(),
+        out_shape=[S((1, 1), f32), S((96, 256), f32), S((8,), f32), S((2, 8), f32), S((2, 8), f32), S((2, 16, TOK), f32),
+                   S((2, 16), f32), S((2, 16, TOK), f32), S((2, 8), f32), S((2, 8), f32), S((2, 32, 1024), f32), S((2, 32), f32),
+                   S((2, 32, 1024), f32), S((2, 8), f32), S((8,), f32), S((8,), f32), S((32, 250), f32), S((250,), f32)],
+        in_specs=[any_spec] * 6 + [vmem] * 2 + [any_spec] * 2, out_specs=[vmem] * 18,
+        scratch_shapes=[pltpu.VMEM((2, rows, 4096), bf16), pltpu.VMEM((2, rows, 1024), bf16), reduce_scratch(), small_scratch(),
                         pltpu.SemaphoreType.DMA((REDUCE_COPIES,)), pltpu.SemaphoreType.DMA((REDUCE_COPIES,)),
-                        pltpu.SemaphoreType.DMA((2, 2)), pltpu.SemaphoreType.REGULAR((3,))],
+                        pltpu.SemaphoreType.DMA((3, 2)), pltpu.SemaphoreType.REGULAR((3,))],
         compiler_params=pltpu.CompilerParams(collective_id=1, has_side_effects=True, vmem_limit_bytes=64 * 1024 * 1024 - 65536),
         cost_estimate=pl.CostEstimate(flops=100_000_000_000, bytes_accessed=80_000_000, transcendentals=0),
     )(*operands)
@@ -414,9 +515,35 @@
         out.wait(n - 1, 1 - n % 2)
 
 
-def backward_kernel(xin, xmid, pre_in, wc, wt, vec, dx0,
-                    dpre, dout, dstem, gvec, gbch1, gt1, gt2, gbt,
-                    x_v, d_v, dv_v, do_v, w1_v, w2_v, pre_v, dp_v, g_v, dh_v, sem, sem_w, sem_o):
+def small_pack(flat, turn, gvec, hstat, gbch1, gbh):
+    turn[...] = jnp.zeros_like(turn)
+    turn[pl.ds(0, 16), :] = gvec[...]
+    turn[pl.ds(11, 2), :] = hstat[pl.ds(0, 2), :]
+    for n in range(8):
+        flat[pl.ds(128 * n, 128), :] = turn[:, pl.ds(128 * n, 128)].T
+    for l in range(2):
+        total = jnp.zeros((384, 128), f32)
+        for n in range(8):
+            lane = lax.broadcasted_iota(jnp.int32, (128, 512), 0)
+            col = lax.broadcasted_iota(jnp.int32, (128, 512), 1)
+            mine = jnp.where(lane == n * 16 + col // 32, gbch1[l:l + 1, 512 * n:512 * (n + 1)], 0.0)
+            pick = jnp.where(lane == 32 + col % 32, 1.0, 0.0).astype(bf16)
+            total += lax.dot_general(jnp.concatenate(three_parts(mine), axis=0), pick, (((1,), (1,)), ((), ())),
+                                     preferred_element_type=f32)
+        flat[pl.ds(l, 128, stride=8), :] += total[0:128] + total[128:256] + total[256:384]
+    high = lax.broadcasted_iota(jnp.int32, (1, 128), 1) >= 64
+    for t in range(4):
+        for q in range(4):
+            tile = gbh[0:1, t * 256 + q // 2 * 128:t * 256 + q // 2 * 128 + 128]
+            if q % 2 == 0:
+                tile = jnp.concatenate([tile[:, 64:], tile[:, :64]], axis=1)
+            flat[pl.ds(t * 256 + 2 + q, 32, stride=8), :] += jnp.where(high, tile, 0.0)
+    at64 = lax.broadcasted_iota(jnp.int32, (1, 128), 1) == 64
+    flat[pl.ds(6, 128, stride=8), :] += jnp.where(at64, hstat[2:3, 0:128], 0.0)
+
+
+def backward_kernel(xin, xmid, pre_in, wc, wt, vec, dx0, hstat, gbh,
+                    dpre, dout, dstem, flat, tk, gvec, gbch1, turn, x_v, d_v, dv_v, do_v, w1_v, w2_v, pre_v, dp_v, g_v, dh_v, sem, sem_w, sem_o):
     mask = row_mask()
     rest = pl.ds(ROWS, XROWS - ROWS)
     put(d_v, rest, jnp.zeros((XROWS - ROWS, CH), f32))
@@ -426,9 +553,7 @@
     def _(s):
         put(d_v, pl.ds(pl.multiple_of(s * IMG, IMG), IMG), dx0[...])
     gvec[...] = jnp.zeros_like(gvec)
-    gt1[...] = jnp.zeros_like(gt1)
-    gt2[...] = jnp.zeros_like(gt2)
-    gbt[...] = jnp.zeros_like(gbt)
+    tk[...] = jnp.zeros_like(tk)
 
     def add(row, value):
         gvec[row:row + 1, :] += jnp.sum(value, axis=0, keepdims=True)
@@ -495,10 +620,10 @@
             act, slope = gelu_both(dot_nn(wt[l, :, 0:TPAD], a))
             g_v[...] = act.astype(bf16)
             dh = dot_nn(wt[2 + l, :, 0:TPAD], dm) * slope
-            gbt[l] += jnp.sum(dh, axis=-1, keepdims=True)
+            tk[l, :, pl.ds(64, 1)] += jnp.sum(dh, axis=-1, keepdims=True)
             dh_v[...] = dh.astype(bf16)
-            gt2[l] += dot_nt(g_v[...], dm)
-            gt1[l] += dot_nt(dh_v[...], a)
+            tk[2 + l, :, pl.ds(0, TPAD)] += dot_nt(g_v[...], dm)
+            tk[l, :, pl.ds(0, TPAD)] += dot_nt(dh_v[...], a)
             d = jnp.where(mask, dot_tn(wt[l, :, 0:TPAD], dh_v[...]), 0.0)
             add(r, d * std)
             add(r + 1, d)
@@ -510,6 +635,7 @@
         do_v[pl.ds(at, size), :] = d.astype(bf16)
     send = pltpu.make_async_copy(do_v, dstem, sem.at[1])
     send.start()
+    small_pack(flat, turn, gvec, hstat, gbch1, gbh)
     send.wait()
 
 
@@ -518,11 +644,12 @@
     S = jax.ShapeDtypeStruct
     return pl.pallas_call(
         backward_kernel, name='backward',
-        in_specs=[a] * 4 + [v] * 3,
-        out_specs=[a] * 3 + [v] * 5,
-        out_shape=[S((2, ROWS, CHH), bf16), S((2, ROWS, CH), bf16), S((ROWS, CH), bf16), S((16, CH), f32), S((2, CHH), f32),
-                   S((2, TOKH, TPAD), f32), S((2, TOKH, TPAD), f32), S((2, TOKH, 1), f32)],
-        scratch_shapes=[pltpu.VMEM((CH // 128, XROWS, 128), f32), pltpu.VMEM((CH // 128, XROWS, 128), f32), pltpu.VMEM((ROWS, CH), f32),
+        in_specs=[a] * 4 + [v] * 5,
+        out_specs=[a] * 3 + [v] * 2,
+        out_shape=[S((2, ROWS, CHH), bf16), S((2, ROWS, CH), bf16), S((ROWS, CH), bf16), S((1024, 128), f32),
+                   S((4, TOKH, 128), f32)],
+        scratch_shapes=[pltpu.VMEM((16, CH), f32), pltpu.VMEM((2, CHH), f32), pltpu.VMEM((128, 1024), f32),
+                        pltpu.VMEM((CH // 128, XROWS, 128), f32), pltpu.VMEM((CH // 128, XROWS, 128), f32), pltpu.VMEM((ROWS, CH), f32),
                         pltpu.VMEM((ROWS, CH), bf16), pltpu.VMEM((2, 4, 4, 2, 32, BLK), bf16),
                         pltpu.VMEM((2, 2, 4, 2, 32, CH), bf16),
                         pltpu.VMEM((2, ROWS, BLK), f32), pltpu.VMEM((2, ROWS, BLK), bf16), pltpu.VMEM((TOKH, CH), bf16),
@@ -946,51 +1073,18 @@
 
 
 def solution(mesh):
-    fs = mesh.shape['fsdp']
-    tp = mesh.shape['tp']
-    nd = fs * tp
-
     def step(patches, labels, w_stem, b_stem, ln1_g, ln1_b, w_tok1, b_tok1, w_tok2,
              ln2_g, ln2_b, w_ch1, b_ch1, w_ch2, b_ch2, lnf_g, lnf_b, w_head, b_head):
-        t = lax.axis_index('tp')
-        nl = w_tok1.shape[0]
-        total_images = IMG * nd
-        classes = w_head.shape[1]
         wc, pat, xin, xmid, vin, pre, act, hl, hr, dx0, hstat, gbh, vec, wt = front(
             labels, patches.transpose(1, 0, 2), w_stem, w_ch1, w_ch2, w_head, w_tok1.transpose(0, 2, 1), w_tok2, b_tok1, b_ch1,
             b_head, b_stem, ln1_g, ln1_b, ln2_g, ln2_b, b_ch2, lnf_g, lnf_b)
         pat = pat.reshape(ROWS, -1)
-        dpre, dout, dstem, gvec, gbch1, gt1, gt2, gbt = backward(xin, xmid, pre, wc, wt, vec, dx0)
-
-        gvec = jnp.concatenate([gvec[:11], hstat[:2]], axis=0)
-        parts = [gvec, gbch1, gbt[:, :, 0], gbh, gt1, gt2, hstat[2, :1]]
-        flat = jnp.concatenate([p.reshape(-1) for p in parts])
-        flat = jnp.pad(flat, (0, (-flat.shape[0]) % 1024))
-        tot = lax.psum(flat, CHANNEL_AXES)
-
-        g_c, g_s, g_h = reduce_gradients(dpre, act, pat, vin, dout, dstem, hl, hr)
-
-        out = []
-        o = 0
-        for p in parts:
-            out.append(tot[o:o + p.size].reshape(p.shape))
-            o += p.size
-        f = lax.axis_index('fsdp')
-
-        def own(x, n, i, ax):
-            size = x.shape[ax] // n
-            return lax.dynamic_slice_in_dim(x, i * size, size, ax)
-        dev = t * fs + f
-        gv = own(out[0], nd, dev, 1)
-        gc1 = own(out[1], nd, dev, 1)
-        gtb = own(out[2], fs, f, 1)
-        gbh = own(out[3].reshape(tp, 256), tp, t, 0)[0, :classes]
-        gw1 = own(out[4], fs, f, 1)[:, :, :TOK].transpose(0, 2, 1)
-        gw2 = own(out[5], fs, f, 1)[:, :, :TOK]
-        loss = out[6][0] / total_images
-        per = [jnp.stack([gv[1 + i], gv[6 + i]]) for i in range(5)]
-        return (loss, g_s, gv[0], per[0], per[1], gw1, gtb, gw2, per[2], per[3], g_c[0::2], gc1, g_c[1::2], per[4],
-                gv[11], gv[12], g_h[:, :classes], gbh)
+        dpre, dout, dstem, sm, tk = backward(xin, xmid, pre, wc, wt, vec, dx0, hstat, gbh)
+
+        loss, g_s, g_bs, g_1g, g_1b, g_t1, g_bt, g_t2, g_2g, g_2b, g_c1, g_b1, g_c2, g_b2, g_fg, g_fb, g_h, g_bh = reduce_gradients(
+            dpre, act, pat, vin, dout, dstem, hl, hr, sm.reshape(4, 4, 4, 2, 8, 128), tk.reshape(4, 4, 4, 2, 16, 128))
+        return (loss.reshape(()), g_s, g_bs, g_1g, g_1b, g_t1.transpose(0, 2, 1), g_bt, g_t2, g_2g, g_2b, g_c1, g_b1, g_c2, g_b2,
+                g_fg, g_fb, g_h, g_bh)
 
     specs = weight_specs()
     return jax.shard_map(step, mesh=mesh, in_specs=(P('fsdp', None, None), P('fsdp')) + specs,

time: 402 us -> 391 us (0.973)
  between operations: 16 us -> 2.46 us
  Pallas kernels: 360 us -> 365 us
    unnamed x12 -> x17, local copies, waits for them, and re-layouts: 3.74 us -> 22 us
    slice x12 -> x0, local copies, waits for them, and re-layouts: 8.97 us -> none  [the longest x8 4.57 us: step(): out.append(tot[o:o + p.size].reshape(p.shape))]
  transfers between devices with their start and end apart: 1 -> 0, of which waited for: 0 -> 0; matrix products, arithmetic and copies ran while one was open for 0% -> 0% of each run, Pallas kernels for 37% -> 0%
where the time goes in v7:
time: 391 us; the launch traced here: 389 us
  Pallas kernels  365 us (93%)
  local copies, waits for them, and re-layouts  22 us (6%)
    pallas_call x1, Pallas kernels, reduce_gradients(): pl.pallas_call(reduce_kernel, name='reduce_gradients', out_shape=[S((1, 1...  150 us
    pallas_call x1, Pallas kernels, front(): pl.pallas_call(front_kernel, name='front', in_specs=[pl.BlockSpec(memory_...  128 us
    pallas_call x1, Pallas kernels, backward(): pl.pallas_call(backward_kernel, name='backward', in_specs=[a] * 4 + [v] *...  86.4 us
    unnamed x17, local copies, waits for them, and re-layouts  22 us

profile of v7, /device:TPU:0, one launch (start us, length us, event | category | flops | bytes accessed | tf_op | source)
XLA Modules:
  0.0 389.1 jit_solution(550619369111717794)
XLA Ops:
  0.7 128.2 %front.1 = (bf16[4,4,4,4,2,32,1024]{6,5,4,3,2,1,0:T(8,128)(2,1)}, bf16[49,8,3072]{2,1,0:T(8,128)(2,1)}, f32[2,8,392,128]{3,2,1,0:T(8,128)}, f32[2,8,392,128]{3,2...) custom-call(s32[32]{0:T(128)} %labels.1, ...), custom_call_target="tpu_custom_call" | custom-call | flops 89999998976 | bytes 180000000 | tf_op jit(solution)/shard_map/front/pallas_call | solution.py:1043
  128.8 86.4 %backward.1 = (bf16[2,392,4096]{2,1,0:T(8,128)(2,1)}, bf16[2,392,1024]{2,1,0:T(8,128)(2,1)}, bf16[392,1024]{1,0:T(8,128)(2,1)}, f32[1024,128]{1,0:T(8,128)}, f32[4,512,128]{2,1,0:T(8,128)}) custom-call(f32[2,8,392,128]{3,2,1,0:T(8,128)} %get-tuple-element.55.xin, f32[2,8,392,128]{3,2,1,0:T(8,128)} %get-tuple-element.56.xmid, ...), custom_call_target="tpu_custom_call" | custom-call | flops 49999998976 | bytes 100000000 | tf_op jit(solution)/shard_map/backward/pallas_call | solution.py:645
  215.3 150.1 %reduce_gradients.1 = (f32[1,1]{1,0:T(1,128)}, f32[96,256]{1,0:T(8,128)}, f32[8]{0:T(128)}, f32[2,8]{1,0:T(2,128)}, f32[2,8]{1,0:T(2,128)}, /*index=5*/f32[2,16,...) custom-call(bf16[2,392,4096]{2,1,0:T(8,128)(2,1)} %get-tuple-element, ...), custom_call_target="tpu_custom_call" | custom-call | flops 99999997952 | bytes 80000000 | tf_op jit(solution)/shard_map/reduce_gradients/pallas_call | solution.py:396
  366.0 1.5 copy.56
  367.5 1.1 copy.57
  368.7 1.2 copy.58
  369.9 1.2 copy.59
  371.1 1.3 copy.60
  372.4 1.2 copy.61
  373.6 1.3 copy.62
  375.0 1.2 copy.63
  376.2 1.2 copy.64
  377.4 1.7 copy.65
  379.1 1.2 copy.66
  380.3 1.7 copy.67
  382.0 1.2 copy.68
  383.2 1.1 copy.69
  384.4 1.1 copy.70
  385.5 1.4 copy.71
  386.9 1.2 copy.72

commit v8 on v7

--- a/solution.py
+++ b/solution.py
@@ -83,10 +83,9 @@
     sm_in, tk_in, refs = refs[8], refs[9], refs[:8] + refs[10:]
     wides = [dpre.at[0], act.at[0], dpre.at[1], act.at[1], pat]
     narrows = [vin.at[0], dout.at[0], vin.at[1], dout.at[1], dstem]
-    (loss, out_s, o_bstem, o_ln1g, o_ln1b, o_wt1, o_bt1, o_wt2, o_ln2g, o_ln2b, out_c1, o_bch1, out_c2, o_bch2, o_lnfg, o_lnfb,
-     out_h, o_bhead) = refs[8:26]
-    wide, narrow, per, small, send_sems, recv_sems, load_sems, credit = refs[26:]
-    out_c = (out_c1, out_c2)
+    out_c, out_s, out_h, sm_own, tk_own = refs[8:13]
+    wide, narrow, per, small, send_sems, recv_sems, load_sems, credit = refs[13:]
+    small.update(sm_own=sm_own, tk_own=tk_own)
     me = my_place()
     other = moved(me, 'k', 1)
     k = me['k']
@@ -263,9 +262,9 @@
                 elif self.g == STEM:
                     out_s[pl.ds(32 * self.c, 32), :] = value
                 elif self.g == HEAD:
-                    out_h[...] = value[:, 0:250]
+                    out_h[...] = value
                 else:
-                    out_c[self.g % 2][self.g // 2, :, pl.ds(*COLS[self.c])] = value
+                    out_c[self.g, :, pl.ds(*COLS[self.c])] = value
             self.each(phase, body)
             if phase == 0 and not self.last:
                 pl.semaphore_signal(credit.at[self.c], inc=1, device_id=device(other), device_id_type=MESH)
@@ -294,8 +293,6 @@
         stage_of[u] += 1
     assert stage_of == [8] * len(units)
     sums.wait_sent()
-    small_unpack(small, loss, (o_bstem, o_lnfg, o_lnfb), (o_ln1g, o_ln1b, o_ln2g, o_ln2b, o_bch2), o_bch1, o_bhead, o_wt1,
-                 o_wt2, o_bt1)
     for key in list(busy):
         free(key)
     assert sender.count == REDUCE_COPIES, sender.count
@@ -307,8 +304,8 @@
 
 def small_scratch():
     b = {f'{kind}{n}': pltpu.VMEM(shape, f32) for kind, shapes in SMALL.items() for n, shape in enumerate(shapes)}
-    b.update(sm_s1=pltpu.VMEM((4, 4, 8, 128), f32), sm_s2=pltpu.VMEM((4, 8, 128), f32), sm_own=pltpu.VMEM((8, 128), f32),
-             tk_s1=pltpu.VMEM((4, 4, 16, 128), f32), tk_s2=pltpu.VMEM((4, 16, 128), f32), tk_own=pltpu.VMEM((4, 16, 128), f32))
+    b.update(sm_s1=pltpu.VMEM((4, 4, 8, 128), f32), sm_s2=pltpu.VMEM((4, 8, 128), f32),
+             tk_s1=pltpu.VMEM((4, 4, 16, 128), f32), tk_s2=pltpu.VMEM((4, 16, 128), f32))
     return b
 
 
@@ -368,24 +365,40 @@
             b['tk_own'][...] = (ordered[0] + ordered[1]) + (ordered[2] + ordered[3])
 
 
-def small_unpack(b, loss, singles, pairs, o_bch1, o_bhead, o_wt1, o_wt2, o_bt1):
-    own = b['sm_own'][...]
+def finish_kernel(c, stem, head, sm, tk, loss, o_stem, o_bstem, o_ln1g, o_ln1b, o_wt1, o_bt1, o_wt2, o_ln2g, o_ln2b, o_ch1,
+                  o_bch1, o_ch2, o_bch2, o_lnfg, o_lnfb, o_head, o_bhead):
+    for l in range(2):
+        o_ch1[l] = c[2 * l]
+        o_ch2[l] = c[2 * l + 1]
+    o_stem[...] = stem[...]
+    o_head[...] = head[:, 0:250]
+    own = sm[...]
     turned = jnp.concatenate([own, jnp.zeros((120, 128), f32)], axis=0).T
-    for ref, n in zip(singles, (0, 11, 12)):
+    for ref, n in ((o_bstem, 0), (o_lnfg, 11), (o_lnfb, 12)):
         ref[...] = turned[n, 0:8]
-    for n, ref in enumerate(pairs):
+    for n, ref in enumerate((o_ln1g, o_ln1b, o_ln2g, o_ln2b, o_bch2)):
         for l in range(2):
             ref[pl.ds(l, 1), :] = turned[1 + 5 * l + n:2 + 5 * l + n, 0:8]
     o_bch1[...] = own[0:2, 32:64]
     classes = jnp.concatenate([own[2 + q:3 + q, 64:128] for q in range(4)], axis=1)
     o_bhead[...] = classes[0, 0:250]
     loss[...] = own[6:7, 64:65] * (1.0 / 1024)
-    tk = b['tk_own'][...]
     for l in range(2):
         o_wt1[l] = tk[l, :, 0:TOK]
         o_wt2[l] = tk[2 + l, :, 0:TOK]
         tall = jnp.concatenate([tk[l], jnp.zeros((112, 128), f32)], axis=0).T
         o_bt1[pl.ds(l, 1), :] = tall[64:65, 0:16]
+
+
+def finish(*operands):
+    S = jax.ShapeDtypeStruct
+    v = pl.BlockSpec(memory_space=pltpu.VMEM)
+    return pl.pallas_call(
+        finish_kernel, name='finish', in_specs=[v] * 5, out_specs=[v] * 18,
+        out_shape=[S((1, 1), f32), S((96, 256), f32), S((8,), f32), S((2, 8), f32), S((2, 8), f32), S((2, 16, TOK), f32),
+                   S((2, 16), f32), S((2, 16, TOK), f32), S((2, 8), f32), S((2, 8), f32), S((2, 32, 1024), f32), S((2, 32), f32),
+                   S((2, 32, 1024), f32), S((2, 8), f32), S((8,), f32), S((8,), f32), S((32, 250), f32), S((250,), f32)],
+    )(*operands)
 
 
 def reduce_gradients(*operands):
@@ -395,10 +408,8 @@
     S = jax.ShapeDtypeStruct
     return pl.pallas_call(
         reduce_kernel, name='reduce_gradients',
-        out_shape=[S((1, 1), f32), S((96, 256), f32), S((8,), f32), S((2, 8), f32), S((2, 8), f32), S((2, 16, TOK), f32),
-                   S((2, 16), f32), S((2, 16, TOK), f32), S((2, 8), f32), S((2, 8), f32), S((2, 32, 1024), f32), S((2, 32), f32),
-                   S((2, 32, 1024), f32), S((2, 8), f32), S((8,), f32), S((8,), f32), S((32, 250), f32), S((250,), f32)],
-        in_specs=[any_spec] * 6 + [vmem] * 2 + [any_spec] * 2, out_specs=[vmem] * 18,
+        out_shape=[S((N_CH, 32, 1024), f32), S((96, 256), f32), S((32, 256), f32), S((8, 128), f32), S((4, 16, 128), f32)],
+        in_specs=[any_spec] * 6 + [vmem] * 2 + [any_spec] * 2, out_specs=[vmem] * 5,
         scratch_shapes=[pltpu.VMEM((2, rows, 4096), bf16), pltpu.VMEM((2, rows, 1024), bf16), reduce_scratch(), small_scratch(),
                         pltpu.SemaphoreType.DMA((REDUCE_COPIES,)), pltpu.SemaphoreType.DMA((REDUCE_COPIES,)),
                         pltpu.SemaphoreType.DMA((3, 2)), pltpu.SemaphoreType.REGULAR((3,))],
@@ -1081,8 +1092,8 @@
         pat = pat.reshape(ROWS, -1)
         dpre, dout, dstem, sm, tk = backward(xin, xmid, pre, wc, wt, vec, dx0, hstat, gbh)
 
-        loss, g_s, g_bs, g_1g, g_1b, g_t1, g_bt, g_t2, g_2g, g_2b, g_c1, g_b1, g_c2, g_b2, g_fg, g_fb, g_h, g_bh = reduce_gradients(
-            dpre, act, pat, vin, dout, dstem, hl, hr, sm.reshape(4, 4, 4, 2, 8, 128), tk.reshape(4, 4, 4, 2, 16, 128))
+        loss, g_s, g_bs, g_1g, g_1b, g_t1, g_bt, g_t2, g_2g, g_2b, g_c1, g_b1, g_c2, g_b2, g_fg, g_fb, g_h, g_bh = finish(*reduce_gradients(
+            dpre, act, pat, vin, dout, dstem, hl, hr, sm.reshape(4, 4, 4, 2, 8, 128), tk.reshape(4, 4, 4, 2, 16, 128)))
         return (loss.reshape(()), g_s, g_bs, g_1g, g_1b, g_t1.transpose(0, 2, 1), g_bt, g_t2, g_2g, g_2b, g_c1, g_b1, g_c2, g_b2,
                 g_fg, g_fb, g_h, g_bh)
 

time: 391 us -> 369 us (0.944)
  local copies, waits for them, and re-layouts: 22 us -> 0 us
    unnamed x17 -> x0, local copies, waits for them, and re-layouts: 22 us -> none
    pallas_call x1 -> x2, Pallas kernels: 150 us -> 152 us  [the longest x1 150 us: reduce_gradients(): pl.pallas_call(reduce_kernel, name='reduce_gradients', out_shape=[S((N_CH...]
where the time goes in v8:
time: 369 us; the launch traced here: 368 us
  Pallas kernels  367 us (99%)
    pallas_call x1, Pallas kernels, reduce_gradients(): pl.pallas_call(reduce_kernel, name='reduce_gradients', out_shape=[S((N_CH...  150 us
    pallas_call x1, Pallas kernels, front(): pl.pallas_call(front_kernel, name='front', in_specs=[pl.BlockSpec(memory_...  128 us
    pallas_call x1, Pallas kernels, backward(): pl.pallas_call(backward_kernel, name='backward', in_specs=[a] * 4 + [v] *...  86.5 us

profile of v8, /device:TPU:0, one launch (start us, length us, event | category | flops | bytes accessed | tf_op | source)
XLA Modules:
  0.0 367.6 jit_solution(12008956762142202860)
XLA Ops:
  0.7 128.2 %front.1 = (bf16[4,4,4,4,2,32,1024]{6,5,4,3,2,1,0:T(8,128)(2,1)}, bf16[49,8,3072]{2,1,0:T(8,128)(2,1)}, f32[2,8,392,128]{3,2,1,0:T(8,128)}, f32[2,8,392,128]{3,2...) custom-call(s32[32]{0:T(128)} %labels.1, ...), custom_call_target="tpu_custom_call" | custom-call | flops 89999998976 | bytes 180000000 | tf_op jit(solution)/shard_map/front/pallas_call | solution.py:1054
  128.9 86.5 %backward.1 = (bf16[2,392,4096]{2,1,0:T(8,128)(2,1)}, bf16[2,392,1024]{2,1,0:T(8,128)(2,1)}, bf16[392,1024]{1,0:T(8,128)(2,1)}, f32[1024,128]{1,0:T(8,128)}, f32[4,512,128]{2,1,0:T(8,128)}) custom-call(f32[2,8,392,128]{3,2,1,0:T(8,128)} %get-tuple-element.60.xin, f32[2,8,392,128]{3,2,1,0:T(8,128)} %get-tuple-element.61.xmid, ...), custom_call_target="tpu_custom_call" | custom-call | flops 49999998976 | bytes 100000000 | tf_op jit(solution)/shard_map/backward/pallas_call | solution.py:656
  215.4 150.0 %reduce_gradients.1 = (f32[4,32,1024]{2,1,0:T(8,128)}, f32[96,256]{1,0:T(8,128)}, f32[32,256]{1,0:T(8,128)}, f32[8,128]{1,0:T(8,128)}, f32[4,16,128]{2,1,0:T(8,128)}) custom-call(bf16[2,392,4096]{2,1,0:T(8,128)(2,1)} %get-tuple-element.69.refs_0_, bf16[2,392,4096]{2,1,0:T(8,128)(2,1)} %get-tuple-element.70.refs_1_, bf16[392,3072]{1,0:T(8,128)(2,1)} %bitcast.10, ...), custom_call_target="tpu_custom_call" | custom-call | flops 99999997952 | bytes 80000000 | tf_op jit(solution)/shard_map/reduce_gradients/pallas_call | solution.py:409
  365.4 2.0 finish.1

commit v9 on v6

v9 whole, which is shorter than its diff:
```python
import functools

import jax
import jax.numpy as jnp
from jax import lax
from jax.experimental import pallas as pl
from jax.experimental.pallas import tpu as pltpu
from jax.sharding import PartitionSpec as P

MESH = pl.DeviceIdType.MESH
ORDERS = (('x', 'y', 'z'), ('y', 'z', 'x'), ('z', 'x', 'y'))
COLS = ((0, 384), (384, 384), (768, 256))
N_CH = 4
STEM, HEAD = 4, 5
bf16, f32 = jnp.bfloat16, jnp.float32


def my_place():
    f = lax.axis_index('fsdp')
    return {'x': lax.axis_index('tp'), 'z': f // 8, 'y': (f // 2) % 4, 'k': f % 2}


def moved(place, dim, step):
    new = dict(place)
    new[dim] = 1 - place['k'] if dim == 'k' else (place[dim] + step) % 4
    return new


def device(place):
    return {'tp': place['x'], 'fsdp': (place['z'] * 4 + place['y']) * 2 + place['k']}


EPS = 1e-6
TOK, TPAD = 49, 56
IMG = 8
ROWS, XROWS = IMG * TOK, IMG * TPAD
CHUNKS = ((0, 112), (112, 112), (224, 112), (336, 56))
CH, TOKH, CHH = 1024, 512, 4096
BLK = 512
NBLK = CHH // BLK
GELU_C, GELU_A = 0.7978845608028654, 0.044715


def dot_nn(a, b):
    return lax.dot_general(a, b, (((1,), (0,)), ((), ())), preferred_element_type=f32)


def dot_nt(a, b):
    return lax.dot_general(a, b, (((1,), (1,)), ((), ())), preferred_element_type=f32)


def dot_tn(a, b):
    return lax.dot_general(a, b, (((0,), (0,)), ((), ())), preferred_element_type=f32)


def gelu(x):
    half = 0.5 * x
    return half + half * jnp.tanh(x * (GELU_C + (GELU_C * GELU_A) * (x * x)))


def gelu_both(x):
    sq = x * x
    th = jnp.tanh(x * (GELU_C + (GELU_C * GELU_A) * sq))
    half = 0.5 * x
    rise = 0.5 + 0.5 * th
    slope = (1.0 - th * th) * (GELU_C + (3.0 * GELU_C * GELU_A) * sq)
    return x * rise, rise + half * slope


def standardize(x):
    mean = jnp.mean(x, axis=-1, keepdims=True)
    cent = x - mean
    inv = lax.rsqrt(jnp.mean(cent * cent, axis=-1, keepdims=True) + EPS)
    return cent * inv, inv


def norm_grad(d, gain, std, inv):
    gs = d * gain
    m0 = jnp.mean(gs, axis=-1, keepdims=True)
    m1 = jnp.mean(gs * std, axis=-1, keepdims=True)
    return inv * (gs - m0 - std * m1)


def row_mask(rows=TPAD):
    return lax.broadcasted_iota(jnp.int32, (rows, 1), 0) < TOK


def image(b):
    return pl.ds(b, TPAD, stride=IMG)


def get(ref, rows):
    return jnp.concatenate([ref[n, rows, :] for n in range(CH // 128)], axis=1)


def put(ref, rows, value):
    for n in range(CH // 128):
        ref[n, rows, :] = value[:, 128 * n:128 * (n + 1)]


class Stream:
    def __init__(self, sem, copies, count):
        self.sem, self.copies, self.count = sem, copies, count

    def make(self, i, slot):
        return [pltpu.make_async_copy(src, dst, self.sem.at[slot, n]) for n, (src, dst) in enumerate(self.copies(i, slot))]

    def start(self, i, slot):
        for copy in self.make(i, slot):
            copy.start()

    def wait(self, i, slot):
        for copy in self.make(i, slot):
            copy.wait()


def for_blocks(stream, body, out=None):
    n = stream.count
    stream.start(0, 0)

    @pl.loop(0, n)
    def _(i):
        slot = i % 2
        stream.wait(i, slot)

        @pl.when(i + 1 < n)
        def _():
            stream.start(i + 1, 1 - slot)
        if out is not None:
            @pl.when(i >= 2)
            def _():
                out.wait(i - 2, slot)
        body(i, slot)
        if out is not None:
            out.start(i, slot)
    if out is not None:
        out.wait(n - 2, n % 2)
        out.wait(n - 1, 1 - n % 2)


FRONT_COPIES = 240
EARLY = [('stem', 0), ('stem', 1), ('stem', 2), ('ch', 0), ('ch', 1), ('ch', 2), ('head', 2)]
LATE = [('stem', c, None) for c in range(3)] + [('ch', c, g) for g in range(N_CH) for c in range(3)] + [('head', 2, None)]
UNIT_GROUP = {('stem', None): 0, ('ch', 0): 1, ('ch', 1): 2, ('ch', 2): 3, ('ch', 3): 4, ('head', None): 5}
EVERY = pl.ds(0, 4)
FRONT_ORDER = (
    ('prep', (('M0', ('sm',)), ('M0', ('tk',)), ('A0', ('stem', 0)), ('A0', ('stem', 1)), ('A0', ('stem', 2)),
        ('A0', ('ch', 0)), ('A0', ('ch', 1)), ('A0', ('ch', 2)), ('A0', ('head', 2)),)),
    ('unpack', (('M1', ('sm',)), ('M1', ('tk',)), ('A', ('stem', 0)), ('A', ('stem', 1)), ('A', ('stem', 2)),
        ('A', ('head', 2)), ('A', ('ch', 2)), ('A', ('ch', 0)), ('A', ('ch', 1)), ('B', ('stem', 0)), ('M2', ('sm',)),
        ('B', ('stem', 1)), ('M2', ('tk',)), ('B', ('stem', 2)), ('B', ('ch', 0)), ('B', ('head', 2)), ('B', ('ch', 1)),
        ('C', ('stem', 0)), ('B', ('ch', 2)), ('M3', ('sm',)), ('C', ('stem', 2)), ('C', ('stem', 1)), ('C', ('head', 2)),)),
    ('stem0', (('D', ('stem', 2, None)), ('D', ('stem', 0, None)), ('C', ('ch', 2)), ('C', ('ch', 0)),
        ('D', ('stem', 1, None)), ('C', ('ch', 1)), ('D', ('ch', 2, 0)), ('D', ('ch', 2, 1)), ('E', ('stem', 2, None)),
        ('E', ('stem', 0, None)), ('E', ('stem', 1, None)), ('D', ('ch', 0, 0)), ('D', ('ch', 0, 1)), ('D', ('ch', 1, 0)),
        ('D', ('ch', 1, 1)), ('F', ('stem', 0, None)), ('F', ('stem', 1, None)), ('E', ('ch', 2, 0)), ('E', ('ch', 2, 1)),
        ('E', ('ch', 0, 0)), ('E', ('ch', 1, 0)), ('F', ('stem', 2, None)), ('F', ('ch', 2, 0)),)),
    ('stem1', (('F', ('ch', 2, 1)), ('E', ('ch', 0, 1)), ('E', ('ch', 1, 1)), ('D', ('ch', 0, 2)), ('D', ('ch', 1, 2)),
        ('D', ('ch', 2, 2)), ('D', ('ch', 0, 3)), ('D', ('ch', 1, 3)), ('D', ('ch', 2, 3)),)),
    ('stem3', (('F', ('ch', 0, 0)),)),
    ('tok0_0', (('F', ('ch', 1, 0)),)),
    ('tok0_3', (('F', ('ch', 0, 1)),)),
    ('tok0_4', (('F', ('ch', 1, 1)),)),
    ('tok0_5', (('E', ('ch', 2, 2)),)),
    ('ch0_0', (('E', ('ch', 2, 3)), ('E', ('ch', 0, 2)), ('E', ('ch', 1, 2)), ('F', ('ch', 2, 2)),)),
    ('ch0_3', (('F', ('ch', 2, 3)),)),
    ('ch0_5', (('E', ('ch', 0, 3)), ('E', ('ch', 1, 3)), ('D', ('head', 2, None)),)),
    ('ch0_7', (('F', ('ch', 0, 2)), ('F', ('ch', 1, 2)),)),
    ('tok1_2', (('F', ('ch', 0, 3)),)),
    ('tok1_3', (('F', ('ch', 1, 3)), ('E', ('head', 2, None)),)),
    ('ln1', (('F', ('head', 2, None)),)),
)


class Net:
    def __init__(self, send_sems, recv_sems):
        self.send_sems, self.recv_sems, self.names, self.builds, self.done = send_sems, recv_sems, {}, [], set()

    def copy(self, name):
        n = self.names[name]
        src, dst, target = self.builds[n]()
        return pltpu.make_async_remote_copy(src_ref=src, dst_ref=dst, send_sem=self.send_sems.at[n],
                                            recv_sem=self.recv_sems.at[n], device_id=target, device_id_type=MESH)

    def start(self, name, build):
        self.names[name] = len(self.builds)
        self.builds.append(build)
        self.copy(name).start()

    def arrived(self, *names):
        for name in names:
            self.copy(name).wait_recv()

    def finish(self):
        for name in self.names:
            if name not in self.done:
                self.copy(name).wait_send()


def core_first(size, cols, each):
    half = cols // 2
    row = lax.broadcasted_iota(jnp.int32, (size, size), 0)
    col = lax.broadcasted_iota(jnp.int32, (size, size), 1)
    source = col % half // each * (2 * each) + col // half * each + col % each
    return jnp.where(row == source, 1.0, 0.0).astype(bf16)


def three_parts(x):
    hi = x.astype(bf16)
    rest = x - hi.astype(f32)
    mid = rest.astype(bf16)
    return hi, mid, (rest - mid.astype(f32)).astype(bf16)


def with_bias_rows(a):
    row = lax.broadcasted_iota(jnp.int32, (TPAD, 1), 0)
    return jnp.where(row < TOK, a, jnp.where(row < TOK + 3, 1.0, 0.0)).astype(bf16)


def front_kernel(labels, patches, w_stem, w_ch1, w_ch2, w_head, w_tok1, w_tok2, b_tok1, b_ch1, b_head, b_stem, ln1_g, ln1_b,
                 ln2_g, ln2_b, b_ch2, lnf_g, lnf_b,
                 wc, pat_out, xin, xmid, vout, pre_out, act_out, hl, hr, dx0, hstat, gbh, vec, wt,
                 pc, ps, ph, tk_f, tk_p, sm_p, bh_p, ws, wh, tk_v, sm_v, sm_2, bh_v, bch1,
                 turn, p_v, pk_v, x_v, v_v, w1_v, w2_v, pre_v, act_v, g_v,
                 send_sems, recv_sems, sem, sem_w, sem_o, sem_x):
    me = my_place()
    other = moved(me, 'k', 1)
    load_p = pltpu.make_async_copy(patches.at[:, pl.ds(pl.multiple_of(me['x'] * IMG, IMG), IMG)], p_v, sem.at[0])
    load_p.start()

    barrier = pltpu.get_barrier_semaphore()
    for dim in 'xyz':
        for step in (1, 2, 3):
            pl.semaphore_signal(barrier, inc=1, device_id=device(moved(me, dim, step)), device_id_type=MESH)
    pl.semaphore_signal(barrier, inc=1, device_id=device(other), device_id_type=MESH)

    stem = dot_nn(w_stem[...].astype(bf16), core_first(256, 256, 32)).astype(bf16)
    ps[0], ps[1] = stem[:, 0:128], stem[:, 128:256]
    pick = core_first(1024, 1024, 32)
    for l in range(2):
        pc[2 * l] = dot_nn(w_ch1[l].astype(bf16), pick).astype(bf16)
        pc[2 * l + 1] = dot_nn(w_ch2[l].astype(bf16), pick).astype(bf16)
    ph[...] = jnp.zeros_like(ph)
    ph[:, pl.ds(0, 250)] = w_head[...].astype(bf16)
    turn[...] = jnp.zeros_like(turn)
    for n, ref in ((0, b_stem), (11, lnf_g), (12, lnf_b)):
        turn[n, pl.ds(0, 8)] = ref[...]
    for n, ref in enumerate((ln1_g, ln1_b, ln2_g, ln2_b, b_ch2)):
        for l in range(2):
            turn[pl.ds(1 + 5 * l + n, 1), pl.ds(0, 8)] = ref[pl.ds(l, 1), :]
    turn[pl.ds(16, 2), pl.ds(0, 16)] = b_tok1[...]
    turned = turn[...].T
    tk_f[...] = jnp.zeros_like(tk_f)
    for l in range(2):
        tk_f[l, :, pl.ds(0, TOK)] = w_tok1[l]
        tk_f[2 + l, :, pl.ds(0, TOK)] = w_tok2[l]
        for n, part in enumerate(three_parts(turned[0:16, 16 + l:17 + l])):
            tk_f[l, :, pl.ds(TOK + n, 1)] = part.astype(f32)
    tk_p[...] = tk_f[...].astype(bf16)
    sm_p[...] = jnp.zeros_like(sm_p)
    sm_p[:, pl.ds(0, 16)] = turned[0:8, 0:16]
    sm_p[pl.ds(0, 2), pl.ds(32, 32)] = b_ch1[...]
    bh_p[...] = jnp.full_like(bh_p, -1e30)
    bh_p[0, pl.ds(0, 250)] = b_head[...]

    net = Net(send_sems, recv_sems)
    core = me['k']
    ring = {d: [moved(me, d, n)[d] for n in range(4)] for d in 'xyz'}
    columns = [pl.ds(pl.multiple_of(x * 256, 256), 256) for x in ring['x']]
    stem_columns = [pl.ds(pl.multiple_of(x * 128, 128), 128) for x in ring['x']]
    peers = {(d, n): device(moved(me, d, n)) for d in 'xyz' for n in (1, 2, 3)}
    partner = device(other)
    here = {'x': 0, 'y': 0, 'z': 0}

    def view(unit, block, half=None):
        kind, colour = unit[:2]
        x, z, y = (EVERY if block[d] is None else ring[d][block[d]] for d in 'xzy')
        r0, rn = (0, 32) if half is None else (16 * half, 16)
        if kind == 'ch':
            c0, cn = COLS[colour]
            g = EVERY if len(unit) == 2 else unit[2]
            return wc.at[g, x, core, z, y, pl.ds(r0, rn), pl.ds(c0, cn)]
        if kind == 'stem':
            cols = pl.ds(0, 512) if x is EVERY else stem_columns[block['x']]
            return ws.at[:, z, y, core, pl.ds(32 * colour + r0, rn), cols]
        cols = pl.ds(0, CH) if x is EVERY else columns[block['x']]
        return wh.at[core, z, y, pl.ds(r0, rn), cols]

    def piece(unit):
        kind, colour = unit
        if kind == 'ch':
            return pc.at[:, :, pl.ds(*COLS[colour])]
        return ps.at[:, pl.ds(32 * colour, 32), :] if kind == 'stem' else ph.at[:, :]

    def exchange(unit, tag, dim, block):
        for side, step in (('l', 1), ('r', 3)):
            def build(step=step):
                part = view(unit, block)
                return (piece(unit) if tag == '1' else part), part, peers[dim, step]
            net.start((unit, tag, side), build)

    def forward_half(unit, tag, dim, block):
        for half, (origin, target, side) in enumerate(((3, 1, 'l'), (1, 3, 'r'))):
            def build(half=half, origin=origin, target=target):
                part = view(unit, {**block, dim: origin}, half)
                return part, part, peers[dim, target]
            net.start((unit, tag, side), build)

    def swap(unit, tag, block):
        def build():
            part = view(unit, block)
            return part, part, partner
        net.start((unit, tag), build)

    own = pltpu.make_async_copy(pc, wc.at[:, me['x'], me['k'], me['z'], me['y']], sem.at[1])
    own.start()
    mine = pl.ds(pl.multiple_of(me['x'] * 256, 256), 256)
    for n in range(2):
        ws[n, me['z'], me['y'], me['k'], :, stem_columns[0]] = ps[n]
    wh[me['k'], me['z'], me['y'], :, mine] = ph[...]
    sm_v[me['x'], me['z'], me['y'], me['k']] = sm_p[...]
    tk_v[:, me['z'], me['y'], me['k']] = tk_p[...]
    bh_v[:, mine] = bh_p[...]
    own.wait()
    pl.semaphore_wait(barrier, 10)

    def small(kind, n):
        dims = 'xyz' if kind == 'sm' else 'yz'
        at = {d: EVERY if d in dims[:n] else ring[d][0] for d in 'xyz'}

        def part():
            if kind == 'sm':
                return sm_v.at[at['x'], at['z'], at['y'], core]
            return tk_v.at[:, at['z'], at['y'], core]
        if n > 0:
            net.arrived(*[(kind, n - 1, s) for s in (1, 2, 3)])
        if n < len(dims):
            for s in (1, 2, 3):
                net.start((kind, n, s), lambda s=s: (part(), part(), peers[dims[n], s]))
            if kind == 'sm' and n == 0:
                def head_bias():
                    return bh_v.at[:, columns[0]]
                for s in (1, 2, 3):
                    net.start(('bh', s), lambda s=s: (head_bias(), head_bias(), peers['x', s]))
        else:
            net.start((kind, 'k'), lambda: (part(), part(), partner))

    def step(name, unit):
        if name[0] == 'M':
            small(unit[0], int(name[1]))
            return
        d1, d2, d3 = ORDERS[unit[1]]
        early = unit[:2]
        plane = {**here, d1: None, d2: None}
        if name == 'A0':
            exchange(unit, '1', d1, here)
        elif name == 'A':
            net.arrived((unit, '1', 'l'), (unit, '1', 'r'))
            forward_half(unit, '1h', d1, here)
        elif name == 'B':
            net.arrived((unit, '1h', 'l'), (unit, '1h', 'r'))
            exchange(unit, '2', d2, {**here, d1: None})
        elif name == 'C':
            net.arrived((unit, '2', 'l'), (unit, '2', 'r'))
            forward_half(unit, '2h', d2, {**here, d1: None})
        elif name == 'D':
            if early not in planes:
                planes.add(early)
                net.arrived((early, '2h', 'l'), (early, '2h', 'r'))
            exchange(unit, '3', d3, plane)
            swap(unit, 'k0', plane)
        elif name == 'E':
            net.arrived((unit, '3', 'l'), (unit, '3', 'r'))
            forward_half(unit, '3h', d3, plane)
            for n in (1, 3):
                swap(unit, f'k{n}', {**plane, d3: n})
        else:
            net.arrived((unit, '3h', 'l'), (unit, '3h', 'r'))
            swap(unit, 'k2', {**plane, d3: 2})

    planes = set()
    awaited = set()

    def need(group):
        for u in LATE:
            if UNIT_GROUP[u[0], u[2]] <= group and u not in awaited:
                awaited.add(u)
                net.arrived(*[(u, f'k{n}') for n in range(4)])

    bursts = {name: steps for name, steps in FRONT_ORDER}

    def burst(name):
        for s in bursts.get(name, ()):
            step(*s)

    def during(name, count):
        def run(i):
            for n in range(1, count):
                if bursts.get(f'{name}{n}'):
                    pl.when(i == n)(functools.partial(burst, f'{name}{n}'))
        return run

    burst('prep')
    load_p.wait()
    pick = core_first(768, 768, 96)
    for g in range(4):
        part = dot_nn(p_v[:, :, pl.ds(768 * g, 768)].reshape(ROWS, 768), pick).astype(bf16)
        for n in range(2):
            pk_v[n, :, pl.ds(384 * g, 384)] = part[:, 384 * n:384 * n + 384]
    keep_p = pltpu.make_async_copy(pk_v, pat_out, sem.at[0])
    keep_p.start()

    burst('unpack')
    net.arrived(('sm', 'k'), ('tk', 'k'), ('bh', 1), ('bh', 2), ('bh', 3))
    sm_2[...] = sm_v[...].reshape(1024, 128)
    for n in range(8):
        tile = jnp.concatenate([sm_2[pl.ds((n % 4 * 4 + i) * 64 + n // 4 * 32, 32), :] for i in range(4)], axis=0)
        vec[:, pl.ds(128 * n, 128)] = tile.T[0:16, :]
    wt[...] = tk_v[...].reshape(4, TOKH, 128)
    for l in range(2):
        rows = jnp.concatenate(three_parts(sm_2[pl.ds(l, 128, stride=8), :]), axis=0)

        @pl.loop(0, 8)
        def _(n):
            lane = lax.broadcasted_iota(jnp.int32, (128, 512), 0)
            col = lax.broadcasted_iota(jnp.int32, (128, 512), 1)
            pick = jnp.where(lane == 32 + col % 32, 1.0, 0.0).astype(bf16)
            spread = dot_nn(rows, pick)
            value = spread[0:128] + spread[128:256] + spread[256:384]
            mine = lane == n // 2 * 32 + col // 32 * 2 + n % 2
            bch1[l:l + 1, pl.ds(pl.multiple_of(n * 512, 512), 512)] = jnp.sum(jnp.where(mine, value, 0.0), axis=0, keepdims=True)

    burst('stem0')
    need(0)
    run = during('stem', 4)
    put(x_v, pl.ds(ROWS, XROWS - ROWS), jnp.zeros((XROWS - ROWS, CH), f32))

    @pl.loop(0, 4)
    def _(i):
        run(i)
        cols = pl.ds(pl.multiple_of(i * 256, 256), 256)
        w = ws[i // 2, :, :, :, :, pl.ds(pl.multiple_of(i % 2 * 256, 256), 256)].reshape(3072, 256)
        value = dot_nn(p_v[...].reshape(ROWS, 3072), w) + vec[0:1, cols]
        for n in range(2):
            x_v[2 * i + n, pl.ds(0, ROWS), :] = value[:, 128 * n:128 * (n + 1)]

    wc_all = wc

    def add_rows(value):
        for n in range(CH // 128):
            x_v[n, pl.ds(0, ROWS), :] += value[:, 128 * n:128 * (n + 1)]

    for l in range(2):
        r = 1 + 5 * l
        burst(f'tok{l}_0')
        run = during(f'tok{l}_', IMG)
        save_in = pltpu.make_async_copy(x_v.at[:, pl.ds(0, ROWS)], xin.at[l], sem_x.at[0])
        save_in.start()
        save_in.wait()

        @pl.loop(0, IMG)
        def _(b):
            run(b)
            x = get(x_v, image(b))
            std, _ = standardize(x)
            a = with_bias_rows(std * vec[r:r + 1, :] + vec[r + 1:r + 2, :])
            g_v[...] = gelu(dot_nn(wt[l, :, 0:TPAD], a)).astype(bf16)
            put(x_v, image(b), x + dot_tn(wt[2 + l, :, 0:TPAD], g_v[...]))
        save_mid = pltpu.make_async_copy(x_v.at[:, pl.ds(0, ROWS)], xmid.at[l], sem_x.at[0])
        save_mid.start()
        burst(f'ln{l}')

        for at, size in CHUNKS:
            std, _ = standardize(get(x_v, pl.ds(at, size)))
            v_v[pl.ds(at, size), :] = (std * vec[r + 2:r + 3, :] + vec[r + 3:r + 4, :]).astype(bf16)
        save_v = [pltpu.make_async_copy(v_v.at[:, pl.ds(512 * n, 512)], vout.at[l, n], sem_x.at[1 + n]) for n in range(2)]
        for copy in save_v:
            copy.start()
        burst(f'ch{l}_0')
        need(2 + 2 * l)
        save_mid.wait()

        def blocks(i, slot):
            t, h = i // 2, i % 2
            part = pl.ds(pl.multiple_of(h * BLK, BLK), BLK)
            return [(wc_all.at[2 * l, t, :, :, :, :, part], w1_v.at[slot]), (wc_all.at[2 * l + 1, t, h], w2_v.at[slot])]

        def outs(i, slot):
            part = pl.ds(pl.multiple_of(i * BLK, BLK), BLK)
            half = pl.ds(pl.multiple_of(i // 2 * BLK, BLK), BLK)
            return [(pre_v.at[slot], pre_out.at[l, :, part]), (act_v.at[slot], act_out.at[l, i % 2, :, half])]
        run = during(f'ch{l}_', NBLK)

        def channel(i, slot):
            run(i)
            part = pl.ds(pl.multiple_of(i * BLK, BLK), BLK)
            h = dot_nn(v_v[...], w1_v[slot].reshape(CH, BLK)) + bch1[l:l + 1, part]
            pre_v[slot] = h
            act_v[slot] = gelu(h).astype(bf16)
            add_rows(dot_nn(act_v[slot], w2_v[slot].reshape(BLK, CH)))
        for_blocks(Stream(sem_w, blocks, NBLK), channel, Stream(sem_o, outs, NBLK))
        add_rows(jnp.broadcast_to(vec[r + 4:r + 5, :], (ROWS, CH)))
        for copy in save_v:
            copy.wait()

    burst('head')
    need(5)
    keep_p.wait()
    last = 11
    pooled = jnp.sum(get(x_v, pl.ds(0, ROWS)).reshape(TOK, IMG, CH), axis=0) * (1.0 / TOK)
    std, inv = standardize(pooled)
    head_in = (std * vec[last:last + 1, :] + vec[last + 1:last + 2, :]).astype(bf16)
    hl[...] = head_in
    w_h = wh[...].reshape(CH, CH)
    logits = dot_nn(head_in, w_h) + bh_v[0:1, :]
    row = lax.broadcasted_iota(jnp.int32, (IMG, 1), 0)
    label = jnp.zeros((IMG, 1), jnp.int32)
    for b in range(IMG):
        value = labels[me['x'] * IMG + b]
        label = jnp.where(row == b, value, label)
    label = label + 6 * sum(jnp.where(label >= edge, 1, 0) for edge in (250, 500, 750))
    is_label = lax.broadcasted_iota(jnp.int32, logits.shape, 1) == label
    top = jnp.max(logits, axis=-1, keepdims=True)
    ex = jnp.exp(logits - top)
    es = jnp.sum(ex, axis=-1, keepdims=True)
    nll = top + jnp.log(es) - jnp.sum(jnp.where(is_label, logits, 0.0), axis=-1, keepdims=True)
    d_logits = (ex / es - jnp.where(is_label, 1.0, 0.0)) * (1.0 / 1024)
    gbh[...] = jnp.sum(d_logits, axis=0, keepdims=True)
    d_bf = d_logits.astype(bf16)
    hr[...] = d_bf
    d_in = dot_nt(d_bf, w_h)
    hstat[0:1, :] = jnp.sum(d_in * std, axis=0, keepdims=True)
    hstat[1:2, :] = jnp.sum(d_in, axis=0, keepdims=True)
    hstat[2:3, :] = jnp.broadcast_to(jnp.sum(nll, axis=0, keepdims=True), (1, CH))
    dx0[...] = norm_grad(d_in, vec[last:last + 1, :], std, inv) * (1.0 / TOK)
    burst('end')
    net.finish()
    assert len(net.builds) <= FRONT_COPIES, len(net.builds)


def front(*operands):
    a, v = pl.BlockSpec(memory_space=pl.ANY), pl.BlockSpec(memory_space=pltpu.VMEM)
    S, V, DMA = jax.ShapeDtypeStruct, pltpu.VMEM, pltpu.SemaphoreType.DMA
    return pl.pallas_call(
        front_kernel, name='front',
        in_specs=[pl.BlockSpec(memory_space=pltpu.SMEM), a] + [v] * 17,
        out_specs=[a] * 7 + [v] * 7,
        out_shape=[S((N_CH, 4, 2, 4, 4, 32, 1024), bf16), S((2, ROWS, 1536), bf16), S((2, CH // 128, ROWS, 128), f32),
                   S((2, CH // 128, ROWS, 128), f32),
                   S((2, 2, ROWS, 512), bf16), S((2, ROWS, CHH), f32), S((2, 2, ROWS, 2048), bf16), S((IMG, CH), bf16),
                   S((IMG, CH), bf16), S((IMG, CH), f32), S((8, CH), f32), S((1, CH), f32), S((16, CH), f32),
                   S((4, TOKH, 128), bf16)],
        scratch_shapes=[V((N_CH, 32, 1024), bf16), V((2, 96, 128), bf16), V((32, 256), bf16), V((4, 16, 128), f32),
                        V((4, 16, 128), bf16), V((8, 128), f32), V((8, 256), f32), V((2, 4, 4, 2, 96, 512), bf16),
                        V((2, 4, 4, 32, CH), bf16), V((4, 4, 4, 2, 16, 128), bf16), V((4, 4, 4, 2, 8, 128), f32),
                        V((1024, 128), f32), V((8, CH), f32), V((2, CHH), f32),
                        V((128, 128), f32), V((TOK, IMG, 3072), bf16), V((2, ROWS, 1536), bf16), V((CH // 128, XROWS, 128), f32),
                        V((ROWS, CH), bf16), V((2, 2, 4, 4, 32, BLK), bf16), V((2, 4, 4, 32, CH), bf16),
                        V((2, ROWS, BLK), f32), V((2, ROWS, BLK), bf16), V((TOKH, CH), bf16),
                        DMA((FRONT_COPIES,)), DMA((FRONT_COPIES,)), DMA((2,)), DMA((2, 2)), DMA((2, 2)), DMA((3,))],
        compiler_params=pltpu.CompilerParams(collective_id=0, has_side_effects=True, vmem_limit_bytes=62 * 1024 * 1024),
        cost_estimate=pl.CostEstimate(flops=90_000_000_000, bytes_accessed=180_000_000, transcendentals=0),
    )(*operands)


TOK_CUTS = 4
GROUPS = (HEAD, 3, 2, 1, 0, STEM)
UNITS = tuple((g, c) for g in GROUPS for c in (2, 0, 1) if g != HEAD or c == 2)
BACK_COPIES = 18 * len(UNITS) + 40
NEEDS = {3: ('act1', 'dout1'), 2: ('vin1', 'dpre1'), 1: ('act0', 'dout0'), 0: ('vin0', 'dpre0'), STEM: ('pat', 'dres'),
         HEAD: ('hl', 'hr')}
BACK_ORDER = (
    ('c1_7', ((3, 'L'), (0, 0), (0, 1),)),
    ('l1', ((1, 0), (1, 1),)),
    ('t1_0', ((0, 2),)),
    ('t1_3', ((1, 2),)),
    ('t1_4', ((0, 3), (2, 0), (2, 1), (0, 4),)),
    ('t1_7', ((2, 2),)),
    ('c0_0', ((0, 5), (1, 3), (3, 0), (2, 'L'), (3, 1), (0, 6), (2, 3), (1, 4),)),
    ('c0_1', ((4, 0), (4, 1), (1, 5),)),
    ('c0_2', ((3, 2),)),
    ('c0_4', ((4, 2), (0, 7),)),
    ('c0_5', ((2, 4),)),
    ('c0_6', ((1, 6),)),
    ('c0_7', ((4, 3), (5, 0), (5, 1), (1, 7), (2, 5), (3, 3), (4, 4), (6, 0), (1, 'L'), (6, 1), (2, 6), (3, 4),)),
    ('l0', ((5, 2),)),
    ('t0_0', ((2, 7), (3, 5),)),
    ('t0_1', ((6, 2), (4, 5),)),
    ('t0_3', ((3, 6), (5, 3), (7, 0), (7, 1), (3, 7), (4, 6), (6, 3), (5, 4), (8, 0), (8, 1), (4, 7), (5, 5), (7, 2),)),
    ('t0_5', ((5, 6), (6, 4),)),
    ('t0_6', ((8, 2), (5, 7), (7, 3), (9, 0), (0, 'L'), (9, 1), (6, 5),)),
    ('t0_7', ((8, 3), (7, 4), (10, 0), (10, 1), (6, 6),)),
    ('fin', ((9, 2), (6, 7), (7, 5),)),
    ('end', ((11, 0), (10, 2), (11, 1), (8, 4), (12, 0), (4, 'L'), (12, 1), (7, 6), (8, 5), (9, 3), (10, 3), (13, 0),
        (11, 2), (12, 2), (13, 1), (7, 7), (8, 6), (9, 4), (10, 4), (14, 0), (14, 1), (15, 0), (15, 1), (13, 2), (11, 3),
        (10, 5), (8, 7), (9, 5), (15, 2), (14, 2), (12, 3), (13, 3), (9, 6), (11, 4), (12, 4), (10, 6), (13, 4), (9, 7),
        (12, 5), (15, 3), (11, 5), (10, 7), (14, 3), (13, 5), (12, 6), (15, 4), (14, 4), (11, 6), (13, 6), (12, 7), (15, 5),
        (11, 7), (14, 5), (13, 7), (15, 6), (14, 6), (15, 7), (14, 7),)),
)
SMALL = dict(sm=((4, 4, 4, 8, 128), (3, 4, 4, 8, 128), (3, 4, 8, 128), (3, 8, 128)),
             tk=((4, 4, 4, 16, 128), (3, 4, 4, 16, 128), (3, 4, 16, 128), (3, 4, 16, 128)))


def reduce_scratch():
    per = []
    for c in range(3):
        n = COLS[c][1]
        many = sum(1 for u in UNITS if u[1] == c)
        lead = ((4, 4), (4,), ())
        b = {'C': pltpu.VMEM((2, 4, 4, 4, 32, n), bf16), 'S1': pltpu.VMEM((4, 4, 32, n), f32), 'S2': pltpu.VMEM((2, 4, 32, n), f32)}
        for ph in range(3):
            if ph:
                b[f'opp{ph}'] = pltpu.VMEM(lead[ph] + (32, n), bf16)
                b[f'pr{ph}'] = pltpu.VMEM(lead[ph] + (16, n), bf16)
                b[f'pl{ph}'] = pltpu.VMEM(lead[ph] + (16, n), bf16)
            for name in ('rig', 'lef'):
                b[f'{name}{ph}'] = pltpu.VMEM(lead[ph] + (16, n), bf16)
            for name in ('half0', 'half1'):
                b[f'{name}{ph}'] = pltpu.VMEM((many,) + lead[ph] + (16, n), bf16)
            for name in ('froml', 'fromr'):
                b[f'{name}{ph}'] = pltpu.VMEM((many,) + lead[ph] + (32, n), bf16)
        per.append(b)
    return per


def small_scratch():
    b = {f'{kind}{n + 1}': pltpu.VMEM(shape, f32) for kind, shapes in SMALL.items() for n, shape in enumerate(shapes)}
    b.update(sm=pltpu.VMEM((4, 4, 4, 2, 8, 128), f32), tk=pltpu.VMEM((4, 4, 4, 2, 16, 128), f32),
             sm_s1=pltpu.VMEM((4, 4, 8, 128), f32), sm_s2=pltpu.VMEM((4, 8, 128), f32),
             tk_s1=pltpu.VMEM((4, 4, 16, 128), f32), tk_s2=pltpu.VMEM((4, 16, 128), f32))
    return b


def small_pack(b, flat, turn, gvec, hstat, gbch1, gbh):
    for n in range(8):
        cols = pl.ds(128 * n, 128)
        turn[n, pl.ds(0, 128), :] = jnp.zeros((128, 128), f32)
        turn[n, pl.ds(0, 16), :] = gvec[:, cols]
        turn[n, pl.ds(11, 2), :] = hstat[pl.ds(0, 2), cols]
    for n in range(8):
        tile = turn[n, pl.ds(0, 128), :].T
        for i in range(4):
            a = n % 4 * 4 + i
            flat[a // 2, pl.ds(a % 2 * 64 + n // 4 * 32, 32), :] = tile[32 * i:32 * i + 32]
    for l in range(2):
        def gather(n, total):
            lane = lax.broadcasted_iota(jnp.int32, (128, 512), 0)
            col = lax.broadcasted_iota(jnp.int32, (128, 512), 1)
            sums = gbch1[l:l + 1, pl.ds(pl.multiple_of(512 * n, 512), 512)]
            mine = jnp.where(lane == n // 2 * 32 + col // 32 * 2 + n % 2, sums, 0.0)
            pick = jnp.where(lane == 32 + col % 32, 1.0, 0.0).astype(bf16)
            return total + dot_nt(jnp.concatenate(three_parts(mine), axis=0), pick)
        total = lax.fori_loop(0, 8, gather, jnp.zeros((384, 128), f32))
        total = total[0:128] + total[128:256] + total[256:384]
        for n in range(8):
            flat[n, pl.ds(l, 16, stride=8), :] += total[16 * n:16 * n + 16]
    lane = lax.broadcasted_iota(jnp.int32, (1, 128), 1)
    for t in range(4):
        for q in range(4):
            tile = gbh[0:1, t * 256 + q // 2 * 128:t * 256 + q // 2 * 128 + 128]
            if q % 2 == 0:
                tile = jnp.concatenate([tile[:, 64:], tile[:, :64]], axis=1)
            tile = jnp.where(lane >= 64, tile, 0.0)
            for n in (2 * t, 2 * t + 1):
                flat[n, pl.ds(2 + q, 16, stride=8), :] += tile
    for n in range(8):
        flat[n, pl.ds(6, 16, stride=8), :] += jnp.where(lane == 64, hstat[2:3, 0:128], 0.0)
        b['sm'][n // 2, pl.ds(n % 2 * 2, 2)] = flat[n, pl.ds(0, 128), :].reshape(2, 4, 2, 8, 128)


def back_kernel(*refs):
    xin, xmid, pre_in, wc, act, vin, pat = refs[:7]
    hl, hr, dx0, hstat, gbh, wt, vec = refs[7:14]
    out_c, out_s, out_h, sm_own, tk_own = refs[14:19]
    dpre, dout, dres, x_act, x_vin, x_pat, x_dpre, x_dout, x_dres = refs[19:28]
    (per, b, big, little, x_hl, x_hr, gvec, gbch1, x_v, d_v, dv_v, do_v, w1_v, w2_v, pre_v, dp_v,
     send_sems, recv_sems, load_sems, sem, sem_w, sem_o) = refs[28:]
    me = my_place()
    other = moved(me, 'k', 1)
    k, k2 = me['k'], 1 - me['k']
    barrier = pltpu.get_barrier_semaphore()
    for dim in 'xyz':
        for step in (1, 2, 3):
            pl.semaphore_signal(barrier, inc=1, device_id=device(moved(me, dim, step)), device_id_type=MESH)
    pl.semaphore_signal(barrier, inc=1, device_id=device(other), device_id_type=MESH)
    net = Net(send_sems, recv_sems)
    ring = {d: [moved(me, d, n)[d] for n in range(4)] for d in 'xyz'}
    peers = {(d, n): device(moved(me, d, n)) for d in 'xyz' for n in (1, 2, 3)}
    partner = device(other)
    half_at = pl.ds(pl.multiple_of(k * 512, 512), 512)
    half_to = pl.ds(pl.multiple_of(k2 * 512, 512), 512)
    swaps = {'act1': (act.at[1, k2], x_act.at[1]), 'act0': (act.at[0, k2], x_act.at[0]), 'vin1': (vin.at[1, k2], x_vin.at[1]),
             'vin0': (vin.at[0, k2], x_vin.at[0]), 'pat': (pat.at[k2], x_pat), 'dpre1': (dpre.at[1], x_dpre.at[1]),
             'dpre0': (dpre.at[0], x_dpre.at[0]), 'dout1': (dout.at[1], x_dout.at[1]), 'dout0': (dout.at[0], x_dout.at[0]),
             'dres': (dres, x_dres), 'hl': (hl.at[:, half_to], x_hl), 'hr': (hr, x_hr)}

    def swap(*names):
        for name in names:
            net.start(name, lambda name=name: (*swaps[name], partner))
    busy = {}

    def free(key):
        for name in busy.pop(key, ()):
            net.copy(name).wait_send()
            net.done.add(name)

    def loads(g):
        l = g // 2
        if g == STEM:
            wide, tall = (pat.at[k], x_pat, 1536), (dres, x_dres, CH)
        elif g % 2:
            wide, tall = (act.at[l, k], x_act.at[l], 2048), (dout.at[l], x_dout.at[l], CH)
        else:
            wide, tall = (dpre.at[l], x_dpre.at[l], CHH), (vin.at[l, k], x_vin.at[l], 512)
        out = []
        for n, (buf, (own, far, cols)) in enumerate(((big, wide), (little, tall))):
            out += [pltpu.make_async_copy(own, buf.at[0, :, pl.ds(0, cols)], load_sems.at[2 * n]),
                    pltpu.make_async_copy(far, buf.at[1, :, pl.ds(0, cols)], load_sems.at[2 * n + 1])]
        return out

    def product(u):
        g, c, slot = u.g, u.c, u.slot
        first = c == 2
        if first and g != HEAD:
            for copy in loads(g):
                copy.wait()
        if g == STEM and not first:
            return
        for v in (units if g == STEM else (u,)):
            if v.g == g:
                free(('C', v.c, v.slot))
        if g == HEAD:
            net.arrived(*NEEDS[g])
            for t in range(4):
                cols = pl.ds(256 * t, 256)
                prod = dot_tn(hl[:, half_at], hr[:, cols]) + dot_tn(x_hl[...], x_hr[:, cols])
                per[c]['C'][slot, t] = prod.astype(bf16).reshape(4, 4, 32, 256)
        elif g == STEM:
            slots = {v.c: v.slot for v in units if v.g == STEM}

            @pl.loop(0, 4)
            def _(z):
                rows = pl.ds(pl.multiple_of(z * 384, 384), 384)
                for t in range(4):
                    def right(s):
                        return jnp.concatenate([little[s, :, 128 * t:128 * t + 128], little[s, :, 512 + 128 * t:640 + 128 * t]], axis=1)
                    prod = dot_tn(big[0, :, rows], right(0)) + dot_tn(big[1, :, rows], right(1))
                    prod = prod.astype(bf16).reshape(4, 3, 32, 256)
                    for d in range(3):
                        per[d]['C'][slots[d], t, z, :, :, pl.ds(0, 256)] = prod[:, d]
        else:
            c0, n = COLS[c]

            @pl.loop(0, 4)
            def _(t):
                for h in range(2):
                    if g % 2:
                        left = pl.ds(pl.multiple_of(t * 512 + h * 256, 256), 256)
                        prod = dot_tn(big[0, :, left], little[0, :, c0:c0 + n]) + dot_tn(big[1, :, left], little[1, :, c0:c0 + n])
                    else:
                        right = pl.ds(pl.multiple_of(t * 1024 + c0, 128), n)
                        rows = slice(256 * h, 256 * h + 256)
                        prod = dot_tn(little[0, :, rows], big[0, :, right]) + dot_tn(little[1, :, rows], big[1, :, right])
                    per[c]['C'][slot, t, 2 * h:2 * h + 2] = prod.astype(bf16).reshape(2, 4, 32, n)

    class Unit:
        def __init__(self, g, c):
            self.g, self.c = g, c
            self.index = [u for u in UNITS if u[1] == c].index((g, c))
            self.slot = self.index % 2
            self.n = COLS[c][1] if g < N_CH else 256
            self.cols = pl.ds(0, self.n)
            self.buf = per[c]
            self.dims = ORDERS[c]
            self.rest = [d for d in 'xzy' if d != self.dims[0]]

        def cut(self, name, *at, rows=slice(None)):
            ref = self.buf[name]
            inner = [slice(None)] * (len(ref.shape) - len(at) - 2)
            return ref.at[(*at, *inner, rows, self.cols)]

        def block(self, p, rows):
            at = {d: EVERY for d in 'xzy'}
            at[self.dims[0]] = p
            return self.buf['C'].at[self.slot, at['x'], at['z'], at['y'], rows, self.cols]

        def share(self, phase, p, e, rows):
            if phase == 0:
                at = dict(zip(self.rest, e))
                at[self.dims[0]] = p
                return self.buf['C'][self.slot, at['x'], at['z'], at['y'], rows, self.cols].astype(f32)
            if phase == 1:
                at = (p, e[0]) if self.dims[1] == self.rest[0] else (e[0], p)
                return self.buf['S1'][(*at, rows, self.cols)]
            return self.buf['S2'][self.slot, p, rows, self.cols]

        def each(self, phase, body):
            if phase == 2:
                body(())
            elif phase == 1:
                pl.loop(0, 4)(lambda i: body((i,)))
            else:
                @pl.loop(0, 4)
                def _(i):
                    pl.loop(0, 4)(lambda j: body((i, j)))

        def send(self, tag, phase, src, dst, step):
            name = (self.g, self.c, tag, phase)
            net.start(name, lambda: (src(), dst(), peers[self.dims[phase], step]))
            return name

        def arrived(self, phase, *tags):
            net.arrived(*[(self.g, self.c, tag, phase) for tag in tags])

        def opposite(self, phase):
            places = ring[self.dims[phase]]
            low, high = pl.ds(0, 16), pl.ds(16, 16)
            if phase == 0:
                sources = [lambda: self.block(places[2], low), lambda: self.block(places[2], high),
                           lambda: self.block(places[1], high), lambda: self.block(places[3], low)]
            else:
                names = (f'opp{phase}', f'pr{phase}', f'pl{phase}')
                for name in names:
                    free((name, self.c))
                opp, right, left = (self.buf[name] for name in names)

                def body(e):
                    opp[(*e, slice(None), self.cols)] = self.share(phase, places[2], e, pl.ds(0, 32)).astype(bf16)
                    right[(*e, slice(None), self.cols)] = self.share(phase, places[1], e, high).astype(bf16)
                    left[(*e, slice(None), self.cols)] = self.share(phase, places[3], e, low).astype(bf16)
                self.each(phase, body)
                sources = [lambda: self.cut(names[0], rows=low), lambda: self.cut(names[0], rows=high),
                           lambda: self.cut(names[1]), lambda: self.cut(names[2])]
            targets = [lambda: self.cut(f'half0{phase}', self.index), lambda: self.cut(f'half1{phase}', self.index),
                       lambda: self.cut(f'froml{phase}', self.index, rows=high),
                       lambda: self.cut(f'fromr{phase}', self.index, rows=low)]
            sent = [self.send(tag, phase, src, dst, step)
                    for tag, src, dst, step in zip(('h0', 'h1', 'p0', 'p1'), sources, targets, (1, 3, 1, 3))]
            if phase == 0:
                busy['C', self.c, self.slot] = sent
            else:
                busy[names[0], self.c] = sent[:2]
                busy[names[1], self.c] = sent[2:3]
                busy[names[2], self.c] = sent[3:]

        def beside(self, phase):
            places = ring[self.dims[phase]]
            for half, step, name, dst in ((0, 1, 'rig', 'froml'), (1, 3, 'lef', 'fromr')):
                self.arrived(phase, f'h{half}')
                key = f'{name}{phase}'
                free((key, self.c))
                out, got = self.buf[key], self.buf[f'half{half}{phase}']
                rows = pl.ds(16 * half, 16)

                def body(e):
                    value = self.share(phase, places[step], e, rows) + got[(self.index, *e, slice(None), self.cols)].astype(f32)
                    out[(*e, slice(None), self.cols)] = value.astype(bf16)
                self.each(phase, body)
                busy[key, self.c] = [self.send(f'f{half}', phase, lambda key=key: self.cut(key),
                                               lambda dst=dst, rows=rows: self.cut(f'{dst}{phase}', self.index, rows=rows), step)]

        def total(self, phase):
            self.arrived(phase, 'p0', 'p1', 'f0', 'f1')
            p = ring[self.dims[phase]][0]

            def body(e):
                got = [self.buf[f'{name}{phase}'][(self.index, *e, slice(None), self.cols)].astype(f32)
                       for name in ('froml', 'fromr')]
                value = self.share(phase, p, e, pl.ds(0, 32)) + got[0] + got[1]
                if phase == 0:
                    self.buf['S1'][(*e, slice(None), self.cols)] = value
                elif phase == 1:
                    self.buf['S2'][(self.slot, *e, slice(None), self.cols)] = value
                elif self.g == STEM:
                    out_s[pl.ds(32 * self.c, 32), :] = value
                elif self.g == HEAD:
                    out_h[...] = value
                else:
                    out_c[self.g, :, pl.ds(*COLS[self.c])] = value
            self.each(phase, body)

        def run(self, stage):
            if stage == 0:
                product(self)
            elif stage == 7:
                self.total(2)
            elif stage % 2 == 0:
                self.beside(stage // 2 - 1)
            else:
                if stage > 1:
                    self.total(stage // 2 - 1)
                self.opposite(stage // 2)

    units = [Unit(g, c) for g, c in UNITS]
    bursts = dict(BACK_ORDER)

    def step(which, stage):
        if stage == 'L':
            net.arrived(*NEEDS[which])
            for copy in loads(which):
                copy.start()
        else:
            units[which].run(stage)

    def burst(name):
        for s in bursts.get(name, ()):
            step(*s)

    def during(name, count):
        def run(i):
            for n in range(1, count):
                if bursts.get(f'{name}{n}'):
                    pl.when(i == n)(functools.partial(burst, f'{name}{n}'))
        return run

    load = pltpu.make_async_copy(xmid.at[1], x_v.at[:, pl.ds(0, ROWS)], sem.at[0])
    load.start()
    mask = row_mask()
    rest = pl.ds(ROWS, XROWS - ROWS)
    put(d_v, rest, jnp.zeros((XROWS - ROWS, CH), f32))
    put(x_v, rest, jnp.zeros((XROWS - ROWS, CH), f32))
    gvec[...] = jnp.zeros_like(gvec)
    tk = b['tk']
    tk[...] = jnp.zeros_like(tk)

    @pl.loop(0, TOK)
    def _(s):
        put(d_v, pl.ds(pl.multiple_of(s * IMG, IMG), IMG), dx0[...])

    def add(row, value):
        gvec[row:row + 1, :] += jnp.sum(value, axis=0, keepdims=True)

    def add_token(n, value, start=0):
        tk[n, :, :, :, :, pl.ds(start, value.shape[1])] += value.reshape(4, 4, 2, 16, value.shape[1])

    for l in (1, 0):
        r = 1 + 5 * l
        for at, size in CHUNKS:
            d = get(d_v, pl.ds(at, size))
            add(r + 4, d)
            do_v[pl.ds(at, size), :] = d.astype(bf16)
        keep = pltpu.make_async_copy(do_v, dout.at[l], sem.at[1])
        keep.start()
        keep.wait()
        if l == 1:
            pl.semaphore_wait(barrier, 10)
            swap('hl', 'hr', 'dout1', 'act1', 'vin1', 'act0', 'vin0', 'pat')
        else:
            swap('dout0')
        burst(f'c{l}_0')
        run = during(f'c{l}_', NBLK)

        def blocks(i, slot):
            t, h = i // 2, i % 2
            part = pl.ds(pl.multiple_of(h * BLK, BLK), BLK)
            whole = pl.ds(pl.multiple_of(i * BLK, BLK), BLK)
            return [(wc.at[2 * l, t, :, :, :, :, part], w1_v.at[slot]), (wc.at[2 * l + 1, t, h], w2_v.at[slot]),
                    (pre_in.at[l, :, whole], pre_v.at[slot])]

        def outs(i, slot):
            return [(dp_v.at[slot], dpre.at[l, :, pl.ds(pl.multiple_of(i * BLK, BLK), BLK)])]

        def channel(i, slot):
            run(i)
            for n in range(2):
                cols = slice(256 * n, 256 * n + 256)
                _, slope = gelu_both(pre_v[slot, :, cols])
                d = dot_nt(do_v[...], w2_v[slot, 2 * n:2 * n + 2].reshape(256, CH)) * slope
                gbch1[l:l + 1, pl.ds(pl.multiple_of(i * BLK + 256 * n, 256), 256)] = jnp.sum(d, axis=0, keepdims=True)
                dp_v[slot, :, cols] = d.astype(bf16)

            @pl.when(i == 0)
            def _():
                dv_v[...] = jnp.zeros_like(dv_v)
            for n in range(2):
                cols = slice(512 * n, 512 * n + 512)
                dv_v[:, cols] += dot_nt(dp_v[slot], w1_v[slot, n].reshape(512, BLK))
        for_blocks(Stream(sem_w, blocks, NBLK), channel, Stream(sem_o, outs, NBLK))
        swap(f'dpre{l}')
        burst(f'l{l}')
        load.wait()

        @pl.loop(0, ROWS // TPAD)
        def _(n):
            rows = pl.ds(pl.multiple_of(n * TPAD, TPAD), TPAD)
            std, inv = standardize(get(x_v, rows))
            d = dv_v[rows, :]
            add(r + 2, d * std)
            add(r + 3, d)
            put(d_v, rows, get(d_v, rows) + norm_grad(d, vec[r + 2:r + 3, :], std, inv))
        load = pltpu.make_async_copy(xin.at[l], x_v.at[:, pl.ds(0, ROWS)], sem.at[0])
        load.start()
        burst(f't{l}_0')
        load.wait()
        run = during(f't{l}_', IMG)

        @pl.loop(0, IMG)
        def _(m):
            run(m)
            std, inv = standardize(get(x_v, image(m)))
            a = with_bias_rows(std * vec[r:r + 1, :] + vec[r + 1:r + 2, :])
            d_mid = get(d_v, image(m))
            dm = d_mid.astype(bf16)
            parts = []
            for n in range(TOK_CUTS):
                cols = slice(CH // TOK_CUTS * n, CH // TOK_CUTS * (n + 1))
                value, slope = gelu_both(dot_nn(wt[l, :, 0:TPAD], a[:, cols]))
                add_token(2 + l, dot_nt(value.astype(bf16), dm[:, cols]))
                dh = dot_nn(wt[2 + l, :, 0:TPAD], dm[:, cols]) * slope
                add_token(l, jnp.sum(dh, axis=-1, keepdims=True), 64)
                dh = dh.astype(bf16)
                add_token(l, dot_nt(dh, a[:, cols]))
                parts.append(dot_tn(wt[l, :, 0:TPAD], dh))
            d = jnp.where(mask, jnp.concatenate(parts, axis=1), 0.0)
            add(r, d * std)
            add(r + 1, d)
            put(d_v, image(m), d_mid + norm_grad(d, vec[r:r + 1, :], std, inv))
        if l == 1:
            load = pltpu.make_async_copy(xmid.at[0], x_v.at[:, pl.ds(0, ROWS)], sem.at[0])
            load.start()
            burst('d0')

    burst('fin')
    for at, size in CHUNKS:
        d = get(d_v, pl.ds(at, size))
        add(0, d)
        do_v[pl.ds(at, size), :] = d.astype(bf16)
    keep = pltpu.make_async_copy(do_v, dres, sem.at[1])
    keep.start()
    keep.wait()
    swap('dres')
    small_pack(b, x_v, d_v, gvec, hstat, gbch1, gbh)

    last = []

    def put_small(name, src, dst, target):
        last.append(name)
        net.start(name, lambda: (src, dst, target))

    def small(n):
        x, z, y = (ring[d][0] for d in 'xzy')
        net.arrived(*last)
        last.clear()
        if n == 0:
            put_small(('sm', 0), b['sm'].at[:, :, :, k2], b['sm1'], partner)
            put_small(('tk', 0), b['tk'].at[:, :, :, k2], b['tk1'], partner)
        elif n == 1:
            b['sm1'][...] += b['sm'][:, :, :, k]
            b['tk1'][...] += b['tk'][:, :, :, k]
            for s in (1, 2, 3):
                put_small(('sm', 1, s), b['sm1'].at[ring['x'][s]], b['sm2'].at[s - 1], peers['x', s])
                put_small(('tk', 1, s), b['tk1'].at[:, ring['z'][s]], b['tk2'].at[s - 1], peers['z', s])
        elif n == 2:
            b['sm_s1'][...] = b['sm1'][x] + b['sm2'][0] + b['sm2'][1] + b['sm2'][2]
            b['tk_s1'][...] = b['tk1'][:, z] + b['tk2'][0] + b['tk2'][1] + b['tk2'][2]
            for s in (1, 2, 3):
                put_small(('sm', 2, s), b['sm_s1'].at[ring['z'][s]], b['sm3'].at[s - 1], peers['z', s])
                put_small(('tk', 2, s), b['tk_s1'].at[:, ring['y'][s]], b['tk3'].at[s - 1], peers['y', s])
        elif n == 3:
            b['sm_s2'][...] = b['sm_s1'][z] + b['sm3'][0] + b['sm3'][1] + b['sm3'][2]
            b['tk_s2'][...] = b['tk_s1'][:, y] + b['tk3'][0] + b['tk3'][1] + b['tk3'][2]
            for s in (1, 2, 3):
                put_small(('sm', 3, s), b['sm_s2'].at[ring['y'][s]], b['sm4'].at[s - 1], peers['y', s])
                put_small(('tk', 3, s), b['tk_s2'], b['tk4'].at[s - 1], peers['x', s])
        else:
            sm_own[...] = b['sm_s2'][y] + b['sm4'][0] + b['sm4'][1] + b['sm4'][2]
            ordered = []
            for place in range(4):
                value = b['tk_s2'][...]
                for s in (1, 2, 3):
                    value = jnp.where(ring['x'][4 - s] == place, b['tk4'][s - 1], value)
                ordered.append(value)
            tk_own[...] = (ordered[0] + ordered[1]) + (ordered[2] + ordered[3])

    tail = bursts.get('end', ())
    small(0)
    for n, s in enumerate(tail):
        step(*s)
        if n in (8, 18, 28, 38):
            small(1 + (8, 18, 28, 38).index(n))
    net.finish()
    assert len(net.builds) <= BACK_COPIES, len(net.builds)


def back(*operands):
    a, v = pl.BlockSpec(memory_space=pl.ANY), pl.BlockSpec(memory_space=pltpu.VMEM)
    S, V, DMA = jax.ShapeDtypeStruct, pltpu.VMEM, pltpu.SemaphoreType.DMA
    return pl.pallas_call(
        back_kernel, name='back',
        in_specs=[a] * 7 + [v] * 7, out_specs=[v] * 5 + [a] * 9,
        out_shape=[S((N_CH, 32, 1024), f32), S((96, 256), f32), S((32, 256), f32), S((8, 128), f32), S((4, 16, 128), f32),
                   S((2, ROWS, CHH), bf16), S((2, ROWS, CH), bf16), S((ROWS, CH), bf16), S((2, ROWS, 2048), bf16),
                   S((2, ROWS, 512), bf16), S((ROWS, 1536), bf16), S((2, ROWS, CHH), bf16), S((2, ROWS, CH), bf16),
                   S((ROWS, CH), bf16)],
        scratch_shapes=[reduce_scratch(), small_scratch(), V((2, ROWS, CHH), bf16), V((2, ROWS, CH), bf16), V((IMG, 512), bf16),
                        V((IMG, CH), bf16), V((16, CH), f32), V((2, CHH), f32), V((CH // 128, XROWS, 128), f32),
                        V((CH // 128, XROWS, 128), f32), V((ROWS, CH), f32), V((ROWS, CH), bf16), V((2, 2, 4, 4, 32, BLK), bf16),
                        V((2, 4, 4, 32, CH), bf16), V((2, ROWS, BLK), f32), V((2, ROWS, BLK), bf16), DMA((BACK_COPIES,)), DMA((BACK_COPIES,)), DMA((4,)), DMA((2,)), DMA((2, 3)),
                        DMA((2, 1))],
        compiler_params=pltpu.CompilerParams(collective_id=1, has_side_effects=True, vmem_limit_bytes=64 * 1024 * 1024 - 65536),
        cost_estimate=pl.CostEstimate(flops=120_000_000_000, bytes_accessed=200_000_000, transcendentals=0),
    )(*operands)


def finish_kernel(c, stem, head, sm, tk, loss, o_stem, o_bstem, o_ln1g, o_ln1b, o_wt1, o_bt1, o_wt2, o_ln2g, o_ln2b, o_ch1,
                  o_bch1, o_ch2, o_bch2, o_lnfg, o_lnfb, o_head, o_bhead):
    def core_last(value, pick):
        got = dot_nt(jnp.concatenate(three_parts(value), axis=0), pick)
        n = value.shape[0]
        return got[0:n] + got[n:2 * n] + got[2 * n:3 * n]
    pick = core_first(1024, 1024, 32)
    for l in range(2):
        o_ch1[l] = core_last(c[2 * l], pick)
        o_ch2[l] = core_last(c[2 * l + 1], pick)
    o_stem[...] = core_last(stem[...], core_first(256, 256, 32))
    o_head[...] = head[:, 0:250]
    own = sm[...]
    turned = jnp.concatenate([own, jnp.zeros((120, 128), f32)], axis=0).T
    for ref, n in ((o_bstem, 0), (o_lnfg, 11), (o_lnfb, 12)):
        ref[...] = turned[n, 0:8]
    for n, ref in enumerate((o_ln1g, o_ln1b, o_ln2g, o_ln2b, o_bch2)):
        for l in range(2):
            ref[pl.ds(l, 1), :] = turned[1 + 5 * l + n:2 + 5 * l + n, 0:8]
    o_bch1[...] = own[0:2, 32:64]
    classes = jnp.concatenate([own[2 + q:3 + q, 64:128] for q in range(4)], axis=1)
    o_bhead[...] = classes[0, 0:250]
    loss[...] = own[6:7, 64:65] * (1.0 / 1024)
    for l in range(2):
        o_wt1[l] = tk[l, :, 0:TOK]
        o_wt2[l] = tk[2 + l, :, 0:TOK]
        tall = jnp.concatenate([tk[l], jnp.zeros((112, 128), f32)], axis=0).T
        o_bt1[pl.ds(l, 1), :] = tall[64:65, 0:16]


def finish(*operands):
    S = jax.ShapeDtypeStruct
    v = pl.BlockSpec(memory_space=pltpu.VMEM)
    return pl.pallas_call(
        finish_kernel, name='finish', in_specs=[v] * 5, out_specs=[v] * 18,
        out_shape=[S((1, 1), f32), S((96, 256), f32), S((8,), f32), S((2, 8), f32), S((2, 8), f32), S((2, 16, TOK), f32),
                   S((2, 16), f32), S((2, 16, TOK), f32), S((2, 8), f32), S((2, 8), f32), S((2, 32, 1024), f32), S((2, 32), f32),
                   S((2, 32, 1024), f32), S((2, 8), f32), S((8,), f32), S((8,), f32), S((32, 250), f32), S((250,), f32)],
    )(*operands)

CHANNEL_AXES = ('tp', 'fsdp')


def weight_specs():
    vec_spec = P(CHANNEL_AXES)
    layer_vec = P(None, CHANNEL_AXES)
    return (P('fsdp', 'tp'), vec_spec, layer_vec, layer_vec, P(None, None, 'fsdp'), P(None, 'fsdp'),
            P(None, 'fsdp', None), layer_vec, layer_vec, P(None, 'fsdp', 'tp'), layer_vec,
            P(None, CHANNEL_AXES, None), layer_vec, vec_spec, vec_spec, P('fsdp', 'tp'), P('tp'))


def solution(mesh):
    def step(patches, labels, w_stem, b_stem, ln1_g, ln1_b, w_tok1, b_tok1, w_tok2,
             ln2_g, ln2_b, w_ch1, b_ch1, w_ch2, b_ch2, lnf_g, lnf_b, w_head, b_head):
        wc, pat, xin, xmid, vin, pre, act, hl, hr, dx0, hstat, gbh, vec, wt = front(
            labels, patches.transpose(1, 0, 2), w_stem, w_ch1, w_ch2, w_head, w_tok1.transpose(0, 2, 1), w_tok2, b_tok1, b_ch1,
            b_head, b_stem, ln1_g, ln1_b, ln2_g, ln2_b, b_ch2, lnf_g, lnf_b)
        sums = back(xin, xmid, pre, wc, act, vin, pat, hl, hr, dx0, hstat, gbh, wt, vec)[:5]
        loss, g_s, g_bs, g_1g, g_1b, g_t1, g_bt, g_t2, g_2g, g_2b, g_c1, g_b1, g_c2, g_b2, g_fg, g_fb, g_h, g_bh = finish(*sums)
        return (loss.reshape(()), g_s, g_bs, g_1g, g_1b, g_t1.transpose(0, 2, 1), g_bt, g_t2, g_2g, g_2b, g_c1, g_b1, g_c2, g_b2,
                g_fg, g_fb, g_h, g_bh)

    specs = weight_specs()
    return jax.shard_map(step, mesh=mesh, in_specs=(P('fsdp', None, None), P('fsdp')) + specs,
                         out_specs=(P(),) + specs, check_vma=False)
```

time: 402 us -> 324 us (0.81)
  Pallas kernels: 360 us -> 318 us
  local copies, waits for them, and re-layouts: 20.3 us -> 0 us
  between operations: 16 us -> 0.97 us
    pallas_call x2, Pallas kernels: 232 us -> 190 us  [the longest x1 186 us: back(): pl.pallas_call(back_kernel, name='back', in_specs=[a] * 7 + [v] * 7, out_...]
    slice x12 -> x0, local copies, waits for them, and re-layouts: 8.97 us -> none  [the longest x8 4.57 us: step(): out.append(tot[o:o + p.size].reshape(p.shape))]
  transfers between devices with their start and end apart: 1 -> 0, of which waited for: 0 -> 0; matrix products, arithmetic and copies ran while one was open for 0% -> 0% of each run, Pallas kernels for 37% -> 0%
where the time goes in v9:
time: 324 us; the launch traced here: 319 us
  Pallas kernels  318 us (98%)
    pallas_call x1, Pallas kernels, back(): pl.pallas_call(back_kernel, name='back', in_specs=[a] * 7 + [v] * 7, out_...  186 us
    pallas_call x1, Pallas kernels, front(): pl.pallas_call(front_kernel, name='front', in_specs=[pl.BlockSpec(memory_...  128 us

profile of v9, /device:TPU:0, one launch (start us, length us, event | category | flops | bytes accessed | tf_op | source)
XLA Modules:
  0.0 319.0 jit_solution(1639969695402287122)
XLA Ops:
  0.7 127.6 %front.1 = (bf16[4,4,2,4,4,32,1024]{6,5,4,3,2,1,0:T(8,128)(2,1)}, bf16[2,392,1536]{2,1,0:T(8,128)(2,1)}, f32[2,8,392,128]{3,2,1,0:T(8,128)}, f32[2,8,392,128]{3,...) custom-call(s32[32]{0:T(128)} %labels.1, ...), custom_call_target="tpu_custom_call" | custom-call | flops 89999998976 | bytes 180000000 | tf_op jit(solution)/shard_map/front/pallas_call | solution.py:544
  128.3 185.8 %back.1 = (f32[4,32,1024]{2,1,0:T(8,128)}, f32[96,256]{1,0:T(8,128)}, f32[32,256]{1,0:T(8,128)}, f32[8,128]{1,0:T(8,128)}, f32[4,16,128]{2,1,0:T(8,128)}, /*inde...) custom-call(f32[2,8,392,128]{3,2,1,0:T(8,128)} %get-tuple-element.55, ...), custom_call_target="tpu_custom_call" | custom-call | flops 120000004096 | bytes 200000000 | tf_op jit(solution)/shard_map/back/pallas_call | solution.py:1088
  314.1 4.6 %finish.1 = (f32[1,1]{1,0:T(1,128)}, f32[96,256]{1,0:T(8,128)}, f32[8]{0:T(128)}, f32[2,8]{1,0:T(2,128)}, f32[2,8]{1,0:T(2,128)}, /*index=5*/f32[2,16,49]{2,1,0:...) custom-call(f32[4,32,1024]{2,1,0:T(8,128)} %get-tuple-element.69.c, ...), custom_call_target="tpu_custom_call" | custom-call | tf_op jit(solution)/shard_map/finish/pallas_call | solution.py:1138

commit v10 on v9

--- a/solution.py
+++ b/solution.py
@@ -53,18 +53,12 @@
     return lax.dot_general(a, b, (((0,), (0,)), ((), ())), preferred_element_type=f32)
 
 
-def gelu(x):
-    half = 0.5 * x
-    return half + half * jnp.tanh(x * (GELU_C + (GELU_C * GELU_A) * (x * x)))
-
-
 def gelu_both(x):
     sq = x * x
-    th = jnp.tanh(x * (GELU_C + (GELU_C * GELU_A) * sq))
-    half = 0.5 * x
-    rise = 0.5 + 0.5 * th
-    slope = (1.0 - th * th) * (GELU_C + (3.0 * GELU_C * GELU_A) * sq)
-    return x * rise, rise + half * slope
+    half = 0.5 * jnp.tanh(x * (GELU_C + (GELU_C * GELU_A) * sq))
+    rise = 0.5 + half
+    value = x * rise
+    return value, rise + value * (0.5 - half) * (2.0 * GELU_C + (6.0 * GELU_C * GELU_A) * sq)
 
 
 def standardize(x):
@@ -138,37 +132,45 @@
         out.wait(n - 1, 1 - n % 2)
 
 
-FRONT_COPIES = 240
-EARLY = [('stem', 0), ('stem', 1), ('stem', 2), ('ch', 0), ('ch', 1), ('ch', 2), ('head', 2)]
+TOK_CUTS = 4
+FRONT_COPIES = 270
+EARLY = [('stem', c) for c in range(3)] + [('ch', c, p) for p in 'ab' for c in range(3)] + [('head', 2)]
+PARTS = {'a': pl.ds(0, 2), 'b': pl.ds(2, 2)}
 LATE = [('stem', c, None) for c in range(3)] + [('ch', c, g) for g in range(N_CH) for c in range(3)] + [('head', 2, None)]
 UNIT_GROUP = {('stem', None): 0, ('ch', 0): 1, ('ch', 1): 2, ('ch', 2): 3, ('ch', 3): 4, ('head', None): 5}
 EVERY = pl.ds(0, 4)
 FRONT_ORDER = (
     ('prep', (('M0', ('sm',)), ('M0', ('tk',)), ('A0', ('stem', 0)), ('A0', ('stem', 1)), ('A0', ('stem', 2)),
-        ('A0', ('ch', 0)), ('A0', ('ch', 1)), ('A0', ('ch', 2)), ('A0', ('head', 2)),)),
+        ('A0', ('ch', 0, 'a')), ('A0', ('ch', 0, 'b')), ('A0', ('ch', 1, 'a')), ('A0', ('ch', 1, 'b')),
+        ('A0', ('ch', 2, 'a')), ('A0', ('ch', 2, 'b')), ('A0', ('head', 2)),)),
     ('unpack', (('M1', ('sm',)), ('M1', ('tk',)), ('A', ('stem', 0)), ('A', ('stem', 1)), ('A', ('stem', 2)),
-        ('A', ('head', 2)), ('A', ('ch', 2)), ('A', ('ch', 0)), ('A', ('ch', 1)), ('B', ('stem', 0)), ('M2', ('sm',)),
-        ('B', ('stem', 1)), ('M2', ('tk',)), ('B', ('stem', 2)), ('B', ('ch', 0)), ('B', ('head', 2)), ('B', ('ch', 1)),
-        ('C', ('stem', 0)), ('B', ('ch', 2)), ('M3', ('sm',)), ('C', ('stem', 2)), ('C', ('stem', 1)), ('C', ('head', 2)),)),
-    ('stem0', (('D', ('stem', 2, None)), ('D', ('stem', 0, None)), ('C', ('ch', 2)), ('C', ('ch', 0)),
-        ('D', ('stem', 1, None)), ('C', ('ch', 1)), ('D', ('ch', 2, 0)), ('D', ('ch', 2, 1)), ('E', ('stem', 2, None)),
-        ('E', ('stem', 0, None)), ('E', ('stem', 1, None)), ('D', ('ch', 0, 0)), ('D', ('ch', 0, 1)), ('D', ('ch', 1, 0)),
-        ('D', ('ch', 1, 1)), ('F', ('stem', 0, None)), ('F', ('stem', 1, None)), ('E', ('ch', 2, 0)), ('E', ('ch', 2, 1)),
-        ('E', ('ch', 0, 0)), ('E', ('ch', 1, 0)), ('F', ('stem', 2, None)), ('F', ('ch', 2, 0)),)),
-    ('stem1', (('F', ('ch', 2, 1)), ('E', ('ch', 0, 1)), ('E', ('ch', 1, 1)), ('D', ('ch', 0, 2)), ('D', ('ch', 1, 2)),
-        ('D', ('ch', 2, 2)), ('D', ('ch', 0, 3)), ('D', ('ch', 1, 3)), ('D', ('ch', 2, 3)),)),
-    ('stem3', (('F', ('ch', 0, 0)),)),
-    ('tok0_0', (('F', ('ch', 1, 0)),)),
+        ('A', ('ch', 0, 'a')), ('A', ('ch', 1, 'a')), ('A', ('ch', 2, 'a')), ('A', ('ch', 0, 'b')), ('A', ('ch', 2, 'b')),
+        ('A', ('head', 2)), ('A', ('ch', 1, 'b')), ('B', ('stem', 0)), ('M2', ('sm',)), ('B', ('stem', 1)),
+        ('B', ('ch', 0, 'a')), ('B', ('ch', 1, 'a')), ('B', ('ch', 0, 'b')), ('B', ('ch', 1, 'b')), ('M2', ('tk',)),
+        ('B', ('stem', 2)), ('B', ('head', 2)), ('C', ('stem', 0)), ('B', ('ch', 2, 'a')), ('B', ('ch', 2, 'b')),
+        ('M3', ('sm',)), ('C', ('stem', 2)), ('C', ('stem', 1)), ('C', ('head', 2)),)),
+    ('stem0', (('D', ('stem', 0, None)), ('C', ('ch', 0, 'a')), ('C', ('ch', 1, 'a')), ('C', ('ch', 2, 'a')),
+        ('D', ('stem', 2, None)), ('D', ('stem', 1, None)), ('D', ('ch', 2, 0)), ('D', ('ch', 2, 1)), ('D', ('ch', 0, 0)),
+        ('D', ('ch', 0, 1)), ('E', ('stem', 0, None)), ('E', ('stem', 2, None)), ('E', ('stem', 1, None)),
+        ('D', ('ch', 1, 0)), ('D', ('ch', 1, 1)), ('F', ('stem', 1, None)), ('E', ('ch', 2, 0)), ('E', ('ch', 0, 0)),
+        ('E', ('ch', 2, 1)), ('F', ('stem', 2, None)), ('C', ('ch', 0, 'b')), ('C', ('ch', 1, 'b')), ('C', ('ch', 2, 'b')),
+        ('D', ('head', 2, None)), ('E', ('ch', 1, 0)), ('F', ('ch', 2, 0)), ('E', ('ch', 0, 1)), ('F', ('stem', 0, None)),
+        ('F', ('ch', 2, 1)), ('D', ('ch', 0, 2)), ('D', ('ch', 0, 3)),)),
+    ('stem1', (('E', ('ch', 1, 1)),)),
+    ('stem2', (('F', ('ch', 0, 0)), ('D', ('ch', 2, 2)), ('D', ('ch', 2, 3)),)),
+    ('tok0_0', (('D', ('ch', 1, 2)), ('D', ('ch', 1, 3)), ('E', ('head', 2, None)),)),
+    ('tok0_1', (('F', ('ch', 1, 0)),)),
     ('tok0_3', (('F', ('ch', 0, 1)),)),
-    ('tok0_4', (('F', ('ch', 1, 1)),)),
-    ('tok0_5', (('E', ('ch', 2, 2)),)),
-    ('ch0_0', (('E', ('ch', 2, 3)), ('E', ('ch', 0, 2)), ('E', ('ch', 1, 2)), ('F', ('ch', 2, 2)),)),
-    ('ch0_3', (('F', ('ch', 2, 3)),)),
-    ('ch0_5', (('E', ('ch', 0, 3)), ('E', ('ch', 1, 3)), ('D', ('head', 2, None)),)),
-    ('ch0_7', (('F', ('ch', 0, 2)), ('F', ('ch', 1, 2)),)),
-    ('tok1_2', (('F', ('ch', 0, 3)),)),
-    ('tok1_3', (('F', ('ch', 1, 3)), ('E', ('head', 2, None)),)),
-    ('ln1', (('F', ('head', 2, None)),)),
+    ('tok0_5', (('F', ('ch', 1, 1)), ('E', ('ch', 2, 2)),)),
+    ('ch0_1', (('E', ('ch', 0, 2)), ('E', ('ch', 2, 3)),)),
+    ('ch0_2', (('E', ('ch', 1, 2)), ('F', ('head', 2, None)),)),
+    ('ch0_4', (('F', ('ch', 2, 2)),)),
+    ('ch0_5', (('E', ('ch', 0, 3)), ('F', ('ch', 2, 3)),)),
+    ('ch0_7', (('E', ('ch', 1, 3)),)),
+    ('tok1_0', (('F', ('ch', 0, 2)),)),
+    ('tok1_1', (('F', ('ch', 1, 2)),)),
+    ('tok1_3', (('F', ('ch', 0, 3)),)),
+    ('tok1_5', (('F', ('ch', 1, 3)),)),
 )
 
 
@@ -219,7 +221,7 @@
 
 def front_kernel(labels, patches, w_stem, w_ch1, w_ch2, w_head, w_tok1, w_tok2, b_tok1, b_ch1, b_head, b_stem, ln1_g, ln1_b,
                  ln2_g, ln2_b, b_ch2, lnf_g, lnf_b,
-                 wc, pat_out, xin, xmid, vout, pre_out, act_out, hl, hr, dx0, hstat, gbh, vec, wt,
+                 wc, pat_out, xin, xmid, vout, pre_out, act_out, hl, hr, dx0, hstat, gbh, vec, wt, wt_t,
                  pc, ps, ph, tk_f, tk_p, sm_p, bh_p, ws, wh, tk_v, sm_v, sm_2, bh_v, bch1,
                  turn, p_v, pk_v, x_v, v_v, w1_v, w2_v, pre_v, act_v, g_v,
                  send_sems, recv_sems, sem, sem_w, sem_o, sem_x):
@@ -278,7 +280,7 @@
         r0, rn = (0, 32) if half is None else (16 * half, 16)
         if kind == 'ch':
             c0, cn = COLS[colour]
-            g = EVERY if len(unit) == 2 else unit[2]
+            g = PARTS.get(unit[2], unit[2])
             return wc.at[g, x, core, z, y, pl.ds(r0, rn), pl.ds(c0, cn)]
         if kind == 'stem':
             cols = pl.ds(0, 512) if x is EVERY else stem_columns[block['x']]
@@ -287,9 +289,9 @@
         return wh.at[core, z, y, pl.ds(r0, rn), cols]
 
     def piece(unit):
-        kind, colour = unit
+        kind, colour = unit[:2]
         if kind == 'ch':
-            return pc.at[:, :, pl.ds(*COLS[colour])]
+            return pc.at[PARTS[unit[2]], :, pl.ds(*COLS[colour])]
         return ps.at[:, pl.ds(32 * colour, 32), :] if kind == 'stem' else ph.at[:, :]
 
     def exchange(unit, tag, dim, block):
@@ -350,7 +352,7 @@
             small(unit[0], int(name[1]))
             return
         d1, d2, d3 = ORDERS[unit[1]]
-        early = unit[:2]
+        early = unit[:2] if unit[0] != 'ch' or unit[2] in PARTS else ('ch', unit[1], 'a' if unit[2] < 2 else 'b')
         plane = {**here, d1: None, d2: None}
         if name == 'A0':
             exchange(unit, '1', d1, here)
@@ -417,6 +419,8 @@
         tile = jnp.concatenate([sm_2[pl.ds((n % 4 * 4 + i) * 64 + n // 4 * 32, 32), :] for i in range(4)], axis=0)
         vec[:, pl.ds(128 * n, 128)] = tile.T[0:16, :]
     wt[...] = tk_v[...].reshape(4, TOKH, 128)
+    for n in range(4):
+        wt_t[n] = wt[n].astype(f32).T[0:TPAD].astype(bf16)
     for l in range(2):
         rows = jnp.concatenate(three_parts(sm_2[pl.ds(l, 128, stride=8), :]), axis=0)
 
@@ -464,8 +468,8 @@
             x = get(x_v, image(b))
             std, _ = standardize(x)
             a = with_bias_rows(std * vec[r:r + 1, :] + vec[r + 1:r + 2, :])
-            g_v[...] = gelu(dot_nn(wt[l, :, 0:TPAD], a)).astype(bf16)
-            put(x_v, image(b), x + dot_tn(wt[2 + l, :, 0:TPAD], g_v[...]))
+            g_v[...] = gelu_both(dot_nn(wt[l, :, 0:TPAD], a))[0].astype(bf16)
+            put(x_v, image(b), x + dot_nn(wt_t[2 + l], g_v[...]))
         save_mid = pltpu.make_async_copy(x_v.at[:, pl.ds(0, ROWS)], xmid.at[l], sem_x.at[0])
         save_mid.start()
         burst(f'ln{l}')
@@ -495,8 +499,8 @@
             run(i)
             part = pl.ds(pl.multiple_of(i * BLK, BLK), BLK)
             h = dot_nn(v_v[...], w1_v[slot].reshape(CH, BLK)) + bch1[l:l + 1, part]
-            pre_v[slot] = h
-            act_v[slot] = gelu(h).astype(bf16)
+            value, pre_v[slot] = gelu_both(h)
+            act_v[slot] = value.astype(bf16)
             add_rows(dot_nn(act_v[slot], w2_v[slot].reshape(BLK, CH)))
         for_blocks(Stream(sem_w, blocks, NBLK), channel, Stream(sem_o, outs, NBLK))
         add_rows(jnp.broadcast_to(vec[r + 4:r + 5, :], (ROWS, CH)))
@@ -544,12 +548,12 @@
     return pl.pallas_call(
         front_kernel, name='front',
         in_specs=[pl.BlockSpec(memory_space=pltpu.SMEM), a] + [v] * 17,
-        out_specs=[a] * 7 + [v] * 7,
+        out_specs=[a] * 7 + [v] * 8,
         out_shape=[S((N_CH, 4, 2, 4, 4, 32, 1024), bf16), S((2, ROWS, 1536), bf16), S((2, CH // 128, ROWS, 128), f32),
                    S((2, CH // 128, ROWS, 128), f32),
                    S((2, 2, ROWS, 512), bf16), S((2, ROWS, CHH), f32), S((2, 2, ROWS, 2048), bf16), S((IMG, CH), bf16),
                    S((IMG, CH), bf16), S((IMG, CH), f32), S((8, CH), f32), S((1, CH), f32), S((16, CH), f32),
-                   S((4, TOKH, 128), bf16)],
+                   S((4, TOKH, 128), bf16), S((4, TPAD, TOKH), bf16)],
         scratch_shapes=[V((N_CH, 32, 1024), bf16), V((2, 96, 128), bf16), V((32, 256), bf16), V((4, 16, 128), f32),
                         V((4, 16, 128), bf16), V((8, 128), f32), V((8, 256), f32), V((2, 4, 4, 2, 96, 512), bf16),
                         V((2, 4, 4, 32, CH), bf16), V((4, 4, 4, 2, 16, 128), bf16), V((4, 4, 4, 2, 8, 128), f32),
@@ -563,39 +567,32 @@
     )(*operands)
 
 
-TOK_CUTS = 4
-GROUPS = (HEAD, 3, 2, 1, 0, STEM)
+GROUPS = (3, 2, 1, HEAD, 0, STEM)
 UNITS = tuple((g, c) for g in GROUPS for c in (2, 0, 1) if g != HEAD or c == 2)
 BACK_COPIES = 18 * len(UNITS) + 40
-NEEDS = {3: ('act1', 'dout1'), 2: ('vin1', 'dpre1'), 1: ('act0', 'dout0'), 0: ('vin0', 'dpre0'), STEM: ('pat', 'dres'),
+NEEDS = {3: ('act1', 'dout1'), 2: ('vin1',), 1: ('act0', 'dout0'), 0: ('vin0',), STEM: ('pat', 'dres'),
          HEAD: ('hl', 'hr')}
 BACK_ORDER = (
-    ('c1_7', ((3, 'L'), (0, 0), (0, 1),)),
-    ('l1', ((1, 0), (1, 1),)),
-    ('t1_0', ((0, 2),)),
-    ('t1_3', ((1, 2),)),
-    ('t1_4', ((0, 3), (2, 0), (2, 1), (0, 4),)),
-    ('t1_7', ((2, 2),)),
-    ('c0_0', ((0, 5), (1, 3), (3, 0), (2, 'L'), (3, 1), (0, 6), (2, 3), (1, 4),)),
-    ('c0_1', ((4, 0), (4, 1), (1, 5),)),
-    ('c0_2', ((3, 2),)),
-    ('c0_4', ((4, 2), (0, 7),)),
-    ('c0_5', ((2, 4),)),
-    ('c0_6', ((1, 6),)),
-    ('c0_7', ((4, 3), (5, 0), (5, 1), (1, 7), (2, 5), (3, 3), (4, 4), (6, 0), (1, 'L'), (6, 1), (2, 6), (3, 4),)),
-    ('l0', ((5, 2),)),
-    ('t0_0', ((2, 7), (3, 5),)),
-    ('t0_1', ((6, 2), (4, 5),)),
-    ('t0_3', ((3, 6), (5, 3), (7, 0), (7, 1), (3, 7), (4, 6), (6, 3), (5, 4), (8, 0), (8, 1), (4, 7), (5, 5), (7, 2),)),
-    ('t0_5', ((5, 6), (6, 4),)),
-    ('t0_6', ((8, 2), (5, 7), (7, 3), (9, 0), (0, 'L'), (9, 1), (6, 5),)),
-    ('t0_7', ((8, 3), (7, 4), (10, 0), (10, 1), (6, 6),)),
-    ('fin', ((9, 2), (6, 7), (7, 5),)),
-    ('end', ((11, 0), (10, 2), (11, 1), (8, 4), (12, 0), (4, 'L'), (12, 1), (7, 6), (8, 5), (9, 3), (10, 3), (13, 0),
-        (11, 2), (12, 2), (13, 1), (7, 7), (8, 6), (9, 4), (10, 4), (14, 0), (14, 1), (15, 0), (15, 1), (13, 2), (11, 3),
-        (10, 5), (8, 7), (9, 5), (15, 2), (14, 2), (12, 3), (13, 3), (9, 6), (11, 4), (12, 4), (10, 6), (13, 4), (9, 7),
-        (12, 5), (15, 3), (11, 5), (10, 7), (14, 3), (13, 5), (12, 6), (15, 4), (14, 4), (11, 6), (13, 6), (12, 7), (15, 5),
-        (11, 7), (14, 5), (13, 7), (15, 6), (14, 6), (15, 7), (14, 7),)),
+    ('c1_7', ((3, 'L'),)),
+    ('t1_7', ((0, 0), (0, 1), (1, 0), (1, 1),)),
+    ('d0', ((0, 2),)),
+    ('c0_3', ((1, 2), (0, 3),)),
+    ('l0', ((1, 3), (0, 4),)),
+    ('t0_1', ((1, 4), (0, 5),)),
+    ('t0_3', ((1, 5), (0, 6),)),
+    ('t0_4', ((2, 0), (2, 'L'), (2, 1), (1, 6), (0, 7),)),
+    ('t0_5', ((3, 0), (3, 1), (1, 7), (4, 0), (4, 1), (2, 2),)),
+    ('t0_6', ((3, 2), (5, 0), (1, 'L'), (5, 1),)),
+    ('t0_7', ((4, 2), (2, 3), (3, 3),)),
+    ('fin', ((6, 0), (6, 1), (5, 2), (2, 4), (7, 0), (7, 1), (4, 3), (3, 4), (8, 0), (0, 'L'), (8, 1), (6, 2), (4, 4),
+        (2, 5), (5, 3), (9, 0), (9, 1), (7, 2),)),
+    ('end', ((8, 2), (5, 4), (3, 5), (6, 3), (2, 6), (10, 0), (10, 1), (9, 2), (11, 0), (11, 1), (6, 4), (4, 5), (7, 3),
+        (5, 5), (2, 7), (12, 0), (4, 'L'), (12, 1), (8, 3), (7, 4), (10, 2), (3, 6), (11, 2), (4, 6), (8, 4), (6, 5),
+        (12, 2), (9, 3), (5, 6), (13, 0), (13, 1), (9, 4), (7, 5), (11, 3), (8, 5), (6, 6), (3, 7), (4, 7), (5, 7), (14, 0),
+        (14, 1), (15, 0), (15, 1), (9, 5), (10, 3), (12, 3), (8, 6), (11, 4), (13, 2), (6, 7), (14, 2), (7, 6), (15, 2),
+        (12, 4), (10, 4), (8, 7), (9, 6), (11, 5), (7, 7), (14, 3), (12, 5), (10, 5), (13, 3), (15, 3), (11, 6), (9, 7),
+        (12, 6), (14, 4), (13, 4), (10, 6), (15, 4), (11, 7), (12, 7), (14, 5), (10, 7), (13, 5), (15, 5), (14, 6), (13, 6),
+        (15, 6), (14, 7), (13, 7), (15, 7),)),
 )
 SMALL = dict(sm=((4, 4, 4, 8, 128), (3, 4, 4, 8, 128), (3, 4, 8, 128), (3, 8, 128)),
              tk=((4, 4, 4, 16, 128), (3, 4, 4, 16, 128), (3, 4, 16, 128), (3, 4, 16, 128)))
@@ -670,11 +667,11 @@
 
 def back_kernel(*refs):
     xin, xmid, pre_in, wc, act, vin, pat = refs[:7]
-    hl, hr, dx0, hstat, gbh, wt, vec = refs[7:14]
-    out_c, out_s, out_h, sm_own, tk_own = refs[14:19]
-    dpre, dout, dres, x_act, x_vin, x_pat, x_dpre, x_dout, x_dres = refs[19:28]
+    hl, hr, dx0, hstat, gbh, wt, wt_t, vec = refs[7:15]
+    out_c, out_s, out_h, sm_own, tk_own = refs[15:20]
+    dpre, dout, dres, x_act, x_vin, x_pat, x_dpre, x_dout, x_dres = refs[20:29]
     (per, b, big, little, x_hl, x_hr, gvec, gbch1, x_v, d_v, dv_v, do_v, w1_v, w2_v, pre_v, dp_v,
-     send_sems, recv_sems, load_sems, sem, sem_w, sem_o) = refs[28:]
+     send_sems, recv_sems, load_sems, sem, sem_w, sem_o, ship_sent, ship_got) = refs[29:]
     me = my_place()
     other = moved(me, 'k', 1)
     k, k2 = me['k'], 1 - me['k']
@@ -690,9 +687,8 @@
     half_at = pl.ds(pl.multiple_of(k * 512, 512), 512)
     half_to = pl.ds(pl.multiple_of(k2 * 512, 512), 512)
     swaps = {'act1': (act.at[1, k2], x_act.at[1]), 'act0': (act.at[0, k2], x_act.at[0]), 'vin1': (vin.at[1, k2], x_vin.at[1]),
-             'vin0': (vin.at[0, k2], x_vin.at[0]), 'pat': (pat.at[k2], x_pat), 'dpre1': (dpre.at[1], x_dpre.at[1]),
-             'dpre0': (dpre.at[0], x_dpre.at[0]), 'dout1': (dout.at[1], x_dout.at[1]), 'dout0': (dout.at[0], x_dout.at[0]),
-             'dres': (dres, x_dres), 'hl': (hl.at[:, half_to], x_hl), 'hr': (hr, x_hr)}
+             'vin0': (vin.at[0, k2], x_vin.at[0]), 'pat': (pat.at[k2], x_pat), 'dout1': (do_v, x_dout.at[1]), 'dout0': (do_v, x_dout.at[0]), 'dres': (do_v, x_dres),
+             'hl': (hl.at[:, half_to], x_hl), 'hr': (hr, x_hr)}
 
     def swap(*names):
         for name in names:
@@ -703,6 +699,15 @@
         for name in busy.pop(key, ()):
             net.copy(name).wait_send()
             net.done.add(name)
+
+    def ship(l, i, slot):
+        part = pl.ds(pl.multiple_of(i * BLK, BLK), BLK)
+        return pltpu.make_async_remote_copy(src_ref=dp_v.at[slot], dst_ref=x_dpre.at[l, :, part], send_sem=ship_sent.at[slot],
+                                            recv_sem=ship_got.at[l], device_id=partner, device_id_type=MESH)
+
+    def shipped(l):
+        pltpu.make_async_remote_copy(src_ref=dpre.at[l], dst_ref=x_dpre.at[l], send_sem=ship_sent.at[0],
+                                     recv_sem=ship_got.at[l], device_id=partner, device_id_type=MESH).wait_recv()
 
     def loads(g):
         l = g // 2
@@ -897,6 +902,8 @@
     def step(which, stage):
         if stage == 'L':
             net.arrived(*NEEDS[which])
+            if which in (0, 2):
+                shipped(which // 2)
             for copy in loads(which):
                 copy.start()
         else:
@@ -935,18 +942,20 @@
 
     for l in (1, 0):
         r = 1 + 5 * l
+        free('do')
         for at, size in CHUNKS:
             d = get(d_v, pl.ds(at, size))
             add(r + 4, d)
             do_v[pl.ds(at, size), :] = d.astype(bf16)
         keep = pltpu.make_async_copy(do_v, dout.at[l], sem.at[1])
         keep.start()
-        keep.wait()
         if l == 1:
             pl.semaphore_wait(barrier, 10)
-            swap('hl', 'hr', 'dout1', 'act1', 'vin1', 'act0', 'vin0', 'pat')
+            swap('dout1', 'act1', 'hl', 'hr', 'vin1', 'act0', 'vin0', 'pat')
         else:
             swap('dout0')
+        busy['do'] = [f'dout{l}']
+        keep.wait()
         burst(f'c{l}_0')
         run = during(f'c{l}_', NBLK)
 
@@ -962,12 +971,16 @@
 
         def channel(i, slot):
             run(i)
+
+            @pl.when(i >= 2)
+            def _():
+                ship(l, i - 2, slot).wait_send()
             for n in range(2):
                 cols = slice(256 * n, 256 * n + 256)
-                _, slope = gelu_both(pre_v[slot, :, cols])
-                d = dot_nt(do_v[...], w2_v[slot, 2 * n:2 * n + 2].reshape(256, CH)) * slope
+                d = dot_nt(do_v[...], w2_v[slot, 2 * n:2 * n + 2].reshape(256, CH)) * pre_v[slot, :, cols]
                 gbch1[l:l + 1, pl.ds(pl.multiple_of(i * BLK + 256 * n, 256), 256)] = jnp.sum(d, axis=0, keepdims=True)
                 dp_v[slot, :, cols] = d.astype(bf16)
+            ship(l, i, slot).start()
 
             @pl.when(i == 0)
             def _():
@@ -976,7 +989,8 @@
                 cols = slice(512 * n, 512 * n + 512)
                 dv_v[:, cols] += dot_nt(dp_v[slot], w1_v[slot, n].reshape(512, BLK))
         for_blocks(Stream(sem_w, blocks, NBLK), channel, Stream(sem_o, outs, NBLK))
-        swap(f'dpre{l}')
+        for slot in range(2):
+            ship(l, NBLK - 2 + slot, slot).wait_send()
         burst(f'l{l}')
         load.wait()
 
@@ -1010,7 +1024,7 @@
                 add_token(l, jnp.sum(dh, axis=-1, keepdims=True), 64)
                 dh = dh.astype(bf16)
                 add_token(l, dot_nt(dh, a[:, cols]))
-                parts.append(dot_tn(wt[l, :, 0:TPAD], dh))
+                parts.append(dot_nn(wt_t[l], dh))
             d = jnp.where(mask, jnp.concatenate(parts, axis=1), 0.0)
             add(r, d * std)
             add(r + 1, d)
@@ -1021,14 +1035,15 @@
             burst('d0')
 
     burst('fin')
+    free('do')
     for at, size in CHUNKS:
         d = get(d_v, pl.ds(at, size))
         add(0, d)
         do_v[pl.ds(at, size), :] = d.astype(bf16)
     keep = pltpu.make_async_copy(do_v, dres, sem.at[1])
     keep.start()
+    swap('dres')
     keep.wait()
-    swap('dres')
     small_pack(b, x_v, d_v, gvec, hstat, gbch1, gbh)
 
     last = []
@@ -1087,7 +1102,7 @@
     S, V, DMA = jax.ShapeDtypeStruct, pltpu.VMEM, pltpu.SemaphoreType.DMA
     return pl.pallas_call(
         back_kernel, name='back',
-        in_specs=[a] * 7 + [v] * 7, out_specs=[v] * 5 + [a] * 9,
+        in_specs=[a] * 7 + [v] * 8, out_specs=[v] * 5 + [a] * 9,
         out_shape=[S((N_CH, 32, 1024), f32), S((96, 256), f32), S((32, 256), f32), S((8, 128), f32), S((4, 16, 128), f32),
                    S((2, ROWS, CHH), bf16), S((2, ROWS, CH), bf16), S((ROWS, CH), bf16), S((2, ROWS, 2048), bf16),
                    S((2, ROWS, 512), bf16), S((ROWS, 1536), bf16), S((2, ROWS, CHH), bf16), S((2, ROWS, CH), bf16),
@@ -1096,7 +1111,7 @@
                         V((IMG, CH), bf16), V((16, CH), f32), V((2, CHH), f32), V((CH // 128, XROWS, 128), f32),
                         V((CH // 128, XROWS, 128), f32), V((ROWS, CH), f32), V((ROWS, CH), bf16), V((2, 2, 4, 4, 32, BLK), bf16),
                         V((2, 4, 4, 32, CH), bf16), V((2, ROWS, BLK), f32), V((2, ROWS, BLK), bf16), DMA((BACK_COPIES,)), DMA((BACK_COPIES,)), DMA((4,)), DMA((2,)), DMA((2, 3)),
-                        DMA((2, 1))],
+                        DMA((2, 1)), DMA((2,)), DMA((2,))],
         compiler_params=pltpu.CompilerParams(collective_id=1, has_side_effects=True, vmem_limit_bytes=64 * 1024 * 1024 - 65536),
         cost_estimate=pl.CostEstimate(flops=120_000_000_000, bytes_accessed=200_000_000, transcendentals=0),
     )(*operands)
@@ -1156,10 +1171,10 @@
 def solution(mesh):
     def step(patches, labels, w_stem, b_stem, ln1_g, ln1_b, w_tok1, b_tok1, w_tok2,
              ln2_g, ln2_b, w_ch1, b_ch1, w_ch2, b_ch2, lnf_g, lnf_b, w_head, b_head):
-        wc, pat, xin, xmid, vin, pre, act, hl, hr, dx0, hstat, gbh, vec, wt = front(
+        wc, pat, xin, xmid, vin, pre, act, hl, hr, dx0, hstat, gbh, vec, wt, wt_t = front(
             labels, patches.transpose(1, 0, 2), w_stem, w_ch1, w_ch2, w_head, w_tok1.transpose(0, 2, 1), w_tok2, b_tok1, b_ch1,
             b_head, b_stem, ln1_g, ln1_b, ln2_g, ln2_b, b_ch2, lnf_g, lnf_b)
-        sums = back(xin, xmid, pre, wc, act, vin, pat, hl, hr, dx0, hstat, gbh, wt, vec)[:5]
+        sums = back(xin, xmid, pre, wc, act, vin, pat, hl, hr, dx0, hstat, gbh, wt, wt_t, vec)[:5]
         loss, g_s, g_bs, g_1g, g_1b, g_t1, g_bt, g_t2, g_2g, g_2b, g_c1, g_b1, g_c2, g_b2, g_fg, g_fb, g_h, g_bh = finish(*sums)
         return (loss.reshape(()), g_s, g_bs, g_1g, g_1b, g_t1.transpose(0, 2, 1), g_bt, g_t2, g_2g, g_2b, g_c1, g_b1, g_c2, g_b2,
                 g_fg, g_fb, g_h, g_bh)

time: 324 us -> 325 us (level)
  no operation moved by 1% of the time
where the time goes in v10:
time: 325 us; the launch traced here: 320 us
  Pallas kernels  319 us (98%)
    pallas_call x1, Pallas kernels, back(): pl.pallas_call(back_kernel, name='back', in_specs=[a] * 7 + [v] * 8, out_...  187 us
    pallas_call x1, Pallas kernels, front(): pl.pallas_call(front_kernel, name='front', in_specs=[pl.BlockSpec(memory_...  127 us

profile of v10, /device:TPU:0, one launch (start us, length us, event | category | flops | bytes accessed | tf_op | source)
XLA Modules:
  0.0 320.0 jit_solution(7565030689861901749)
XLA Ops:
  0.7 126.7 %front.1 = (bf16[4,4,2,4,4,32,1024]{6,5,4,3,2,1,0:T(8,128)(2,1)}, bf16[2,392,1536]{2,1,0:T(8,128)(2,1)}, f32[2,8,392,128]{3,2,1,0:T(8,128)}, f32[2,8,392,128]{3,...) custom-call(s32[32]{0:T(128)} %labels.1, ...), custom_call_target="tpu_custom_call" | custom-call | flops 89999998976 | bytes 180000000 | tf_op jit(solution)/shard_map/front/pallas_call | solution.py:548
  127.4 187.5 %back.1 = (f32[4,32,1024]{2,1,0:T(8,128)}, f32[96,256]{1,0:T(8,128)}, f32[32,256]{1,0:T(8,128)}, f32[8,128]{1,0:T(8,128)}, f32[4,16,128]{2,1,0:T(8,128)}, /*inde...) custom-call(f32[2,8,392,128]{3,2,1,0:T(8,128)} %get-tuple-element.56, ...), custom_call_target="tpu_custom_call" | custom-call | flops 120000004096 | bytes 200000000 | tf_op jit(solution)/shard_map/back/pallas_call | solution.py:1103
  314.9 4.6 %finish.1 = (f32[1,1]{1,0:T(1,128)}, f32[96,256]{1,0:T(8,128)}, f32[8]{0:T(128)}, f32[2,8]{1,0:T(2,128)}, f32[2,8]{1,0:T(2,128)}, /*index=5*/f32[2,16,49]{2,1,0:...) custom-call(f32[4,32,1024]{2,1,0:T(8,128)} %get-tuple-element.71.c, ...), custom_call_target="tpu_custom_call" | custom-call | tf_op jit(solution)/shard_map/finish/pallas_call | solution.py:1153

commit v11 on v10

--- a/solution.py
+++ b/solution.py
@@ -142,35 +142,35 @@
 FRONT_ORDER = (
     ('prep', (('M0', ('sm',)), ('M0', ('tk',)), ('A0', ('stem', 0)), ('A0', ('stem', 1)), ('A0', ('stem', 2)),
         ('A0', ('ch', 0, 'a')), ('A0', ('ch', 0, 'b')), ('A0', ('ch', 1, 'a')), ('A0', ('ch', 1, 'b')),
-        ('A0', ('ch', 2, 'a')), ('A0', ('ch', 2, 'b')), ('A0', ('head', 2)),)),
+        ('A0', ('ch', 2, 'a')), ('A0', ('ch', 2, 'b')),)),
     ('unpack', (('M1', ('sm',)), ('M1', ('tk',)), ('A', ('stem', 0)), ('A', ('stem', 1)), ('A', ('stem', 2)),
-        ('A', ('ch', 0, 'a')), ('A', ('ch', 1, 'a')), ('A', ('ch', 2, 'a')), ('A', ('ch', 0, 'b')), ('A', ('ch', 2, 'b')),
-        ('A', ('head', 2)), ('A', ('ch', 1, 'b')), ('B', ('stem', 0)), ('M2', ('sm',)), ('B', ('stem', 1)),
-        ('B', ('ch', 0, 'a')), ('B', ('ch', 1, 'a')), ('B', ('ch', 0, 'b')), ('B', ('ch', 1, 'b')), ('M2', ('tk',)),
-        ('B', ('stem', 2)), ('B', ('head', 2)), ('C', ('stem', 0)), ('B', ('ch', 2, 'a')), ('B', ('ch', 2, 'b')),
-        ('M3', ('sm',)), ('C', ('stem', 2)), ('C', ('stem', 1)), ('C', ('head', 2)),)),
-    ('stem0', (('D', ('stem', 0, None)), ('C', ('ch', 0, 'a')), ('C', ('ch', 1, 'a')), ('C', ('ch', 2, 'a')),
-        ('D', ('stem', 2, None)), ('D', ('stem', 1, None)), ('D', ('ch', 2, 0)), ('D', ('ch', 2, 1)), ('D', ('ch', 0, 0)),
-        ('D', ('ch', 0, 1)), ('E', ('stem', 0, None)), ('E', ('stem', 2, None)), ('E', ('stem', 1, None)),
-        ('D', ('ch', 1, 0)), ('D', ('ch', 1, 1)), ('F', ('stem', 1, None)), ('E', ('ch', 2, 0)), ('E', ('ch', 0, 0)),
-        ('E', ('ch', 2, 1)), ('F', ('stem', 2, None)), ('C', ('ch', 0, 'b')), ('C', ('ch', 1, 'b')), ('C', ('ch', 2, 'b')),
-        ('D', ('head', 2, None)), ('E', ('ch', 1, 0)), ('F', ('ch', 2, 0)), ('E', ('ch', 0, 1)), ('F', ('stem', 0, None)),
-        ('F', ('ch', 2, 1)), ('D', ('ch', 0, 2)), ('D', ('ch', 0, 3)),)),
-    ('stem1', (('E', ('ch', 1, 1)),)),
-    ('stem2', (('F', ('ch', 0, 0)), ('D', ('ch', 2, 2)), ('D', ('ch', 2, 3)),)),
-    ('tok0_0', (('D', ('ch', 1, 2)), ('D', ('ch', 1, 3)), ('E', ('head', 2, None)),)),
-    ('tok0_1', (('F', ('ch', 1, 0)),)),
-    ('tok0_3', (('F', ('ch', 0, 1)),)),
-    ('tok0_5', (('F', ('ch', 1, 1)), ('E', ('ch', 2, 2)),)),
-    ('ch0_1', (('E', ('ch', 0, 2)), ('E', ('ch', 2, 3)),)),
-    ('ch0_2', (('E', ('ch', 1, 2)), ('F', ('head', 2, None)),)),
-    ('ch0_4', (('F', ('ch', 2, 2)),)),
-    ('ch0_5', (('E', ('ch', 0, 3)), ('F', ('ch', 2, 3)),)),
-    ('ch0_7', (('E', ('ch', 1, 3)),)),
-    ('tok1_0', (('F', ('ch', 0, 2)),)),
-    ('tok1_1', (('F', ('ch', 1, 2)),)),
-    ('tok1_3', (('F', ('ch', 0, 3)),)),
-    ('tok1_5', (('F', ('ch', 1, 3)),)),
+        ('A', ('ch', 0, 'a')), ('A', ('ch', 1, 'a')), ('A', ('ch', 2, 'a')), ('B', ('stem', 0)), ('M2', ('sm',)),
+        ('B', ('stem', 1)), ('B', ('ch', 0, 'a')), ('B', ('ch', 1, 'a')), ('M2', ('tk',)), ('B', ('stem', 2)),
+        ('C', ('stem', 0)), ('B', ('ch', 2, 'a')), ('M3', ('sm',)), ('C', ('stem', 2)), ('C', ('stem', 1)),)),
+    ('stem0', (('D', ('stem', 0, None)), ('D', ('stem', 1, None)), ('D', ('stem', 2, None)), ('C', ('ch', 0, 'a')),
+        ('C', ('ch', 1, 'a')), ('C', ('ch', 2, 'a')), ('A', ('ch', 0, 'b')), ('A', ('ch', 1, 'b')), ('A', ('ch', 2, 'b')),
+        ('E', ('stem', 0, None)), ('E', ('stem', 1, None)), ('E', ('stem', 2, None)), ('D', ('ch', 2, 0)),
+        ('B', ('ch', 0, 'b')), ('D', ('ch', 1, 0)), ('D', ('ch', 0, 0)), ('B', ('ch', 2, 'b')), ('B', ('ch', 1, 'b')),
+        ('F', ('stem', 0, None)), ('F', ('stem', 1, None)), ('A0', ('head', 2)), ('F', ('stem', 2, None)),)),
+    ('stem1', (('E', ('ch', 2, 0)), ('D', ('ch', 0, 1)), ('D', ('ch', 1, 1)), ('D', ('ch', 2, 1)),)),
+    ('stem3', (('E', ('ch', 0, 0)), ('E', ('ch', 1, 0)),)),
+    ('tok0_2', (('F', ('ch', 2, 0)), ('A', ('head', 2)),)),
+    ('tok0_7', (('E', ('ch', 2, 1)), ('C', ('ch', 0, 'b')), ('C', ('ch', 1, 'b')), ('C', ('ch', 2, 'b')),)),
+    ('ln0', (('E', ('ch', 1, 1)),)),
+    ('ch0_0', (('E', ('ch', 0, 1)), ('F', ('ch', 1, 0)), ('B', ('head', 2)), ('F', ('ch', 2, 1)), ('D', ('ch', 2, 2)),
+        ('D', ('ch', 2, 3)), ('F', ('ch', 0, 0)), ('D', ('ch', 0, 2)), ('D', ('ch', 0, 3)), ('D', ('ch', 1, 2)),
+        ('D', ('ch', 1, 3)), ('F', ('ch', 1, 1)), ('C', ('head', 2)),)),
+    ('ch0_1', (('F', ('ch', 0, 1)),)),
+    ('ch0_2', (('E', ('ch', 2, 2)),)),
+    ('ch0_7', (('E', ('ch', 1, 2)), ('E', ('ch', 2, 3)),)),
+    ('cb0_0', (('E', ('ch', 0, 2)),)),
+    ('cb0_1', (('F', ('ch', 2, 2)),)),
+    ('tok1_1', (('F', ('ch', 2, 3)),)),
+    ('tok1_2', (('D', ('head', 2, None)), ('E', ('ch', 1, 3)),)),
+    ('tok1_3', (('E', ('ch', 0, 3)),)),
+    ('tok1_6', (('F', ('ch', 1, 2)), ('F', ('ch', 0, 2)),)),
+    ('ch1_0', (('E', ('head', 2, None)), ('F', ('ch', 1, 3)), ('F', ('ch', 0, 3)),)),
+    ('ch1_4', (('F', ('head', 2, None)),)),
 )
 
 
@@ -481,28 +481,34 @@
         for copy in save_v:
             copy.start()
         burst(f'ch{l}_0')
-        need(2 + 2 * l)
+        need(1 + 2 * l)
         save_mid.wait()
 
         def blocks(i, slot):
-            t, h = i // 2, i % 2
-            part = pl.ds(pl.multiple_of(h * BLK, BLK), BLK)
-            return [(wc_all.at[2 * l, t, :, :, :, :, part], w1_v.at[slot]), (wc_all.at[2 * l + 1, t, h], w2_v.at[slot])]
+            part = pl.ds(pl.multiple_of(i % 2 * BLK, BLK), BLK)
+            return [(wc_all.at[2 * l, i // 2, :, :, :, :, part], w1_v.at[slot])]
 
         def outs(i, slot):
             part = pl.ds(pl.multiple_of(i * BLK, BLK), BLK)
             half = pl.ds(pl.multiple_of(i // 2 * BLK, BLK), BLK)
-            return [(pre_v.at[slot], pre_out.at[l, :, part]), (act_v.at[slot], act_out.at[l, i % 2, :, half])]
-        run = during(f'ch{l}_', NBLK)
+            return [(pre_v.at[slot], pre_out.at[l, :, part]), (act_v.at[:, part], act_out.at[l, i % 2, :, half])]
+        run_a = during(f'ch{l}_', NBLK)
 
         def channel(i, slot):
-            run(i)
+            run_a(i)
             part = pl.ds(pl.multiple_of(i * BLK, BLK), BLK)
             h = dot_nn(v_v[...], w1_v[slot].reshape(CH, BLK)) + bch1[l:l + 1, part]
             value, pre_v[slot] = gelu_both(h)
-            act_v[slot] = value.astype(bf16)
-            add_rows(dot_nn(act_v[slot], w2_v[slot].reshape(BLK, CH)))
+            act_v[:, part] = value.astype(bf16)
         for_blocks(Stream(sem_w, blocks, NBLK), channel, Stream(sem_o, outs, NBLK))
+        burst(f'cb{l}_0')
+        need(2 + 2 * l)
+        run_b = during(f'cb{l}_', 4)
+
+        def second(t, slot):
+            run_b(t)
+            add_rows(dot_nn(act_v[:, pl.ds(pl.multiple_of(t * CH, CH), CH)], w2_v[slot].reshape(CH, CH)))
+        for_blocks(Stream(sem_w, lambda t, slot: [(wc_all.at[2 * l + 1, t], w2_v.at[slot])], 4), second)
         add_rows(jnp.broadcast_to(vec[r + 4:r + 5, :], (ROWS, CH)))
         for copy in save_v:
             copy.wait()
@@ -559,8 +565,8 @@
                         V((2, 4, 4, 32, CH), bf16), V((4, 4, 4, 2, 16, 128), bf16), V((4, 4, 4, 2, 8, 128), f32),
                         V((1024, 128), f32), V((8, CH), f32), V((2, CHH), f32),
                         V((128, 128), f32), V((TOK, IMG, 3072), bf16), V((2, ROWS, 1536), bf16), V((CH // 128, XROWS, 128), f32),
-                        V((ROWS, CH), bf16), V((2, 2, 4, 4, 32, BLK), bf16), V((2, 4, 4, 32, CH), bf16),
-                        V((2, ROWS, BLK), f32), V((2, ROWS, BLK), bf16), V((TOKH, CH), bf16),
+                        V((ROWS, CH), bf16), V((2, 2, 4, 4, 32, BLK), bf16), V((2, 2, 4, 4, 32, CH), bf16),
+                        V((2, ROWS, BLK), f32), V((ROWS, CHH), bf16), V((TOKH, CH), bf16),
                         DMA((FRONT_COPIES,)), DMA((FRONT_COPIES,)), DMA((2,)), DMA((2, 2)), DMA((2, 2)), DMA((3,))],
         compiler_params=pltpu.CompilerParams(collective_id=0, has_side_effects=True, vmem_limit_bytes=62 * 1024 * 1024),
         cost_estimate=pl.CostEstimate(flops=90_000_000_000, bytes_accessed=180_000_000, transcendentals=0),
@@ -570,29 +576,37 @@
 GROUPS = (3, 2, 1, HEAD, 0, STEM)
 UNITS = tuple((g, c) for g in GROUPS for c in (2, 0, 1) if g != HEAD or c == 2)
 BACK_COPIES = 18 * len(UNITS) + 40
-NEEDS = {3: ('act1', 'dout1'), 2: ('vin1',), 1: ('act0', 'dout0'), 0: ('vin0',), STEM: ('pat', 'dres'),
+NEEDS = {3: ('act1', 'dout1'), 2: ('vin1', 'dpre1'), 1: ('act0', 'dout0'), 0: ('vin0', 'dpre0'), STEM: ('pat', 'dres'),
          HEAD: ('hl', 'hr')}
 BACK_ORDER = (
     ('c1_7', ((3, 'L'),)),
-    ('t1_7', ((0, 0), (0, 1), (1, 0), (1, 1),)),
-    ('d0', ((0, 2),)),
-    ('c0_3', ((1, 2), (0, 3),)),
-    ('l0', ((1, 3), (0, 4),)),
-    ('t0_1', ((1, 4), (0, 5),)),
-    ('t0_3', ((1, 5), (0, 6),)),
-    ('t0_4', ((2, 0), (2, 'L'), (2, 1), (1, 6), (0, 7),)),
-    ('t0_5', ((3, 0), (3, 1), (1, 7), (4, 0), (4, 1), (2, 2),)),
-    ('t0_6', ((3, 2), (5, 0), (1, 'L'), (5, 1),)),
-    ('t0_7', ((4, 2), (2, 3), (3, 3),)),
-    ('fin', ((6, 0), (6, 1), (5, 2), (2, 4), (7, 0), (7, 1), (4, 3), (3, 4), (8, 0), (0, 'L'), (8, 1), (6, 2), (4, 4),
-        (2, 5), (5, 3), (9, 0), (9, 1), (7, 2),)),
-    ('end', ((8, 2), (5, 4), (3, 5), (6, 3), (2, 6), (10, 0), (10, 1), (9, 2), (11, 0), (11, 1), (6, 4), (4, 5), (7, 3),
-        (5, 5), (2, 7), (12, 0), (4, 'L'), (12, 1), (8, 3), (7, 4), (10, 2), (3, 6), (11, 2), (4, 6), (8, 4), (6, 5),
-        (12, 2), (9, 3), (5, 6), (13, 0), (13, 1), (9, 4), (7, 5), (11, 3), (8, 5), (6, 6), (3, 7), (4, 7), (5, 7), (14, 0),
-        (14, 1), (15, 0), (15, 1), (9, 5), (10, 3), (12, 3), (8, 6), (11, 4), (13, 2), (6, 7), (14, 2), (7, 6), (15, 2),
-        (12, 4), (10, 4), (8, 7), (9, 6), (11, 5), (7, 7), (14, 3), (12, 5), (10, 5), (13, 3), (15, 3), (11, 6), (9, 7),
-        (12, 6), (14, 4), (13, 4), (10, 6), (15, 4), (11, 7), (12, 7), (14, 5), (10, 7), (13, 5), (15, 5), (14, 6), (13, 6),
-        (15, 6), (14, 7), (13, 7), (15, 7),)),
+    ('t1_0', ((0, 0), (0, 1), (1, 0), (1, 1), (2, 0), (2, 1), (0, 2),)),
+    ('t1_2', ((1, 2),)),
+    ('t1_3', ((0, 3), (2, 2),)),
+    ('t1_4', ((2, 'L'),)),
+    ('t1_6', ((1, 3), (0, 4), (3, 0), (3, 1), (2, 3), (4, 0), (4, 1), (1, 4), (0, 5), (5, 0), (5, 1), (3, 2), (1, 5), (0, 6),)),
+    ('t1_7', ((2, 4),)),
+    ('d0', ((4, 2),)),
+    ('c0_1', ((5, 2), (3, 3), (2, 5), (1, 6),)),
+    ('c0_3', ((1, 'L'), (1, 7),)),
+    ('c0_4', ((4, 3), (3, 4), (0, 7), (6, 0), (6, 1), (2, 6), (7, 0), (7, 1), (5, 3), (4, 4), (3, 5), (2, 7), (8, 0), (8, 1),
+        (6, 2), (4, 5), (3, 6), (9, 0), (9, 1),)),
+    ('c0_5', ((7, 2), (5, 4),)),
+    ('c0_7', ((6, 3), (8, 2), (4, 6),)),
+    ('t0_0', ((9, 2),)),
+    ('t0_1', ((7, 3), (6, 4), (3, 7),)),
+    ('t0_2', ((5, 5), (4, 7),)),
+    ('t0_3', ((8, 3), (7, 4), (6, 5), (9, 3), (5, 6),)),
+    ('t0_4', ((0, 'L'),)),
+    ('t0_5', ((8, 4), (9, 4), (7, 5), (6, 6), (5, 7), (10, 0), (10, 1), (11, 0), (11, 1), (8, 5), (9, 5), (7, 6), (6, 7),
+        (12, 0), (12, 1), (10, 2), (9, 6),)),
+    ('t0_6', ((7, 7),)),
+    ('t0_7', ((11, 2),)),
+    ('fin', ((12, 2), (10, 3),)),
+    ('end', ((8, 6), (9, 7), (11, 3), (10, 4), (8, 7), (4, 'L'), (12, 3), (10, 5), (11, 4), (13, 0), (13, 1), (12, 4),
+        (11, 5), (10, 6), (14, 0), (14, 1), (15, 0), (15, 1), (10, 7), (13, 2), (14, 2), (15, 2), (12, 5), (11, 6), (14, 3),
+        (15, 3), (12, 6), (13, 3), (11, 7), (14, 4), (12, 7), (15, 4), (13, 4), (14, 5), (15, 5), (13, 5), (14, 6), (15, 6),
+        (13, 6), (14, 7), (15, 7), (13, 7),)),
 )
 SMALL = dict(sm=((4, 4, 4, 8, 128), (3, 4, 4, 8, 128), (3, 4, 8, 128), (3, 8, 128)),
              tk=((4, 4, 4, 16, 128), (3, 4, 4, 16, 128), (3, 4, 16, 128), (3, 4, 16, 128)))
@@ -671,7 +685,7 @@
     out_c, out_s, out_h, sm_own, tk_own = refs[15:20]
     dpre, dout, dres, x_act, x_vin, x_pat, x_dpre, x_dout, x_dres = refs[20:29]
     (per, b, big, little, x_hl, x_hr, gvec, gbch1, x_v, d_v, dv_v, do_v, w1_v, w2_v, pre_v, dp_v,
-     send_sems, recv_sems, load_sems, sem, sem_w, sem_o, ship_sent, ship_got) = refs[29:]
+     send_sems, recv_sems, load_sems, sem, sem_w, sem_o) = refs[29:]
     me = my_place()
     other = moved(me, 'k', 1)
     k, k2 = me['k'], 1 - me['k']
@@ -687,7 +701,8 @@
     half_at = pl.ds(pl.multiple_of(k * 512, 512), 512)
     half_to = pl.ds(pl.multiple_of(k2 * 512, 512), 512)
     swaps = {'act1': (act.at[1, k2], x_act.at[1]), 'act0': (act.at[0, k2], x_act.at[0]), 'vin1': (vin.at[1, k2], x_vin.at[1]),
-             'vin0': (vin.at[0, k2], x_vin.at[0]), 'pat': (pat.at[k2], x_pat), 'dout1': (do_v, x_dout.at[1]), 'dout0': (do_v, x_dout.at[0]), 'dres': (do_v, x_dres),
+             'vin0': (vin.at[0, k2], x_vin.at[0]), 'pat': (pat.at[k2], x_pat), 'dpre1': (dpre.at[1], x_dpre.at[1]), 'dpre0': (dpre.at[0], x_dpre.at[0]),
+             'dout1': (do_v, x_dout.at[1]), 'dout0': (do_v, x_dout.at[0]), 'dres': (do_v, x_dres),
              'hl': (hl.at[:, half_to], x_hl), 'hr': (hr, x_hr)}
 
     def swap(*names):
@@ -699,15 +714,6 @@
         for name in busy.pop(key, ()):
             net.copy(name).wait_send()
             net.done.add(name)
-
-    def ship(l, i, slot):
-        part = pl.ds(pl.multiple_of(i * BLK, BLK), BLK)
-        return pltpu.make_async_remote_copy(src_ref=dp_v.at[slot], dst_ref=x_dpre.at[l, :, part], send_sem=ship_sent.at[slot],
-                                            recv_sem=ship_got.at[l], device_id=partner, device_id_type=MESH)
-
-    def shipped(l):
-        pltpu.make_async_remote_copy(src_ref=dpre.at[l], dst_ref=x_dpre.at[l], send_sem=ship_sent.at[0],
-                                     recv_sem=ship_got.at[l], device_id=partner, device_id_type=MESH).wait_recv()
 
     def loads(g):
         l = g // 2
@@ -902,8 +908,6 @@
     def step(which, stage):
         if stage == 'L':
             net.arrived(*NEEDS[which])
-            if which in (0, 2):
-                shipped(which // 2)
             for copy in loads(which):
                 copy.start()
         else:
@@ -972,15 +976,11 @@
         def channel(i, slot):
             run(i)
 
-            @pl.when(i >= 2)
-            def _():
-                ship(l, i - 2, slot).wait_send()
             for n in range(2):
                 cols = slice(256 * n, 256 * n + 256)
                 d = dot_nt(do_v[...], w2_v[slot, 2 * n:2 * n + 2].reshape(256, CH)) * pre_v[slot, :, cols]
                 gbch1[l:l + 1, pl.ds(pl.multiple_of(i * BLK + 256 * n, 256), 256)] = jnp.sum(d, axis=0, keepdims=True)
                 dp_v[slot, :, cols] = d.astype(bf16)
-            ship(l, i, slot).start()
 
             @pl.when(i == 0)
             def _():
@@ -989,8 +989,7 @@
                 cols = slice(512 * n, 512 * n + 512)
                 dv_v[:, cols] += dot_nt(dp_v[slot], w1_v[slot, n].reshape(512, BLK))
         for_blocks(Stream(sem_w, blocks, NBLK), channel, Stream(sem_o, outs, NBLK))
-        for slot in range(2):
-            ship(l, NBLK - 2 + slot, slot).wait_send()
+        swap(f'dpre{l}')
         burst(f'l{l}')
         load.wait()
 
@@ -1111,7 +1110,7 @@
                         V((IMG, CH), bf16), V((16, CH), f32), V((2, CHH), f32), V((CH // 128, XROWS, 128), f32),
                         V((CH // 128, XROWS, 128), f32), V((ROWS, CH), f32), V((ROWS, CH), bf16), V((2, 2, 4, 4, 32, BLK), bf16),
                         V((2, 4, 4, 32, CH), bf16), V((2, ROWS, BLK), f32), V((2, ROWS, BLK), bf16), DMA((BACK_COPIES,)), DMA((BACK_COPIES,)), DMA((4,)), DMA((2,)), DMA((2, 3)),
-                        DMA((2, 1)), DMA((2,)), DMA((2,))],
+                        DMA((2, 1))],
         compiler_params=pltpu.CompilerParams(collective_id=1, has_side_effects=True, vmem_limit_bytes=64 * 1024 * 1024 - 65536),
         cost_estimate=pl.CostEstimate(flops=120_000_000_000, bytes_accessed=200_000_000, transcendentals=0),
     )(*operands)

time: 325 us -> 318 us (0.978)
  Pallas kernels: 319 us -> 312 us
    pallas_call x1, Pallas kernels: 187 us -> 175 us  [back(): pl.pallas_call(back_kernel, name='back', in_specs=[a] * 7 + [v] * 8, out_...]
    pallas_call x1, Pallas kernels: 127 us -> 132 us  [front(): pl.pallas_call(front_kernel, name='front', in_specs=[pl.BlockSpec(memory_...]
where the time goes in v11:
time: 318 us; the launch traced here: 313 us
  Pallas kernels  312 us (98%)
    pallas_call x1, Pallas kernels, back(): pl.pallas_call(back_kernel, name='back', in_specs=[a] * 7 + [v] * 8, out_...  175 us
    pallas_call x1, Pallas kernels, front(): pl.pallas_call(front_kernel, name='front', in_specs=[pl.BlockSpec(memory_...  132 us

profile of v11, /device:TPU:0, one launch (start us, length us, event | category | flops | bytes accessed | tf_op | source)
XLA Modules:
  0.0 313.2 jit_solution(6442074266406125518)
XLA Ops:
  0.7 132.4 %front.1 = (bf16[4,4,2,4,4,32,1024]{6,5,4,3,2,1,0:T(8,128)(2,1)}, bf16[2,392,1536]{2,1,0:T(8,128)(2,1)}, f32[2,8,392,128]{3,2,1,0:T(8,128)}, f32[2,8,392,128]{3,...) custom-call(s32[32]{0:T(128)} %labels.1, ...), custom_call_target="tpu_custom_call" | custom-call | flops 89999998976 | bytes 180000000 | tf_op jit(solution)/shard_map/front/pallas_call | solution.py:554
  133.1 175.1 %back.1 = (f32[4,32,1024]{2,1,0:T(8,128)}, f32[96,256]{1,0:T(8,128)}, f32[32,256]{1,0:T(8,128)}, f32[8,128]{1,0:T(8,128)}, f32[4,16,128]{2,1,0:T(8,128)}, /*inde...) custom-call(f32[2,8,392,128]{3,2,1,0:T(8,128)} %get-tuple-element.56, ...), custom_call_target="tpu_custom_call" | custom-call | flops 120000004096 | bytes 200000000 | tf_op jit(solution)/shard_map/back/pallas_call | solution.py:1102
  308.1 4.6 %finish.1 = (f32[1,1]{1,0:T(1,128)}, f32[96,256]{1,0:T(8,128)}, f32[8]{0:T(128)}, f32[2,8]{1,0:T(2,128)}, f32[2,8]{1,0:T(2,128)}, /*index=5*/f32[2,16,49]{2,1,0:...) custom-call(f32[4,32,1024]{2,1,0:T(8,128)} %get-tuple-element.71.c, ...), custom_call_target="tpu_custom_call" | custom-call | tf_op jit(solution)/shard_map/finish/pallas_call | solution.py:1152

commit v12 on v10

--- a/solution.py
+++ b/solution.py
@@ -202,7 +202,7 @@
 def core_first(size, cols, each):
     half = cols // 2
     row = lax.broadcasted_iota(jnp.int32, (size, size), 0)
-    col = lax.broadcasted_iota(jnp.int32, (size, size), 1)
+    col = lax.broadcasted_iota(jnp.int32, (1, size), 1)
     source = col % half // each * (2 * each) + col // half * each + col % each
     return jnp.where(row == source, 1.0, 0.0).astype(bf16)
 
@@ -223,7 +223,7 @@
                  ln2_g, ln2_b, b_ch2, lnf_g, lnf_b,
                  wc, pat_out, xin, xmid, vout, pre_out, act_out, hl, hr, dx0, hstat, gbh, vec, wt, wt_t,
                  pc, ps, ph, tk_f, tk_p, sm_p, bh_p, ws, wh, tk_v, sm_v, sm_2, bh_v, bch1,
-                 turn, p_v, pk_v, x_v, v_v, w1_v, w2_v, pre_v, act_v, g_v,
+                 turn, p_v, pk_v, x_a, x_b, v_v, w1_v, w2_v, pre_v, act_v, g_v,
                  send_sems, recv_sems, sem, sem_w, sem_o, sem_x):
     me = my_place()
     other = moved(me, 'k', 1)
@@ -437,7 +437,7 @@
     burst('stem0')
     need(0)
     run = during('stem', 4)
-    put(x_v, pl.ds(ROWS, XROWS - ROWS), jnp.zeros((XROWS - ROWS, CH), f32))
+    put(x_a, pl.ds(ROWS, XROWS - ROWS), jnp.zeros((XROWS - ROWS, CH), f32))
 
     @pl.loop(0, 4)
     def _(i):
@@ -446,26 +446,26 @@
         w = ws[i // 2, :, :, :, :, pl.ds(pl.multiple_of(i % 2 * 256, 256), 256)].reshape(3072, 256)
         value = dot_nn(p_v[...].reshape(ROWS, 3072), w) + vec[0:1, cols]
         for n in range(2):
-            x_v[2 * i + n, pl.ds(0, ROWS), :] = value[:, 128 * n:128 * (n + 1)]
+            x_a[2 * i + n, pl.ds(0, ROWS), :] = value[:, 128 * n:128 * (n + 1)]
 
     wc_all = wc
 
-    def add_rows(value):
+    def add_rows(x_v, value):
         for n in range(CH // 128):
             x_v[n, pl.ds(0, ROWS), :] += value[:, 128 * n:128 * (n + 1)]
 
     for l in range(2):
         r = 1 + 5 * l
+        x_old, x_v = ((x_a, x_b), (x_b, x_a))[l]
         burst(f'tok{l}_0')
         run = during(f'tok{l}_', IMG)
-        save_in = pltpu.make_async_copy(x_v.at[:, pl.ds(0, ROWS)], xin.at[l], sem_x.at[0])
+        save_in = pltpu.make_async_copy(x_old.at[:, pl.ds(0, ROWS)], xin.at[l], sem_x.at[3])
         save_in.start()
-        save_in.wait()
 
         @pl.loop(0, IMG)
         def _(b):
             run(b)
-            x = get(x_v, image(b))
+            x = get(x_old, image(b))
             std, _ = standardize(x)
             a = with_bias_rows(std * vec[r:r + 1, :] + vec[r + 1:r + 2, :])
             g_v[...] = gelu_both(dot_nn(wt[l, :, 0:TPAD], a))[0].astype(bf16)
@@ -501,17 +501,17 @@
             h = dot_nn(v_v[...], w1_v[slot].reshape(CH, BLK)) + bch1[l:l + 1, part]
             value, pre_v[slot] = gelu_both(h)
             act_v[slot] = value.astype(bf16)
-            add_rows(dot_nn(act_v[slot], w2_v[slot].reshape(BLK, CH)))
+            add_rows(x_v, dot_nn(act_v[slot], w2_v[slot].reshape(BLK, CH)))
         for_blocks(Stream(sem_w, blocks, NBLK), channel, Stream(sem_o, outs, NBLK))
-        add_rows(jnp.broadcast_to(vec[r + 4:r + 5, :], (ROWS, CH)))
-        for copy in save_v:
+        add_rows(x_v, jnp.broadcast_to(vec[r + 4:r + 5, :], (ROWS, CH)))
+        for copy in (save_in, *save_v):
             copy.wait()
 
     burst('head')
     need(5)
     keep_p.wait()
     last = 11
-    pooled = jnp.sum(get(x_v, pl.ds(0, ROWS)).reshape(TOK, IMG, CH), axis=0) * (1.0 / TOK)
+    pooled = jnp.sum(get(x_a, pl.ds(0, ROWS)).reshape(TOK, IMG, CH), axis=0) * (1.0 / TOK)
     std, inv = standardize(pooled)
     head_in = (std * vec[last:last + 1, :] + vec[last + 1:last + 2, :]).astype(bf16)
     hl[...] = head_in
@@ -559,9 +559,10 @@
                         V((2, 4, 4, 32, CH), bf16), V((4, 4, 4, 2, 16, 128), bf16), V((4, 4, 4, 2, 8, 128), f32),
                         V((1024, 128), f32), V((8, CH), f32), V((2, CHH), f32),
                         V((128, 128), f32), V((TOK, IMG, 3072), bf16), V((2, ROWS, 1536), bf16), V((CH // 128, XROWS, 128), f32),
+                        V((CH // 128, XROWS, 128), f32),
                         V((ROWS, CH), bf16), V((2, 2, 4, 4, 32, BLK), bf16), V((2, 4, 4, 32, CH), bf16),
                         V((2, ROWS, BLK), f32), V((2, ROWS, BLK), bf16), V((TOKH, CH), bf16),
-                        DMA((FRONT_COPIES,)), DMA((FRONT_COPIES,)), DMA((2,)), DMA((2, 2)), DMA((2, 2)), DMA((3,))],
+                        DMA((FRONT_COPIES,)), DMA((FRONT_COPIES,)), DMA((2,)), DMA((2, 2)), DMA((2, 2)), DMA((4,))],
         compiler_params=pltpu.CompilerParams(collective_id=0, has_side_effects=True, vmem_limit_bytes=62 * 1024 * 1024),
         cost_estimate=pl.CostEstimate(flops=90_000_000_000, bytes_accessed=180_000_000, transcendentals=0),
     )(*operands)
@@ -570,29 +571,37 @@
 GROUPS = (3, 2, 1, HEAD, 0, STEM)
 UNITS = tuple((g, c) for g in GROUPS for c in (2, 0, 1) if g != HEAD or c == 2)
 BACK_COPIES = 18 * len(UNITS) + 40
-NEEDS = {3: ('act1', 'dout1'), 2: ('vin1',), 1: ('act0', 'dout0'), 0: ('vin0',), STEM: ('pat', 'dres'),
+NEEDS = {3: ('act1', 'dout1'), 2: ('vin1', 'dpre1'), 1: ('act0', 'dout0'), 0: ('vin0', 'dpre0'), STEM: ('pat', 'dres'),
          HEAD: ('hl', 'hr')}
 BACK_ORDER = (
     ('c1_7', ((3, 'L'),)),
-    ('t1_7', ((0, 0), (0, 1), (1, 0), (1, 1),)),
-    ('d0', ((0, 2),)),
-    ('c0_3', ((1, 2), (0, 3),)),
-    ('l0', ((1, 3), (0, 4),)),
-    ('t0_1', ((1, 4), (0, 5),)),
-    ('t0_3', ((1, 5), (0, 6),)),
-    ('t0_4', ((2, 0), (2, 'L'), (2, 1), (1, 6), (0, 7),)),
-    ('t0_5', ((3, 0), (3, 1), (1, 7), (4, 0), (4, 1), (2, 2),)),
-    ('t0_6', ((3, 2), (5, 0), (1, 'L'), (5, 1),)),
-    ('t0_7', ((4, 2), (2, 3), (3, 3),)),
-    ('fin', ((6, 0), (6, 1), (5, 2), (2, 4), (7, 0), (7, 1), (4, 3), (3, 4), (8, 0), (0, 'L'), (8, 1), (6, 2), (4, 4),
-        (2, 5), (5, 3), (9, 0), (9, 1), (7, 2),)),
-    ('end', ((8, 2), (5, 4), (3, 5), (6, 3), (2, 6), (10, 0), (10, 1), (9, 2), (11, 0), (11, 1), (6, 4), (4, 5), (7, 3),
-        (5, 5), (2, 7), (12, 0), (4, 'L'), (12, 1), (8, 3), (7, 4), (10, 2), (3, 6), (11, 2), (4, 6), (8, 4), (6, 5),
-        (12, 2), (9, 3), (5, 6), (13, 0), (13, 1), (9, 4), (7, 5), (11, 3), (8, 5), (6, 6), (3, 7), (4, 7), (5, 7), (14, 0),
-        (14, 1), (15, 0), (15, 1), (9, 5), (10, 3), (12, 3), (8, 6), (11, 4), (13, 2), (6, 7), (14, 2), (7, 6), (15, 2),
-        (12, 4), (10, 4), (8, 7), (9, 6), (11, 5), (7, 7), (14, 3), (12, 5), (10, 5), (13, 3), (15, 3), (11, 6), (9, 7),
-        (12, 6), (14, 4), (13, 4), (10, 6), (15, 4), (11, 7), (12, 7), (14, 5), (10, 7), (13, 5), (15, 5), (14, 6), (13, 6),
-        (15, 6), (14, 7), (13, 7), (15, 7),)),
+    ('t1_0', ((0, 0), (0, 1), (1, 0), (1, 1), (2, 0), (2, 1), (0, 2),)),
+    ('t1_2', ((1, 2),)),
+    ('t1_3', ((0, 3), (2, 2),)),
+    ('t1_4', ((2, 'L'),)),
+    ('t1_6', ((1, 3), (0, 4), (3, 0), (3, 1), (2, 3), (4, 0), (4, 1), (1, 4), (0, 5), (5, 0), (5, 1), (3, 2), (1, 5), (0, 6),)),
+    ('t1_7', ((2, 4),)),
+    ('d0', ((4, 2),)),
+    ('c0_1', ((5, 2), (3, 3), (2, 5), (1, 6),)),
+    ('c0_3', ((1, 'L'), (1, 7),)),
+    ('c0_4', ((4, 3), (3, 4), (0, 7), (6, 0), (6, 1), (2, 6), (7, 0), (7, 1), (5, 3), (4, 4), (3, 5), (2, 7), (8, 0), (8, 1),
+        (6, 2), (4, 5), (3, 6), (9, 0), (9, 1),)),
+    ('c0_5', ((7, 2), (5, 4),)),
+    ('c0_7', ((6, 3), (8, 2), (4, 6),)),
+    ('t0_0', ((9, 2),)),
+    ('t0_1', ((7, 3), (6, 4), (3, 7),)),
+    ('t0_2', ((5, 5), (4, 7),)),
+    ('t0_3', ((8, 3), (7, 4), (6, 5), (9, 3), (5, 6),)),
+    ('t0_4', ((0, 'L'),)),
+    ('t0_5', ((8, 4), (9, 4), (7, 5), (6, 6), (5, 7), (10, 0), (10, 1), (11, 0), (11, 1), (8, 5), (9, 5), (7, 6), (6, 7),
+        (12, 0), (12, 1), (10, 2), (9, 6),)),
+    ('t0_6', ((7, 7),)),
+    ('t0_7', ((11, 2),)),
+    ('fin', ((12, 2), (10, 3),)),
+    ('end', ((8, 6), (9, 7), (11, 3), (10, 4), (8, 7), (4, 'L'), (12, 3), (10, 5), (11, 4), (13, 0), (13, 1), (12, 4),
+        (11, 5), (10, 6), (14, 0), (14, 1), (15, 0), (15, 1), (10, 7), (13, 2), (14, 2), (15, 2), (12, 5), (11, 6), (14, 3),
+        (15, 3), (12, 6), (13, 3), (11, 7), (14, 4), (12, 7), (15, 4), (13, 4), (14, 5), (15, 5), (13, 5), (14, 6), (15, 6),
+        (13, 6), (14, 7), (15, 7), (13, 7),)),
 )
 SMALL = dict(sm=((4, 4, 4, 8, 128), (3, 4, 4, 8, 128), (3, 4, 8, 128), (3, 8, 128)),
              tk=((4, 4, 4, 16, 128), (3, 4, 4, 16, 128), (3, 4, 16, 128), (3, 4, 16, 128)))
@@ -671,7 +680,7 @@
     out_c, out_s, out_h, sm_own, tk_own = refs[15:20]
     dpre, dout, dres, x_act, x_vin, x_pat, x_dpre, x_dout, x_dres = refs[20:29]
     (per, b, big, little, x_hl, x_hr, gvec, gbch1, x_v, d_v, dv_v, do_v, w1_v, w2_v, pre_v, dp_v,
-     send_sems, recv_sems, load_sems, sem, sem_w, sem_o, ship_sent, ship_got) = refs[29:]
+     send_sems, recv_sems, load_sems, sem, sem_w, sem_o) = refs[29:]
     me = my_place()
     other = moved(me, 'k', 1)
     k, k2 = me['k'], 1 - me['k']
@@ -687,7 +696,8 @@
     half_at = pl.ds(pl.multiple_of(k * 512, 512), 512)
     half_to = pl.ds(pl.multiple_of(k2 * 512, 512), 512)
     swaps = {'act1': (act.at[1, k2], x_act.at[1]), 'act0': (act.at[0, k2], x_act.at[0]), 'vin1': (vin.at[1, k2], x_vin.at[1]),
-             'vin0': (vin.at[0, k2], x_vin.at[0]), 'pat': (pat.at[k2], x_pat), 'dout1': (do_v, x_dout.at[1]), 'dout0': (do_v, x_dout.at[0]), 'dres': (do_v, x_dres),
+             'vin0': (vin.at[0, k2], x_vin.at[0]), 'pat': (pat.at[k2], x_pat), 'dpre1': (dpre.at[1], x_dpre.at[1]), 'dpre0': (dpre.at[0], x_dpre.at[0]),
+             'dout1': (do_v, x_dout.at[1]), 'dout0': (do_v, x_dout.at[0]), 'dres': (do_v, x_dres),
              'hl': (hl.at[:, half_to], x_hl), 'hr': (hr, x_hr)}
 
     def swap(*names):
@@ -699,15 +709,6 @@
         for name in busy.pop(key, ()):
             net.copy(name).wait_send()
             net.done.add(name)
-
-    def ship(l, i, slot):
-        part = pl.ds(pl.multiple_of(i * BLK, BLK), BLK)
-        return pltpu.make_async_remote_copy(src_ref=dp_v.at[slot], dst_ref=x_dpre.at[l, :, part], send_sem=ship_sent.at[slot],
-                                            recv_sem=ship_got.at[l], device_id=partner, device_id_type=MESH)
-
-    def shipped(l):
-        pltpu.make_async_remote_copy(src_ref=dpre.at[l], dst_ref=x_dpre.at[l], send_sem=ship_sent.at[0],
-                                     recv_sem=ship_got.at[l], device_id=partner, device_id_type=MESH).wait_recv()
 
     def loads(g):
         l = g // 2
@@ -902,8 +903,6 @@
     def step(which, stage):
         if stage == 'L':
             net.arrived(*NEEDS[which])
-            if which in (0, 2):
-                shipped(which // 2)
             for copy in loads(which):
                 copy.start()
         else:
@@ -972,15 +971,11 @@
         def channel(i, slot):
             run(i)
 
-            @pl.when(i >= 2)
-            def _():
-                ship(l, i - 2, slot).wait_send()
             for n in range(2):
                 cols = slice(256 * n, 256 * n + 256)
                 d = dot_nt(do_v[...], w2_v[slot, 2 * n:2 * n + 2].reshape(256, CH)) * pre_v[slot, :, cols]
                 gbch1[l:l + 1, pl.ds(pl.multiple_of(i * BLK + 256 * n, 256), 256)] = jnp.sum(d, axis=0, keepdims=True)
                 dp_v[slot, :, cols] = d.astype(bf16)
-            ship(l, i, slot).start()
 
             @pl.when(i == 0)
             def _():
@@ -989,8 +984,7 @@
                 cols = slice(512 * n, 512 * n + 512)
                 dv_v[:, cols] += dot_nt(dp_v[slot], w1_v[slot, n].reshape(512, BLK))
         for_blocks(Stream(sem_w, blocks, NBLK), channel, Stream(sem_o, outs, NBLK))
-        for slot in range(2):
-            ship(l, NBLK - 2 + slot, slot).wait_send()
+        swap(f'dpre{l}')
         burst(f'l{l}')
         load.wait()
 
@@ -1111,7 +1105,7 @@
                         V((IMG, CH), bf16), V((16, CH), f32), V((2, CHH), f32), V((CH // 128, XROWS, 128), f32),
                         V((CH // 128, XROWS, 128), f32), V((ROWS, CH), f32), V((ROWS, CH), bf16), V((2, 2, 4, 4, 32, BLK), bf16),
                         V((2, 4, 4, 32, CH), bf16), V((2, ROWS, BLK), f32), V((2, ROWS, BLK), bf16), DMA((BACK_COPIES,)), DMA((BACK_COPIES,)), DMA((4,)), DMA((2,)), DMA((2, 3)),
-                        DMA((2, 1)), DMA((2,)), DMA((2,))],
+                        DMA((2, 1))],
         compiler_params=pltpu.CompilerParams(collective_id=1, has_side_effects=True, vmem_limit_bytes=64 * 1024 * 1024 - 65536),
         cost_estimate=pl.CostEstimate(flops=120_000_000_000, bytes_accessed=200_000_000, transcendentals=0),
     )(*operands)

time: 325 us -> 311 us (0.957)
  Pallas kernels: 319 us -> 305 us
    pallas_call x1, Pallas kernels: 187 us -> 175 us  [back(): pl.pallas_call(back_kernel, name='back', in_specs=[a] * 7 + [v] * 8, out_...]
where the time goes in v12:
time: 311 us; the launch traced here: 306 us
  Pallas kernels  305 us (98%)
    pallas_call x1, Pallas kernels, back(): pl.pallas_call(back_kernel, name='back', in_specs=[a] * 7 + [v] * 8, out_...  175 us
    pallas_call x1, Pallas kernels, front(): pl.pallas_call(front_kernel, name='front', in_specs=[pl.BlockSpec(memory_...  125 us

profile of v12, /device:TPU:0, one launch (start us, length us, event | category | flops | bytes accessed | tf_op | source)
XLA Modules:
  0.0 306.3 jit_solution(13809045841445742032)
XLA Ops:
  0.7 125.5 %front.1 = (bf16[4,4,2,4,4,32,1024]{6,5,4,3,2,1,0:T(8,128)(2,1)}, bf16[2,392,1536]{2,1,0:T(8,128)(2,1)}, f32[2,8,392,128]{3,2,1,0:T(8,128)}, f32[2,8,392,128]{3,...) custom-call(s32[32]{0:T(128)} %labels.1, ...), custom_call_target="tpu_custom_call" | custom-call | flops 89999998976 | bytes 180000000 | tf_op jit(solution)/shard_map/front/pallas_call | solution.py:548
  126.1 175.1 %back.1 = (f32[4,32,1024]{2,1,0:T(8,128)}, f32[96,256]{1,0:T(8,128)}, f32[32,256]{1,0:T(8,128)}, f32[8,128]{1,0:T(8,128)}, f32[4,16,128]{2,1,0:T(8,128)}, /*inde...) custom-call(f32[2,8,392,128]{3,2,1,0:T(8,128)} %get-tuple-element.56, ...), custom_call_target="tpu_custom_call" | custom-call | flops 120000004096 | bytes 200000000 | tf_op jit(solution)/shard_map/back/pallas_call | solution.py:1097
  301.2 4.6 %finish.1 = (f32[1,1]{1,0:T(1,128)}, f32[96,256]{1,0:T(8,128)}, f32[8]{0:T(128)}, f32[2,8]{1,0:T(2,128)}, f32[2,8]{1,0:T(2,128)}, /*index=5*/f32[2,16,49]{2,1,0:...) custom-call(f32[4,32,1024]{2,1,0:T(8,128)} %get-tuple-element.71.c, ...), custom_call_target="tpu_custom_call" | custom-call | tf_op jit(solution)/shard_map/finish/pallas_call | solution.py:1147

commit v13 on v12

--- a/solution.py
+++ b/solution.py
@@ -34,7 +34,6 @@
 TOK, TPAD = 49, 56
 IMG = 8
 ROWS, XROWS = IMG * TOK, IMG * TPAD
-CHUNKS = ((0, 112), (112, 112), (224, 112), (336, 56))
 CH, TOKH, CHH = 1024, 512, 4096
 BLK = 512
 NBLK = CHH // BLK
@@ -474,9 +473,11 @@
         save_mid.start()
         burst(f'ln{l}')
 
-        for at, size in CHUNKS:
-            std, _ = standardize(get(x_v, pl.ds(at, size)))
-            v_v[pl.ds(at, size), :] = (std * vec[r + 2:r + 3, :] + vec[r + 3:r + 4, :]).astype(bf16)
+        @pl.loop(0, ROWS // TPAD)
+        def _(n):
+            rows = pl.ds(pl.multiple_of(n * TPAD, 8), TPAD)
+            std, _ = standardize(get(x_v, rows))
+            v_v[rows, :] = (std * vec[r + 2:r + 3, :] + vec[r + 3:r + 4, :]).astype(bf16)
         save_v = [pltpu.make_async_copy(v_v.at[:, pl.ds(512 * n, 512)], vout.at[l, n], sem_x.at[1 + n]) for n in range(2)]
         for copy in save_v:
             copy.start()
@@ -724,17 +725,30 @@
                     pltpu.make_async_copy(far, buf.at[1, :, pl.ds(0, cols)], load_sems.at[2 * n + 1])]
         return out
 
+    def shares(g, t, h, c0, n):
+        if g % 2:
+            rows, cols = pl.ds(pl.multiple_of(t * 512 + h * 256, 256), 256), slice(c0, c0 + n)
+            prod = sum(dot_tn(big[s, :, rows], little[s, :, cols]) for s in range(2))
+        else:
+            rows, cols = slice(256 * h, 256 * h + 256), pl.ds(pl.multiple_of(t * 1024 + c0, 128), n)
+            prod = sum(dot_tn(little[s, :, rows], big[s, :, cols]) for s in range(2))
+        return prod.astype(bf16).reshape(2, 4, 32, n)
+
     def product(u):
         g, c, slot = u.g, u.c, u.slot
         first = c == 2
         if first and g != HEAD:
             for copy in loads(g):
                 copy.wait()
-        if g == STEM and not first:
+        if g == STEM and not first or g < N_CH and c == 1:
             return
-        for v in (units if g == STEM else (u,)):
-            if v.g == g:
-                free(('C', v.c, v.slot))
+        slot1 = 0
+        for v in units:
+            if v.g == g and (v is u or g == STEM or c == 0):
+                if v.c < 2 or v is u or g == STEM:
+                    free(('C', v.c, v.slot))
+                if v.c == 1:
+                    slot1 = v.slot
         if g == HEAD:
             net.arrived(*NEEDS[g])
             for t in range(4):
@@ -754,20 +768,25 @@
                     prod = prod.astype(bf16).reshape(4, 3, 32, 256)
                     for d in range(3):
                         per[d]['C'][slots[d], t, z, :, :, pl.ds(0, 256)] = prod[:, d]
-        else:
+        elif c == 2:
             c0, n = COLS[c]
 
             @pl.loop(0, 4)
             def _(t):
                 for h in range(2):
-                    if g % 2:
-                        left = pl.ds(pl.multiple_of(t * 512 + h * 256, 256), 256)
-                        prod = dot_tn(big[0, :, left], little[0, :, c0:c0 + n]) + dot_tn(big[1, :, left], little[1, :, c0:c0 + n])
-                    else:
-                        right = pl.ds(pl.multiple_of(t * 1024 + c0, 128), n)
-                        rows = slice(256 * h, 256 * h + 256)
-                        prod = dot_tn(little[0, :, rows], big[0, :, right]) + dot_tn(little[1, :, rows], big[1, :, right])
-                    per[c]['C'][slot, t, 2 * h:2 * h + 2] = prod.astype(bf16).reshape(2, 4, 32, n)
+                    per[c]['C'][slot, t, 2 * h:2 * h + 2] = shares(g, t, h, c0, n)
+        elif c == 0:
+
+            @pl.loop(0, 4)
+            def _(t):
+                for h in range(2):
+                    at = slice(2 * h, 2 * h + 2)
+                    prods = [shares(g, t, h, 256 * m, 256) for m in range(3)]
+                    left, right = per[0]['C'], per[1]['C']
+                    left[slot, t, at, :, :, pl.ds(0, 256)] = prods[0]
+                    left[slot, t, at, :, :, pl.ds(256, 128)] = prods[1][..., 0:128]
+                    right[slot1, t, at, :, :, pl.ds(0, 128)] = prods[1][..., 128:256]
+                    right[slot1, t, at, :, :, pl.ds(128, 256)] = prods[2]
 
     class Unit:
         def __init__(self, g, c):
@@ -936,16 +955,21 @@
     def add(row, value):
         gvec[row:row + 1, :] += jnp.sum(value, axis=0, keepdims=True)
 
+    def cast_out(row):
+        @pl.loop(0, ROWS // TPAD)
+        def _(n):
+            rows = pl.ds(pl.multiple_of(n * TPAD, 8), TPAD)
+            d = get(d_v, rows)
+            add(row, d)
+            do_v[rows, :] = d.astype(bf16)
+
     def add_token(n, value, start=0):
         tk[n, :, :, :, :, pl.ds(start, value.shape[1])] += value.reshape(4, 4, 2, 16, value.shape[1])
 
     for l in (1, 0):
         r = 1 + 5 * l
         free('do')
-        for at, size in CHUNKS:
-            d = get(d_v, pl.ds(at, size))
-            add(r + 4, d)
-            do_v[pl.ds(at, size), :] = d.astype(bf16)
+        cast_out(r + 4)
         keep = pltpu.make_async_copy(do_v, dout.at[l], sem.at[1])
         keep.start()
         if l == 1:
@@ -1030,10 +1054,7 @@
 
     burst('fin')
     free('do')
-    for at, size in CHUNKS:
-        d = get(d_v, pl.ds(at, size))
-        add(0, d)
-        do_v[pl.ds(at, size), :] = d.astype(bf16)
+    cast_out(0)
     keep = pltpu.make_async_copy(do_v, dres, sem.at[1])
     keep.start()
     swap('dres')
@@ -1054,14 +1075,19 @@
             put_small(('sm', 0), b['sm'].at[:, :, :, k2], b['sm1'], partner)
             put_small(('tk', 0), b['tk'].at[:, :, :, k2], b['tk1'], partner)
         elif n == 1:
-            b['sm1'][...] += b['sm'][:, :, :, k]
-            b['tk1'][...] += b['tk'][:, :, :, k]
+            @pl.loop(0, 4)
+            def _(i):
+                b['sm1'][i] += b['sm'][i, :, :, k]
+                b['tk1'][i] += b['tk'][i, :, :, k]
             for s in (1, 2, 3):
                 put_small(('sm', 1, s), b['sm1'].at[ring['x'][s]], b['sm2'].at[s - 1], peers['x', s])
                 put_small(('tk', 1, s), b['tk1'].at[:, ring['z'][s]], b['tk2'].at[s - 1], peers['z', s])
         elif n == 2:
             b['sm_s1'][...] = b['sm1'][x] + b['sm2'][0] + b['sm2'][1] + b['sm2'][2]
-            b['tk_s1'][...] = b['tk1'][:, z] + b['tk2'][0] + b['tk2'][1] + b['tk2'][2]
+
+            @pl.loop(0, 4)
+            def _(i):
+                b['tk_s1'][i] = b['tk1'][i, z] + b['tk2'][0, i] + b['tk2'][1, i] + b['tk2'][2, i]
             for s in (1, 2, 3):
                 put_small(('sm', 2, s), b['sm_s1'].at[ring['z'][s]], b['sm3'].at[s - 1], peers['z', s])
                 put_small(('tk', 2, s), b['tk_s1'].at[:, ring['y'][s]], b['tk3'].at[s - 1], peers['y', s])
@@ -1113,15 +1139,13 @@
 
 def finish_kernel(c, stem, head, sm, tk, loss, o_stem, o_bstem, o_ln1g, o_ln1b, o_wt1, o_bt1, o_wt2, o_ln2g, o_ln2b, o_ch1,
                   o_bch1, o_ch2, o_bch2, o_lnfg, o_lnfb, o_head, o_bhead):
-    def core_last(value, pick):
-        got = dot_nt(jnp.concatenate(three_parts(value), axis=0), pick)
-        n = value.shape[0]
-        return got[0:n] + got[n:2 * n] + got[2 * n:3 * n]
-    pick = core_first(1024, 1024, 32)
+    def core_last(value):
+        half = value.shape[1] // 2
+        return jnp.concatenate([value[:, k * half + a:k * half + a + 32] for a in range(0, half, 32) for k in range(2)], axis=1)
     for l in range(2):
-        o_ch1[l] = core_last(c[2 * l], pick)
-        o_ch2[l] = core_last(c[2 * l + 1], pick)
-    o_stem[...] = core_last(stem[...], core_first(256, 256, 32))
+        o_ch1[l] = core_last(c[2 * l])
+        o_ch2[l] = core_last(c[2 * l + 1])
+    o_stem[...] = core_last(stem[...])
     o_head[...] = head[:, 0:250]
     own = sm[...]
     turned = jnp.concatenate([own, jnp.zeros((120, 128), f32)], axis=0).T

time: 311 us -> 310 us (level); the launches traced: 306 us -> 309 us
    pallas_call x1, Pallas kernels: 175 us -> 178 us  [back(): pl.pallas_call(back_kernel, name='back', in_specs=[a] * 7 + [v] * 8, out_...]
where the time goes in v13:
time: 310 us; the launch traced here: 309 us
  Pallas kernels  308 us (99%)
    pallas_call x1, Pallas kernels, back(): pl.pallas_call(back_kernel, name='back', in_specs=[a] * 7 + [v] * 8, out_...  178 us
    pallas_call x1, Pallas kernels, front(): pl.pallas_call(front_kernel, name='front', in_specs=[pl.BlockSpec(memory_...  127 us

profile of v13, /device:TPU:0, one launch (start us, length us, event | category | flops | bytes accessed | tf_op | source)
XLA Modules:
  0.0 308.6 jit_solution(4582058313526657165)
XLA Ops:
  0.7 126.7 %front.1 = (bf16[4,4,2,4,4,32,1024]{6,5,4,3,2,1,0:T(8,128)(2,1)}, bf16[2,392,1536]{2,1,0:T(8,128)(2,1)}, f32[2,8,392,128]{3,2,1,0:T(8,128)}, f32[2,8,392,128]{3,...) custom-call(s32[32]{0:T(128)} %labels.1, ...), custom_call_target="tpu_custom_call" | custom-call | flops 89999998976 | bytes 180000000 | tf_op jit(solution)/shard_map/front/pallas_call | solution.py:549
  127.4 178.5 %back.1 = (f32[4,32,1024]{2,1,0:T(8,128)}, f32[96,256]{1,0:T(8,128)}, f32[32,256]{1,0:T(8,128)}, f32[8,128]{1,0:T(8,128)}, f32[4,16,128]{2,1,0:T(8,128)}, /*inde...) custom-call(f32[2,8,392,128]{3,2,1,0:T(8,128)} %get-tuple-element.56, ...), custom_call_target="tpu_custom_call" | custom-call | flops 120000004096 | bytes 200000000 | tf_op jit(solution)/shard_map/back/pallas_call | solution.py:1123
  305.9 2.5 finish.1

commit v14 on v13

--- a/solution.py
+++ b/solution.py
@@ -473,11 +473,14 @@
         save_mid.start()
         burst(f'ln{l}')
 
-        @pl.loop(0, ROWS // TPAD)
-        def _(n):
-            rows = pl.ds(pl.multiple_of(n * TPAD, 8), TPAD)
+        def norm_rows(rows):
             std, _ = standardize(get(x_v, rows))
             v_v[rows, :] = (std * vec[r + 2:r + 3, :] + vec[r + 3:r + 4, :]).astype(bf16)
+
+        @pl.loop(0, ROWS // (2 * TPAD))
+        def _(n):
+            norm_rows(pl.ds(pl.multiple_of(n * 2 * TPAD, 16), 2 * TPAD))
+        norm_rows(pl.ds(ROWS // (2 * TPAD) * 2 * TPAD, TPAD))
         save_v = [pltpu.make_async_copy(v_v.at[:, pl.ds(512 * n, 512)], vout.at[l, n], sem_x.at[1 + n]) for n in range(2)]
         for copy in save_v:
             copy.start()
@@ -504,7 +507,10 @@
             act_v[slot] = value.astype(bf16)
             add_rows(x_v, dot_nn(act_v[slot], w2_v[slot].reshape(BLK, CH)))
         for_blocks(Stream(sem_w, blocks, NBLK), channel, Stream(sem_o, outs, NBLK))
-        add_rows(x_v, jnp.broadcast_to(vec[r + 4:r + 5, :], (ROWS, CH)))
+
+        @pl.loop(0, CH // 128)
+        def _(n):
+            x_v[n, pl.ds(0, ROWS), :] += vec[r + 4:r + 5, pl.ds(pl.multiple_of(128 * n, 128), 128)]
         for copy in (save_in, *save_v):
             copy.wait()
 
@@ -639,16 +645,16 @@
 
 
 def small_pack(b, flat, turn, gvec, hstat, gbch1, gbh):
-    for n in range(8):
-        cols = pl.ds(128 * n, 128)
+    @pl.loop(0, 8)
+    def _(n):
+        cols = pl.ds(pl.multiple_of(128 * n, 128), 128)
         turn[n, pl.ds(0, 128), :] = jnp.zeros((128, 128), f32)
         turn[n, pl.ds(0, 16), :] = gvec[:, cols]
         turn[n, pl.ds(11, 2), :] = hstat[pl.ds(0, 2), cols]
-    for n in range(8):
         tile = turn[n, pl.ds(0, 128), :].T
         for i in range(4):
-            a = n % 4 * 4 + i
-            flat[a // 2, pl.ds(a % 2 * 64 + n // 4 * 32, 32), :] = tile[32 * i:32 * i + 32]
+            row = pl.multiple_of(i % 2 * 64 + n // 4 * 32, 32)
+            flat[n % 4 * 2 + i // 2, pl.ds(row, 32), :] = tile[32 * i:32 * i + 32]
     for l in range(2):
         def gather(n, total):
             lane = lax.broadcasted_iota(jnp.int32, (128, 512), 0)
@@ -725,30 +731,17 @@
                     pltpu.make_async_copy(far, buf.at[1, :, pl.ds(0, cols)], load_sems.at[2 * n + 1])]
         return out
 
-    def shares(g, t, h, c0, n):
-        if g % 2:
-            rows, cols = pl.ds(pl.multiple_of(t * 512 + h * 256, 256), 256), slice(c0, c0 + n)
-            prod = sum(dot_tn(big[s, :, rows], little[s, :, cols]) for s in range(2))
-        else:
-            rows, cols = slice(256 * h, 256 * h + 256), pl.ds(pl.multiple_of(t * 1024 + c0, 128), n)
-            prod = sum(dot_tn(little[s, :, rows], big[s, :, cols]) for s in range(2))
-        return prod.astype(bf16).reshape(2, 4, 32, n)
-
     def product(u):
         g, c, slot = u.g, u.c, u.slot
         first = c == 2
         if first and g != HEAD:
             for copy in loads(g):
                 copy.wait()
-        if g == STEM and not first or g < N_CH and c == 1:
+        if g == STEM and not first:
             return
-        slot1 = 0
-        for v in units:
-            if v.g == g and (v is u or g == STEM or c == 0):
-                if v.c < 2 or v is u or g == STEM:
-                    free(('C', v.c, v.slot))
-                if v.c == 1:
-                    slot1 = v.slot
+        for v in (units if g == STEM else (u,)):
+            if v.g == g:
+                free(('C', v.c, v.slot))
         if g == HEAD:
             net.arrived(*NEEDS[g])
             for t in range(4):
@@ -768,25 +761,20 @@
                     prod = prod.astype(bf16).reshape(4, 3, 32, 256)
                     for d in range(3):
                         per[d]['C'][slots[d], t, z, :, :, pl.ds(0, 256)] = prod[:, d]
-        elif c == 2:
+        else:
             c0, n = COLS[c]
 
             @pl.loop(0, 4)
             def _(t):
                 for h in range(2):
-                    per[c]['C'][slot, t, 2 * h:2 * h + 2] = shares(g, t, h, c0, n)
-        elif c == 0:
-
-            @pl.loop(0, 4)
-            def _(t):
-                for h in range(2):
-                    at = slice(2 * h, 2 * h + 2)
-                    prods = [shares(g, t, h, 256 * m, 256) for m in range(3)]
-                    left, right = per[0]['C'], per[1]['C']
-                    left[slot, t, at, :, :, pl.ds(0, 256)] = prods[0]
-                    left[slot, t, at, :, :, pl.ds(256, 128)] = prods[1][..., 0:128]
-                    right[slot1, t, at, :, :, pl.ds(0, 128)] = prods[1][..., 128:256]
-                    right[slot1, t, at, :, :, pl.ds(128, 256)] = prods[2]
+                    if g % 2:
+                        left = pl.ds(pl.multiple_of(t * 512 + h * 256, 256), 256)
+                        prod = dot_tn(big[0, :, left], little[0, :, c0:c0 + n]) + dot_tn(big[1, :, left], little[1, :, c0:c0 + n])
+                    else:
+                        right = pl.ds(pl.multiple_of(t * 1024 + c0, 128), n)
+                        rows = slice(256 * h, 256 * h + 256)
+                        prod = dot_tn(little[0, :, rows], big[0, :, right]) + dot_tn(little[1, :, rows], big[1, :, right])
+                    per[c]['C'][slot, t, 2 * h:2 * h + 2] = prod.astype(bf16).reshape(2, 4, 32, n)
 
     class Unit:
         def __init__(self, g, c):

time: 310 us -> 306 us (0.987)
  Pallas kernels: 308 us -> 304 us
where the time goes in v14:
time: 306 us; the launch traced here: 305 us
  Pallas kernels  304 us (99%)
    pallas_call x1, Pallas kernels, back(): pl.pallas_call(back_kernel, name='back', in_specs=[a] * 7 + [v] * 8, out_...  176 us
    pallas_call x1, Pallas kernels, front(): pl.pallas_call(front_kernel, name='front', in_specs=[pl.BlockSpec(memory_...  126 us

profile of v14, /device:TPU:0, one launch (start us, length us, event | category | flops | bytes accessed | tf_op | source)
XLA Modules:
  0.0 304.6 jit_solution(267746968038103164)
XLA Ops:
  0.7 125.7 %front.1 = (bf16[4,4,2,4,4,32,1024]{6,5,4,3,2,1,0:T(8,128)(2,1)}, bf16[2,392,1536]{2,1,0:T(8,128)(2,1)}, f32[2,8,392,128]{3,2,1,0:T(8,128)}, f32[2,8,392,128]{3,...) custom-call(s32[32]{0:T(128)} %labels.1, ...), custom_call_target="tpu_custom_call" | custom-call | flops 89999998976 | bytes 180000000 | tf_op jit(solution)/shard_map/front/pallas_call | solution.py:555
  126.3 175.6 %back.1 = (f32[4,32,1024]{2,1,0:T(8,128)}, f32[96,256]{1,0:T(8,128)}, f32[32,256]{1,0:T(8,128)}, f32[8,128]{1,0:T(8,128)}, f32[4,16,128]{2,1,0:T(8,128)}, /*inde...) custom-call(f32[2,8,392,128]{3,2,1,0:T(8,128)} %get-tuple-element.56, ...), custom_call_target="tpu_custom_call" | custom-call | flops 120000004096 | bytes 200000000 | tf_op jit(solution)/shard_map/back/pallas_call | solution.py:1111
  301.9 2.5 finish.1
